TPU v7x, 8 devices: a whole 2x2x1 slice. The times are simulated.
8 devices in a mesh: tp: 2 (over z, y), cp: 4 (over x, core).
Axes of the slice: x: 2, y: 2, z: 1, core: 2. Of those that a mesh axis runs over, the one named last changes fastest.
Arguments:
- hidden: bfloat16 [2048, 4608], P('cp')
- g_pre: float32 [4608], replicated
- w_q: bfloat16 [4608, 32, 128], P(None, 'tp')
- w_k: bfloat16 [4608, 16, 128], P(None, 'tp')
- w_v: bfloat16 [4608, 16, 128], P(None, 'tp')
- w_o: bfloat16 [32, 128, 4608], P('tp')
- g_post: float32 [4608], replicated
- d_out: bfloat16 [2048, 4608], P('cp')
Outputs:
- output 1: bfloat16 [2048, 4608], P('cp')
- output 2: bfloat16 [2048, 4608], P('cp')
- output 3: float32 [4608], replicated
- output 4: float32 [4608, 32, 128], P(None, 'tp')
- output 5: float32 [4608, 16, 128], P(None, 'tp')
- output 6: float32 [4608, 16, 128], P(None, 'tp')
- output 7: float32 [32, 128, 4608], P('tp')
- output 8: float32 [4608], replicated
All inputs are finite; a program needn't handle non-finite values.
Results may differ from a plain program's by a relative error of at most 0.0176177.
Values are sent between devices in bfloat16 or wider.
A program may use at most 1 GiB of HBM per device.

v0:
```python
import jax
import jax.numpy as jnp
from jax import lax
from jax.sharding import PartitionSpec as P

SOFT_CAP = 30.0
NORM_EPS = 1e-5
ROPE_THETA = 10000.0
MASK_FILL = -1e30


def rms_norm_fwd(x_val):
    inv_rms = lax.rsqrt(jnp.mean(x_val * x_val, axis=-1, keepdims=True) + NORM_EPS)
    return x_val * inv_rms, inv_rms


def rms_norm_bwd(grad_hat, x_hat, inv_rms):
    return inv_rms * (grad_hat - x_hat * jnp.mean(grad_hat * x_hat, axis=-1, keepdims=True))


def rope_tables(start, length, head_dim):
    half_dim = head_dim // 2
    inv_freq = ROPE_THETA ** (-jnp.arange(half_dim, dtype=jnp.float32) * 2.0 / head_dim)
    positions = (start + jnp.arange(length)).astype(jnp.float32)
    rot_angle = positions[:, None] * inv_freq[None, :]
    return jnp.cos(rot_angle)[:, None, :], jnp.sin(rot_angle)[:, None, :]


def rope_apply(x_val, cos_t, sin_t):
    half_dim = x_val.shape[-1] // 2
    x_lo = x_val[..., :half_dim]
    x_hi = x_val[..., half_dim:]
    return jnp.concatenate([x_lo * cos_t - x_hi * sin_t, x_hi * cos_t + x_lo * sin_t], axis=-1)


def rope_grad(g_val, cos_t, sin_t):
    half_dim = g_val.shape[-1] // 2
    g_lo = g_val[..., :half_dim]
    g_hi = g_val[..., half_dim:]
    return jnp.concatenate([g_lo * cos_t + g_hi * sin_t, g_hi * cos_t - g_lo * sin_t], axis=-1)


def solution(mesh):
    cp_size = mesh.shape['cp']
    shift_perm = [(src_idx, (src_idx + 1) % cp_size) for src_idx in range(cp_size)]

    def device_fn(hidden, g_pre, w_q, w_k, w_v, w_o, g_post, d_out):
        tokens = hidden.shape[0]
        heads_local, head_dim = w_q.shape[1], w_q.shape[2]
        kv_local = w_k.shape[1]
        groups = heads_local // kv_local
        attn_scale = head_dim ** -0.5
        cp_rank = lax.axis_index('cp')
        cos_t, sin_t = rope_tables(cp_rank * tokens, tokens, head_dim)
        local_pos = jnp.arange(tokens)
        query_pos = cp_rank * tokens + local_pos

        h_f32 = hidden.astype(jnp.float32)
        a_hat, inv_pre = rms_norm_fwd(h_f32)
        a_act = (a_hat * g_pre).astype(jnp.bfloat16)
        q_rot = rope_apply(jnp.einsum('td,dhe->the', a_act, w_q, preferred_element_type=jnp.float32), cos_t, sin_t).astype(jnp.bfloat16)
        k_rot = rope_apply(jnp.einsum('td,dhe->the', a_act, w_k, preferred_element_type=jnp.float32), cos_t, sin_t).astype(jnp.bfloat16)
        v_val = jnp.einsum('td,dhe->the', a_act, w_v, preferred_element_type=jnp.float32).astype(jnp.bfloat16)
        q_grp = q_rot.reshape(tokens, kv_local, groups, head_dim)
        wo_grp = w_o.reshape(kv_local, groups, head_dim, w_o.shape[2])

        def block_mask(step_idx):
            key_pos = ((cp_rank - step_idx) % cp_size) * tokens + local_pos
            return (query_pos[:, None] >= key_pos[None, :])[None, None]

        def capped_scores(k_blk):
            logits = jnp.einsum('qhge,khe->hgqk', q_grp, k_blk, preferred_element_type=jnp.float32) * attn_scale
            tanh_val = jnp.tanh(logits / SOFT_CAP)
            return SOFT_CAP * tanh_val, tanh_val

        run_max = jnp.full((kv_local, groups, tokens), MASK_FILL, jnp.float32)
        run_sum = jnp.zeros((kv_local, groups, tokens), jnp.float32)
        run_acc = jnp.zeros((kv_local, groups, tokens, head_dim), jnp.float32)
        k_blk, v_blk = k_rot, v_val
        for step_idx in range(cp_size):
            if step_idx > 0:
                k_blk, v_blk = lax.ppermute((k_blk, v_blk), 'cp', shift_perm)
            visible = block_mask(step_idx)
            capped = jnp.where(visible, capped_scores(k_blk)[0], MASK_FILL)
            new_max = jnp.maximum(run_max, capped.max(axis=-1))
            rescale = jnp.exp(run_max - new_max)
            attn_prob = jnp.where(visible, jnp.exp(capped - new_max[..., None]), 0.0)
            run_sum = run_sum * rescale + attn_prob.sum(axis=-1)
            run_acc = run_acc * rescale[..., None] + jnp.einsum('hgqk,khe->hgqe', attn_prob.astype(jnp.bfloat16), v_blk, preferred_element_type=jnp.float32)
            run_max = new_max
        ctx = (run_acc / run_sum[..., None]).astype(jnp.bfloat16)
        log_norm = run_max + jnp.log(run_sum)

        o_part = jnp.einsum('hgqe,hged->qd', ctx, wo_grp, preferred_element_type=jnp.float32)
        o_sum = lax.psum(o_part.astype(jnp.bfloat16), 'tp').astype(jnp.float32)
        o_hat, inv_post = rms_norm_fwd(o_sum)
        y_blk = (h_f32 + o_hat * g_post).astype(jnp.bfloat16)

        g_out = d_out.astype(jnp.float32)
        grad_gpost = jnp.sum(g_out * o_hat, axis=0)
        grad_o = rms_norm_bwd(g_out * g_post, o_hat, inv_post).astype(jnp.bfloat16)
        grad_wo = jnp.einsum('hgqe,qd->hged', ctx, grad_o, preferred_element_type=jnp.float32).reshape(w_o.shape)
        grad_ctx = jnp.einsum('qd,hged->hgqe', grad_o, wo_grp, preferred_element_type=jnp.float32).astype(jnp.bfloat16)
        row_dot = jnp.einsum('hgqe,hgqe->hgq', grad_ctx, ctx, preferred_element_type=jnp.float32)

        k_blk, v_blk = k_rot, v_val
        grad_k = jnp.zeros((tokens, kv_local, head_dim), jnp.float32)
        grad_v = jnp.zeros((tokens, kv_local, head_dim), jnp.float32)
        grad_q = jnp.zeros((tokens, kv_local, groups, head_dim), jnp.float32)
        for step_idx in range(cp_size):
            if step_idx > 0:
                k_blk, v_blk, grad_k, grad_v = lax.ppermute((k_blk, v_blk, grad_k, grad_v), 'cp', shift_perm)
            visible = block_mask(step_idx)
            capped, tanh_val = capped_scores(k_blk)
            attn_prob = jnp.where(visible, jnp.exp(capped - log_norm[..., None]), 0.0)
            grad_v = grad_v + jnp.einsum('hgqk,hgqe->khe', attn_prob.astype(jnp.bfloat16), grad_ctx, preferred_element_type=jnp.float32)
            grad_p = jnp.einsum('hgqe,khe->hgqk', grad_ctx, v_blk, preferred_element_type=jnp.float32)
            grad_l = (attn_prob * (grad_p - row_dot[..., None]) * (1.0 - tanh_val * tanh_val) * attn_scale).astype(jnp.bfloat16)
            grad_q = grad_q + jnp.einsum('hgqk,khe->qhge', grad_l, k_blk, preferred_element_type=jnp.float32)
            grad_k = grad_k + jnp.einsum('hgqk,qhge->khe', grad_l, q_grp, preferred_element_type=jnp.float32)
        grad_k, grad_v = lax.ppermute((grad_k, grad_v), 'cp', shift_perm)

        dq_pre = rope_grad(grad_q.reshape(tokens, heads_local, head_dim), cos_t, sin_t).astype(jnp.bfloat16)
        dk_pre = rope_grad(grad_k, cos_t, sin_t).astype(jnp.bfloat16)
        dv_pre = grad_v.astype(jnp.bfloat16)
        grad_wq = jnp.einsum('td,the->dhe', a_act, dq_pre, preferred_element_type=jnp.float32)
        grad_wk = jnp.einsum('td,the->dhe', a_act, dk_pre, preferred_element_type=jnp.float32)
        grad_wv = jnp.einsum('td,the->dhe', a_act, dv_pre, preferred_element_type=jnp.float32)
        grad_a_part = (jnp.einsum('the,dhe->td', dq_pre, w_q, preferred_element_type=jnp.float32) + jnp.einsum('the,dhe->td', dk_pre, w_k, preferred_element_type=jnp.float32) + jnp.einsum('the,dhe->td', dv_pre, w_v, preferred_element_type=jnp.float32))
        grad_a = lax.psum(grad_a_part.astype(jnp.bfloat16), 'tp').astype(jnp.float32)
        grad_gpre = jnp.sum(grad_a * a_hat, axis=0)
        grad_h = (g_out + rms_norm_bwd(grad_a * g_pre, a_hat, inv_pre)).astype(jnp.bfloat16)
        grad_gpre, grad_wq, grad_wk, grad_wv, grad_wo, grad_gpost = lax.psum((grad_gpre, grad_wq, grad_wk, grad_wv, grad_wo, grad_gpost), 'cp')
        return y_blk, grad_h, grad_gpre, grad_wq, grad_wk, grad_wv, grad_wo, grad_gpost

    row_spec = P('cp', None)
    head_spec = P(None, 'tp', None)
    out_head_spec = P('tp', None, None)
    return jax.shard_map(device_fn, mesh=mesh, in_specs=(row_spec, P(), head_spec, head_spec, head_spec, out_head_spec, P(), row_spec), out_specs=(row_spec, row_spec, P(), head_spec, head_spec, head_spec, out_head_spec, P()), check_vma=False)
```

profile of v0, /device:TPU:0, one launch (start us, length us, event | category | flops | bytes accessed | tf_op | source)
XLA Modules:
  0.0 2709.0 jit_solution(14833635467933023066)
XLA Ops:
  10.6 10.6 fusion.121
  22.0 12.8 copy.16
  34.8 9.2 fusion.196
  47.7 23.9 copy.17
  71.6 16.7 fusion.194
  102.1 9.5 fusion.18
  111.7 9.4 fusion.19
  122.8 9.4 fusion.20
  137.0 14.2 fusion.39
  151.2 11.6 fusion.74
  168.2 9.8 fusion.43
  184.2 11.1 fusion.70
  195.2 11.7 fusion.72
  206.9 15.0 divide_convert_fusion
  222.0 15.7 bitcast_convert_fusion
  237.7 113.7 %all-reduce.6.cloned.1.call-done = bf16[512,4608]{1,0:T(8,128)(2,1)} async-done(((bf16[512,4608]{1,0:T(8,128)(2,1)}), bf16[512,4608]{1,0:T(8,128)(2,1)}) %all-reduce.6.cloned.1.call-update) | async-done | bytes 4718608 | tf_op jit(solution)/shard_map/psum | solution.py:95
  354.9 10.7 fusion.58
  365.6 14.4 fusion.100
  380.1 10.8 fusion.112
  390.9 12.6 fusion.9
  409.7 13.8 fusion.5
  423.5 13.8 fusion.3
  437.3 14.2 fusion.7
  451.5 22.8 fusion.187
  483.2 6.8 fusion.138
  502.3 6.9 bitcast_add_fusion.7
  512.1 11.0 bitcast_add_fusion.4
  523.7 10.9 collective-permute-done.7
  538.5 9.5 fusion.62
  548.0 9.1 collective-permute-done.11
  557.6 22.0 collective-permute-done.8
  580.1 16.8 fusion.126
  596.9 9.3 fusion.60
  607.4 17.1 collective-permute-done.9
  626.4 7.7 fusion.150
  636.8 13.8 fusion.59
  650.7 17.8 fusion.97
  668.5 11.4 fusion.93
  679.8 11.5 fusion.95
  691.4 71.8 %all-reduce.8.cloned.1.call-done = bf16[512,4608]{1,0:T(8,128)(2,1)} async-done(((bf16[512,4608]{1,0:T(8,128)(2,1)}), bf16[512,4608]{1,0:T(8,128)(2,1)}) %all-reduce.8.cloned.1.call-update) | async-done | bytes 4718608 | tf_op jit(solution)/shard_map/psum | solution.py:130
  763.2 8.2 fusion.54
  771.4 13.5 all-reduce
  784.9 8.3 fusion.57
  793.2 1809.6 %all-reduce.10.cloned.1.call-done = (f32[4608,16,128]{2,0,1:T(8,128)}, f32[4608,8,128]{2,0,1:T(8,128)}, f32[4608,8,128]{2,0,1:T(8,128)}, f32[16,128,4608]{2,1,0:T(8,128)}) async-done(((f32[4608,16,128]{2,0,1:T(8,128)}, f32[4608,8,128]{2,0,1:T(8,128)}, f32[4608,8,128]{2,0,1:T(8,128)}, f32[16,128,4608]{2,1,0:T(8,128)}), (f32[4608,16,128]{2,0,1:T(8,128)}, f32[4608,8,128]{2,0,1:T(8,128)}, ...) | async-done | bytes 113246224 | tf_op jit(solution)/shard_map/psum | solution.py:133
  2602.8 36.9 %copy.68 = f32[4608,16,128]{2,1,0:T(8,128)} copy(f32[4608,16,128]{2,0,1:T(8,128)} %get-tuple-element.22) | data formatting | bytes 75497472
  2639.7 26.2 copy.69
  2666.0 22.9 copy.70
  2689.0 13.1 copy.167
  (199 shorter events, 84.7 us)
Async XLA Ops:
  7.2 344.2 %all-reduce.6.cloned.1.call-start = ((), (), s32[]{:S(2)}) async-start(), calls=%async_computation | async-start | bytes 9437184 | tf_op jit(solution)/shard_map/psum | solution.py:95
  10.6 61.1 %copy-start.32 = (f32[512]{0:T(512)}, f32[512]{0:T(512)S(1)}, u32[]{:S(2)}) copy-start(f32[512]{0:T(512)S(1)} %add_rsqrt_fusion.1) | copy-start | bytes 6148
  21.2 80.8 %collective-permute-start.1 = (bf16[512,8,128]{2,0,1:T(8,128)(2,1)}, bf16[512,8,128]{2,0,1:T(8,128)(2,1)}, u32[]{:S(2)}, u32[]{:S(2)}) collective-permute-start(bf16[512,8,128]{2,0,1:T(8,128)(2,1)} %fusion.121), channel_id=1, source_target_pairs={{0,1},{1,2},{2,3},{3,0},{4,5},{5,6},{6,7},{7,4}} | collective-permute-start | bytes 3145736 | tf_op jit(solution)/shard_map/ppermute | solution.py:82
  44.6 43.8 %copy-start.11 = (f32[512,64]{0,1:T(8,128)}, f32[512,64]{0,1:T(8,128)S(1)}, u32[]{:S(2)}) copy-start(f32[512,64]{0,1:T(8,128)S(1)} %get-tuple-element.45) | copy-start | bytes 393220
  44.6 43.8 %copy-start.13 = (f32[512,64]{0,1:T(8,128)}, f32[512,64]{0,1:T(8,128)S(1)}, u32[]{:S(2)}) copy-start(f32[512,64]{0,1:T(8,128)S(1)} %get-tuple-element.46) | copy-start | bytes 393220
  45.0 57.1 %copy-start.7 = (bf16[512,8,64]{0,2,1:T(8,128)(2,1)}, bf16[512,8,64]{0,2,1:T(8,128)(2,1)S(1)}, u32[]{:S(2)}) copy-start(bf16[512,8,64]{0,2,1:T(8,128)(2,1)S(1)} %get-tuple-element.41) | copy-start | bytes 1572868
  45.0 57.1 %copy-start.9 = (bf16[512,8,64]{0,2,1:T(8,128)(2,1)}, bf16[512,8,64]{0,2,1:T(8,128)(2,1)S(1)}, u32[]{:S(2)}) copy-start(bf16[512,8,64]{0,2,1:T(8,128)(2,1)S(1)} %get-tuple-element.42) | copy-start | bytes 1572868
  45.1 47.6 %collective-permute-start = (bf16[512,8,128]{0,2,1:T(8,128)(2,1)S(1)}, bf16[512,8,128]{0,2,1:T(8,128)(2,1)}, u32[]{:S(2)}, u32[]{:S(2)}) collective-permute-start(bf16[512,8,128]{0,2,1:T(8,128)(2,1)S(1)} %pad_maximum_fusion.4), channel_id=1, source_target_pairs={{0,1},{1,2},{2,3},{3,0},{4,5},{5,6},{6,7},{7,4}} | collective-permute-start | bytes 3145736 | tf_op jit(solution)/shard_map/ppermute | solution.py:82
  92.6 18.9 collective-permute-start.2
  102.0 30.3 %copy-start = (bf16[512,8,2,128]{3,0,2,1:T(8,128)(2,1)}, bf16[512,8,2,128]{3,0,2,1:T(8,128)(2,1)S(1)}, u32[]{:S(2)}) copy-start(bf16[512,8,2,128]{3,0,2,1:T(8,128)(2,1)S(1)} %pad_maximum_fusion) | copy-start | bytes 6291460
  102.0 19.1 collective-permute-start.3
  111.6 20.6 collective-permute-start.4
  121.1 63.1 %copy-start.34 = (bf16[512,8,128]{2,0,1:T(8,128)(2,1)}, bf16[512,8,128]{2,0,1:T(8,128)(2,1)S(1)}, u32[]{:S(2)}) copy-start(bf16[512,8,128]{2,0,1:T(8,128)(2,1)S(1)} %collective-permute-done.3) | copy-start | bytes 3145732
  121.1 85.8 %collective-permute-start.5 = (bf16[512,8,128]{2,0,1:T(8,128)(2,1)S(1)}, bf16[512,8,128]{2,0,1:T(8,128)(2,1)S(1)}, u32[]{:S(2)}, u32[]{:S(2)}) collective-permute-start(bf16[512,8,128]{2,0,1:T(8,128)(2,1)S(1)} %collective-permute-done.3), channel_id=1, source_target_pairs={{0,1},{1,2},{2,3},{3,0},{4,5},{5,6},{6,7},{7,4}} | collective-permute-start | bytes 3145736 | tf_op jit(solution)/shard_map/ppermute | solution.py:82
  136.9 70.0 %copy-start.6 = (f32[8,512,512,2]{2,1,3,0:T(8,128)}, f32[8,512,512,2]{2,1,3,0:T(8,128)S(1)}, u32[]{:S(2)}) copy-start(f32[8,512,512,2]{2,1,3,0:T(8,128)S(1)} %get-tuple-element.52) | copy-start | bytes 50331652
  221.9 143.6 %copy-start.15 = (bf16[8,2,512,128]{3,2,1,0:T(8,128)(2,1)}, bf16[8,2,512,128]{3,2,1,0:T(8,128)(2,1)S(1)}, u32[]{:S(2)}) copy-start(bf16[8,2,512,128]{3,2,1,0:T(8,128)(2,1)S(1)} %divide_convert_fusion) | copy-start | bytes 6291460
  237.6 117.3 %copy-start.28 = (f32[4608]{0:T(1024)S(1)}, f32[4608]{0:T(1024)}, u32[]{:S(2)}) copy-start(f32[4608]{0:T(1024)} %param.14) | copy-start | bytes 55300
  237.6 128.0 %slice-start.2 = ((s8[4718592]{0:T(1024)(128)(4,1)}), s8[524288]{0:T(1024)(128)(4,1)S(1)}, s32[]{:S(2)}) async-start(s8[4718592]{0:T(1024)(128)(4,1)} %bitcast.326), calls=%async_computation.5 | async-start | bytes 1048576
  237.6 525.6 %all-reduce.8.cloned.1.call-start = ((), (), s32[]{:S(2)}) async-start(), calls=%async_computation.1 | async-start | bytes 9437184 | tf_op jit(solution)/shard_map/psum | solution.py:130
  408.1 94.1 %collective-permute-start.6 = (f32[512,8,128]{0,2,1:T(8,128)}, f32[512,8,128]{0,2,1:T(8,128)}, u32[]{:S(2)}, u32[]{:S(2)}) collective-permute-start(f32[512,8,128]{0,2,1:T(8,128)} %convolution_bitcast_fusion), channel_id=1, source_target_pairs={{0,1},{1,2},{2,3},{3,0},{4,5},{5,6},{6,7},{7,4}} | collective-permute-start | bytes 6291464 | tf_op jit(solution)/shard_map/ppermute | solution.py:112
  408.1 104.0 %collective-permute-start.10 = (f32[512,8,128]{0,2,1:T(8,128)}, f32[512,8,128]{0,2,1:T(8,128)}, u32[]{:S(2)}, u32[]{:S(2)}) collective-permute-start(f32[512,8,128]{0,2,1:T(8,128)} %fusion.112), channel_id=1, source_target_pairs={{0,1},{1,2},{2,3},{3,0},{4,5},{5,6},{6,7},{7,4}} | collective-permute-start | bytes 6291464 | tf_op jit(solution)/shard_map/ppermute | solution.py:112
  509.1 25.5 collective-permute-start.7
  512.1 24.7 copy-start.4
  512.1 24.7 copy-start.12
  512.1 24.7 copy-start.14
  523.1 34.0 %collective-permute-start.11 = (f32[512,8,128]{0,2,1:T(8,128)}, f32[512,8,128]{0,2,1:T(8,128)S(1)}, u32[]{:S(2)}, u32[]{:S(2)}) collective-permute-start(f32[512,8,128]{0,2,1:T(8,128)} %bitcast_add_fusion.4), channel_id=1, source_target_pairs={{0,1},{1,2},{2,3},{3,0},{4,5},{5,6},{6,7},{7,4}} | collective-permute-start | bytes 6291464 | tf_op jit(solution)/shard_map/ppermute | solution.py:112
  536.7 42.9 %collective-permute-start.8 = (f32[512,8,128]{0,2,1:T(8,128)S(1)}, f32[512,8,128]{0,2,1:T(8,128)S(1)}, u32[]{:S(2)}, u32[]{:S(2)}) collective-permute-start(f32[512,8,128]{0,2,1:T(8,128)S(1)} %bitcast_add_fusion.6), channel_id=1, source_target_pairs={{0,1},{1,2},{2,3},{3,0},{4,5},{5,6},{6,7},{7,4}} | collective-permute-start | bytes 6291464 | tf_op jit(solution)/shard_map/ppermute | solution.py:112
  538.5 41.6 %copy-start.22 = (bf16[512,16,64]{0,2,1:T(8,128)(2,1)}, bf16[512,16,64]{0,2,1:T(8,128)(2,1)S(1)}, u32[]{:S(2)}) copy-start(bf16[512,16,64]{0,2,1:T(8,128)(2,1)S(1)} %get-tuple-element.35) | copy-start | bytes 3145732
  548.0 32.1 %copy-start.24 = (bf16[512,16,64]{0,2,1:T(8,128)(2,1)S(1)}, bf16[512,16,64]{0,2,1:T(8,128)(2,1)}, u32[]{:S(2)}) copy-start(bf16[512,16,64]{0,2,1:T(8,128)(2,1)} %get-tuple-element.36) | copy-start | bytes 3145732
  557.6 48.6 %collective-permute-start.12 = (f32[512,8,128]{0,2,1:T(8,128)S(1)}, f32[512,8,128]{0,2,1:T(8,128)S(1)}, u32[]{:S(2)}, u32[]{:S(2)}) collective-permute-start(f32[512,8,128]{0,2,1:T(8,128)S(1)} %bitcast_add_fusion.3), channel_id=1, source_target_pairs={{0,1},{1,2},{2,3},{3,0},{4,5},{5,6},{6,7},{7,4}} | collective-permute-start | bytes 6291464 | tf_op jit(solution)/shard_map/ppermute | solution.py:112
  580.1 44.5 %collective-permute-start.9 = (f32[512,8,128]{0,2,1:T(8,128)S(1)}, f32[512,8,128]{0,2,1:T(8,128)}, u32[]{:S(2)}, u32[]{:S(2)}) collective-permute-start(f32[512,8,128]{0,2,1:T(8,128)S(1)} %bitcast_add_fusion.5), channel_id=1, source_target_pairs={{0,1},{1,2},{2,3},{3,0},{4,5},{5,6},{6,7},{7,4}} | collective-permute-start | bytes 6291464 | tf_op jit(solution)/shard_map/ppermute | solution.py:121
  580.1 46.3 %slice-start.15 = ((s8[9437184]{0:T(1024)(128)(4,1)}), s8[4194304]{0:T(1024)(128)(4,1)S(1)}, s32[]{:S(2)}) async-start(s8[9437184]{0:T(1024)(128)(4,1)} %bitcast.333), calls=%async_computation.18 | async-start | bytes 8388608
  580.1 46.3 %slice-start.16 = ((s8[9437184]{0:T(1024)(128)(4,1)}), s8[4194304]{0:T(1024)(128)(4,1)S(1)}, s32[]{:S(2)}) async-start(s8[9437184]{0:T(1024)(128)(4,1)} %bitcast.333), calls=%async_computation.19 | async-start | bytes 8388608
  596.9 29.5 %slice-start.17 = ((s8[9437184]{0:T(1024)(128)(4,1)}), s8[1048576]{0:T(1024)(128)(4,1)S(1)}, s32[]{:S(2)}) async-start(s8[9437184]{0:T(1024)(128)(4,1)} %bitcast.333), calls=%async_computation.20 | async-start | bytes 2097152
  606.8 29.0 %collective-permute-start.13 = (bf16[512,8,128]{0,2,1:T(8,128)(2,1)S(1)}, bf16[512,8,128]{0,2,1:T(8,128)(2,1)S(1)}, u32[]{:S(2)}, u32[]{:S(2)}) collective-permute-start(bf16[512,8,128]{0,2,1:T(8,128)(2,1)S(1)} %bitcast_add_fusion.2), channel_id=1, source_target_pairs={{0,1},{1,2},{2,3},{3,0},{4,5},{5,6},{6,7},{7,4}} | collective-permute-start | bytes 3145736 | tf_op jit(solution)/shard_map/ppermute | solution.py:121
  650.6 1952.2 %all-reduce.10.cloned.1.call-start = ((), (), s32[]{:S(2)}) async-start(), calls=%async_computation.2 | async-start | bytes 226492416 | tf_op jit(solution)/shard_map/psum | solution.py:133
  650.7 17.8 copy-start.39
  691.4 80.0 %copy-start.29 = (f32[4608]{0:T(1024)S(1)}, f32[4608]{0:T(1024)}, u32[]{:S(2)}) copy-start(f32[4608]{0:T(1024)} %get-tuple-element.16) | copy-start | bytes 55300
  2602.8 36.9 %copy-start.5 = (f32[4608,8,128]{2,0,1:T(8,128)S(1)}, f32[4608,8,128]{2,0,1:T(8,128)}, u32[]{:S(2)}) copy-start(f32[4608,8,128]{2,0,1:T(8,128)} %get-tuple-element.23) | copy-start | bytes 56623108
  2639.7 49.2 %slice-start.6 = ((s8[37748736]{0:T(1024)(128)(4,1)}), s8[4194304]{0:T(1024)(128)(4,1)S(1)}, s32[]{:S(2)}) async-start(s8[37748736]{0:T(1024)(128)(4,1)} %bitcast.330), calls=%async_computation.9 | async-start | bytes 8388608
  2639.7 49.2 %slice-start.7 = ((s8[37748736]{0:T(1024)(128)(4,1)}), s8[4194304]{0:T(1024)(128)(4,1)S(1)}, s32[]{:S(2)}) async-start(s8[37748736]{0:T(1024)(128)(4,1)} %bitcast.330), calls=%async_computation.10 | async-start | bytes 8388608
  2639.7 49.2 %slice-start.8 = ((s8[37748736]{0:T(1024)(128)(4,1)}), s8[4194304]{0:T(1024)(128)(4,1)S(1)}, s32[]{:S(2)}) async-start(s8[37748736]{0:T(1024)(128)(4,1)} %bitcast.330), calls=%async_computation.11 | async-start | bytes 8388608
  2639.7 49.2 %slice-start.9 = ((s8[37748736]{0:T(1024)(128)(4,1)}), s8[4194304]{0:T(1024)(128)(4,1)S(1)}, s32[]{:S(2)}) async-start(s8[37748736]{0:T(1024)(128)(4,1)} %bitcast.330), calls=%async_computation.12 | async-start | bytes 8388608
  2639.7 49.2 %slice-start.10 = ((s8[37748736]{0:T(1024)(128)(4,1)}), s8[4194304]{0:T(1024)(128)(4,1)S(1)}, s32[]{:S(2)}) async-start(s8[37748736]{0:T(1024)(128)(4,1)} %bitcast.330), calls=%async_computation.13 | async-start | bytes 8388608
  2665.9 23.0 slice-start.11
  2666.0 23.0 slice-start.12
  2666.0 23.0 slice-start.13
  2666.0 23.0 slice-start.14
  (33 other events, 355.2 us)
Sparse Core Ops, SparseCore 0:
  237.8 113.5 all-reduce.5
  650.7 112.4 all-reduce.7
  766.6 1836.1 all-reduce.9
where the time goes:
time: 2720 us; the launch traced here: 2710 us
  waiting for transfers between devices  2060 us (76%)
  matrix products  387 us (14%)
  local copies, waits for them, and re-layouts  143 us (5%)
  other arithmetic  86.1 us (3%)
    psum x1, waiting for transfers between devices, device_fn(): lax.psum((grad_gpre, grad_wq, grad_wk, grad_wv, grad_wo, grad_gpost), 'cp')  1810 us
    unnamed x134, local copies, waits for them, and re-layouts  138 us
    psum x1, waiting for transfers between devices, device_fn(): o_sum = lax.psum(o_part.astype(jnp.bfloat16), 'tp').astype(jnp.float32)  114 us
    psum x1, waiting for transfers between devices, device_fn(): lax.psum(grad_a_part.astype(jnp.bfloat16), 'tp').astype(jnp.float32)  71.8 us
    dot_general x4, matrix products, device_fn(): jnp.einsum('hgqe,khe->hgqk', grad_ctx, v_blk, preferred_element_type=jnp....  54.4 us
  transfers between devices with their start and end apart: 17, of which 8 were waited for; matrix products, arithmetic and copies ran while one was open for 15% of the time, Pallas kernels for 0%

commit v1 on v0

v1 whole, which is shorter than its diff:
```python
import functools

import jax
import jax.numpy as jnp
from jax import lax
from jax.experimental import pallas as pl
from jax.experimental.pallas import tpu as pltpu
from jax.sharding import PartitionSpec as P

SOFT_CAP = 30.0
NORM_EPS = 1e-5
ROPE_THETA = 10000.0
HEAD = 128
LOG2E = 1.4426950408889634
NEG = -1e30
F32 = jnp.float32
BF16 = jnp.bfloat16

NT = (((1,), (1,)), ((), ()))
NN = (((1,), (0,)), ((), ()))
TN = (((0,), (0,)), ((), ()))


def dotf(a, b, dims):
    return lax.dot_general(a, b, dims, preferred_element_type=F32)


def rope_tables(length):
    half = HEAD // 2
    inv_freq = ROPE_THETA ** (-jnp.arange(half, dtype=F32) * 2.0 / HEAD)
    ang = jnp.arange(length).astype(F32)[:, None] * inv_freq[None, :]
    cos, sin = jnp.cos(ang), jnp.sin(ang)
    return jnp.concatenate([cos, cos], axis=-1), jnp.concatenate([-sin, sin], axis=-1)


QB = 256
KB = 256


def attn_fwd_kernel(q_ref, k_ref, v_ref, ctx_ref, lse_ref, acc_ref, sum_ref, *, k1, k2):
    i = pl.program_id(1)
    q = jnp.concatenate([q_ref[:, :HEAD], q_ref[:, HEAD:]], axis=0)
    acc_ref[...] = jnp.zeros_like(acc_ref)
    sum_ref[...] = jnp.zeros_like(sum_ref)

    def chunk(row0, mask):
        k = k_ref[pl.ds(row0, KB), :]
        v = v_ref[pl.ds(row0, KB), :]
        s = dotf(q, k, NT)
        p = jnp.exp2(jnp.tanh(s * k1) * k2)
        if mask is not None:
            p = jnp.where(mask, p, 0.0)
        part = p[:, :128]
        for c in range(1, KB // 128):
            part = part + p[:, c * 128:(c + 1) * 128]
        return part, dotf(p.astype(BF16), v, NN)

    def pair(j, carry):
        s0, a0 = chunk(pl.multiple_of(j * (2 * KB), 2 * KB), None)
        s1, a1 = chunk(pl.multiple_of(j * (2 * KB) + KB, KB), None)
        acc_ref[...] += a0 + a1
        sum_ref[...] += s0 + s1
        return carry

    lax.fori_loop(0, i // 2, pair, 0)

    @pl.when(i % 2 == 1)
    def _():
        s0, a0 = chunk(pl.multiple_of((i - 1) * KB, KB), None)
        acc_ref[...] += a0
        sum_ref[...] += s0

    rows = lax.broadcasted_iota(jnp.int32, (2 * QB, KB), 0) % QB
    cols = lax.broadcasted_iota(jnp.int32, (2 * QB, KB), 1)
    s0, a0 = chunk(pl.multiple_of(i * KB, KB), rows >= cols)
    total = jnp.sum(sum_ref[...] + s0, axis=1, keepdims=True)
    ctx = ((acc_ref[...] + a0) / total).astype(BF16)
    ctx_ref[:, :HEAD] = ctx[:QB]
    ctx_ref[:, HEAD:] = ctx[QB:]
    lse = jnp.broadcast_to(jnp.log2(total), (2 * QB, 128)).T
    lse_ref[0, 0:1, :] = lse[0:1, :QB]
    lse_ref[0, 1:2, :] = lse[0:1, QB:]


def attn_fwd(q, k, v):
    T, kvh = q.shape[0], k.shape[1] // HEAD
    scale = HEAD ** -0.5
    return pl.pallas_call(
        functools.partial(attn_fwd_kernel, k1=scale / SOFT_CAP, k2=SOFT_CAP * LOG2E),
        grid=(kvh, T // QB),
        in_specs=[
            pl.BlockSpec((QB, 2 * HEAD), lambda h, i: (i, h)),
            pl.BlockSpec((T, HEAD), lambda h, i: (0, h)),
            pl.BlockSpec((T, HEAD), lambda h, i: (0, h)),
        ],
        out_specs=[
            pl.BlockSpec((QB, 2 * HEAD), lambda h, i: (i, h)),
            pl.BlockSpec((1, 2, QB), lambda h, i: (h, 0, i)),
        ],
        out_shape=[
            jax.ShapeDtypeStruct(q.shape, BF16),
            jax.ShapeDtypeStruct((kvh, 2, T), F32),
        ],
        scratch_shapes=[pltpu.VMEM((2 * QB, HEAD), F32), pltpu.VMEM((2 * QB, 128), F32)],
        compiler_params=pltpu.CompilerParams(dimension_semantics=("arbitrary", "arbitrary")),
        cost_estimate=pl.CostEstimate(flops=int(2 * 2 * T * T * HEAD * kvh * 2), bytes_accessed=4 * q.size * 2, transcendentals=0),
        name="attn_fwd",
    )(q, k, v)


BQ = 256
BK = 512


def attn_bwd_kernel(q_ref, k_ref, v_ref, do_ref, ctx_ref, lse_ref, cos_ref, sin_ref, dq_ref, dk_ref, dv_ref,
                    dqa_ref, dka_ref, dva_ref, dd_ref, *, k1, k2, scale):
    J = pl.program_id(1)
    nq = q_ref.shape[0] // BQ
    r = BK // BQ

    @pl.when(J == 0)
    def _():
        dqa_ref[...] = jnp.zeros_like(dqa_ref)
        for g in range(2):
            for i in range(nq):
                sl = slice(i * BQ, (i + 1) * BQ)
                prod = do_ref[sl, g * HEAD:(g + 1) * HEAD].astype(F32) * ctx_ref[sl, g * HEAD:(g + 1) * HEAD].astype(F32)
                dd_ref[g, 0:1, sl] = jnp.sum(prod.T, axis=0, keepdims=True)

    dka_ref[...] = jnp.zeros_like(dka_ref)
    dva_ref[...] = jnp.zeros_like(dva_ref)
    k = k_ref[...]
    v = v_ref[...]

    def tile(i, mask):
        row0 = pl.multiple_of(i * BQ, BQ)
        rs = pl.ds(row0, BQ)
        dks, dvs = [], []
        for g in range(2):
            q = q_ref[rs, g * HEAD:(g + 1) * HEAD]
            do = do_ref[rs, g * HEAD:(g + 1) * HEAD]
            lse = lse_ref[0, g:g + 1, rs]
            dd = dd_ref[g, 0:1, rs]
            s = dotf(k, q, NT)
            u = jnp.tanh(s * k1)
            p = jnp.exp2(u * k2 - lse)
            if mask is not None:
                p = jnp.where(mask, p, 0.0)
            dp = dotf(v, do, NT)
            ds = (p * (dp - dd) * (1.0 - u * u)).astype(BF16)
            dvs.append(dotf(p.astype(BF16), do, NN))
            dks.append(dotf(ds, q, NN))
            dqa_ref[g, rs, :] += dotf(ds, k, TN)
        dva_ref[...] += dvs[0] + dvs[1]
        dka_ref[...] += dks[0] + dks[1]

    kpos = lax.broadcasted_iota(jnp.int32, (BK, BQ), 0)
    qpos = lax.broadcasted_iota(jnp.int32, (BK, BQ), 1)
    for m in range(r):
        tile(J * r + m, qpos + m * BQ >= kpos)

    def body(i, carry):
        tile(i, None)
        return carry

    lax.fori_loop(J * r + r, nq, body, 0)

    krow = pl.ds(pl.multiple_of(J * BK, BK), BK)

    def unrope(g, cos, sin):
        return (g * cos - pltpu.roll(g, HEAD // 2, 1) * sin) * scale

    dk_ref[...] = unrope(dka_ref[...], cos_ref[krow, :], sin_ref[krow, :]).astype(BF16)
    dv_ref[...] = dva_ref[...].astype(BF16)
    for g in range(2):
        dq_ref[:, g * HEAD:(g + 1) * HEAD] = unrope(dqa_ref[g, krow, :], cos_ref[krow, :], sin_ref[krow, :]).astype(BF16)


def attn_bwd(q, k, v, do, ctx, lse, cos, sin):
    T, kvh = q.shape[0], k.shape[1] // HEAD
    scale = HEAD ** -0.5
    full2 = pl.BlockSpec((T, 2 * HEAD), lambda h, j: (0, h))
    kblk = pl.BlockSpec((BK, HEAD), lambda h, j: (j, h))
    tab = pl.BlockSpec((T, HEAD), lambda h, j: (0, 0))
    return pl.pallas_call(
        functools.partial(attn_bwd_kernel, k1=scale / SOFT_CAP, k2=SOFT_CAP * LOG2E, scale=scale),
        grid=(kvh, T // BK),
        in_specs=[full2, kblk, kblk, full2, full2, pl.BlockSpec((1, 2, T), lambda h, j: (h, 0, 0)), tab, tab],
        out_specs=[pl.BlockSpec((BK, 2 * HEAD), lambda h, j: (j, h)), kblk, kblk],
        out_shape=[
            jax.ShapeDtypeStruct(q.shape, BF16),
            jax.ShapeDtypeStruct(k.shape, BF16),
            jax.ShapeDtypeStruct(v.shape, BF16),
        ],
        scratch_shapes=[
            pltpu.VMEM((2, T, HEAD), F32),
            pltpu.VMEM((BK, HEAD), F32),
            pltpu.VMEM((BK, HEAD), F32),
            pltpu.VMEM((2, 1, T), F32),
        ],
        compiler_params=pltpu.CompilerParams(dimension_semantics=("arbitrary", "arbitrary")),
        cost_estimate=pl.CostEstimate(flops=int(5 * 2 * T * T * HEAD * kvh), bytes_accessed=6 * q.size * 2, transcendentals=0),
        name="attn_bwd",
    )(q, k, v, do, ctx, lse, cos, sin)


def dw_kernel(a_ref, g0_ref, g1_ref, out_ref, *, nh):
    db = a_ref.shape[1]
    half = nh // 2
    at = a_ref[...].T
    for c, g_ref in enumerate((g0_ref, g1_ref)):
        res = dotf(at, g_ref[...], NN)
        for h in range(half):
            out_ref[pl.ds(c * half + h, db, stride=nh), :] = res[:, h * HEAD:(h + 1) * HEAD]


def dw_proj(a, g0, g1, db):
    T, D = a.shape
    cols = g0.shape[1]
    nh = 2 * cols // HEAD
    out = pl.pallas_call(
        functools.partial(dw_kernel, nh=nh),
        grid=(D // db,),
        in_specs=[
            pl.BlockSpec((T, db), lambda i: (0, i)),
            pl.BlockSpec((T, cols), lambda i: (0, 0)),
            pl.BlockSpec((T, cols), lambda i: (0, 0)),
        ],
        out_specs=pl.BlockSpec((db * nh, HEAD), lambda i: (i, 0)),
        out_shape=jax.ShapeDtypeStruct((D * nh, HEAD), F32),
        compiler_params=pltpu.CompilerParams(dimension_semantics=("arbitrary",)),
        cost_estimate=pl.CostEstimate(flops=int(2 * T * D * nh * HEAD), bytes_accessed=D * nh * HEAD * 4 + 2 * a.size, transcendentals=0),
        name="dw_proj",
    )(a, g0, g1)
    return out.reshape(D, nh, HEAD)


def solution(mesh):
    core_perm = [(0, 1), (1, 0), (2, 3), (3, 2)]
    x_perm = [(0, 2), (2, 0), (1, 3), (3, 1)]
    tp_perm = [(0, 1), (1, 0)]

    def gather(blk, me):
        b1 = lax.ppermute(blk, 'cp', core_perm)
        b2 = lax.ppermute(blk, 'cp', x_perm)
        b3 = lax.ppermute(b2, 'cp', core_perm)
        n = blk.shape[0]
        out = jnp.zeros((4 * n,) + blk.shape[1:], blk.dtype)
        for rel, b in enumerate((blk, b1, b2, b3)):
            out = lax.dynamic_update_slice_in_dim(out, b, (me ^ rel) * n, 0)
        return out

    def device_fn(hidden, g_pre, w_q, w_k, w_v, w_o, g_post, d_out):
        tokens, D = hidden.shape
        T = 4 * tokens
        me = lax.axis_index('cp')
        core = me % 2
        HL = w_q.shape[1] // 2
        KL = w_k.shape[1] // 2
        cos, sin = rope_tables(T)
        row0 = me * tokens

        h_f32 = hidden.astype(F32)
        inv_pre = lax.rsqrt(jnp.mean(h_f32 * h_f32, axis=-1, keepdims=True) + NORM_EPS)
        a_loc = (h_f32 * inv_pre * g_pre).astype(BF16)
        a_all = gather(a_loc, me)

        def split(w, n):
            return [w[:, c * n:(c + 1) * n].reshape(D, n * HEAD) for c in range(2)]

        wq, wk, wv = split(w_q, HL), split(w_k, KL), split(w_v, KL)
        w_cat = [jnp.concatenate([wq[c], wk[c], wv[c]], axis=1) for c in range(2)]
        w_own = jnp.where(core == 0, w_cat[0], w_cat[1])
        qkv = jnp.dot(a_all, w_own, preferred_element_type=F32)

        def rope(x):
            x3 = x.reshape(T, -1, HEAD)
            lo, hi = x3[..., :HEAD // 2], x3[..., HEAD // 2:]
            c, s = cos[:, None, :HEAD // 2], sin[:, None, HEAD // 2:]
            return jnp.concatenate([lo * c - hi * s, hi * c + lo * s], axis=-1).reshape(x.shape).astype(BF16)

        q = rope(qkv[:, :HL * HEAD])
        k = rope(qkv[:, HL * HEAD:(HL + KL) * HEAD])
        v = qkv[:, (HL + KL) * HEAD:].astype(BF16)

        ctx, lse = attn_fwd(q, k, v)
        ctx_p = lax.ppermute(ctx, 'cp', core_perm)
        ctx_c = [jnp.where(core == 0, ctx, ctx_p), jnp.where(core == 0, ctx_p, ctx)]
        ctx_all = jnp.concatenate(ctx_c, axis=1)
        wo2 = w_o.reshape(2 * HL * HEAD, D)
        ctx_rows = lax.dynamic_slice_in_dim(ctx_all, row0, tokens, 0)
        o_part = jnp.dot(ctx_rows, wo2, preferred_element_type=F32).astype(BF16)
        o_peer = lax.ppermute(o_part, 'tp', tp_perm)
        o_sum = o_part.astype(F32) + o_peer.astype(F32)
        inv_post = lax.rsqrt(jnp.mean(o_sum * o_sum, axis=-1, keepdims=True) + NORM_EPS)
        o_hat = o_sum * inv_post
        y_blk = (h_f32 + o_hat * g_post).astype(BF16)

        g_out = d_out.astype(F32)
        dgpost = jnp.sum(g_out * o_hat, axis=0)
        gg = g_out * g_post
        grad_o = (inv_post * (gg - o_hat * jnp.mean(gg * o_hat, axis=-1, keepdims=True))).astype(BF16)
        go_all = gather(grad_o, me)

        wo_own = lax.dynamic_slice_in_dim(wo2, core * HL * HEAD, HL * HEAD, 0)
        dctx = lax.dot_general(go_all, wo_own, NT, preferred_element_type=F32).astype(BF16)
        dq, dk, dv = attn_bwd(q, k, v, dctx, ctx, lse, cos, sin)

        def both(g):
            gp = lax.ppermute(g, 'cp', core_perm)
            return jnp.where(core == 0, g, gp), jnp.where(core == 0, gp, g)

        dqs, dks, dvs = both(dq), both(dk), both(dv)
        rows = [lax.dynamic_slice_in_dim(g, row0, tokens, 0) for c in range(2) for g in (dqs[c], dks[c], dvs[c])]
        drow = jnp.concatenate(rows, axis=1)
        w_all = jnp.concatenate(w_cat, axis=1)
        ga_part = lax.dot_general(drow, w_all, NT, preferred_element_type=F32).astype(BF16)
        ga_peer = lax.ppermute(ga_part, 'tp', tp_perm)

        dwo = lax.dot_general(ctx_all, go_all, TN, preferred_element_type=F32).reshape(w_o.shape)
        dwq = dw_proj(a_all, dqs[0], dqs[1], 256)
        dwk = dw_proj(a_all, dks[0], dks[1], 256)
        dwv = dw_proj(a_all, dvs[0], dvs[1], 256)

        ga = ga_part.astype(F32) + ga_peer.astype(F32)
        a_hat = h_f32 * inv_pre
        dgpre = jnp.sum(ga * a_hat, axis=0)
        gh = ga * g_pre
        grad_h = (g_out + inv_pre * (gh - a_hat * jnp.mean(gh * a_hat, axis=-1, keepdims=True))).astype(BF16)
        dg = jnp.stack([dgpre, dgpost])
        dg = dg + lax.ppermute(dg, 'cp', core_perm)
        dg = dg + lax.ppermute(dg, 'cp', x_perm)
        return y_blk, grad_h, dg[0], dwq, dwk, dwv, dwo, dg[1]

    row_spec = P('cp', None)
    head_spec = P(None, 'tp', None)
    out_head_spec = P('tp', None, None)
    return jax.shard_map(device_fn, mesh=mesh, in_specs=(row_spec, P(), head_spec, head_spec, head_spec, out_head_spec, P(), row_spec), out_specs=(row_spec, row_spec, P(), head_spec, head_spec, head_spec, out_head_spec, P()), check_vma=False)
```

time: 2720 us -> 1020 us (0.38)
  waiting for transfers between devices: 2060 us -> 238 us
  Pallas kernels: 0 us -> 272 us
  matrix products: 387 us -> 167 us
  local copies, waits for them, and re-layouts: 143 us -> 231 us
    psum x3 -> x0, waiting for transfers between devices: 2000 us -> none  [the longest x1 1810 us: device_fn(): lax.psum((grad_gpre, grad_wq, grad_wk, grad_wv, grad_wo, grad_gpost), 'cp')]
    pallas_call x0 -> x5, Pallas kernels: none -> 272 us  [the longest x3 117 us: dw_proj(): pl.pallas_call(functools.partial(dw_kernel, nh=nh), grid=(D // db,), in_s...]
    dot_general x34 -> x5, matrix products: 361 us -> 167 us  [the longest x1 51.1 us: device_fn(): qkv = jnp.dot(a_all, w_own, preferred_element_type=F32)]
    ppermute x14, waiting for transfers between devices: 60.7 us -> 238 us  [the longest x2 111 us: gather(): b2 = lax.ppermute(blk, 'cp', x_perm)]
    reduce_sum x8 -> x4, other arithmetic: 60.4 us -> 19 us  [the longest x1 7.3 us: device_fn(): dgpre = jnp.sum(ga * a_hat, axis=0)]
    reshape x0 -> x5, local copies, waits for them, and re-layouts: none -> 39 us  [split(): return [w[:, c * n:(c + 1) * n].reshape(D, n * HEAD) for c in range(2)]]
    slice x0 -> x10, local copies, waits for them, and re-layouts: none -> 33.3 us  [the longest x3 18.6 us: split(): return [w[:, c * n:(c + 1) * n].reshape(D, n * HEAD) for c in range(2)]]
    unnamed x134 -> x79, local copies, waits for them, and re-layouts: 138 us -> 110 us
  transfers between devices with their start and end apart: 17 -> 14, of which waited for: 8 -> 6; matrix products, arithmetic and copies ran while one was open for 15% -> 22% of each run, Pallas kernels for 0% -> 12%
where the time goes in v1:
time: 1020 us; the launch traced here: 1010 us
  Pallas kernels  272 us (27%)
  waiting for transfers between devices  238 us (23%)
  local copies, waits for them, and re-layouts  231 us (23%)
  matrix products  167 us (16%)
  other arithmetic  87.2 us (9%)
  starting transfers between devices  11.9 us (1%)
    pallas_call x3, Pallas kernels, dw_proj(): pl.pallas_call(functools.partial(dw_kernel, nh=nh), grid=(D // db,), in_s...  117 us
    ppermute x2, waiting for transfers between devices, gather(): b2 = lax.ppermute(blk, 'cp', x_perm)  111 us
    unnamed x79, local copies, waits for them, and re-layouts  110 us
    ppermute x1, waiting for transfers between devices, device_fn(): o_peer = lax.ppermute(o_part, 'tp', tp_perm)  102 us
    pallas_call x1, Pallas kernels, attn_bwd(): pl.pallas_call(functools.partial(attn_bwd_kernel, k1=scale / SOFT_CAP, k2...  99.6 us
    pallas_call x1, Pallas kernels, attn_fwd(): pl.pallas_call(functools.partial(attn_fwd_kernel, k1=scale / SOFT_CAP, k2...  55.6 us
    dot_general x1, matrix products, device_fn(): qkv = jnp.dot(a_all, w_own, preferred_element_type=F32)  51.1 us
    dot_general x1, matrix products, device_fn(): lax.dot_general(ctx_all, go_all, TN, preferred_element_type=F32)  48.6 us
  transfers between devices with their start and end apart: 14, of which 6 were waited for; matrix products, arithmetic and copies ran while one was open for 22% of the time, Pallas kernels for 12%

profile of v1, /device:TPU:0, one launch (start us, length us, event | category | flops | bytes accessed | tf_op | source)
XLA Modules:
  0.0 1008.7 jit_solution(12904477653743296777)
XLA Ops:
  4.1 9.3 broadcast.87.clone
  13.4 5.4 constant_dynamic-update-slice_fusion.13
  22.2 5.6 fusion.50
  27.8 5.6 fusion.49
  33.4 8.4 copy.39
  41.7 6.7 copy.24
  48.4 8.4 copy.38
  56.8 6.7 copy.23
  63.5 8.4 copy.41
  71.9 6.6 copy.28
  78.5 8.4 copy.40
  86.9 6.7 copy.27
  93.5 5.4 fusion.39
  98.9 24.9 %collective-permute-done.1 = bf16[512,4608]{1,0:T(8,128)(2,1)} collective-permute-done((bf16[512,4608]{1,0:T(8,128)(2,1)}, bf16[512,4608]{1,0:T(8,128)(2,1)}, u32[]{:S(2)}, u32[]{:S(2)}) %collective-permute-start.1) | collective-permute-done | bytes 4718624 | tf_op jit(solution)/shard_map/ppermute | solution.py:245
  123.9 7.4 fusion.48
  131.3 12.3 %copy_bitcast_fusion = (bf16[4608,1024]{1,0:T(8,128)(2,1)}, bf16[4608,1024]{1,0:T(8,128)(2,1)}) fusion(bf16[576,8,8,128]{3,2,1,0:T(8,128)(2,1)S(1)} %bitcast.40, bf16[576,8,8,128]{3,2,1,0:T(8,128)(2,1)S(1)} %bitcast.42), kind=kLoop, calls=%fused_computation.39 | loop fusion | bytes 37748736 | tf_op jit(solution)/shard_map/reshape | solution.py:269
  148.4 5.0 constant_dynamic-update-slice_fusion.11
  155.9 51.1 %fusion = f32[2048,2048]{0,1:T(8,128)} fusion(bf16[2048,4608]{1,0:T(8,128)(2,1)} %constant_dynamic-update-slice_fusion.10.a_ref, bf16[4608,512]{1,0:T(8,128)(2,1)} %copy.24, bf16[4608,512]{1,0:T(8,128)(2,1)} %copy.23, bf16[4608,1024]{1,0:T(8,128)(2,1)} %get-tuple-element.55, bf16[4608,512]{1,0:T(8,128)(2,1)S(1)} %bitcast.48, bf16[4608,512]{1,0:T(8,128)(2,1)} %copy.27, ...), kind=kOutput, calls=%fused_computation.1 | convolution fusion | flops 38777389056 | bytes 73400320 | tf_op jit(solution)/shard_map/dot_general | solution.py:274
  218.8 6.9 copy.43
  225.7 6.9 copy.42
  232.6 7.4 subtract_convert_fusion
  257.3 15.1 %subtract_convert_fusion.1 = (bf16[2048,4,64]{2,1,0:T(4,128)(2,1)S(1)}, bf16[2048,4,64]{2,1,0:T(4,128)(2,1)S(1)}) fusion(f32[2048,4,64]{2,1,0:T(4,128)} %copy.45, f32[2048,4,64]{2,1,0:T(4,128)} %copy.44, f32[2048,64]{1,0:T(8,128)S(1)} %get-tuple-element.52, f32[2048,64]{1,0:T(8,128)S(1)} %get-tuple-element.53), kind=kLoop, calls=%fused_computation.56 | loop fusion | flops 4194304 | bytes 7340032 | tf_op jit(solution)/shard_map/convert.1
  281.0 55.6 %attn_fwd.1 = (bf16[2048,1024]{1,0:T(8,128)(2,1)}, f32[4,2,2048]{2,1,0:T(2,128)}) custom-call(bf16[2048,1024]{1,0:T(8,128)(2,1)} %bitcast.60, bf16[2048,512]{1,0:T(8,128)(2,1)} %bitcast.62, bf16[2048,512]{1,0:T(8,128)(2,1)} %copy.46.v_ref), custom_call_target="tpu_custom_call" | custom-call | flops 17179869184 | bytes 16777216 | tf_op jit(solution)/shard_map/attn_fwd/pallas_call | solution.py:88
  337.1 6.8 collective-permute-done.3
  343.8 5.1 broadcast_select_fusion.2
  348.9 14.5 %convolution_convert_fusion.1 = bf16[512,4608]{1,0:T(8,128)(2,1)S(1)} fusion(bf16[2048,4608]{1,0:T(8,128)(2,1)} %bitcast.64, s32[]{:T(128)S(6)} %select_n.83, bf16[2048,1024]{1,0:T(8,128)(2,1)} %get-tuple-element.42, bf16[2048,1024]{1,0:T(8,128)(2,1)} %get-tuple-element.41), kind=kOutput, calls=%fused_computation.52 | convolution fusion | flops 9670230016 | bytes 31981572 | tf_op jit(solution)/shard_map/dot_general | solution.py:292
  365.3 102.3 %collective-permute-done.4 = bf16[512,4608]{1,0:T(8,128)(2,1)S(1)} collective-permute-done((bf16[512,4608]{1,0:T(8,128)(2,1)S(1)}, bf16[512,4608]{1,0:T(8,128)(2,1)S(1)}, u32[]{:S(2)}, u32[]{:S(2)}) %collective-permute-start.4) | collective-permute-done | bytes 4718624 | tf_op jit(solution)/shard_map/ppermute | solution.py:293
  469.3 6.7 fusion.28
  476.0 6.6 broadcast.87
  482.6 6.2 constant_dynamic-update-slice_fusion.9
  490.5 10.5 %constant_dynamic-update-slice_fusion.5 = bf16[4608,4096]{1,0:T(8,128)(2,1)} fusion(bf16[576,8,8,128]{3,2,1,0:T(8,128)(2,1)} %bitcast.43), kind=kLoop, calls=%fused_computation.86 | loop fusion | bytes 18874368
  501.0 4.9 constant_dynamic-update-slice_fusion.4
  505.9 86.2 %collective-permute-done.6 = bf16[512,4608]{1,0:T(8,128)(2,1)} collective-permute-done((bf16[512,4608]{1,0:T(8,128)(2,1)}, bf16[512,4608]{1,0:T(8,128)(2,1)}, u32[]{:S(2)}, u32[]{:S(2)}) %collective-permute-start.6) | collective-permute-done | bytes 4718624 | tf_op jit(solution)/shard_map/ppermute | solution.py:245
  592.1 4.8 constant_dynamic-update-slice_fusion.3
  598.8 10.5 %constant_dynamic-update-slice_fusion.2 = bf16[4608,4096]{1,0:T(8,128)(2,1)} fusion(bf16[4608,4096]{1,0:T(8,128)(2,1)} %constant_dynamic-update-slice_fusion.3, bf16[576,8,8,128]{3,2,1,0:T(8,128)(2,1)} %bitcast.41), kind=kLoop, calls=%fused_computation.83 | loop fusion | bytes 18874368
  609.3 4.8 constant_dynamic-update-slice_fusion.1
  619.6 4.8 constant_dynamic-update-slice_fusion.8
  629.2 4.8 constant_dynamic-update-slice_fusion.6
  634.1 26.3 %fusion.34.do_ref = bf16[2048,1024]{1,0:T(8,128)(2,1)} fusion(bf16[2048,4608]{1,0:T(8,128)(2,1)} %constant_dynamic-update-slice_fusion.6, bf16[2048,4608]{1,0:T(8,128)(2,1)} %bitcast.65, s32[]{:T(128)S(6)} %select_n.91), kind=kOutput, calls=%fused_computation.61 | convolution fusion | flops 19329449984 | bytes 32505860 | tf_op jit(solution)/shard_map/dot_general | solution.py:306
  660.4 99.6 %attn_bwd.1 = (bf16[2048,1024]{1,0:T(8,128)(2,1)}, bf16[2048,512]{1,0:T(8,128)(2,1)}, bf16[2048,512]{1,0:T(8,128)(2,1)}) custom-call(bf16[2048,1024]{1,0:T(8,128)(2,1)} %bitcast.61, bf16[2048,512]{1,0:T(8,128)(2,1)} %bitcast.63, bf16[2048,512]{1,0:T(8,128)(2,1)} %copy.46.v_ref, bf16[2048,1024]{1,0:T(8,128)(2,1)} %fusion.34.do_ref, ...), custom_call_target="tpu_custom_call" | custom-call | flops 21474836480 | bytes 25165824 | tf_op jit(solution)/shard_map/attn_bwd/pallas_call | solution.py:185
  761.0 48.6 %fusion.33 = f32[2048,4608]{1,0:T(8,128)} fusion(bf16[2048,4608]{1,0:T(8,128)(2,1)} %constant_dynamic-update-slice_fusion.6, bf16[2048,1024]{1,0:T(8,128)(2,1)} %get-tuple-element.41, bf16[2048,1024]{1,0:T(8,128)(2,1)} %get-tuple-element.42), kind=kOutput, calls=%fused_computation.48 | convolution fusion | flops 38671482880 | bytes 65011712 | tf_op jit(solution)/shard_map/dot_general | solution.py:320
  813.6 30.9 %dw_proj.4 = f32[36864,128]{1,0:T(8,128)} custom-call(bf16[2048,4608]{1,0:T(8,128)(2,1)} %constant_dynamic-update-slice_fusion.10.a_ref, bf16[2048,512]{1,0:T(8,128)(2,1)} %get-tuple-element.48.g0_ref, bf16[2048,512]{1,0:T(8,128)(2,1)} %get-tuple-element.47.g1_ref), custom_call_target="tpu_custom_call" | custom-call | flops 19327352832 | bytes 37748736 | tf_op jit(solution)/shard_map/dw_proj/pallas_call | solution.py:221
  857.7 27.0 %convolution_convert_fusion = bf16[512,4608]{1,0:T(8,128)(2,1)} fusion(bf16[512,4096]{1,0:T(8,128)(2,1)} %dynamic-slice_dynamic-update-slice_fusion.2, bf16[4608,4096]{1,0:T(8,128)(2,1)} %constant_dynamic-update-slice_fusion), kind=kOutput, calls=%fused_computation.51 | convolution fusion | flops 19329712128 | bytes 46661632 | tf_op jit(solution)/shard_map/dot_general | solution.py:317
  886.3 30.2 %dw_proj.5 = f32[36864,128]{1,0:T(8,128)} custom-call(bf16[2048,4608]{1,0:T(8,128)(2,1)} %constant_dynamic-update-slice_fusion.10.a_ref, bf16[2048,512]{1,0:T(8,128)(2,1)} %get-tuple-element.46.g0_ref, bf16[2048,512]{1,0:T(8,128)(2,1)} %copy-done.6), custom_call_target="tpu_custom_call" | custom-call | flops 19327352832 | bytes 37748736 | tf_op jit(solution)/shard_map/dw_proj/pallas_call | solution.py:221
  916.6 55.4 %dw_proj.3 = f32[73728,128]{1,0:T(8,128)} custom-call(bf16[2048,4608]{1,0:T(8,128)(2,1)} %constant_dynamic-update-slice_fusion.10.a_ref, bf16[2048,1024]{1,0:T(8,128)(2,1)} %copy-done.4, bf16[2048,1024]{1,0:T(8,128)(2,1)} %copy-done.3), custom_call_target="tpu_custom_call" | custom-call | flops 38654705664 | bytes 56623104 | tf_op jit(solution)/shard_map/dw_proj/pallas_call | solution.py:221
  972.0 16.4 %collective-permute-done.11 = bf16[512,4608]{1,0:T(8,128)(2,1)} collective-permute-done((bf16[512,4608]{1,0:T(8,128)(2,1)}, bf16[512,4608]{1,0:T(8,128)(2,1)}, u32[]{:S(2)}, u32[]{:S(2)}) %collective-permute-start.11) | collective-permute-done | bytes 4718624 | tf_op jit(solution)/shard_map/ppermute | solution.py:318
  988.4 7.3 fusion.24
  998.7 8.8 fusion.27
  (128 shorter events, 93.2 us)
Async XLA Ops:
  0.6 12.7 %slice-start = ((s8[4718592]{0:T(1024)(128)(4,1)}), s8[524288]{0:T(1024)(128)(4,1)S(1)}, s32[]{:S(2)}) async-start(s8[4718592]{0:T(1024)(128)(4,1)} %bitcast.36), calls=%async_computation | async-start | bytes 1048576
  4.1 9.3 copy-start.13
  4.1 9.3 slice-start.1
  4.1 9.3 copy-start.10
  4.1 18.1 %slice-start.9 = ((s8[9437184]{0:T(1024)(128)(4,1)}), s8[4194304]{0:T(1024)(128)(4,1)S(1)}, s32[]{:S(2)}) async-start(s8[9437184]{0:T(1024)(128)(4,1)} %bitcast.55), calls=%async_computation.9 | async-start | bytes 8388608
  4.1 18.1 %slice-start.10 = ((s8[9437184]{0:T(1024)(128)(4,1)}), s8[4194304]{0:T(1024)(128)(4,1)S(1)}, s32[]{:S(2)}) async-start(s8[9437184]{0:T(1024)(128)(4,1)} %bitcast.55), calls=%async_computation.10 | async-start | bytes 8388608
  13.4 8.8 slice-start.11
  18.8 9.0 slice-start.12
  18.8 9.0 slice-start.13
  18.8 9.0 slice-start.14
  18.8 105.1 %collective-permute-start.1 = (bf16[512,4608]{1,0:T(8,128)(2,1)}, bf16[512,4608]{1,0:T(8,128)(2,1)}, u32[]{:S(2)}, u32[]{:S(2)}) collective-permute-start(bf16[512,4608]{1,0:T(8,128)(2,1)} %get-tuple-element.27), channel_id=1, source_target_pairs={{0,2},{2,0},{1,3},{3,1},{4,6},{6,4},{5,7},{7,5}} | collective-permute-start | bytes 14155784 | tf_op jit(solution)/shard_map/ppermute | solution.py:245
  22.2 121.5 %collective-permute-start = (bf16[512,4608]{1,0:T(8,128)(2,1)}, bf16[512,4608]{1,0:T(8,128)(2,1)}, u32[]{:S(2)}, u32[]{:S(2)}) collective-permute-start(bf16[512,4608]{1,0:T(8,128)(2,1)} %get-tuple-element.27), channel_id=1, source_target_pairs={{0,1},{1,0},{2,3},{3,2},{4,5},{5,4},{6,7},{7,6}} | collective-permute-start | bytes 14155784 | tf_op jit(solution)/shard_map/ppermute | solution.py:244
  123.9 29.6 %collective-permute-start.2 = (bf16[512,4608]{1,0:T(8,128)(2,1)}, bf16[512,4608]{1,0:T(8,128)(2,1)S(1)}, u32[]{:S(2)}, u32[]{:S(2)}) collective-permute-start(bf16[512,4608]{1,0:T(8,128)(2,1)} %collective-permute-done.1), channel_id=1, source_target_pairs={{0,1},{1,0},{2,3},{3,2},{4,5},{5,4},{6,7},{7,6}} | collective-permute-start | bytes 14155784 | tf_op jit(solution)/shard_map/ppermute | solution.py:246
  131.3 12.3 %copy-start = (bf16[4608,8,128]{2,1,0:T(8,128)(2,1)}, bf16[4608,8,128]{2,1,0:T(8,128)(2,1)S(1)}, u32[]{:S(2)}) copy-start(bf16[4608,8,128]{2,1,0:T(8,128)(2,1)S(1)} %get-tuple-element.30) | copy-start | bytes 28311556
  131.3 12.3 %copy-start.1 = (bf16[4608,8,128]{2,1,0:T(8,128)(2,1)}, bf16[4608,8,128]{2,1,0:T(8,128)(2,1)S(1)}, u32[]{:S(2)}) copy-start(bf16[4608,8,128]{2,1,0:T(8,128)(2,1)S(1)} %get-tuple-element.31) | copy-start | bytes 28311556
  148.4 7.5 slice-start.6
  153.5 2.5 slice-start.7
  240.0 5.5 slice-start.8
  336.5 7.3 collective-permute-start.3
  348.9 120.3 %slice-start.2 = ((s8[4718592]{0:T(1024)(128)(4,1)}), s8[4194304]{0:T(1024)(128)(4,1)S(1)}, s32[]{:S(2)}) async-start(s8[4718592]{0:T(1024)(128)(4,1)} %bitcast.38), calls=%async_computation.2 | async-start | bytes 8388608
  348.9 120.3 %slice-start.4 = ((s8[4718592]{0:T(1024)(128)(4,1)}), s8[4194304]{0:T(1024)(128)(4,1)S(1)}, s32[]{:S(2)}) async-start(s8[4718592]{0:T(1024)(128)(4,1)} %bitcast.44), calls=%async_computation.4 | async-start | bytes 8388608
  348.9 120.3 %slice-start.3 = ((s8[4718592]{0:T(1024)(128)(4,1)}), s8[524288]{0:T(1024)(128)(4,1)S(1)}, s32[]{:S(2)}) async-start(s8[4718592]{0:T(1024)(128)(4,1)} %bitcast.38), calls=%async_computation.3 | async-start | bytes 1048576
  348.9 120.3 %slice-start.5 = ((s8[4718592]{0:T(1024)(128)(4,1)}), s8[524288]{0:T(1024)(128)(4,1)S(1)}, s32[]{:S(2)}) async-start(s8[4718592]{0:T(1024)(128)(4,1)} %bitcast.44), calls=%async_computation.5 | async-start | bytes 1048576
  363.4 105.8 %copy-start.12 = (f32[4608]{0:T(1024)S(1)}, f32[4608]{0:T(1024)}, u32[]{:S(2)}) copy-start(f32[4608]{0:T(1024)} %param.14) | copy-start | bytes 55300
  363.4 104.2 %collective-permute-start.4 = (bf16[512,4608]{1,0:T(8,128)(2,1)S(1)}, bf16[512,4608]{1,0:T(8,128)(2,1)S(1)}, u32[]{:S(2)}, u32[]{:S(2)}) collective-permute-start(bf16[512,4608]{1,0:T(8,128)(2,1)S(1)} %convolution_convert_fusion.1), channel_id=1, source_target_pairs={{0,4},{4,0},{1,5},{5,1},{2,6},{6,2},{3,7},{7,3}} | collective-permute-start | bytes 14155784 | tf_op jit(solution)/shard_map/ppermute | solution.py:293
  488.8 103.3 %collective-permute-start.6 = (bf16[512,4608]{1,0:T(8,128)(2,1)}, bf16[512,4608]{1,0:T(8,128)(2,1)}, u32[]{:S(2)}, u32[]{:S(2)}) collective-permute-start(bf16[512,4608]{1,0:T(8,128)(2,1)} %get-tuple-element.25), channel_id=1, source_target_pairs={{0,2},{2,0},{1,3},{3,1},{4,6},{6,4},{5,7},{7,5}} | collective-permute-start | bytes 14155784 | tf_op jit(solution)/shard_map/ppermute | solution.py:245
  490.5 129.1 %collective-permute-start.5 = (bf16[512,4608]{1,0:T(8,128)(2,1)}, bf16[512,4608]{1,0:T(8,128)(2,1)}, u32[]{:S(2)}, u32[]{:S(2)}) collective-permute-start(bf16[512,4608]{1,0:T(8,128)(2,1)} %get-tuple-element.25), channel_id=1, source_target_pairs={{0,1},{1,0},{2,3},{3,2},{4,5},{5,4},{6,7},{7,6}} | collective-permute-start | bytes 14155784 | tf_op jit(solution)/shard_map/ppermute | solution.py:244
  501.0 95.9 %copy-start.5 = (f32[2048,64]{1,0:T(8,128)S(1)}, f32[2048,64]{1,0:T(8,128)}, u32[]{:S(2)}) copy-start(f32[2048,64]{1,0:T(8,128)} %get-tuple-element.51) | copy-start | bytes 1572868
  592.1 37.2 %collective-permute-start.7 = (bf16[512,4608]{1,0:T(8,128)(2,1)}, bf16[512,4608]{1,0:T(8,128)(2,1)}, u32[]{:S(2)}, u32[]{:S(2)}) collective-permute-start(bf16[512,4608]{1,0:T(8,128)(2,1)} %collective-permute-done.6), channel_id=1, source_target_pairs={{0,1},{1,0},{2,3},{3,2},{4,5},{5,4},{6,7},{7,6}} | collective-permute-start | bytes 14155784 | tf_op jit(solution)/shard_map/ppermute | solution.py:246
  760.0 84.5 %collective-permute-start.8 = (bf16[2048,1024]{1,0:T(8,128)(2,1)}, bf16[2048,1024]{1,0:T(8,128)(2,1)}, u32[]{:S(2)}, u32[]{:S(2)}) collective-permute-start(bf16[2048,1024]{1,0:T(8,128)(2,1)} %get-tuple-element.15), channel_id=1, source_target_pairs={{0,1},{1,0},{2,3},{3,2},{4,5},{5,4},{6,7},{7,6}} | collective-permute-start | bytes 12582920 | tf_op jit(solution)/shard_map/ppermute | solution.py:310
  760.5 49.1 %collective-permute-start.9 = (bf16[2048,512]{1,0:T(8,128)(2,1)}, bf16[2048,512]{1,0:T(8,128)(2,1)S(1)}, u32[]{:S(2)}, u32[]{:S(2)}) collective-permute-start(bf16[2048,512]{1,0:T(8,128)(2,1)} %get-tuple-element.16), channel_id=1, source_target_pairs={{0,1},{1,0},{2,3},{3,2},{4,5},{5,4},{6,7},{7,6}} | collective-permute-start | bytes 6291464 | tf_op jit(solution)/shard_map/ppermute | solution.py:310
  760.6 49.1 %copy-start.8 = (bf16[2048,512]{1,0:T(8,128)(2,1)S(1)}, bf16[2048,512]{1,0:T(8,128)(2,1)}, u32[]{:S(2)}) copy-start(bf16[2048,512]{1,0:T(8,128)(2,1)} %get-tuple-element.16) | copy-start | bytes 6291460
  760.6 51.3 %collective-permute-start.10 = (bf16[2048,512]{1,0:T(8,128)(2,1)}, bf16[2048,512]{1,0:T(8,128)(2,1)S(1)}, u32[]{:S(2)}, u32[]{:S(2)}) collective-permute-start(bf16[2048,512]{1,0:T(8,128)(2,1)} %get-tuple-element.17), channel_id=1, source_target_pairs={{0,1},{1,0},{2,3},{3,2},{4,5},{5,4},{6,7},{7,6}} | collective-permute-start | bytes 6291464 | tf_op jit(solution)/shard_map/ppermute | solution.py:310
  809.6 2.4 copy-start.7
  813.6 43.3 %copy-start.6 = (bf16[2048,512]{1,0:T(8,128)(2,1)}, bf16[2048,512]{1,0:T(8,128)(2,1)S(1)}, u32[]{:S(2)}) copy-start(bf16[2048,512]{1,0:T(8,128)(2,1)S(1)} %get-tuple-element.45.g1_ref) | copy-start | bytes 6291460
  848.3 5.6 copy-start.3
  848.3 6.7 copy-start.4
  884.7 103.7 %collective-permute-start.11 = (bf16[512,4608]{1,0:T(8,128)(2,1)}, bf16[512,4608]{1,0:T(8,128)(2,1)}, u32[]{:S(2)}, u32[]{:S(2)}) collective-permute-start(bf16[512,4608]{1,0:T(8,128)(2,1)} %convolution_convert_fusion), channel_id=1, source_target_pairs={{0,4},{4,0},{1,5},{5,1},{2,6},{6,2},{3,7},{7,3}} | collective-permute-start | bytes 14155784 | tf_op jit(solution)/shard_map/ppermute | solution.py:318
  916.6 71.8 %copy-start.11 = (f32[4608]{0:T(1024)S(1)}, f32[4608]{0:T(1024)}, u32[]{:S(2)}) copy-start(f32[4608]{0:T(1024)} %param.9) | copy-start | bytes 55300
  916.6 71.8 %copy-start.14 = (f32[512]{0:T(512)S(1)}, f32[512]{0:T(512)}, u32[]{:S(2)}) copy-start(f32[512]{0:T(512)} %copy-done.13) | copy-start | bytes 6148
  972.0 23.7 %copy-start.9 = (f32[1,4608]{1,0:T(1,128)S(1)}, f32[1,4608]{1,0:T(1,128)}, u32[]{:S(2)}) copy-start(f32[1,4608]{1,0:T(1,128)} %stack.10) | copy-start | bytes 55300
  972.0 26.7 %copy-start.2 = (bf16[512,4608]{1,0:T(8,128)(2,1)S(1)}, bf16[512,4608]{1,0:T(8,128)(2,1)}, u32[]{:S(2)}) copy-start(bf16[512,4608]{1,0:T(8,128)(2,1)} %convolution_convert_fusion) | copy-start | bytes 14155780
  995.8 1.2 collective-permute-start.12
  997.1 10.4 %collective-permute-start.13 = (f32[2,4608]{1,0:T(2,128)S(1)}, f32[2,4608]{1,0:T(2,128)S(1)}, u32[]{:S(2)}, u32[]{:S(2)}) collective-permute-start(f32[2,4608]{1,0:T(2,128)S(1)} %fusion.45), channel_id=1, source_target_pairs={{0,2},{2,0},{1,3},{3,1},{4,6},{6,4},{5,7},{7,5}} | collective-permute-start | bytes 110600 | tf_op jit(solution)/shard_map/ppermute | solution.py:332

commit v2 on v1

v2 whole, which is shorter than its diff:
```python
import functools

import jax
import jax.numpy as jnp
from jax import lax
from jax.experimental import pallas as pl
from jax.experimental.pallas import tpu as pltpu
from jax.sharding import PartitionSpec as P


SOFT_CAP = 30.0
NORM_EPS = 1e-5
ROPE_THETA = 10000.0
HEAD = 128
LOG2E = 1.4426950408889634
F32 = jnp.float32
BF16 = jnp.bfloat16

NT = (((1,), (1,)), ((), ()))
NN = (((1,), (0,)), ((), ()))
TN = (((0,), (0,)), ((), ()))


def dotf(a, b, dims):
    return lax.dot_general(a, b, dims, preferred_element_type=F32)


def rope_tables(length):
    half = HEAD // 2
    inv_freq = ROPE_THETA ** (-jnp.arange(half, dtype=F32) * 2.0 / HEAD)
    ang = jnp.arange(length).astype(F32)[:, None] * inv_freq[None, :]
    cos, sin = jnp.cos(ang), jnp.sin(ang)
    return jnp.concatenate([cos, cos], axis=-1), jnp.concatenate([-sin, sin], axis=-1)


QB = 256
KB = 256


def attn_fwd_kernel(q_ref, k_ref, v_ref, ctx_ref, lse_ref, acc_ref, sum_ref, *, k1, k2):
    i = pl.program_id(1)
    q = jnp.concatenate([q_ref[:, :HEAD], q_ref[:, HEAD:]], axis=0)
    acc_ref[...] = jnp.zeros_like(acc_ref)
    sum_ref[...] = jnp.zeros_like(sum_ref)

    def chunk(row0, mask):
        k = k_ref[pl.ds(row0, KB), :]
        v = v_ref[pl.ds(row0, KB), :]
        s = dotf(q, k, NT)
        p = jnp.exp2(jnp.tanh(s * k1) * k2)
        if mask is not None:
            p = jnp.where(mask, p, 0.0)
        part = p[:, :128]
        for c in range(1, KB // 128):
            part = part + p[:, c * 128:(c + 1) * 128]
        return part, dotf(p.astype(BF16), v, NN)

    def pair(j, carry):
        s0, a0 = chunk(pl.multiple_of(j * (2 * KB), 2 * KB), None)
        s1, a1 = chunk(pl.multiple_of(j * (2 * KB) + KB, KB), None)
        acc_ref[...] += a0 + a1
        sum_ref[...] += s0 + s1
        return carry

    lax.fori_loop(0, i // 2, pair, 0)

    @pl.when(i % 2 == 1)
    def _():
        s0, a0 = chunk(pl.multiple_of((i - 1) * KB, KB), None)
        acc_ref[...] += a0
        sum_ref[...] += s0

    rows = lax.broadcasted_iota(jnp.int32, (2 * QB, KB), 0) % QB
    cols = lax.broadcasted_iota(jnp.int32, (2 * QB, KB), 1)
    s0, a0 = chunk(pl.multiple_of(i * KB, KB), rows >= cols)
    total = jnp.sum(sum_ref[...] + s0, axis=1, keepdims=True)
    ctx = ((acc_ref[...] + a0) / total).astype(BF16)
    ctx_ref[:, :HEAD] = ctx[:QB]
    ctx_ref[:, HEAD:] = ctx[QB:]
    lse = jnp.broadcast_to(jnp.log2(total), (2 * QB, 128)).T
    lse_ref[0, 0:1, :] = lse[0:1, :QB]
    lse_ref[0, 1:2, :] = lse[0:1, QB:]


def attn_fwd(qkv, kvh, nq):
    T = qkv.shape[0]
    scale = HEAD ** -0.5
    return pl.pallas_call(
        functools.partial(attn_fwd_kernel, k1=scale / SOFT_CAP, k2=SOFT_CAP * LOG2E),
        grid=(kvh, T // QB),
        in_specs=[
            pl.BlockSpec((QB, 2 * HEAD), lambda h, i: (i, h)),
            pl.BlockSpec((T, HEAD), lambda h, i: (0, nq + h)),
            pl.BlockSpec((T, HEAD), lambda h, i: (0, nq + kvh + h)),
        ],
        out_specs=[
            pl.BlockSpec((QB, 2 * HEAD), lambda h, i: (i, h)),
            pl.BlockSpec((1, 2, QB), lambda h, i: (h, 0, i)),
        ],
        out_shape=[
            jax.ShapeDtypeStruct((T, nq * HEAD), BF16),
            jax.ShapeDtypeStruct((kvh, 2, T), F32),
        ],
        scratch_shapes=[pltpu.VMEM((2 * QB, HEAD), F32), pltpu.VMEM((2 * QB, 128), F32)],
        compiler_params=pltpu.CompilerParams(dimension_semantics=("arbitrary", "arbitrary")),
        cost_estimate=pl.CostEstimate(flops=int(2 * 2 * T * T * HEAD * kvh * 2), bytes_accessed=2 * qkv.size * 2, transcendentals=0),
        name="attn_fwd",
    )(qkv, qkv, qkv)


BQ = 256
BK = 512


def attn_bwd_kernel(q_ref, k_ref, v_ref, do_ref, ctx_ref, lse_ref, cos_ref, sin_ref, dq_ref, dk_ref, dv_ref,
                    dqa_ref, dka_ref, dva_ref, dd_ref, *, k1, k2, scale):
    J = pl.program_id(1)
    nq = q_ref.shape[0] // BQ
    r = BK // BQ

    @pl.when(J == 0)
    def _():
        dqa_ref[...] = jnp.zeros_like(dqa_ref)
        for g in range(2):
            for i in range(nq):
                sl = slice(i * BQ, (i + 1) * BQ)
                prod = do_ref[sl, g * HEAD:(g + 1) * HEAD].astype(F32) * ctx_ref[sl, g * HEAD:(g + 1) * HEAD].astype(F32)
                dd_ref[g, 0:1, sl] = jnp.sum(prod.T, axis=0, keepdims=True)

    dka_ref[...] = jnp.zeros_like(dka_ref)
    dva_ref[...] = jnp.zeros_like(dva_ref)
    k = k_ref[...]
    v = v_ref[...]

    def tile(i, mask):
        row0 = pl.multiple_of(i * BQ, BQ)
        rs = pl.ds(row0, BQ)
        dks, dvs = [], []
        for g in range(2):
            q = q_ref[rs, g * HEAD:(g + 1) * HEAD]
            do = do_ref[rs, g * HEAD:(g + 1) * HEAD]
            lse = lse_ref[0, g:g + 1, rs]
            dd = dd_ref[g, 0:1, rs]
            s = dotf(k, q, NT)
            u = jnp.tanh(s * k1)
            p = jnp.exp2(u * k2 - lse)
            if mask is not None:
                p = jnp.where(mask, p, 0.0)
            dp = dotf(v, do, NT)
            ds = (p * (dp - dd) * (1.0 - u * u)).astype(BF16)
            dvs.append(dotf(p.astype(BF16), do, NN))
            dks.append(dotf(ds, q, NN))
            dqa_ref[g, rs, :] += dotf(ds, k, TN)
        dva_ref[...] += dvs[0] + dvs[1]
        dka_ref[...] += dks[0] + dks[1]

    kpos = lax.broadcasted_iota(jnp.int32, (BK, BQ), 0)
    qpos = lax.broadcasted_iota(jnp.int32, (BK, BQ), 1)
    for m in range(r):
        tile(J * r + m, qpos + m * BQ >= kpos)

    def body(i, carry):
        tile(i, None)
        return carry

    lax.fori_loop(J * r + r, nq, body, 0)

    krow = pl.ds(pl.multiple_of(J * BK, BK), BK)

    def unrope(g, cos, sin):
        return (g * cos - pltpu.roll(g, HEAD // 2, 1) * sin) * scale

    dk_ref[...] = unrope(dka_ref[...], cos_ref[krow, :], sin_ref[krow, :]).astype(BF16)
    dv_ref[...] = dva_ref[...].astype(BF16)
    for g in range(2):
        dq_ref[:, g * HEAD:(g + 1) * HEAD] = unrope(dqa_ref[g, krow, :], cos_ref[krow, :], sin_ref[krow, :]).astype(BF16)


def attn_bwd(qkv, kvh, nq, do, ctx, lse, cos, sin):
    T = qkv.shape[0]
    scale = HEAD ** -0.5
    full2 = pl.BlockSpec((T, 2 * HEAD), lambda h, j: (0, h))
    kblk = pl.BlockSpec((BK, HEAD), lambda h, j: (j, h))
    tab = pl.BlockSpec((T, HEAD), lambda h, j: (0, 0))
    return pl.pallas_call(
        functools.partial(attn_bwd_kernel, k1=scale / SOFT_CAP, k2=SOFT_CAP * LOG2E, scale=scale),
        grid=(kvh, T // BK),
        in_specs=[full2, pl.BlockSpec((BK, HEAD), lambda h, j: (j, nq + h)), pl.BlockSpec((BK, HEAD), lambda h, j: (j, nq + kvh + h)), full2, full2, pl.BlockSpec((1, 2, T), lambda h, j: (h, 0, 0)), tab, tab],
        out_specs=[pl.BlockSpec((BK, 2 * HEAD), lambda h, j: (j, h)), kblk, kblk],
        out_shape=[
            jax.ShapeDtypeStruct((T, nq * HEAD), BF16),
            jax.ShapeDtypeStruct((T, kvh * HEAD), BF16),
            jax.ShapeDtypeStruct((T, kvh * HEAD), BF16),
        ],
        scratch_shapes=[
            pltpu.VMEM((2, T, HEAD), F32),
            pltpu.VMEM((BK, HEAD), F32),
            pltpu.VMEM((BK, HEAD), F32),
            pltpu.VMEM((2, 1, T), F32),
        ],
        compiler_params=pltpu.CompilerParams(dimension_semantics=("arbitrary", "arbitrary")),
        cost_estimate=pl.CostEstimate(flops=int(5 * 2 * T * T * HEAD * kvh), bytes_accessed=3 * qkv.size * 2, transcendentals=0),
        name="attn_bwd",
    )(qkv, qkv, qkv, do, ctx, lse, cos, sin)


VMEM_LIMIT = 64_000_000


def gmm_kernel(sc_ref, *refs, layout, rope_blocks, n_w, w_of, aliased):
    np_ = len(layout)
    pieces = refs[:np_]
    ws = refs[np_:np_ + n_w]
    cos_ref, sin_ref = refs[np_ + n_w:np_ + n_w + 2]
    rest = refs[np_ + n_w + 2:]
    if aliased:
        rest = rest[2:]
    out_ref, all_ref, x_ref, sem_in, sem_out = rest
    n = pl.program_id(0)
    last = pl.num_programs(0) - 1
    half = x_ref.shape[0]
    xt = sc_ref[0]
    dst = pl.multiple_of(xt * half, half)

    def off(i):
        return pl.multiple_of(sc_ref[1 + i], 16)

    def cp_in(i):
        return pltpu.make_async_copy(pieces[i], x_ref.at[pl.ds(off(i), layout[i])], sem_in.at[i])

    def cp_out():
        return pltpu.make_async_copy(x_ref, all_ref.at[pl.ds(dst, half)], sem_out)

    @pl.when(n == 0)
    def _():
        for i in range(np_):
            cp_in(i).start()
        for i in range(np_):
            cp_in(i).wait()
        cp_out().start()

    for b, wi in enumerate(w_of):
        @pl.when(n == b)
        def _(b=b, wi=wi):
            res = dotf(x_ref[...], ws[wi][...], NT)
            if b in rope_blocks:
                c, s = cos_ref[...], sin_ref[...]
                for h in range(res.shape[1] // HEAD):
                    r = res[:, h * HEAD:(h + 1) * HEAD]
                    out_ref[:, h * HEAD:(h + 1) * HEAD] = (r * c + pltpu.roll(r, HEAD // 2, 1) * s).astype(BF16)
            else:
                out_ref[...] = res.astype(BF16)

    @pl.when(n == last)
    def _():
        cp_out().wait()


def gather_matmul(scal, pieces, ws, w_maps, w_of, rope_blocks, cos, sin, T, nb, bufs=None):
    D = pieces[0].shape[1]
    half = T // 2
    nblk = len(w_of)
    layout = tuple(p.shape[0] for p in pieces)
    anyspec = pl.BlockSpec(memory_space=pl.ANY)
    tab = pl.BlockSpec((half, HEAD), lambda n, s: (s[0], 0), pipeline_mode=pl.Buffered(1))
    in_specs = [anyspec] * len(pieces) + [pl.BlockSpec((nb, D), m) for m in w_maps] + [tab, tab]
    args = list(pieces) + list(ws) + [cos, sin]
    aliases = {}
    if bufs is not None:
        aliases = {1 + len(args): 0, 2 + len(args): 1}
        in_specs += [anyspec, anyspec]
        args += list(bufs)
    return pl.pallas_call(
        functools.partial(gmm_kernel, layout=layout, rope_blocks=rope_blocks, n_w=len(ws), w_of=w_of, aliased=bufs is not None),
        grid_spec=pltpu.PrefetchScalarGridSpec(
            num_scalar_prefetch=1,
            grid=(nblk,),
            in_specs=in_specs,
            out_specs=[pl.BlockSpec((half, nb), lambda n, s: (s[0], n)), anyspec],
            scratch_shapes=[
                pltpu.VMEM((half, D), BF16),
                pltpu.SemaphoreType.DMA((len(pieces),)),
                pltpu.SemaphoreType.DMA,
            ],
        ),
        out_shape=[jax.ShapeDtypeStruct((T, nblk * nb), BF16), jax.ShapeDtypeStruct((T, D), BF16)],
        input_output_aliases=aliases,
        compiler_params=pltpu.CompilerParams(dimension_semantics=("arbitrary",), vmem_limit_bytes=VMEM_LIMIT),
        cost_estimate=pl.CostEstimate(flops=2 * half * D * nblk * nb, bytes_accessed=half * D * 4 + nblk * nb * D * 2, transcendentals=0),
    )(scal, *args)


def rows_kernel(sc_ref, *refs, parts):
    n_l = len(parts)
    n_w = 1 + max(p[0] for p in parts)
    lhs = refs[:n_l]
    ws = refs[n_l:n_l + n_w]
    out_ref = refs[n_l + n_w]
    core = sc_ref[1]
    acc = None
    for ref, (wi, other, rows) in zip(lhs, parts):
        c = 1 - core if other else core
        d = dotf(ref[...], ws[wi][pl.ds(pl.multiple_of(c * rows, rows), rows), :], NN)
        acc = d if acc is None else acc + d
    out_ref[...] = acc.astype(BF16)


def rows_matmul(scal, lhs, lhs_maps, ws, parts, M, db):
    D = ws[0].shape[1]
    flops = 2 * M * D * sum(p[2] for p in parts)
    return pl.pallas_call(
        functools.partial(rows_kernel, parts=tuple(parts)),
        grid_spec=pltpu.PrefetchScalarGridSpec(
            num_scalar_prefetch=1,
            grid=(D // db,),
            in_specs=[pl.BlockSpec((M, l.shape[1]), m) for l, m in zip(lhs, lhs_maps)]
            + [pl.BlockSpec((w.shape[0], db), lambda i, s: (0, i)) for w in ws],
            out_specs=pl.BlockSpec((M, db), lambda i, s: (0, i)),
        ),
        out_shape=jax.ShapeDtypeStruct((M, D), BF16),
        compiler_params=pltpu.CompilerParams(dimension_semantics=("arbitrary",), vmem_limit_bytes=VMEM_LIMIT),
        cost_estimate=pl.CostEstimate(flops=flops, bytes_accessed=sum(w.size for w in ws) * 2, transcendentals=0),
    )(scal, *lhs, *ws)


def dw_kernel(sc_ref, a_ref, q0, q1, k0, k1, v0, v1, oq_ref, ok_ref, ov_ref):
    db = a_ref.shape[1]
    core = sc_ref[1]
    at = a_ref[...].T
    for pair, out_ref in (((q0, q1), oq_ref), ((k0, k1), ok_ref), ((v0, v1), ov_ref)):
        hh = pair[0].shape[1] // HEAD
        nh = 2 * hh
        for other, g_ref in enumerate(pair):
            c = 1 - core if other else core
            res = dotf(at, g_ref[...], NN)
            for h in range(hh):
                out_ref[pl.ds(c * hh + h, db, stride=nh), :] = res[:, h * HEAD:(h + 1) * HEAD]


def dw_proj(scal, a, gs, db):
    T, D = a.shape
    nhs = [2 * gs[0].shape[1] // HEAD, 2 * gs[2].shape[1] // HEAD, 2 * gs[4].shape[1] // HEAD]
    outs = pl.pallas_call(
        dw_kernel,
        grid_spec=pltpu.PrefetchScalarGridSpec(
            num_scalar_prefetch=1,
            grid=(D // db,),
            in_specs=[pl.BlockSpec((T, db), lambda i, s: (0, i))]
            + [pl.BlockSpec(g.shape, lambda i, s: (0, 0), pipeline_mode=pl.Buffered(1)) for g in gs],
            out_specs=[pl.BlockSpec((db * nh, HEAD), lambda i, s: (i, 0)) for nh in nhs],
        ),
        out_shape=[jax.ShapeDtypeStruct((D * nh, HEAD), F32) for nh in nhs],
        compiler_params=pltpu.CompilerParams(dimension_semantics=("arbitrary",), vmem_limit_bytes=VMEM_LIMIT),
        cost_estimate=pl.CostEstimate(flops=2 * T * D * sum(nhs) * HEAD, bytes_accessed=D * sum(nhs) * HEAD * 4, transcendentals=0),
        name="dw_proj",
    )(scal, a, *gs)
    return [o.reshape(D, nh, HEAD) for o, nh in zip(outs, nhs)]


def dwo_kernel(sc_ref, c0_ref, c1_ref, g_ref, out_ref, t_ref):
    core = sc_ref[1]
    n = c0_ref.shape[1]

    @pl.when(pl.program_id(0) == 0)
    def _():
        t_ref[pl.ds(pl.multiple_of(core * n, n), n), :] = c0_ref[...].T
        t_ref[pl.ds(pl.multiple_of((1 - core) * n, n), n), :] = c1_ref[...].T

    out_ref[...] = dotf(t_ref[...], g_ref[...], NN)


def dwo_proj(scal, c0, c1, go, db):
    T, D = go.shape
    n = c0.shape[1]
    return pl.pallas_call(
        dwo_kernel,
        grid_spec=pltpu.PrefetchScalarGridSpec(
            num_scalar_prefetch=1,
            grid=(D // db,),
            in_specs=[pl.BlockSpec((T, n), lambda i, s: (0, 0), pipeline_mode=pl.Buffered(1))] * 2
            + [pl.BlockSpec((T, db), lambda i, s: (0, i))],
            out_specs=pl.BlockSpec((2 * n, db), lambda i, s: (0, i)),
            scratch_shapes=[pltpu.VMEM((2 * n, T), BF16)],
        ),
        out_shape=jax.ShapeDtypeStruct((2 * n, D), F32),
        compiler_params=pltpu.CompilerParams(dimension_semantics=("arbitrary",), vmem_limit_bytes=VMEM_LIMIT),
        cost_estimate=pl.CostEstimate(flops=4 * T * D * n, bytes_accessed=2 * n * D * 4, transcendentals=0),
        name="dwo_proj",
    )(scal, c0, c1, go)


RB = 64


def post_kernel(p_ref, r_ref, h_ref, dy_ref, g_ref, *rest):
    y_ref, go_ref, dg_ref = rest[-3:]
    o = p_ref[...].astype(F32) + r_ref[...].astype(F32)
    inv = lax.rsqrt(jnp.mean(o * o, axis=-1, keepdims=True) + NORM_EPS)
    hat = o * inv
    g = g_ref[...]
    dy = dy_ref[...].astype(F32)
    y_ref[...] = (h_ref[...].astype(F32) + hat * g).astype(BF16)
    gg = dy * g
    go_ref[...] = (inv * (gg - hat * jnp.mean(gg * hat, axis=-1, keepdims=True))).astype(BF16)

    @pl.when(pl.program_id(0) == 0)
    def _():
        dg_ref[...] = jnp.zeros_like(dg_ref)

    dg_ref[...] += jnp.sum((dy * hat).reshape(RB // 8, 8, -1), axis=0)


def pre_kernel(p_ref, r_ref, h_ref, dy_ref, g_ref, *rest):
    dh_ref, dg_ref = rest[-2:]
    ga = p_ref[...].astype(F32) + r_ref[...].astype(F32)
    h = h_ref[...].astype(F32)
    inv = lax.rsqrt(jnp.mean(h * h, axis=-1, keepdims=True) + NORM_EPS)
    hat = h * inv
    gh = ga * g_ref[...]
    dh_ref[...] = (dy_ref[...].astype(F32) + inv * (gh - hat * jnp.mean(gh * hat, axis=-1, keepdims=True))).astype(BF16)

    @pl.when(pl.program_id(0) == 0)
    def _():
        dg_ref[...] = jnp.zeros_like(dg_ref)

    dg_ref[...] += jnp.sum((ga * hat).reshape(RB // 8, 8, -1), axis=0)


def norm_call(kernel, part, peer, hidden, d_out, g, c, buf, extra):
    M, D = part.shape
    n = M // RB
    loc = pl.BlockSpec((RB, D), lambda i: (i, 0))
    row = pl.BlockSpec((RB, D), lambda i: (c * n + i, 0))
    in_specs = [loc, loc, row, row, pl.BlockSpec((1, D), lambda i: (0, 0))]
    args = [part, peer, hidden, d_out, g.reshape(1, D)]
    aliases = {}
    if buf is not None:
        aliases = {len(args): 0}
        args.append(buf)
        in_specs.append(pl.BlockSpec(memory_space=pl.ANY))
    out_specs = [row] + ([loc] if extra else []) + [pl.BlockSpec((8, D), lambda i: (0, 0))]
    out_shape = [jax.ShapeDtypeStruct(hidden.shape, BF16)]
    if extra:
        out_shape.append(jax.ShapeDtypeStruct((M, D), BF16))
    out_shape.append(jax.ShapeDtypeStruct((8, D), F32))
    return pl.pallas_call(
        kernel, grid=(n,), in_specs=in_specs, out_specs=out_specs, out_shape=out_shape, input_output_aliases=aliases,
        compiler_params=pltpu.CompilerParams(dimension_semantics=("arbitrary",), vmem_limit_bytes=VMEM_LIMIT),
        cost_estimate=pl.CostEstimate(flops=M * D * 2000, bytes_accessed=M * D * 12, transcendentals=0),
    )(*args)


def a_kernel(h_ref, g_ref, a_ref):
    h = h_ref[...].astype(F32)
    inv = lax.rsqrt(jnp.mean(h * h, axis=-1, keepdims=True) + NORM_EPS)
    a_ref[...] = (h * inv * g_ref[...]).astype(BF16)


def a_call(hidden, g):
    M, D = hidden.shape
    row = pl.BlockSpec((RB, D), lambda i: (i, 0))
    return pl.pallas_call(
        a_kernel, grid=(M // RB,), in_specs=[row, pl.BlockSpec((1, D), lambda i: (0, 0))], out_specs=row,
        out_shape=jax.ShapeDtypeStruct((M, D), BF16),
        compiler_params=pltpu.CompilerParams(dimension_semantics=("arbitrary",)),
        cost_estimate=pl.CostEstimate(flops=M * D * 1000, bytes_accessed=M * D * 4, transcendentals=0),
        name="a_norm",
    )(hidden, g.reshape(1, D))


def solution(mesh):
    core_perm = [(0, 1), (1, 0), (2, 3), (3, 2)]
    x_perm = [(0, 2), (2, 0), (1, 3), (3, 1)]
    tp_perm = [(0, 1), (1, 0)]

    def to_core(v):
        return lax.ppermute(v, 'cp', core_perm)

    def to_x(v):
        return lax.ppermute(v, 'cp', x_perm)

    def to_tp(v):
        return lax.ppermute(v, 'tp', tp_perm)

    def device_fn(hidden, g_pre, w_q, w_k, w_v, w_o, g_post, d_out):
        tokens, D = hidden.shape
        T = 4 * tokens
        me = lax.axis_index('cp')
        tp = lax.axis_index('tp')
        core, xi = me % 2, me // 2
        HL = w_q.shape[1] // 2
        KL = w_k.shape[1] // 2
        cos, sin = rope_tables(T)
        base = jnp.stack([xi, core, me, me ^ 1]).astype(jnp.int32)
        mine, other = core * tokens, (1 - core) * tokens

        def two_way(blk, n):
            r1 = to_x(lax.dynamic_slice_in_dim(blk, tp * n, n, 0))
            r3 = to_x(blk[2 * n:])
            r2 = to_tp(r1)
            return [r1, r2, r3], [tp * n, (1 - tp) * n, 2 * n]

        def scalars(x_t, offs):
            return jnp.stack([x_t] + [jnp.asarray(o) for o in offs]).astype(jnp.int32)

        a_loc = a_call(hidden, g_pre)
        a_x, a_off = two_way(a_loc, 176)
        a_p = to_core(a_loc)
        a_xp = [to_core(r) for r in a_x]

        def w_t(w):
            return jnp.transpose(w, (1, 2, 0)).reshape(-1, D)

        wqt = w_t(w_q)
        wkt, wvt = w_t(w_k), w_t(w_v)
        wo2 = w_o.reshape(-1, D)
        nb = KL * HEAD
        ws = (wqt, wkt, wvt)
        nq = HL // KL

        def maps(ncore):
            return [
                lambda n, s: (s[ncore] * nq + jnp.minimum(n, nq - 1), 0),
                lambda n, s: (s[ncore], 0),
                lambda n, s: (s[ncore], 0),
            ]

        w_of = (0,) * nq + (1, 2)
        ropes = tuple(range(nq + 1))
        qkv, a_all = gather_matmul(scalars(xi, [mine, other, core]), [a_loc, a_p], ws, maps(3), w_of, ropes, cos, sin, T, nb)
        offs = [mine + o for o in a_off] + [other + o for o in a_off]
        qkv, a_all = gather_matmul(scalars(1 - xi, offs + [core]), a_x + a_xp, ws, maps(7), w_of, ropes, cos, sin, T, nb, bufs=(qkv, a_all))

        ctx, lse = attn_fwd(qkv, KL, HL)
        ctx_pr = to_core(lax.dynamic_slice_in_dim(ctx, (me ^ 1) * tokens, tokens, 0))
        nc = 2
        M = tokens // nc
        o_parts, o_peers = [], []
        for c in range(nc):
            op = rows_matmul(base, [ctx, ctx_pr], [lambda i, s, c=c: (s[2] * nc + c, 0), lambda i, s, c=c: (c, 0)],
                             [wo2], [(0, False, HL * HEAD), (0, True, HL * HEAD)], M, 768)
            o_parts.append(op)
            o_peers.append(to_tp(op))
        ctx_p = to_core(ctx)

        y_blk, gos, dgp = None, [], []
        for c in range(nc):
            y_blk, go, dg_ = norm_call(post_kernel, o_parts[c], o_peers[c], hidden, d_out, g_post, c, y_blk, True)
            gos.append(go)
            dgp.append(dg_)

        gx = [to_x(gos[0])]
        gx_off = [0]
        gp = [to_core(g) for g in gos]
        r, ro = two_way(gos[1], 96)
        gx += r
        gx_off += [M + o for o in ro]
        gxp = [to_core(g) for g in gx]
        own_off = [c * M for c in range(nc)]
        wo_map = lambda idx: [lambda n, s: (s[idx] * nq + n, 0)]
        offs = [mine + o for o in own_off] + [other + o for o in own_off]
        dctx, go_all = gather_matmul(scalars(xi, offs + [core]), gos + gp, (wo2,), wo_map(5), (0,) * nq, (), cos, sin, T, nb)
        offs = [mine + o for o in gx_off] + [other + o for o in gx_off]
        dctx, go_all = gather_matmul(scalars(1 - xi, offs + [core]), gx + gxp, (wo2,), wo_map(9), (0,) * nq, (), cos, sin, T, nb, bufs=(dctx, go_all))

        dqkv = attn_bwd(qkv, KL, HL, dctx, ctx, lse, cos, sin)
        dqkv_pr = [to_core(lax.dynamic_slice_in_dim(g, (me ^ 1) * tokens, tokens, 0)) for g in dqkv]
        dqkv_p = [to_core(g) for g in dqkv]
        ga_parts, ga_peers = [], []
        sizes = [HL * HEAD, KL * HEAD, KL * HEAD]
        for c in range(nc):
            gp_ = rows_matmul(base, list(dqkv) + dqkv_pr,
                              [lambda i, s, c=c: (s[2] * nc + c, 0)] * 3 + [lambda i, s, c=c: (c, 0)] * 3,
                              [wqt, wkt, wvt], [(j, o, sizes[j]) for o in (False, True) for j in range(3)], M, 512)
            ga_parts.append(gp_)
            ga_peers.append(to_tp(gp_))

        dwo = dwo_proj(base, ctx, ctx_p, go_all, 512).reshape(w_o.shape)
        dwq, dwk, dwv = dw_proj(base, a_all, [g for pair in zip(dqkv, dqkv_p) for g in pair], 256)

        grad_h, dgr = None, []
        for c in range(nc):
            grad_h, dg_ = norm_call(pre_kernel, ga_parts[c], ga_peers[c], hidden, d_out, g_pre, c, grad_h, False)
            dgr.append(dg_)
        dg = jnp.stack([sum(jnp.sum(v, axis=0) for v in dgr), sum(jnp.sum(v, axis=0) for v in dgp)])
        dg = dg + to_core(dg)
        dg = dg + to_x(dg)
        return y_blk, grad_h, dg[0], dwq, dwk, dwv, dwo, dg[1]


    row_spec = P('cp', None)
    head_spec = P(None, 'tp', None)
    out_head_spec = P('tp', None, None)
    return jax.shard_map(device_fn, mesh=mesh, in_specs=(row_spec, P(), head_spec, head_spec, head_spec, out_head_spec, P(), row_spec), out_specs=(row_spec, row_spec, P(), head_spec, head_spec, head_spec, out_head_spec, P()), check_vma=False)
```

time: 1020 us -> 854 us (0.84)
  Pallas kernels: 272 us -> 514 us
  matrix products: 167 us -> 0 us
  local copies, waits for them, and re-layouts: 231 us -> 72.3 us
  other arithmetic: 87.2 us -> 9.22 us
    pallas_call x3 -> x15, Pallas kernels: 117 us -> 359 us  [the longest x4 104 us: gather_matmul(): pl.pallas_call(functools.partial(gmm_kernel, layout=layout, rope_blocks=r...]
    dot_general x5 -> x0, matrix products: 167 us -> none  [the longest x1 51.1 us: device_fn(): qkv = jnp.dot(a_all, w_own, preferred_element_type=F32)]
    unnamed x79 -> x26, local copies, waits for them, and re-layouts: 110 us -> 7.09 us
    transpose x0 -> x3, local copies, waits for them, and re-layouts: none -> 49.6 us  [w_t(): return jnp.transpose(w, (1, 2, 0)).reshape(-1, D)]
    reshape x5 -> x2, local copies, waits for them, and re-layouts: 39 us -> 1.97 us  [the longest x1 1.35 us: a_call(): g.reshape(1, D)]
    slice x9 -> x2, local copies, waits for them, and re-layouts: 32.7 us -> 3.68 us  [two_way(): r3 = to_x(blk[2 * n:])]
    dynamic_update_slice x6 -> x0, local copies, waits for them, and re-layouts: 26.8 us -> none  [gather(): out = lax.dynamic_update_slice_in_dim(out, b, (me ^ rel) * n, 0)]
    another operation x3, other arithmetic: 22.5 us -> 1.36 us  [the longest x1 0.67 us: scalars(): return jnp.stack([x_t] + [jnp.asarray(o) for o in offs]).astype(jnp.int32)]
  transfers between devices with their start and end apart: 14 -> 31, of which waited for: 6 -> 12; matrix products, arithmetic and copies ran while one was open for 22% -> 8% of each run, Pallas kernels for 12% -> 20%
where the time goes in v2:
time: 854 us; the launch traced here: 847 us
  Pallas kernels  514 us (60%)
  waiting for transfers between devices  233 us (27%)
  local copies, waits for them, and re-layouts  72.3 us (8%)
  starting transfers between devices  16.8 us (2%)
  other arithmetic  9.22 us (1%)
    ppermute x6, waiting for transfers between devices, to_tp(): return lax.ppermute(v, 'tp', tp_perm)  159 us
    pallas_call x4, Pallas kernels, gather_matmul(): pl.pallas_call(functools.partial(gmm_kernel, layout=layout, rope_blocks=r...  104 us
    pallas_call x1, Pallas kernels, dw_proj(): pl.pallas_call(dw_kernel, grid_spec=pltpu.PrefetchScalarGridSpec(num_scal...  100 us
    pallas_call x1, Pallas kernels, attn_bwd(): pl.pallas_call(functools.partial(attn_bwd_kernel, k1=scale / SOFT_CAP, k2...  99.4 us
    ppermute x6, waiting for transfers between devices, to_x(): return lax.ppermute(v, 'cp', x_perm)  70.4 us
    pallas_call x4, Pallas kernels, rows_matmul(): pl.pallas_call(functools.partial(rows_kernel, parts=tuple(parts)), grid_s...  64.8 us
    pallas_call x1, Pallas kernels, attn_fwd(): pl.pallas_call(functools.partial(attn_fwd_kernel, k1=scale / SOFT_CAP, k2...  55.8 us
    pallas_call x1, Pallas kernels, dwo_proj(): pl.pallas_call(dwo_kernel, grid_spec=pltpu.PrefetchScalarGridSpec(num_sca...  50.1 us
  transfers between devices with their start and end apart: 31, of which 12 were waited for; matrix products, arithmetic and copies ran while one was open for 8% of the time, Pallas kernels for 20%

profile of v2, /device:TPU:0, one launch (start us, length us, event | category | flops | bytes accessed | tf_op | source)
XLA Modules:
  0.0 846.8 jit_solution(12169298856936785078)
XLA Ops:
  0.6 1.3 reshape.83.g_ref
  2.0 7.8 a_norm.1.refs_0_
  10.6 1.5 constant_dynamic-slice_fusion.5
  12.2 2.5 collective-permute-start
  14.7 36.1 %collective-permute-done.refs_0_ = bf16[176,4608]{1,0:T(8,128)(2,1)S(1)} collective-permute-done((bf16[176,4608]{1,0:T(8,128)(2,1)S(1)}, bf16[176,4608]{1,0:T(8,128)(2,1)S(1)}, u32[]{:S(2)}, u32[]{:S(2)}) %collective-permute-start) | collective-permute-done | bytes 1622048 | tf_op jit(solution)/shard_map/ppermute | solution.py:480
  50.8 1.8 collective-permute-start.1
  52.6 2.6 slice.16
  55.1 1.5 collective-permute-start.2
  56.6 24.1 %copy.22 = bf16[16,128,4608]{2,1,0:T(8,128)(2,1)} copy(bf16[16,128,4608]{1,0,2:T(8,128)(2,1)} %bitcast.48) | data formatting | bytes 37748736 | tf_op jit(solution)/shard_map/transpose | solution.py:512
  80.7 12.7 %copy.23 = bf16[8,128,4608]{2,1,0:T(8,128)(2,1)} copy(bf16[8,128,4608]{1,0,2:T(8,128)(2,1)} %bitcast.49) | data formatting | bytes 18874368 | tf_op jit(solution)/shard_map/transpose | solution.py:512
  93.5 12.7 %copy.24 = bf16[8,128,4608]{2,1,0:T(8,128)(2,1)} copy(bf16[8,128,4608]{1,0,2:T(8,128)(2,1)} %bitcast.50) | data formatting | bytes 18874368 | tf_op jit(solution)/shard_map/transpose | solution.py:512
  107.5 3.7 fusion
  111.2 2.0 pad_maximum_fusion
  113.8 33.0 %shard_map.143 = (bf16[2048,2048]{1,0:T(8,128)(2,1)}, bf16[2048,4608]{1,0:T(8,128)(2,1)}) custom-call(s32[4]{0:T(128)} %pad_add_fusion.1.sc_ref, bf16[512,4608]{1,0:T(8,128)(2,1)} %a_norm.1.refs_0_, bf16[512,4608]{1,0:T(8,128)(2,1)} %collective-permute-done.6.refs_1_, bf16[2048,4608]{1,0:T(8,128)(2,1)} %bitcast.32, bf16[1024,4608]{1,0:T(8,128)(2,1)} %bitcast.40, ...), custom_call_target="tpu_custom_call" | custom-call | flops 19327352832 | bytes 37748736 | tf_op jit(solution)/shard_map/pallas_call | solution.py:273
  146.8 33.3 %shard_map.144 = (bf16[2048,2048]{1,0:T(8,128)(2,1)}, bf16[2048,4608]{1,0:T(8,128)(2,1)}) custom-call(s32[8]{0:T(128)} %stack.106.sc_ref, bf16[176,4608]{1,0:T(8,128)(2,1)} %copy-done.8, bf16[176,4608]{1,0:T(8,128)(2,1)} %collective-permute-done.1.refs_1_, ...), custom_call_target="tpu_custom_call", output_to_operand_aliasing={{0}: (12, {}), {1}: (13, {})} | custom-call | flops 19327352832 | bytes 37748736 | tf_op jit(solution)/shard_map/pallas_call | solution.py:273
  180.1 55.8 %attn_fwd.1 = (bf16[2048,1024]{1,0:T(8,128)(2,1)}, f32[4,2,2048]{2,1,0:T(2,128)}) custom-call(bf16[2048,2048]{1,0:T(8,128)(2,1)} %get-tuple-element.36.q_ref.k_ref.v_ref, bf16[2048,2048]{1,0:T(8,128)(2,1)} %get-tuple-element.36.q_ref.k_ref.v_ref, bf16[2048,2048]{1,0:T(8,128)(2,1)} %get-tuple-element.36.q_ref.k_ref.v_ref), custom_call_target="tpu_custom_call" | custom-call | flops 17179869184 | bytes 16777216 | tf_op jit(solution)/shard_map/attn_fwd/pallas_call | solution.py:88
  235.9 1.3 constant_dynamic-slice_fusion.4
  238.4 1.6 collective-permute-done.7.refs_1_
  241.0 12.2 %shard_map.146.p_ref = bf16[256,4608]{1,0:T(8,128)(2,1)} custom-call(s32[4]{0:T(128)} %pad_add_fusion.sc_ref, bf16[2048,1024]{1,0:T(8,128)(2,1)} %get-tuple-element.37.refs_0_.ctx_ref.c0_ref, bf16[512,1024]{1,0:T(8,128)(2,1)} %copy-done.2, bf16[2048,4608]{1,0:T(8,128)(2,1)} %bitcast.36), custom_call_target="tpu_custom_call" | custom-call | flops 4831838208 | bytes 18874368 | tf_op jit(solution)/shard_map/pallas_call | solution.py:311
  253.7 12.1 %shard_map.145.p_ref = bf16[256,4608]{1,0:T(8,128)(2,1)} custom-call(s32[4]{0:T(128)} %pad_add_fusion.sc_ref, bf16[2048,1024]{1,0:T(8,128)(2,1)} %get-tuple-element.37.refs_0_.ctx_ref.c0_ref, bf16[512,1024]{1,0:T(8,128)(2,1)} %copy-done.2, bf16[2048,4608]{1,0:T(8,128)(2,1)} %bitcast.37), custom_call_target="tpu_custom_call" | custom-call | flops 4831838208 | bytes 18874368 | tf_op jit(solution)/shard_map/pallas_call | solution.py:311
  265.8 1.5 collective-permute-start.8
  267.9 39.7 %collective-permute-done.9.r_ref = bf16[256,4608]{1,0:T(8,128)(2,1)} collective-permute-done((bf16[256,4608]{1,0:T(8,128)(2,1)}, bf16[256,4608]{1,0:T(8,128)(2,1)}, u32[]{:S(2)}, u32[]{:S(2)}) %collective-permute-start.9) | collective-permute-done | bytes 2359328 | tf_op jit(solution)/shard_map/ppermute | solution.py:483
  307.6 8.4 shard_map.147
  316.5 40.9 %collective-permute-done.8.r_ref = bf16[256,4608]{1,0:T(8,128)(2,1)S(1)} collective-permute-done((bf16[256,4608]{1,0:T(8,128)(2,1)}, bf16[256,4608]{1,0:T(8,128)(2,1)S(1)}, u32[]{:S(2)}, u32[]{:S(2)}) %collective-permute-start.8) | collective-permute-done | bytes 2359328 | tf_op jit(solution)/shard_map/ppermute | solution.py:483
  357.4 1.4 copy-done.4
  358.8 8.2 shard_map.148
  367.1 1.2 constant_dynamic-slice_fusion.3
  369.1 21.4 %collective-permute-done.11.refs_1_ = bf16[96,4608]{1,0:T(8,128)(2,1)} collective-permute-done((bf16[96,4608]{1,0:T(8,128)(2,1)S(1)}, bf16[96,4608]{1,0:T(8,128)(2,1)}, u32[]{:S(2)}, u32[]{:S(2)}) %collective-permute-start.11) | collective-permute-done | bytes 884768 | tf_op jit(solution)/shard_map/ppermute | solution.py:480
  391.0 1.1 slice.13
  394.0 12.9 %collective-permute-done.13.refs_3_ = bf16[64,4608]{1,0:T(8,128)(2,1)} collective-permute-done((bf16[64,4608]{1,0:T(8,128)(2,1)S(1)}, bf16[64,4608]{1,0:T(8,128)(2,1)}, u32[]{:S(2)}, u32[]{:S(2)}) %collective-permute-start.13) | collective-permute-done | bytes 589856 | tf_op jit(solution)/shard_map/ppermute | solution.py:480
  406.8 5.1 collective-permute-done.12.refs_2_
  412.5 18.8 %shard_map.149 = (bf16[2048,1024]{1,0:T(8,128)(2,1)}, bf16[2048,4608]{1,0:T(8,128)(2,1)}) custom-call(s32[6]{0:T(128)} %stack.119.sc_ref, bf16[256,4608]{1,0:T(8,128)(2,1)} %get-tuple-element.40.refs_0_, bf16[256,4608]{1,0:T(8,128)(2,1)} %get-tuple-element.41.refs_1_, bf16[256,4608]{1,0:T(8,128)(2,1)} %collective-permute-done.18.refs_2_, ...), custom_call_target="tpu_custom_call" | custom-call | flops 9663676416 | bytes 28311552 | tf_op jit(solution)/shard_map/pallas_call | solution.py:273
  432.9 18.9 %shard_map.150 = (bf16[2048,1024]{1,0:T(8,128)(2,1)}, bf16[2048,4608]{1,0:T(8,128)(2,1)}) custom-call(s32[10]{0:T(128)} %stack.116.sc_ref, bf16[256,4608]{1,0:T(8,128)(2,1)} %collective-permute-done.10.refs_0_, bf16[96,4608]{1,0:T(8,128)(2,1)} %collective-permute-done.11.refs_1_, ...), custom_call_target="tpu_custom_call", output_to_operand_aliasing={{0}: (12, {}), {1}: (13, {})} | custom-call | flops 9663676416 | bytes 28311552 | tf_op jit(solution)/shard_map/pallas_call | solution.py:273
  451.9 99.4 %attn_bwd.1 = (bf16[2048,1024]{1,0:T(8,128)(2,1)}, bf16[2048,512]{1,0:T(8,128)(2,1)}, bf16[2048,512]{1,0:T(8,128)(2,1)}) custom-call(bf16[2048,2048]{1,0:T(8,128)(2,1)} %get-tuple-element.36.q_ref.k_ref.v_ref, bf16[2048,2048]{1,0:T(8,128)(2,1)} %get-tuple-element.36.q_ref.k_ref.v_ref, bf16[2048,2048]{1,0:T(8,128)(2,1)} %get-tuple-element.36.q_ref.k_ref.v_ref, ...), custom_call_target="tpu_custom_call" | custom-call | flops 21474836480 | bytes 25165824 | tf_op jit(solution)/shard_map/attn_bwd/pallas_call | solution.py:185
  551.3 1.3 constant_dynamic-slice_fusion.2
  552.6 1.1 constant_dynamic-slice_fusion.1
  554.2 1.1 constant_dynamic-slice_fusion
  556.0 1.2 collective-permute-done.22.refs_5_
  559.0 20.3 %shard_map.152.p_ref = bf16[256,4608]{1,0:T(8,128)(2,1)} custom-call(s32[4]{0:T(128)} %pad_add_fusion.sc_ref, bf16[2048,1024]{1,0:T(8,128)(2,1)} %get-tuple-element.46.refs_0_.q0, bf16[2048,512]{1,0:T(8,128)(2,1)} %get-tuple-element.47.refs_1_.k0, bf16[2048,512]{1,0:T(8,128)(2,1)} %get-tuple-element.48.refs_2_.v0, bf16[512,1024]{1,0:T(8,128)(2,1)} %copy-done.1, ...), custom_call_target="tpu_custom_call" | custom-call | flops 9663676416 | bytes 37748736 | tf_op jit(solution)/shard_map/pallas_call | solution.py:311
  579.8 20.3 %shard_map.151.p_ref = bf16[256,4608]{1,0:T(8,128)(2,1)} custom-call(s32[4]{0:T(128)} %pad_add_fusion.sc_ref, bf16[2048,1024]{1,0:T(8,128)(2,1)} %get-tuple-element.46.refs_0_.q0, bf16[2048,512]{1,0:T(8,128)(2,1)} %get-tuple-element.47.refs_1_.k0, bf16[2048,512]{1,0:T(8,128)(2,1)} %get-tuple-element.48.refs_2_.v0, bf16[512,1024]{1,0:T(8,128)(2,1)} %copy-done.1, ...), custom_call_target="tpu_custom_call" | custom-call | flops 9663676416 | bytes 37748736 | tf_op jit(solution)/shard_map/pallas_call | solution.py:311
  600.1 1.5 collective-permute-start.23
  601.7 32.0 %collective-permute-done.24.r_ref = bf16[256,4608]{1,0:T(8,128)(2,1)} collective-permute-done((bf16[256,4608]{1,0:T(8,128)(2,1)}, bf16[256,4608]{1,0:T(8,128)(2,1)}, u32[]{:S(2)}, u32[]{:S(2)}) %collective-permute-start.24) | collective-permute-done | bytes 2359328 | tf_op jit(solution)/shard_map/ppermute | solution.py:483
  633.7 7.5 shard_map.153
  642.2 41.1 %collective-permute-done.23.r_ref = bf16[256,4608]{1,0:T(8,128)(2,1)S(1)} collective-permute-done((bf16[256,4608]{1,0:T(8,128)(2,1)}, bf16[256,4608]{1,0:T(8,128)(2,1)S(1)}, u32[]{:S(2)}, u32[]{:S(2)}) %collective-permute-start.23) | collective-permute-done | bytes 2359328 | tf_op jit(solution)/shard_map/ppermute | solution.py:483
  683.3 1.4 copy-done.3
  684.7 7.5 shard_map.154
  695.1 50.1 %dwo_proj.1 = f32[2048,4608]{1,0:T(8,128)} custom-call(s32[4]{0:T(128)} %pad_add_fusion.sc_ref, bf16[2048,1024]{1,0:T(8,128)(2,1)} %get-tuple-element.37.refs_0_.ctx_ref.c0_ref, bf16[2048,1024]{1,0:T(8,128)(2,1)} %collective-permute-done.30.c1_ref, bf16[2048,4608]{1,0:T(8,128)(2,1)} %get-tuple-element.59.g_ref), custom_call_target="tpu_custom_call" | custom-call | flops 38654705664 | bytes 37748736 | tf_op jit(solution)/shard_map/dwo_proj/pallas_call | solution.py:375
  745.9 100.4 %dw_proj.1 = (f32[73728,128]{1,0:T(8,128)}, f32[36864,128]{1,0:T(8,128)}, f32[36864,128]{1,0:T(8,128)}) custom-call(s32[4]{0:T(128)} %pad_add_fusion.sc_ref, bf16[2048,4608]{1,0:T(8,128)(2,1)} %get-tuple-element.55.a_ref, bf16[2048,1024]{1,0:T(8,128)(2,1)} %get-tuple-element.46.refs_0_.q0, bf16[2048,1024]{1,0:T(8,128)(2,1)} %collective-permute-done.27.q1, ...), custom_call_target="tpu_custom_call" | custom-call | flops 77309411328 | bytes 75497472 | tf_op jit(solution)/shard_map/dw_proj/pallas_call | solution.py:343
  (91 shorter events, 20.0 us)
Async XLA Ops:
  9.8 104.0 %collective-permute-start.6 = (bf16[512,4608]{1,0:T(8,128)(2,1)}, bf16[512,4608]{1,0:T(8,128)(2,1)}, u32[]{:S(2)}, u32[]{:S(2)}) collective-permute-start(bf16[512,4608]{1,0:T(8,128)(2,1)} %a_norm.1.refs_0_), channel_id=1, source_target_pairs={{0,1},{1,0},{2,3},{3,2},{4,5},{5,4},{6,7},{7,6}} | collective-permute-start | bytes 14155784 | tf_op jit(solution)/shard_map/ppermute | solution.py:477
  12.2 38.6 %collective-permute-start = (bf16[176,4608]{1,0:T(8,128)(2,1)S(1)}, bf16[176,4608]{1,0:T(8,128)(2,1)S(1)}, u32[]{:S(2)}, u32[]{:S(2)}) collective-permute-start(bf16[176,4608]{1,0:T(8,128)(2,1)S(1)} %constant_dynamic-slice_fusion.5), channel_id=1, source_target_pairs={{0,2},{2,0},{1,3},{3,1},{4,6},{6,4},{5,7},{7,5}} | collective-permute-start | bytes 4866056 | tf_op jit(solution)/shard_map/ppermute | solution.py:480
  50.8 62.4 %copy-start.8 = (bf16[176,4608]{1,0:T(8,128)(2,1)}, bf16[176,4608]{1,0:T(8,128)(2,1)S(1)}, u32[]{:S(2)}) copy-start(bf16[176,4608]{1,0:T(8,128)(2,1)S(1)} %collective-permute-done.refs_0_) | copy-start | bytes 4866052
  50.8 62.9 %collective-permute-start.1 = (bf16[176,4608]{1,0:T(8,128)(2,1)S(1)}, bf16[176,4608]{1,0:T(8,128)(2,1)}, u32[]{:S(2)}, u32[]{:S(2)}) collective-permute-start(bf16[176,4608]{1,0:T(8,128)(2,1)S(1)} %collective-permute-done.refs_0_), channel_id=1, source_target_pairs={{0,4},{4,0},{1,5},{5,1},{2,6},{6,2},{3,7},{7,3}} | collective-permute-start | bytes 4866056 | tf_op jit(solution)/shard_map/ppermute | solution.py:483
  55.1 58.1 %collective-permute-start.2 = (bf16[160,4608]{1,0:T(8,128)(2,1)}, bf16[160,4608]{1,0:T(8,128)(2,1)}, u32[]{:S(2)}, u32[]{:S(2)}) collective-permute-start(bf16[160,4608]{1,0:T(8,128)(2,1)} %slice.16), channel_id=1, source_target_pairs={{0,2},{2,0},{1,3},{3,1},{4,6},{6,4},{5,7},{7,5}} | collective-permute-start | bytes 4423688 | tf_op jit(solution)/shard_map/ppermute | solution.py:480
  113.2 33.6 %collective-permute-start.5 = (bf16[160,4608]{1,0:T(8,128)(2,1)}, bf16[160,4608]{1,0:T(8,128)(2,1)}, u32[]{:S(2)}, u32[]{:S(2)}) collective-permute-start(bf16[160,4608]{1,0:T(8,128)(2,1)} %collective-permute-done.2.refs_2_), channel_id=1, source_target_pairs={{0,1},{1,0},{2,3},{3,2},{4,5},{5,4},{6,7},{7,6}} | collective-permute-start | bytes 4423688 | tf_op jit(solution)/shard_map/ppermute | solution.py:477
  113.2 33.6 %collective-permute-start.3 = (bf16[176,4608]{1,0:T(8,128)(2,1)S(1)}, bf16[176,4608]{1,0:T(8,128)(2,1)}, u32[]{:S(2)}, u32[]{:S(2)}) collective-permute-start(bf16[176,4608]{1,0:T(8,128)(2,1)S(1)} %collective-permute-done.refs_0_), channel_id=1, source_target_pairs={{0,1},{1,0},{2,3},{3,2},{4,5},{5,4},{6,7},{7,6}} | collective-permute-start | bytes 4866056 | tf_op jit(solution)/shard_map/ppermute | solution.py:477
  113.7 33.1 %collective-permute-start.4 = (bf16[176,4608]{1,0:T(8,128)(2,1)}, bf16[176,4608]{1,0:T(8,128)(2,1)}, u32[]{:S(2)}, u32[]{:S(2)}) collective-permute-start(bf16[176,4608]{1,0:T(8,128)(2,1)} %collective-permute-done.1.refs_1_), channel_id=1, source_target_pairs={{0,1},{1,0},{2,3},{3,2},{4,5},{5,4},{6,7},{7,6}} | collective-permute-start | bytes 4866056 | tf_op jit(solution)/shard_map/ppermute | solution.py:477
  237.2 2.8 collective-permute-start.7
  240.0 1.0 copy-start.2
  253.2 14.1 %copy-start.12 = (f32[4608]{0:T(1024)S(1)}, f32[4608]{0:T(1024)}, u32[]{:S(2)}) copy-start(f32[4608]{0:T(1024)} %param.14) | copy-start | bytes 55300
  253.2 54.4 %collective-permute-start.9 = (bf16[256,4608]{1,0:T(8,128)(2,1)}, bf16[256,4608]{1,0:T(8,128)(2,1)}, u32[]{:S(2)}, u32[]{:S(2)}) collective-permute-start(bf16[256,4608]{1,0:T(8,128)(2,1)} %shard_map.146.p_ref), channel_id=1, source_target_pairs={{0,4},{4,0},{1,5},{5,1},{2,6},{6,2},{3,7},{7,3}} | collective-permute-start | bytes 7077896 | tf_op jit(solution)/shard_map/ppermute | solution.py:483
  265.8 91.5 %collective-permute-start.8 = (bf16[256,4608]{1,0:T(8,128)(2,1)}, bf16[256,4608]{1,0:T(8,128)(2,1)S(1)}, u32[]{:S(2)}, u32[]{:S(2)}) collective-permute-start(bf16[256,4608]{1,0:T(8,128)(2,1)} %shard_map.145.p_ref), channel_id=1, source_target_pairs={{0,4},{4,0},{1,5},{5,1},{2,6},{6,2},{3,7},{7,3}} | collective-permute-start | bytes 7077896 | tf_op jit(solution)/shard_map/ppermute | solution.py:483
  316.0 52.8 %collective-permute-start.10 = (bf16[256,4608]{1,0:T(8,128)(2,1)}, bf16[256,4608]{1,0:T(8,128)(2,1)}, u32[]{:S(2)}, u32[]{:S(2)}) collective-permute-start(bf16[256,4608]{1,0:T(8,128)(2,1)} %get-tuple-element.40.refs_0_), channel_id=1, source_target_pairs={{0,2},{2,0},{1,3},{3,1},{4,6},{6,4},{5,7},{7,5}} | collective-permute-start | bytes 7077896 | tf_op jit(solution)/shard_map/ppermute | solution.py:480
  316.5 95.5 %collective-permute-start.18 = (bf16[256,4608]{1,0:T(8,128)(2,1)}, bf16[256,4608]{1,0:T(8,128)(2,1)}, u32[]{:S(2)}, u32[]{:S(2)}) collective-permute-start(bf16[256,4608]{1,0:T(8,128)(2,1)} %get-tuple-element.40.refs_0_), channel_id=1, source_target_pairs={{0,1},{1,0},{2,3},{3,2},{4,5},{5,4},{6,7},{7,6}} | collective-permute-start | bytes 7077896 | tf_op jit(solution)/shard_map/ppermute | solution.py:477
  357.4 1.4 copy-start.4
  367.0 45.5 %collective-permute-start.19 = (bf16[256,4608]{1,0:T(8,128)(2,1)}, bf16[256,4608]{1,0:T(8,128)(2,1)}, u32[]{:S(2)}, u32[]{:S(2)}) collective-permute-start(bf16[256,4608]{1,0:T(8,128)(2,1)} %get-tuple-element.41.refs_1_), channel_id=1, source_target_pairs={{0,1},{1,0},{2,3},{3,2},{4,5},{5,4},{6,7},{7,6}} | collective-permute-start | bytes 7077896 | tf_op jit(solution)/shard_map/ppermute | solution.py:477
  368.3 22.2 %collective-permute-start.11 = (bf16[96,4608]{1,0:T(8,128)(2,1)S(1)}, bf16[96,4608]{1,0:T(8,128)(2,1)}, u32[]{:S(2)}, u32[]{:S(2)}) collective-permute-start(bf16[96,4608]{1,0:T(8,128)(2,1)S(1)} %constant_dynamic-slice_fusion.3), channel_id=1, source_target_pairs={{0,2},{2,0},{1,3},{3,1},{4,6},{6,4},{5,7},{7,5}} | collective-permute-start | bytes 2654216 | tf_op jit(solution)/shard_map/ppermute | solution.py:480
  368.9 62.5 %collective-permute-start.14 = (bf16[256,4608]{1,0:T(8,128)(2,1)}, bf16[256,4608]{1,0:T(8,128)(2,1)S(1)}, u32[]{:S(2)}, u32[]{:S(2)}) collective-permute-start(bf16[256,4608]{1,0:T(8,128)(2,1)} %collective-permute-done.10.refs_0_), channel_id=1, source_target_pairs={{0,1},{1,0},{2,3},{3,2},{4,5},{5,4},{6,7},{7,6}} | collective-permute-start | bytes 7077896 | tf_op jit(solution)/shard_map/ppermute | solution.py:477
  390.5 21.5 %collective-permute-start.12 = (bf16[96,4608]{1,0:T(8,128)(2,1)}, bf16[96,4608]{1,0:T(8,128)(2,1)}, u32[]{:S(2)}, u32[]{:S(2)}) collective-permute-start(bf16[96,4608]{1,0:T(8,128)(2,1)} %collective-permute-done.11.refs_1_), channel_id=1, source_target_pairs={{0,4},{4,0},{1,5},{5,1},{2,6},{6,2},{3,7},{7,3}} | collective-permute-start | bytes 2654216 | tf_op jit(solution)/shard_map/ppermute | solution.py:483
  392.1 14.7 %collective-permute-start.13 = (bf16[64,4608]{1,0:T(8,128)(2,1)S(1)}, bf16[64,4608]{1,0:T(8,128)(2,1)}, u32[]{:S(2)}, u32[]{:S(2)}) collective-permute-start(bf16[64,4608]{1,0:T(8,128)(2,1)S(1)} %slice.13), channel_id=1, source_target_pairs={{0,2},{2,0},{1,3},{3,1},{4,6},{6,4},{5,7},{7,5}} | collective-permute-start | bytes 1769480 | tf_op jit(solution)/shard_map/ppermute | solution.py:480
  406.8 24.5 %collective-permute-start.17 = (bf16[64,4608]{1,0:T(8,128)(2,1)}, bf16[64,4608]{1,0:T(8,128)(2,1)S(1)}, u32[]{:S(2)}, u32[]{:S(2)}) collective-permute-start(bf16[64,4608]{1,0:T(8,128)(2,1)} %collective-permute-done.13.refs_3_), channel_id=1, source_target_pairs={{0,1},{1,0},{2,3},{3,2},{4,5},{5,4},{6,7},{7,6}} | collective-permute-start | bytes 1769480 | tf_op jit(solution)/shard_map/ppermute | solution.py:477
  412.0 19.4 %collective-permute-start.15 = (bf16[96,4608]{1,0:T(8,128)(2,1)}, bf16[96,4608]{1,0:T(8,128)(2,1)}, u32[]{:S(2)}, u32[]{:S(2)}) collective-permute-start(bf16[96,4608]{1,0:T(8,128)(2,1)} %collective-permute-done.11.refs_1_), channel_id=1, source_target_pairs={{0,1},{1,0},{2,3},{3,2},{4,5},{5,4},{6,7},{7,6}} | collective-permute-start | bytes 2654216 | tf_op jit(solution)/shard_map/ppermute | solution.py:477
  412.0 19.4 %collective-permute-start.16 = (bf16[96,4608]{1,0:T(8,128)(2,1)}, bf16[96,4608]{1,0:T(8,128)(2,1)}, u32[]{:S(2)}, u32[]{:S(2)}) collective-permute-start(bf16[96,4608]{1,0:T(8,128)(2,1)} %collective-permute-done.12.refs_2_), channel_id=1, source_target_pairs={{0,1},{1,0},{2,3},{3,2},{4,5},{5,4},{6,7},{7,6}} | collective-permute-start | bytes 2654216 | tf_op jit(solution)/shard_map/ppermute | solution.py:477
  431.3 0.9 copy-start.9
  431.4 1.5 copy-start.5
  552.6 4.6 collective-permute-start.20
  553.7 2.3 collective-permute-start.21
  555.3 1.9 collective-permute-start.22
  556.0 1.2 copy-start.6
  557.2 0.8 copy-start.7
  558.0 1.0 copy-start.1
  579.2 22.3 %copy-start.10 = (f32[8,4608]{1,0:T(8,128)S(1)}, f32[8,4608]{1,0:T(8,128)}, u32[]{:S(2)}) copy-start(f32[8,4608]{1,0:T(8,128)} %get-tuple-element.53) | copy-start | bytes 442372
  579.2 22.4 %copy-start.11 = (f32[8,4608]{1,0:T(8,128)S(1)}, f32[8,4608]{1,0:T(8,128)}, u32[]{:S(2)}) copy-start(f32[8,4608]{1,0:T(8,128)} %get-tuple-element.54) | copy-start | bytes 442372
  579.2 54.5 %collective-permute-start.24 = (bf16[256,4608]{1,0:T(8,128)(2,1)}, bf16[256,4608]{1,0:T(8,128)(2,1)}, u32[]{:S(2)}, u32[]{:S(2)}) collective-permute-start(bf16[256,4608]{1,0:T(8,128)(2,1)} %shard_map.152.p_ref), channel_id=1, source_target_pairs={{0,4},{4,0},{1,5},{5,1},{2,6},{6,2},{3,7},{7,3}} | collective-permute-start | bytes 7077896 | tf_op jit(solution)/shard_map/ppermute | solution.py:483
  600.1 83.2 %collective-permute-start.23 = (bf16[256,4608]{1,0:T(8,128)(2,1)}, bf16[256,4608]{1,0:T(8,128)(2,1)S(1)}, u32[]{:S(2)}, u32[]{:S(2)}) collective-permute-start(bf16[256,4608]{1,0:T(8,128)(2,1)} %shard_map.151.p_ref), channel_id=1, source_target_pairs={{0,4},{4,0},{1,5},{5,1},{2,6},{6,2},{3,7},{7,3}} | collective-permute-start | bytes 7077896 | tf_op jit(solution)/shard_map/ppermute | solution.py:483
  601.6 93.5 %collective-permute-start.30 = (bf16[2048,1024]{1,0:T(8,128)(2,1)}, bf16[2048,1024]{1,0:T(8,128)(2,1)}, u32[]{:S(2)}, u32[]{:S(2)}) collective-permute-start(bf16[2048,1024]{1,0:T(8,128)(2,1)} %get-tuple-element.37.refs_0_.ctx_ref.c0_ref), channel_id=1, source_target_pairs={{0,1},{1,0},{2,3},{3,2},{4,5},{5,4},{6,7},{7,6}} | collective-permute-start | bytes 12582920 | tf_op jit(solution)/shard_map/ppermute | solution.py:477
  683.3 1.4 copy-start.3
  684.7 9.0 %copy-start = (bf16[2048,512]{1,0:T(8,128)(2,1)S(1)}, bf16[2048,512]{1,0:T(8,128)(2,1)}, u32[]{:S(2)}) copy-start(bf16[2048,512]{1,0:T(8,128)(2,1)} %get-tuple-element.47.refs_1_.k0) | copy-start | bytes 6291460
  693.2 1.2 collective-permute-start.25
  693.3 52.6 %collective-permute-start.27 = (bf16[2048,1024]{1,0:T(8,128)(2,1)}, bf16[2048,1024]{1,0:T(8,128)(2,1)}, u32[]{:S(2)}, u32[]{:S(2)}) collective-permute-start(bf16[2048,1024]{1,0:T(8,128)(2,1)} %get-tuple-element.46.refs_0_.q0), channel_id=1, source_target_pairs={{0,1},{1,0},{2,3},{3,2},{4,5},{5,4},{6,7},{7,6}} | collective-permute-start | bytes 12582920 | tf_op jit(solution)/shard_map/ppermute | solution.py:477
  693.8 52.1 %collective-permute-start.28 = (bf16[2048,512]{1,0:T(8,128)(2,1)S(1)}, bf16[2048,512]{1,0:T(8,128)(2,1)}, u32[]{:S(2)}, u32[]{:S(2)}) collective-permute-start(bf16[2048,512]{1,0:T(8,128)(2,1)S(1)} %copy-done), channel_id=1, source_target_pairs={{0,1},{1,0},{2,3},{3,2},{4,5},{5,4},{6,7},{7,6}} | collective-permute-start | bytes 6291464 | tf_op jit(solution)/shard_map/ppermute | solution.py:477
  693.8 52.1 %collective-permute-start.29 = (bf16[2048,512]{1,0:T(8,128)(2,1)}, bf16[2048,512]{1,0:T(8,128)(2,1)}, u32[]{:S(2)}, u32[]{:S(2)}) collective-permute-start(bf16[2048,512]{1,0:T(8,128)(2,1)} %get-tuple-element.48.refs_2_.v0), channel_id=1, source_target_pairs={{0,1},{1,0},{2,3},{3,2},{4,5},{5,4},{6,7},{7,6}} | collective-permute-start | bytes 6291464 | tf_op jit(solution)/shard_map/ppermute | solution.py:477
  694.5 50.6 %collective-permute-start.26 = (f32[2,4608]{1,0:T(2,128)S(1)}, f32[2,4608]{1,0:T(2,128)S(1)}, u32[]{:S(2)}, u32[]{:S(2)}) collective-permute-start(f32[2,4608]{1,0:T(2,128)S(1)} %fusion.1), channel_id=1, source_target_pairs={{0,2},{2,0},{1,3},{3,1},{4,6},{6,4},{5,7},{7,5}} | collective-permute-start | bytes 110600 | tf_op jit(solution)/shard_map/ppermute | solution.py:480

commit v3 on v2

--- a/solution.py
+++ b/solution.py
@@ -205,122 +205,193 @@
 
 
 VMEM_LIMIT = 64_000_000
-
-
-def gmm_kernel(sc_ref, *refs, layout, rope_blocks, n_w, w_of, aliased):
+KD = 512
+
+
+def load_pieces(pieces, layout, sc_ref, x_ref, sem):
+    cps = []
+    for i, (slot, n) in enumerate(layout):
+        blk = sc_ref[slot]
+        off = pl.multiple_of(sc_ref[slot + 1], 16)
+        cps.append(pltpu.make_async_copy(pieces[i], x_ref.at[blk, pl.ds(off, n)], sem.at[i]))
+    return cps
+
+
+def gmm_kernel(sc_ref, *refs, layout, mode, n_w, R, r0, aliased):
     np_ = len(layout)
     pieces = refs[:np_]
     ws = refs[np_:np_ + n_w]
-    cos_ref, sin_ref = refs[np_ + n_w:np_ + n_w + 2]
-    rest = refs[np_ + n_w + 2:]
+    rest = refs[np_ + n_w:]
+    if mode == "qkv":
+        cos_ref, sin_ref = rest[:2]
+        rest = rest[2:]
     if aliased:
         rest = rest[2:]
-    out_ref, all_ref, x_ref, sem_in, sem_out = rest
-    n = pl.program_id(0)
+    out_ref, all_ref, x_ref, acc_ref, w_ref, sem_in, sem_out = rest
+    i = pl.program_id(0)
     last = pl.num_programs(0) - 1
-    half = x_ref.shape[0]
-    xt = sc_ref[0]
-    dst = pl.multiple_of(xt * half, half)
-
-    def off(i):
-        return pl.multiple_of(sc_ref[1 + i], 16)
-
-    def cp_in(i):
-        return pltpu.make_async_copy(pieces[i], x_ref.at[pl.ds(off(i), layout[i])], sem_in.at[i])
-
-    def cp_out():
-        return pltpu.make_async_copy(x_ref, all_ref.at[pl.ds(dst, half)], sem_out)
-
-    @pl.when(n == 0)
-    def _():
-        for i in range(np_):
-            cp_in(i).start()
-        for i in range(np_):
-            cp_in(i).wait()
-        cp_out().start()
-
-    for b, wi in enumerate(w_of):
-        @pl.when(n == b)
-        def _(b=b, wi=wi):
-            res = dotf(x_ref[...], ws[wi][...], NT)
-            if b in rope_blocks:
-                c, s = cos_ref[...], sin_ref[...]
-                for h in range(res.shape[1] // HEAD):
-                    r = res[:, h * HEAD:(h + 1) * HEAD]
-                    out_ref[:, h * HEAD:(h + 1) * HEAD] = (r * c + pltpu.roll(r, HEAD // 2, 1) * s).astype(BF16)
+    B = x_ref.shape[0]
+    core = sc_ref[1]
+    cps = load_pieces(pieces, layout, sc_ref, x_ref, sem_in)
+    outs = [pltpu.make_async_copy(x_ref.at[b], all_ref.at[sc_ref[0] * B + b, pl.ds(r0, R)], sem_out.at[b]) for b in range(B)]
+
+    @pl.when(i == 0)
+    def _():
+        for c in cps:
+            c.start()
+        for c in cps:
+            c.wait()
+        for c in outs:
+            c.start()
+
+    ks = pl.ds(pl.multiple_of(i * KD, KD), KD)
+
+    def products(b):
+        x = x_ref[b, :, ks]
+        if mode == "qkv":
+            n = w_ref.shape[2] // 2
+            half = pl.ds(pl.multiple_of(core * n, n), n)
+            return [dotf(x, w_ref[0], NN), dotf(x, w_ref[1, :, half], NN), dotf(x, w_ref[2, :, half], NN)]
+        return [dotf(x, ws[0][...], NT)]
+
+    if mode == "qkv":
+        for j in range(3):
+            w_ref[j] = ws[j][...].reshape(w_ref.shape[1:])
+
+    @pl.when(i == 0)
+    def _():
+        for b in range(B):
+            o = 0
+            for d in products(b):
+                acc_ref[b, :, o:o + d.shape[1]] = d
+                o += d.shape[1]
+
+    @pl.when(i > 0)
+    def _():
+        for b in range(B):
+            o = 0
+            for d in products(b):
+                acc_ref[b, :, o:o + d.shape[1]] += d
+                o += d.shape[1]
+
+    @pl.when(i == last)
+    def _():
+        N = acc_ref.shape[2]
+        for b in range(B):
+            if mode == "qkv":
+                n_rope = N * 3 // 4
+                c, s = cos_ref[b], sin_ref[b]
+                for h in range(n_rope // HEAD):
+                    r = acc_ref[b, :, h * HEAD:(h + 1) * HEAD]
+                    out_ref[b, :, h * HEAD:(h + 1) * HEAD] = (r * c + pltpu.roll(r, HEAD // 2, 1) * s).astype(BF16)
+                out_ref[b, :, n_rope:] = acc_ref[b, :, n_rope:].astype(BF16)
             else:
-                out_ref[...] = res.astype(BF16)
-
-    @pl.when(n == last)
-    def _():
-        cp_out().wait()
-
-
-def gather_matmul(scal, pieces, ws, w_maps, w_of, rope_blocks, cos, sin, T, nb, bufs=None):
+                out_ref[b] = acc_ref[b].astype(BF16)
+        for c in outs:
+            c.wait()
+
+
+def gather_matmul(chip, core, places, pieces, ws, mode, tabs, B, R, r0, N, bufs=None):
     D = pieces[0].shape[1]
-    half = T // 2
-    nblk = len(w_of)
-    layout = tuple(p.shape[0] for p in pieces)
+    tokens = 512
+    nk = D // KD
+    scal = jnp.stack([jnp.asarray(v, jnp.int32) for v in [chip, core] + [v for p in places for v in p]])
+    layout = tuple((2 + 2 * i, p.shape[0]) for i, p in enumerate(pieces))
     anyspec = pl.BlockSpec(memory_space=pl.ANY)
-    tab = pl.BlockSpec((half, HEAD), lambda n, s: (s[0], 0), pipeline_mode=pl.Buffered(1))
-    in_specs = [anyspec] * len(pieces) + [pl.BlockSpec((nb, D), m) for m in w_maps] + [tab, tab]
-    args = list(pieces) + list(ws) + [cos, sin]
+    if mode == "qkv":
+        hb = ws[1].shape[1]
+        w_specs = [pl.BlockSpec((KD, hb, HEAD), lambda i, s: (i, s[1], 0))] + [pl.BlockSpec((KD, hb, HEAD), lambda i, s: (i, 0, 0))] * 2
+        w_specs += [pl.BlockSpec((B, R, HEAD), lambda i, s: (s[0], 0, 0), pipeline_mode=pl.Buffered(1))] * 2
+        wscr = pltpu.VMEM((3, KD, hb * HEAD), BF16)
+    else:
+        w_specs = [pl.BlockSpec((N, KD), lambda i, s: (s[1], i))]
+        wscr = pltpu.VMEM((1, 16, HEAD), BF16)
+    in_specs = [anyspec] * len(pieces) + w_specs
+    args = list(pieces) + list(ws) + [t.reshape(4, tokens, HEAD) for t in tabs]
     aliases = {}
     if bufs is not None:
         aliases = {1 + len(args): 0, 2 + len(args): 1}
         in_specs += [anyspec, anyspec]
         args += list(bufs)
     return pl.pallas_call(
-        functools.partial(gmm_kernel, layout=layout, rope_blocks=rope_blocks, n_w=len(ws), w_of=w_of, aliased=bufs is not None),
+        functools.partial(gmm_kernel, layout=layout, mode=mode, n_w=len(ws), R=R, r0=r0, aliased=bufs is not None),
         grid_spec=pltpu.PrefetchScalarGridSpec(
             num_scalar_prefetch=1,
-            grid=(nblk,),
+            grid=(nk,),
             in_specs=in_specs,
-            out_specs=[pl.BlockSpec((half, nb), lambda n, s: (s[0], n)), anyspec],
+            out_specs=[pl.BlockSpec((B, R, N), lambda i, s: (s[0], r0 // R, 0), pipeline_mode=pl.Buffered(1)), anyspec],
             scratch_shapes=[
-                pltpu.VMEM((half, D), BF16),
+                pltpu.VMEM((B, R, D), BF16),
+                pltpu.VMEM((B, R, N), F32),
+                wscr,
                 pltpu.SemaphoreType.DMA((len(pieces),)),
-                pltpu.SemaphoreType.DMA,
+                pltpu.SemaphoreType.DMA((B,)),
             ],
         ),
-        out_shape=[jax.ShapeDtypeStruct((T, nblk * nb), BF16), jax.ShapeDtypeStruct((T, D), BF16)],
+        out_shape=[jax.ShapeDtypeStruct((4, tokens, N), BF16), jax.ShapeDtypeStruct((4, tokens, D), BF16)],
         input_output_aliases=aliases,
         compiler_params=pltpu.CompilerParams(dimension_semantics=("arbitrary",), vmem_limit_bytes=VMEM_LIMIT),
-        cost_estimate=pl.CostEstimate(flops=2 * half * D * nblk * nb, bytes_accessed=half * D * 4 + nblk * nb * D * 2, transcendentals=0),
+        cost_estimate=pl.CostEstimate(flops=2 * B * R * D * N, bytes_accessed=B * R * D * 4 + N * D * 2, transcendentals=0),
     )(scal, *args)
 
 
-def rows_kernel(sc_ref, *refs, parts):
-    n_l = len(parts)
-    n_w = 1 + max(p[0] for p in parts)
-    lhs = refs[:n_l]
-    ws = refs[n_l:n_l + n_w]
-    out_ref = refs[n_l + n_w]
+def orow_kernel(sc_ref, c0_ref, c1_ref, w_ref, out_ref):
     core = sc_ref[1]
-    acc = None
-    for ref, (wi, other, rows) in zip(lhs, parts):
-        c = 1 - core if other else core
-        d = dotf(ref[...], ws[wi][pl.ds(pl.multiple_of(c * rows, rows), rows), :], NN)
-        acc = d if acc is None else acc + d
-    out_ref[...] = acc.astype(BF16)
-
-
-def rows_matmul(scal, lhs, lhs_maps, ws, parts, M, db):
-    D = ws[0].shape[1]
-    flops = 2 * M * D * sum(p[2] for p in parts)
-    return pl.pallas_call(
-        functools.partial(rows_kernel, parts=tuple(parts)),
+    n = c0_ref.shape[1]
+    own = w_ref[pl.ds(pl.multiple_of(core * n, n), n), :]
+    oth = w_ref[pl.ds(pl.multiple_of((1 - core) * n, n), n), :]
+    out_ref[...] = (dotf(c0_ref[...], own, NN) + dotf(c1_ref[...], oth, NN)).astype(BF16)
+
+
+def o_rows(scal, ctx, ctx_pr, w, c, nc, M, db):
+    n, D = ctx.shape[1], w.shape[1]
+    return pl.pallas_call(
+        orow_kernel,
         grid_spec=pltpu.PrefetchScalarGridSpec(
             num_scalar_prefetch=1,
             grid=(D // db,),
-            in_specs=[pl.BlockSpec((M, l.shape[1]), m) for l, m in zip(lhs, lhs_maps)]
-            + [pl.BlockSpec((w.shape[0], db), lambda i, s: (0, i)) for w in ws],
+            in_specs=[
+                pl.BlockSpec((M, n), lambda i, s: (s[2] * nc + c, 0)),
+                pl.BlockSpec((M, n), lambda i, s: (c, 0)),
+                pl.BlockSpec((2 * n, db), lambda i, s: (0, i)),
+            ],
             out_specs=pl.BlockSpec((M, db), lambda i, s: (0, i)),
         ),
         out_shape=jax.ShapeDtypeStruct((M, D), BF16),
         compiler_params=pltpu.CompilerParams(dimension_semantics=("arbitrary",), vmem_limit_bytes=VMEM_LIMIT),
-        cost_estimate=pl.CostEstimate(flops=flops, bytes_accessed=sum(w.size for w in ws) * 2, transcendentals=0),
-    )(scal, *lhs, *ws)
+        cost_estimate=pl.CostEstimate(flops=4 * M * D * n, bytes_accessed=w.size * 2, transcendentals=0),
+    )(scal, ctx, ctx_pr, w)
+
+
+def ga_kernel(sc_ref, q0, k0, v0, q1, k1, v1, wq_ref, wk_ref, wv_ref, out_ref, wq_s, wk_s, wv_s):
+    core = sc_ref[1]
+    acc = None
+    for w_ref, s_ref, own, oth in ((wq_ref, wq_s, q0, q1), (wk_ref, wk_s, k0, k1), (wv_ref, wv_s, v0, v1)):
+        s_ref[...] = w_ref[...].reshape(s_ref.shape)
+        n = own.shape[1]
+        for c, g in ((core, own), (1 - core, oth)):
+            d = dotf(g[...], s_ref[:, pl.ds(pl.multiple_of(c * n, n), n)], NT)
+            acc = d if acc is None else acc + d
+    out_ref[...] = acc.astype(BF16)
+
+
+def ga_rows(scal, own, oth, ws, M, db):
+    D = ws[0].shape[0]
+    return pl.pallas_call(
+        ga_kernel,
+        grid_spec=pltpu.PrefetchScalarGridSpec(
+            num_scalar_prefetch=1,
+            grid=(D // db,),
+            in_specs=[pl.BlockSpec((M, g.shape[1]), lambda i, s: (s[2], 0)) for g in own]
+            + [pl.BlockSpec((M, g.shape[1]), lambda i, s: (0, 0)) for g in oth]
+            + [pl.BlockSpec((db,) + w.shape[1:], lambda i, s: (i, 0, 0)) for w in ws],
+            out_specs=pl.BlockSpec((M, db), lambda i, s: (0, i)),
+            scratch_shapes=[pltpu.VMEM((db, w.shape[1] * HEAD), BF16) for w in ws],
+        ),
+        out_shape=jax.ShapeDtypeStruct((M, D), BF16),
+        compiler_params=pltpu.CompilerParams(dimension_semantics=("arbitrary",), vmem_limit_bytes=VMEM_LIMIT),
+        cost_estimate=pl.CostEstimate(flops=2 * M * sum(w.size for w in ws), bytes_accessed=sum(w.size for w in ws) * 2, transcendentals=0),
+    )(scal, *own, *oth, *ws)
 
 
 def dw_kernel(sc_ref, a_ref, q0, q1, k0, k1, v0, v1, oq_ref, ok_ref, ov_ref):
@@ -490,9 +561,8 @@
         core, xi = me % 2, me // 2
         HL = w_q.shape[1] // 2
         KL = w_k.shape[1] // 2
-        cos, sin = rope_tables(T)
+        cos, sin = lax.optimization_barrier(rope_tables(T))
         base = jnp.stack([xi, core, me, me ^ 1]).astype(jnp.int32)
-        mine, other = core * tokens, (1 - core) * tokens
 
         def two_way(blk, n):
             r1 = to_x(lax.dynamic_slice_in_dim(blk, tp * n, n, 0))
@@ -500,45 +570,26 @@
             r2 = to_tp(r1)
             return [r1, r2, r3], [tp * n, (1 - tp) * n, 2 * n]
 
-        def scalars(x_t, offs):
-            return jnp.stack([x_t] + [jnp.asarray(o) for o in offs]).astype(jnp.int32)
-
         a_loc = a_call(hidden, g_pre)
         a_x, a_off = two_way(a_loc, 176)
         a_p = to_core(a_loc)
         a_xp = [to_core(r) for r in a_x]
-
-        def w_t(w):
-            return jnp.transpose(w, (1, 2, 0)).reshape(-1, D)
-
-        wqt = w_t(w_q)
-        wkt, wvt = w_t(w_k), w_t(w_v)
         wo2 = w_o.reshape(-1, D)
-        nb = KL * HEAD
-        ws = (wqt, wkt, wvt)
-        nq = HL // KL
-
-        def maps(ncore):
-            return [
-                lambda n, s: (s[ncore] * nq + jnp.minimum(n, nq - 1), 0),
-                lambda n, s: (s[ncore], 0),
-                lambda n, s: (s[ncore], 0),
-            ]
-
-        w_of = (0,) * nq + (1, 2)
-        ropes = tuple(range(nq + 1))
-        qkv, a_all = gather_matmul(scalars(xi, [mine, other, core]), [a_loc, a_p], ws, maps(3), w_of, ropes, cos, sin, T, nb)
-        offs = [mine + o for o in a_off] + [other + o for o in a_off]
-        qkv, a_all = gather_matmul(scalars(1 - xi, offs + [core]), a_x + a_xp, ws, maps(7), w_of, ropes, cos, sin, T, nb, bufs=(qkv, a_all))
+        N = (HL + 2 * KL) * HEAD
+        qkv_args = ((w_q, w_k, w_v), "qkv", (cos, sin), 2, tokens, 0, N)
+        bufs = gather_matmul(xi, core, [(core, 0), (1 - core, 0)], [a_loc, a_p], *qkv_args)
+        places = [(core, o) for o in a_off] + [(1 - core, o) for o in a_off]
+        qkv, a_all = gather_matmul(1 - xi, core, places, a_x + a_xp, *qkv_args, bufs=bufs)
+        qkv = qkv.reshape(T, N)
+        a_all = a_all.reshape(T, D)
 
         ctx, lse = attn_fwd(qkv, KL, HL)
         ctx_pr = to_core(lax.dynamic_slice_in_dim(ctx, (me ^ 1) * tokens, tokens, 0))
-        nc = 2
+        nc = 4
         M = tokens // nc
         o_parts, o_peers = [], []
         for c in range(nc):
-            op = rows_matmul(base, [ctx, ctx_pr], [lambda i, s, c=c: (s[2] * nc + c, 0), lambda i, s, c=c: (c, 0)],
-                             [wo2], [(0, False, HL * HEAD), (0, True, HL * HEAD)], M, 768)
+            op = o_rows(base, ctx, ctx_pr, wo2, c, nc, M, 1536)
             o_parts.append(op)
             o_peers.append(to_tp(op))
         ctx_p = to_core(ctx)
@@ -549,40 +600,33 @@
             gos.append(go)
             dgp.append(dg_)
 
-        gx = [to_x(gos[0])]
-        gx_off = [0]
+        gx = [to_x(g) for g in gos[:-1]]
         gp = [to_core(g) for g in gos]
-        r, ro = two_way(gos[1], 96)
-        gx += r
-        gx_off += [M + o for o in ro]
+        r, r_off = two_way(gos[-1], 48)
         gxp = [to_core(g) for g in gx]
-        own_off = [c * M for c in range(nc)]
-        wo_map = lambda idx: [lambda n, s: (s[idx] * nq + n, 0)]
-        offs = [mine + o for o in own_off] + [other + o for o in own_off]
-        dctx, go_all = gather_matmul(scalars(xi, offs + [core]), gos + gp, (wo2,), wo_map(5), (0,) * nq, (), cos, sin, T, nb)
-        offs = [mine + o for o in gx_off] + [other + o for o in gx_off]
-        dctx, go_all = gather_matmul(scalars(1 - xi, offs + [core]), gx + gxp, (wo2,), wo_map(9), (0,) * nq, (), cos, sin, T, nb, bufs=(dctx, go_all))
+        rp = [to_core(g) for g in r]
+        HN = HL * HEAD
+        early = [c * M for c in range(nc - 1)]
+        RE = (nc - 1) * M
+        places = [(core, o) for o in early] + [(1 - core, o) for o in early]
+        bufs = gather_matmul(xi, core, places, gos[:-1] + gp[:-1], (wo2,), "nt", (), 2, RE, 0, HN)
+        bufs = gather_matmul(1 - xi, core, places, gx + gxp, (wo2,), "nt", (), 2, RE, 0, HN, bufs=bufs)
+        places = [(me, 0), (me ^ 1, 0)] + [(me ^ 2, o) for o in r_off] + [(me ^ 3, o) for o in r_off]
+        dctx, go_all = gather_matmul(0, core, places, [gos[-1], gp[-1]] + r + rp, (wo2,), "nt", (), 4, M, RE, HN, bufs=bufs)
+        dctx = dctx.reshape(T, HN)
+        go_all = go_all.reshape(T, D)
 
         dqkv = attn_bwd(qkv, KL, HL, dctx, ctx, lse, cos, sin)
         dqkv_pr = [to_core(lax.dynamic_slice_in_dim(g, (me ^ 1) * tokens, tokens, 0)) for g in dqkv]
         dqkv_p = [to_core(g) for g in dqkv]
-        ga_parts, ga_peers = [], []
-        sizes = [HL * HEAD, KL * HEAD, KL * HEAD]
-        for c in range(nc):
-            gp_ = rows_matmul(base, list(dqkv) + dqkv_pr,
-                              [lambda i, s, c=c: (s[2] * nc + c, 0)] * 3 + [lambda i, s, c=c: (c, 0)] * 3,
-                              [wqt, wkt, wvt], [(j, o, sizes[j]) for o in (False, True) for j in range(3)], M, 512)
-            ga_parts.append(gp_)
-            ga_peers.append(to_tp(gp_))
+        ga_part = ga_rows(base, dqkv, dqkv_pr, (w_q, w_k, w_v), tokens, 512)
+        ga_peer = to_tp(ga_part)
 
         dwo = dwo_proj(base, ctx, ctx_p, go_all, 512).reshape(w_o.shape)
         dwq, dwk, dwv = dw_proj(base, a_all, [g for pair in zip(dqkv, dqkv_p) for g in pair], 256)
 
-        grad_h, dgr = None, []
-        for c in range(nc):
-            grad_h, dg_ = norm_call(pre_kernel, ga_parts[c], ga_peers[c], hidden, d_out, g_pre, c, grad_h, False)
-            dgr.append(dg_)
-        dg = jnp.stack([sum(jnp.sum(v, axis=0) for v in dgr), sum(jnp.sum(v, axis=0) for v in dgp)])
+        grad_h, dgr = norm_call(pre_kernel, ga_part, ga_peer, hidden, d_out, g_pre, 0, None, False)
+        dg = jnp.stack([jnp.sum(dgr, axis=0), jnp.sum(sum(dgp), axis=0)])
         dg = dg + to_core(dg)
         dg = dg + to_x(dg)
         return y_blk, grad_h, dg[0], dwq, dwk, dwv, dwo, dg[1]

time: 854 us -> 893 us (1.046)
  local copies, waits for them, and re-layouts: 72.3 us -> 21.6 us
  waiting for transfers between devices: 233 us -> 283 us
  Pallas kernels: 514 us -> 545 us
  starting transfers between devices: 16.8 us -> 25.9 us
    ppermute x6 -> x8, waiting for transfers between devices: 70.4 us -> 124 us  [to_x(): return lax.ppermute(v, 'cp', x_perm)]
    transpose x3 -> x0, local copies, waits for them, and re-layouts: 49.6 us -> none  [w_t(): return jnp.transpose(w, (1, 2, 0)).reshape(-1, D)]
    pallas_call x8 -> x10, Pallas kernels: 169 us -> 198 us  [the longest x5 124 us: gather_matmul(): pl.pallas_call(functools.partial(gmm_kernel, layout=layout, mode=mode, n_...]
    ppermute x6 -> x7, waiting for transfers between devices: 159 us -> 154 us  [to_tp(): return lax.ppermute(v, 'tp', tp_perm)]
    pallas_call x4 -> x5, Pallas kernels: 31.7 us -> 33.3 us  [norm_call(): pl.pallas_call(kernel, grid=(n,), in_specs=in_specs, out_specs=out_specs,...]
  transfers between devices with their start and end apart: 31 -> 38, of which waited for: 12 -> 13; matrix products, arithmetic and copies ran while one was open for 8% -> 2% of each run, Pallas kernels for 20% -> 32%
where the time goes in v3:
time: 893 us; the launch traced here: 884 us
  Pallas kernels  545 us (61%)
  waiting for transfers between devices  283 us (32%)
  starting transfers between devices  25.9 us (3%)
  local copies, waits for them, and re-layouts  21.6 us (2%)
    ppermute x7, waiting for transfers between devices, to_tp(): return lax.ppermute(v, 'tp', tp_perm)  154 us
    pallas_call x5, Pallas kernels, gather_matmul(): pl.pallas_call(functools.partial(gmm_kernel, layout=layout, mode=mode, n_...  124 us
    ppermute x8, waiting for transfers between devices, to_x(): return lax.ppermute(v, 'cp', x_perm)  124 us
    pallas_call x1, Pallas kernels, dw_proj(): pl.pallas_call(dw_kernel, grid_spec=pltpu.PrefetchScalarGridSpec(num_scal...  100 us
    pallas_call x1, Pallas kernels, attn_bwd(): pl.pallas_call(functools.partial(attn_bwd_kernel, k1=scale / SOFT_CAP, k2...  99.8 us
    pallas_call x1, Pallas kernels, attn_fwd(): pl.pallas_call(functools.partial(attn_fwd_kernel, k1=scale / SOFT_CAP, k2...  55.6 us
    pallas_call x1, Pallas kernels, dwo_proj(): pl.pallas_call(dwo_kernel, grid_spec=pltpu.PrefetchScalarGridSpec(num_sca...  50.2 us
    pallas_call x4, Pallas kernels, o_rows(): pl.pallas_call(orow_kernel, grid_spec=pltpu.PrefetchScalarGridSpec(num_sc...  38 us
  transfers between devices with their start and end apart: 38, of which 13 were waited for; matrix products, arithmetic and copies ran while one was open for 2% of the time, Pallas kernels for 32%

profile of v3, /device:TPU:0, one launch (start us, length us, event | category | flops | bytes accessed | tf_op | source)
XLA Modules:
  0.0 883.9 jit_solution(8032971186459268785)
XLA Ops:
  0.6 1.3 reshape.71.g_ref
  2.0 7.8 a_norm.1.refs_0_
  10.6 1.5 constant_dynamic-slice_fusion.5
  12.2 2.5 collective-permute-start
  14.7 36.1 %collective-permute-done.refs_0_ = bf16[176,4608]{1,0:T(8,128)(2,1)S(1)} collective-permute-done((bf16[176,4608]{1,0:T(8,128)(2,1)S(1)}, bf16[176,4608]{1,0:T(8,128)(2,1)S(1)}, u32[]{:S(2)}, u32[]{:S(2)}) %collective-permute-start) | collective-permute-done | bytes 1622048 | tf_op jit(solution)/shard_map/ppermute | solution.py:551
  50.8 1.8 collective-permute-start.1
  52.6 2.6 slice.16
  55.1 1.5 collective-permute-start.2
  56.6 3.7 fusion
  60.4 2.0 pad_maximum_fusion
  63.6 25.4 %collective-permute-done.2.refs_2_ = bf16[160,4608]{1,0:T(8,128)(2,1)} collective-permute-done((bf16[160,4608]{1,0:T(8,128)(2,1)}, bf16[160,4608]{1,0:T(8,128)(2,1)}, u32[]{:S(2)}, u32[]{:S(2)}) %collective-permute-start.2) | collective-permute-done | bytes 1474592 | tf_op jit(solution)/shard_map/ppermute | solution.py:551
  89.6 35.0 %shard_map.143 = (bf16[4,512,2048]{2,1,0:T(8,128)(2,1)}, bf16[4,512,4608]{2,1,0:T(8,128)(2,1)}) custom-call(s32[6]{0:T(128)} %stack.52.sc_ref, bf16[512,4608]{1,0:T(8,128)(2,1)} %a_norm.1.refs_0_, bf16[512,4608]{1,0:T(8,128)(2,1)} %collective-permute-done.6.refs_1_, bf16[4608,16,128]{2,1,0:T(8,128)(2,1)} %wq_ref.1, bf16[4608,8,128]{2,1,0:T(8,128)(2,1)} %wk_ref.1, ...), custom_call_target="tpu_custom_call" | custom-call | flops 19327352832 | bytes 37748736 | tf_op jit(solution)/shard_map/pallas_call | solution.py:316
  124.6 35.3 %shard_map.144 = (bf16[4,512,2048]{2,1,0:T(8,128)(2,1)}, bf16[4,512,4608]{2,1,0:T(8,128)(2,1)}) custom-call(s32[14]{0:T(128)} %stack.51.sc_ref, bf16[176,4608]{1,0:T(8,128)(2,1)} %copy-done.1, bf16[176,4608]{1,0:T(8,128)(2,1)} %collective-permute-done.1.refs_1_, ...), custom_call_target="tpu_custom_call", output_to_operand_aliasing={{0}: (12, {}), {1}: (13, {})} | custom-call | flops 19327352832 | bytes 37748736 | tf_op jit(solution)/shard_map/pallas_call | solution.py:316
  159.9 55.6 %attn_fwd.1 = (bf16[2048,1024]{1,0:T(8,128)(2,1)}, f32[4,2,2048]{2,1,0:T(2,128)}) custom-call(bf16[2048,2048]{1,0:T(8,128)(2,1)} %bitcast.33, bf16[2048,2048]{1,0:T(8,128)(2,1)} %bitcast.34, bf16[2048,2048]{1,0:T(8,128)(2,1)} %bitcast.35), custom_call_target="tpu_custom_call" | custom-call | flops 17179869184 | bytes 16777216 | tf_op jit(solution)/shard_map/attn_fwd/pallas_call | solution.py:88
  215.5 1.3 constant_dynamic-slice_fusion.4
  218.0 1.7 collective-permute-done.7.c1_ref
  220.7 9.5 %shard_map.146.p_ref = bf16[128,4608]{1,0:T(8,128)(2,1)} custom-call(s32[4]{0:T(128)} %pad_add_fusion.sc_ref, bf16[2048,1024]{1,0:T(8,128)(2,1)} %get-tuple-element.47.c0_ref.ctx_ref, bf16[512,1024]{1,0:T(8,128)(2,1)} %copy-done, bf16[2048,4608]{1,0:T(8,128)(2,1)} %bitcast.23), custom_call_target="tpu_custom_call" | custom-call | flops 2415919104 | bytes 18874368 | tf_op jit(solution)/shard_map/pallas_call | solution.py:348
  231.1 9.5 %shard_map.148.p_ref = bf16[128,4608]{1,0:T(8,128)(2,1)} custom-call(s32[4]{0:T(128)} %pad_add_fusion.sc_ref, bf16[2048,1024]{1,0:T(8,128)(2,1)} %get-tuple-element.47.c0_ref.ctx_ref, bf16[512,1024]{1,0:T(8,128)(2,1)} %copy-done, bf16[2048,4608]{1,0:T(8,128)(2,1)} %bitcast.24), custom_call_target="tpu_custom_call" | custom-call | flops 2415919104 | bytes 18874368 | tf_op jit(solution)/shard_map/pallas_call | solution.py:348
  240.6 1.2 collective-permute-start.11
  241.7 9.5 %shard_map.147.p_ref = bf16[128,4608]{1,0:T(8,128)(2,1)} custom-call(s32[4]{0:T(128)} %pad_add_fusion.sc_ref, bf16[2048,1024]{1,0:T(8,128)(2,1)} %get-tuple-element.47.c0_ref.ctx_ref, bf16[512,1024]{1,0:T(8,128)(2,1)} %copy-done, bf16[2048,4608]{1,0:T(8,128)(2,1)} %bitcast.25), custom_call_target="tpu_custom_call" | custom-call | flops 2415919104 | bytes 18874368 | tf_op jit(solution)/shard_map/pallas_call | solution.py:348
  252.1 9.5 %shard_map.145.p_ref = bf16[128,4608]{1,0:T(8,128)(2,1)} custom-call(s32[4]{0:T(128)} %pad_add_fusion.sc_ref, bf16[2048,1024]{1,0:T(8,128)(2,1)} %get-tuple-element.47.c0_ref.ctx_ref, bf16[512,1024]{1,0:T(8,128)(2,1)} %copy-done, bf16[2048,4608]{1,0:T(8,128)(2,1)} %bitcast.26), custom_call_target="tpu_custom_call" | custom-call | flops 2415919104 | bytes 18874368 | tf_op jit(solution)/shard_map/pallas_call | solution.py:348
  263.4 21.1 %collective-permute-done.11.r_ref = bf16[128,4608]{1,0:T(8,128)(2,1)S(1)} collective-permute-done((bf16[128,4608]{1,0:T(8,128)(2,1)}, bf16[128,4608]{1,0:T(8,128)(2,1)S(1)}, u32[]{:S(2)}, u32[]{:S(2)}) %collective-permute-start.11) | collective-permute-done | bytes 1179680 | tf_op jit(solution)/shard_map/ppermute | solution.py:554
  285.6 5.0 shard_map.149
  290.6 1.5 collective-permute-start.19
  292.1 17.8 %collective-permute-done.10.r_ref = bf16[128,4608]{1,0:T(8,128)(2,1)} collective-permute-done((bf16[128,4608]{1,0:T(8,128)(2,1)}, bf16[128,4608]{1,0:T(8,128)(2,1)}, u32[]{:S(2)}, u32[]{:S(2)}) %collective-permute-start.10) | collective-permute-done | bytes 1179680 | tf_op jit(solution)/shard_map/ppermute | solution.py:554
  309.9 5.3 shard_map.150
  316.2 5.0 shard_map.151
  321.2 13.4 %collective-permute-done.8.r_ref = bf16[128,4608]{1,0:T(8,128)(2,1)} collective-permute-done((bf16[128,4608]{1,0:T(8,128)(2,1)}, bf16[128,4608]{1,0:T(8,128)(2,1)}, u32[]{:S(2)}, u32[]{:S(2)}) %collective-permute-start.8) | collective-permute-done | bytes 1179680 | tf_op jit(solution)/shard_map/ppermute | solution.py:554
  334.6 5.1 shard_map.152
  340.6 1.5 collective-permute-start.15
  342.7 1.5 collective-permute-start.21
  345.2 5.3 collective-permute-done.15.refs_4_
  350.6 1.5 collective-permute-start.13
  352.1 57.1 %collective-permute-done.13.refs_2_ = bf16[48,4608]{1,0:T(8,128)(2,1)S(1)} collective-permute-done((bf16[48,4608]{1,0:T(8,128)(2,1)S(1)}, bf16[48,4608]{1,0:T(8,128)(2,1)S(1)}, u32[]{:S(2)}, u32[]{:S(2)}) %collective-permute-start.13) | collective-permute-done | bytes 442400 | tf_op jit(solution)/shard_map/ppermute | solution.py:551
  412.7 1.3 collective-permute-done.27.refs_5_
  414.9 17.3 %shard_map.153 = (bf16[4,512,1024]{2,1,0:T(8,128)(2,1)}, bf16[4,512,4608]{2,1,0:T(8,128)(2,1)}) custom-call(s32[14]{0:T(128)} %stack.117.sc_ref, bf16[128,4608]{1,0:T(8,128)(2,1)} %get-tuple-element.53.refs_0_, bf16[128,4608]{1,0:T(8,128)(2,1)} %get-tuple-element.54.refs_1_, bf16[128,4608]{1,0:T(8,128)(2,1)} %get-tuple-element.55.refs_2_, ...), custom_call_target="tpu_custom_call" | custom-call | flops 7247757312 | bytes 23592960 | tf_op jit(solution)/shard_map/pallas_call | solution.py:316
  432.8 17.3 %shard_map.154 = (bf16[4,512,1024]{2,1,0:T(8,128)(2,1)}, bf16[4,512,4608]{2,1,0:T(8,128)(2,1)}) custom-call(s32[14]{0:T(128)} %stack.116.sc_ref, bf16[128,4608]{1,0:T(8,128)(2,1)} %copy-done.2, bf16[128,4608]{1,0:T(8,128)(2,1)} %copy-done.3, bf16[128,4608]{1,0:T(8,128)(2,1)} %collective-permute-done.21.refs_2_, ...), custom_call_target="tpu_custom_call", output_to_operand_aliasing={{0}: (8, {}), {1}: (9, {})} | custom-call | flops 7247757312 | bytes 23592960 | tf_op jit(solution)/shard_map/pallas_call | solution.py:316
  451.1 19.4 %shard_map.155 = (bf16[4,512,1024]{2,1,0:T(8,128)(2,1)}, bf16[4,512,4608]{2,1,0:T(8,128)(2,1)}) custom-call(s32[18]{0:T(128)} %stack.57.sc_ref, bf16[128,4608]{1,0:T(8,128)(2,1)} %get-tuple-element.52.refs_0_, bf16[128,4608]{1,0:T(8,128)(2,1)} %collective-permute-done.12.refs_1_, ...), custom_call_target="tpu_custom_call", output_to_operand_aliasing={{0}: (10, {}), {1}: (11, {})} | custom-call | flops 4831838208 | bytes 18874368 | tf_op jit(solution)/shard_map/pallas_call | solution.py:316
  470.5 99.8 %attn_bwd.1 = (bf16[2048,1024]{1,0:T(8,128)(2,1)}, bf16[2048,512]{1,0:T(8,128)(2,1)}, bf16[2048,512]{1,0:T(8,128)(2,1)}) custom-call(bf16[2048,2048]{1,0:T(8,128)(2,1)} %bitcast.36, bf16[2048,2048]{1,0:T(8,128)(2,1)} %bitcast.37, bf16[2048,2048]{1,0:T(8,128)(2,1)} %bitcast.38, bf16[2048,1024]{1,0:T(8,128)(2,1)} %bitcast.32, ...), custom_call_target="tpu_custom_call" | custom-call | flops 21474836480 | bytes 25165824 | tf_op jit(solution)/shard_map/attn_bwd/pallas_call | solution.py:185
  570.3 1.3 constant_dynamic-slice_fusion.2
  575.1 1.3 collective-permute-done.30.v1
  577.2 35.2 %shard_map.156.p_ref = bf16[512,4608]{1,0:T(8,128)(2,1)} custom-call(s32[4]{0:T(128)} %pad_add_fusion.sc_ref, bf16[2048,1024]{1,0:T(8,128)(2,1)} %get-tuple-element.62.q0, bf16[2048,512]{1,0:T(8,128)(2,1)} %get-tuple-element.63.k0, bf16[2048,512]{1,0:T(8,128)(2,1)} %get-tuple-element.64.v0, bf16[512,1024]{1,0:T(8,128)(2,1)} %collective-permute-done.28.q1, ...), custom_call_target="tpu_custom_call" | custom-call | flops 19327352832 | bytes 37748736 | tf_op jit(solution)/shard_map/pallas_call | solution.py:380
  612.4 1.2 collective-permute-start.31
  614.7 102.2 %collective-permute-done.31.r_ref = bf16[512,4608]{1,0:T(8,128)(2,1)} collective-permute-done((bf16[512,4608]{1,0:T(8,128)(2,1)}, bf16[512,4608]{1,0:T(8,128)(2,1)}, u32[]{:S(2)}, u32[]{:S(2)}) %collective-permute-start.31) | collective-permute-done | bytes 4718624 | tf_op jit(solution)/shard_map/ppermute | solution.py:554
  716.9 12.9 %shard_map.157 = (bf16[512,4608]{1,0:T(8,128)(2,1)}, f32[8,4608]{1,0:T(8,128)}) custom-call(bf16[512,4608]{1,0:T(8,128)(2,1)} %shard_map.156.p_ref, bf16[512,4608]{1,0:T(8,128)(2,1)} %collective-permute-done.31.r_ref, bf16[512,4608]{1,0:T(8,128)(2,1)} %h_ref.11, bf16[512,4608]{1,0:T(8,128)(2,1)} %dy_ref.9, f32[1,4608]{1,0:T(1,128)} %reshape.71.g_ref), custom_call_target="tpu_custom_call" | custom-call | flops 4718592000 | bytes 28311552 | tf_op jit(solution)/shard_map/pallas_call | solution.py:517
  730.8 50.2 %dwo_proj.1 = f32[2048,4608]{1,0:T(8,128)} custom-call(s32[4]{0:T(128)} %pad_add_fusion.sc_ref, bf16[2048,1024]{1,0:T(8,128)(2,1)} %get-tuple-element.47.c0_ref.ctx_ref, bf16[2048,1024]{1,0:T(8,128)(2,1)} %collective-permute-done.37.c1_ref, bf16[2048,4608]{1,0:T(8,128)(2,1)} %bitcast.30), custom_call_target="tpu_custom_call" | custom-call | flops 38654705664 | bytes 37748736 | tf_op jit(solution)/shard_map/dwo_proj/pallas_call | solution.py:446
  781.1 1.4 collective-permute-start.33
  782.6 100.4 %dw_proj.1 = (f32[73728,128]{1,0:T(8,128)}, f32[36864,128]{1,0:T(8,128)}, f32[36864,128]{1,0:T(8,128)}) custom-call(s32[4]{0:T(128)} %pad_add_fusion.sc_ref, bf16[2048,4608]{1,0:T(8,128)(2,1)} %bitcast.31, bf16[2048,1024]{1,0:T(8,128)(2,1)} %get-tuple-element.62.q0, bf16[2048,1024]{1,0:T(8,128)(2,1)} %collective-permute-done.34.q1, ...), custom_call_target="tpu_custom_call" | custom-call | flops 77309411328 | bytes 75497472 | tf_op jit(solution)/shard_map/dw_proj/pallas_call | solution.py:414
  (112 shorter events, 26.1 us)
Async XLA Ops:
  9.8 79.8 %collective-permute-start.6 = (bf16[512,4608]{1,0:T(8,128)(2,1)}, bf16[512,4608]{1,0:T(8,128)(2,1)}, u32[]{:S(2)}, u32[]{:S(2)}) collective-permute-start(bf16[512,4608]{1,0:T(8,128)(2,1)} %a_norm.1.refs_0_), channel_id=1, source_target_pairs={{0,1},{1,0},{2,3},{3,2},{4,5},{5,4},{6,7},{7,6}} | collective-permute-start | bytes 14155784 | tf_op jit(solution)/shard_map/ppermute | solution.py:548
  12.2 38.6 %collective-permute-start = (bf16[176,4608]{1,0:T(8,128)(2,1)S(1)}, bf16[176,4608]{1,0:T(8,128)(2,1)S(1)}, u32[]{:S(2)}, u32[]{:S(2)}) collective-permute-start(bf16[176,4608]{1,0:T(8,128)(2,1)S(1)} %constant_dynamic-slice_fusion.5), channel_id=1, source_target_pairs={{0,2},{2,0},{1,3},{3,1},{4,6},{6,4},{5,7},{7,5}} | collective-permute-start | bytes 4866056 | tf_op jit(solution)/shard_map/ppermute | solution.py:551
  50.8 38.2 %copy-start.1 = (bf16[176,4608]{1,0:T(8,128)(2,1)}, bf16[176,4608]{1,0:T(8,128)(2,1)S(1)}, u32[]{:S(2)}) copy-start(bf16[176,4608]{1,0:T(8,128)(2,1)S(1)} %collective-permute-done.refs_0_) | copy-start | bytes 4866052
  50.8 38.7 %collective-permute-start.1 = (bf16[176,4608]{1,0:T(8,128)(2,1)S(1)}, bf16[176,4608]{1,0:T(8,128)(2,1)}, u32[]{:S(2)}, u32[]{:S(2)}) collective-permute-start(bf16[176,4608]{1,0:T(8,128)(2,1)S(1)} %collective-permute-done.refs_0_), channel_id=1, source_target_pairs={{0,4},{4,0},{1,5},{5,1},{2,6},{6,2},{3,7},{7,3}} | collective-permute-start | bytes 4866056 | tf_op jit(solution)/shard_map/ppermute | solution.py:554
  55.1 33.9 %collective-permute-start.2 = (bf16[160,4608]{1,0:T(8,128)(2,1)}, bf16[160,4608]{1,0:T(8,128)(2,1)}, u32[]{:S(2)}, u32[]{:S(2)}) collective-permute-start(bf16[160,4608]{1,0:T(8,128)(2,1)} %slice.16), channel_id=1, source_target_pairs={{0,2},{2,0},{1,3},{3,1},{4,6},{6,4},{5,7},{7,5}} | collective-permute-start | bytes 4423688 | tf_op jit(solution)/shard_map/ppermute | solution.py:551
  89.0 35.5 %collective-permute-start.5 = (bf16[160,4608]{1,0:T(8,128)(2,1)}, bf16[160,4608]{1,0:T(8,128)(2,1)}, u32[]{:S(2)}, u32[]{:S(2)}) collective-permute-start(bf16[160,4608]{1,0:T(8,128)(2,1)} %collective-permute-done.2.refs_2_), channel_id=1, source_target_pairs={{0,1},{1,0},{2,3},{3,2},{4,5},{5,4},{6,7},{7,6}} | collective-permute-start | bytes 4423688 | tf_op jit(solution)/shard_map/ppermute | solution.py:548
  89.0 35.5 %collective-permute-start.3 = (bf16[176,4608]{1,0:T(8,128)(2,1)S(1)}, bf16[176,4608]{1,0:T(8,128)(2,1)}, u32[]{:S(2)}, u32[]{:S(2)}) collective-permute-start(bf16[176,4608]{1,0:T(8,128)(2,1)S(1)} %collective-permute-done.refs_0_), channel_id=1, source_target_pairs={{0,1},{1,0},{2,3},{3,2},{4,5},{5,4},{6,7},{7,6}} | collective-permute-start | bytes 4866056 | tf_op jit(solution)/shard_map/ppermute | solution.py:548
  89.5 35.0 %collective-permute-start.4 = (bf16[176,4608]{1,0:T(8,128)(2,1)}, bf16[176,4608]{1,0:T(8,128)(2,1)}, u32[]{:S(2)}, u32[]{:S(2)}) collective-permute-start(bf16[176,4608]{1,0:T(8,128)(2,1)} %collective-permute-done.1.refs_1_), channel_id=1, source_target_pairs={{0,1},{1,0},{2,3},{3,2},{4,5},{5,4},{6,7},{7,6}} | collective-permute-start | bytes 4866056 | tf_op jit(solution)/shard_map/ppermute | solution.py:548
  216.8 2.9 collective-permute-start.7
  230.2 85.0 %collective-permute-start.9 = (bf16[128,4608]{1,0:T(8,128)(2,1)}, bf16[128,4608]{1,0:T(8,128)(2,1)S(1)}, u32[]{:S(2)}, u32[]{:S(2)}) collective-permute-start(bf16[128,4608]{1,0:T(8,128)(2,1)} %shard_map.146.p_ref), channel_id=1, source_target_pairs={{0,4},{4,0},{1,5},{5,1},{2,6},{6,2},{3,7},{7,3}} | collective-permute-start | bytes 3538952 | tf_op jit(solution)/shard_map/ppermute | solution.py:554
  240.6 43.9 %collective-permute-start.11 = (bf16[128,4608]{1,0:T(8,128)(2,1)}, bf16[128,4608]{1,0:T(8,128)(2,1)S(1)}, u32[]{:S(2)}, u32[]{:S(2)}) collective-permute-start(bf16[128,4608]{1,0:T(8,128)(2,1)} %shard_map.148.p_ref), channel_id=1, source_target_pairs={{0,4},{4,0},{1,5},{5,1},{2,6},{6,2},{3,7},{7,3}} | collective-permute-start | bytes 3538952 | tf_op jit(solution)/shard_map/ppermute | solution.py:554
  251.2 58.7 %collective-permute-start.10 = (bf16[128,4608]{1,0:T(8,128)(2,1)}, bf16[128,4608]{1,0:T(8,128)(2,1)}, u32[]{:S(2)}, u32[]{:S(2)}) collective-permute-start(bf16[128,4608]{1,0:T(8,128)(2,1)} %shard_map.147.p_ref), channel_id=1, source_target_pairs={{0,4},{4,0},{1,5},{5,1},{2,6},{6,2},{3,7},{7,3}} | collective-permute-start | bytes 3538952 | tf_op jit(solution)/shard_map/ppermute | solution.py:554
  261.6 73.0 %collective-permute-start.8 = (bf16[128,4608]{1,0:T(8,128)(2,1)}, bf16[128,4608]{1,0:T(8,128)(2,1)}, u32[]{:S(2)}, u32[]{:S(2)}) collective-permute-start(bf16[128,4608]{1,0:T(8,128)(2,1)} %shard_map.145.p_ref), channel_id=1, source_target_pairs={{0,4},{4,0},{1,5},{5,1},{2,6},{6,2},{3,7},{7,3}} | collective-permute-start | bytes 3538952 | tf_op jit(solution)/shard_map/ppermute | solution.py:554
  290.6 118.5 %collective-permute-start.19 = (bf16[128,4608]{1,0:T(8,128)(2,1)}, bf16[128,4608]{1,0:T(8,128)(2,1)S(1)}, u32[]{:S(2)}, u32[]{:S(2)}) collective-permute-start(bf16[128,4608]{1,0:T(8,128)(2,1)} %get-tuple-element.53.refs_0_), channel_id=1, source_target_pairs={{0,2},{2,0},{1,3},{3,1},{4,6},{6,4},{5,7},{7,5}} | collective-permute-start | bytes 3538952 | tf_op jit(solution)/shard_map/ppermute | solution.py:551
  292.1 118.0 %collective-permute-start.25 = (bf16[128,4608]{1,0:T(8,128)(2,1)}, bf16[128,4608]{1,0:T(8,128)(2,1)}, u32[]{:S(2)}, u32[]{:S(2)}) collective-permute-start(bf16[128,4608]{1,0:T(8,128)(2,1)} %get-tuple-element.53.refs_0_), channel_id=1, source_target_pairs={{0,1},{1,0},{2,3},{3,2},{4,5},{5,4},{6,7},{7,6}} | collective-permute-start | bytes 3538952 | tf_op jit(solution)/shard_map/ppermute | solution.py:548
  340.6 9.9 %collective-permute-start.15 = (bf16[32,4608]{1,0:T(8,128)(2,1)S(1)}, bf16[32,4608]{1,0:T(8,128)(2,1)S(1)}, u32[]{:S(2)}, u32[]{:S(2)}) collective-permute-start(bf16[32,4608]{1,0:T(8,128)(2,1)S(1)} %slice.13), channel_id=1, source_target_pairs={{0,2},{2,0},{1,3},{3,1},{4,6},{6,4},{5,7},{7,5}} | collective-permute-start | bytes 884744 | tf_op jit(solution)/shard_map/ppermute | solution.py:551
  342.2 67.5 %collective-permute-start.20 = (bf16[128,4608]{1,0:T(8,128)(2,1)}, bf16[128,4608]{1,0:T(8,128)(2,1)S(1)}, u32[]{:S(2)}, u32[]{:S(2)}) collective-permute-start(bf16[128,4608]{1,0:T(8,128)(2,1)} %get-tuple-element.54.refs_1_), channel_id=1, source_target_pairs={{0,2},{2,0},{1,3},{3,1},{4,6},{6,4},{5,7},{7,5}} | collective-permute-start | bytes 3538952 | tf_op jit(solution)/shard_map/ppermute | solution.py:551
  342.7 67.0 %collective-permute-start.21 = (bf16[128,4608]{1,0:T(8,128)(2,1)}, bf16[128,4608]{1,0:T(8,128)(2,1)}, u32[]{:S(2)}, u32[]{:S(2)}) collective-permute-start(bf16[128,4608]{1,0:T(8,128)(2,1)} %get-tuple-element.55.refs_2_), channel_id=1, source_target_pairs={{0,2},{2,0},{1,3},{3,1},{4,6},{6,4},{5,7},{7,5}} | collective-permute-start | bytes 3538952 | tf_op jit(solution)/shard_map/ppermute | solution.py:551
  350.6 59.2 %copy-start.9 = (bf16[32,4608]{1,0:T(8,128)(2,1)}, bf16[32,4608]{1,0:T(8,128)(2,1)S(1)}, u32[]{:S(2)}) copy-start(bf16[32,4608]{1,0:T(8,128)(2,1)S(1)} %collective-permute-done.15.refs_4_) | copy-start | bytes 884740
  350.6 58.6 %collective-permute-start.13 = (bf16[48,4608]{1,0:T(8,128)(2,1)S(1)}, bf16[48,4608]{1,0:T(8,128)(2,1)S(1)}, u32[]{:S(2)}, u32[]{:S(2)}) collective-permute-start(bf16[48,4608]{1,0:T(8,128)(2,1)S(1)} %constant_dynamic-slice_fusion.3), channel_id=1, source_target_pairs={{0,2},{2,0},{1,3},{3,1},{4,6},{6,4},{5,7},{7,5}} | collective-permute-start | bytes 1327112 | tf_op jit(solution)/shard_map/ppermute | solution.py:551
  409.1 23.1 %copy-start.6 = (bf16[48,4608]{1,0:T(8,128)(2,1)}, bf16[48,4608]{1,0:T(8,128)(2,1)S(1)}, u32[]{:S(2)}) copy-start(bf16[48,4608]{1,0:T(8,128)(2,1)S(1)} %collective-permute-done.13.refs_2_) | copy-start | bytes 1327108
  409.1 3.2 collective-permute-start.26
  409.1 23.0 %copy-start.2 = (bf16[128,4608]{1,0:T(8,128)(2,1)}, bf16[128,4608]{1,0:T(8,128)(2,1)S(1)}, u32[]{:S(2)}) copy-start(bf16[128,4608]{1,0:T(8,128)(2,1)S(1)} %collective-permute-done.19.refs_0_) | copy-start | bytes 3538948
  409.2 4.9 collective-permute-start.27
  409.7 22.5 %copy-start.3 = (bf16[128,4608]{1,0:T(8,128)(2,1)}, bf16[128,4608]{1,0:T(8,128)(2,1)S(1)}, u32[]{:S(2)}) copy-start(bf16[128,4608]{1,0:T(8,128)(2,1)S(1)} %collective-permute-done.20.refs_1_) | copy-start | bytes 3538948
  409.7 22.6 %collective-permute-start.22 = (bf16[128,4608]{1,0:T(8,128)(2,1)S(1)}, bf16[128,4608]{1,0:T(8,128)(2,1)}, u32[]{:S(2)}, u32[]{:S(2)}) collective-permute-start(bf16[128,4608]{1,0:T(8,128)(2,1)S(1)} %collective-permute-done.19.refs_0_), channel_id=1, source_target_pairs={{0,1},{1,0},{2,3},{3,2},{4,5},{5,4},{6,7},{7,6}} | collective-permute-start | bytes 3538952 | tf_op jit(solution)/shard_map/ppermute | solution.py:548
  409.7 23.0 %collective-permute-start.23 = (bf16[128,4608]{1,0:T(8,128)(2,1)S(1)}, bf16[128,4608]{1,0:T(8,128)(2,1)}, u32[]{:S(2)}, u32[]{:S(2)}) collective-permute-start(bf16[128,4608]{1,0:T(8,128)(2,1)S(1)} %collective-permute-done.20.refs_1_), channel_id=1, source_target_pairs={{0,1},{1,0},{2,3},{3,2},{4,5},{5,4},{6,7},{7,6}} | collective-permute-start | bytes 3538952 | tf_op jit(solution)/shard_map/ppermute | solution.py:548
  410.2 22.6 %collective-permute-start.24 = (bf16[128,4608]{1,0:T(8,128)(2,1)}, bf16[128,4608]{1,0:T(8,128)(2,1)}, u32[]{:S(2)}, u32[]{:S(2)}) collective-permute-start(bf16[128,4608]{1,0:T(8,128)(2,1)} %collective-permute-done.21.refs_2_), channel_id=1, source_target_pairs={{0,1},{1,0},{2,3},{3,2},{4,5},{5,4},{6,7},{7,6}} | collective-permute-start | bytes 3538952 | tf_op jit(solution)/shard_map/ppermute | solution.py:548
  412.3 37.8 %collective-permute-start.12 = (bf16[128,4608]{1,0:T(8,128)(2,1)}, bf16[128,4608]{1,0:T(8,128)(2,1)}, u32[]{:S(2)}, u32[]{:S(2)}) collective-permute-start(bf16[128,4608]{1,0:T(8,128)(2,1)} %get-tuple-element.52.refs_0_), channel_id=1, source_target_pairs={{0,1},{1,0},{2,3},{3,2},{4,5},{5,4},{6,7},{7,6}} | collective-permute-start | bytes 3538952 | tf_op jit(solution)/shard_map/ppermute | solution.py:548
  414.0 18.2 %collective-permute-start.14 = (bf16[48,4608]{1,0:T(8,128)(2,1)S(1)}, bf16[48,4608]{1,0:T(8,128)(2,1)}, u32[]{:S(2)}, u32[]{:S(2)}) collective-permute-start(bf16[48,4608]{1,0:T(8,128)(2,1)S(1)} %collective-permute-done.13.refs_2_), channel_id=1, source_target_pairs={{0,4},{4,0},{1,5},{5,1},{2,6},{6,2},{3,7},{7,3}} | collective-permute-start | bytes 1327112 | tf_op jit(solution)/shard_map/ppermute | solution.py:554
  432.2 17.9 %collective-permute-start.18 = (bf16[32,4608]{1,0:T(8,128)(2,1)}, bf16[32,4608]{1,0:T(8,128)(2,1)}, u32[]{:S(2)}, u32[]{:S(2)}) collective-permute-start(bf16[32,4608]{1,0:T(8,128)(2,1)} %copy-done.9), channel_id=1, source_target_pairs={{0,1},{1,0},{2,3},{3,2},{4,5},{5,4},{6,7},{7,6}} | collective-permute-start | bytes 884744 | tf_op jit(solution)/shard_map/ppermute | solution.py:548
  432.3 17.9 %collective-permute-start.16 = (bf16[48,4608]{1,0:T(8,128)(2,1)S(1)}, bf16[48,4608]{1,0:T(8,128)(2,1)S(1)}, u32[]{:S(2)}, u32[]{:S(2)}) collective-permute-start(bf16[48,4608]{1,0:T(8,128)(2,1)S(1)} %collective-permute-done.13.refs_2_), channel_id=1, source_target_pairs={{0,1},{1,0},{2,3},{3,2},{4,5},{5,4},{6,7},{7,6}} | collective-permute-start | bytes 1327112 | tf_op jit(solution)/shard_map/ppermute | solution.py:548
  432.7 17.4 %collective-permute-start.17 = (bf16[48,4608]{1,0:T(8,128)(2,1)}, bf16[48,4608]{1,0:T(8,128)(2,1)S(1)}, u32[]{:S(2)}, u32[]{:S(2)}) collective-permute-start(bf16[48,4608]{1,0:T(8,128)(2,1)} %collective-permute-done.14.refs_3_), channel_id=1, source_target_pairs={{0,1},{1,0},{2,3},{3,2},{4,5},{5,4},{6,7},{7,6}} | collective-permute-start | bytes 1327112 | tf_op jit(solution)/shard_map/ppermute | solution.py:548
  571.6 5.6 collective-permute-start.28
  573.2 2.0 collective-permute-start.29
  574.3 39.4 %copy-start.10 = (f32[8,4608]{1,0:T(8,128)S(1)}, f32[8,4608]{1,0:T(8,128)}, u32[]{:S(2)}) copy-start(f32[8,4608]{1,0:T(8,128)} %get-tuple-element.67) | copy-start | bytes 442372
  574.3 39.4 %copy-start.11 = (f32[8,4608]{1,0:T(8,128)S(1)}, f32[8,4608]{1,0:T(8,128)}, u32[]{:S(2)}) copy-start(f32[8,4608]{1,0:T(8,128)} %get-tuple-element.68) | copy-start | bytes 442372
  574.3 39.4 %copy-start.12 = (f32[8,4608]{1,0:T(8,128)S(1)}, f32[8,4608]{1,0:T(8,128)}, u32[]{:S(2)}) copy-start(f32[8,4608]{1,0:T(8,128)} %get-tuple-element.69) | copy-start | bytes 442372
  574.4 39.4 %copy-start.13 = (f32[8,4608]{1,0:T(8,128)S(1)}, f32[8,4608]{1,0:T(8,128)}, u32[]{:S(2)}) copy-start(f32[8,4608]{1,0:T(8,128)} %get-tuple-element.70) | copy-start | bytes 442372
  574.4 39.8 %copy-start.14 = (bf16[2048,512]{1,0:T(8,128)(2,1)S(1)}, bf16[2048,512]{1,0:T(8,128)(2,1)}, u32[]{:S(2)}) copy-start(bf16[2048,512]{1,0:T(8,128)(2,1)} %get-tuple-element.63.k0) | copy-start | bytes 6291460
  574.4 2.0 collective-permute-start.30
  612.4 104.5 %collective-permute-start.31 = (bf16[512,4608]{1,0:T(8,128)(2,1)}, bf16[512,4608]{1,0:T(8,128)(2,1)}, u32[]{:S(2)}, u32[]{:S(2)}) collective-permute-start(bf16[512,4608]{1,0:T(8,128)(2,1)} %shard_map.156.p_ref), channel_id=1, source_target_pairs={{0,4},{4,0},{1,5},{5,1},{2,6},{6,2},{3,7},{7,3}} | collective-permute-start | bytes 14155784 | tf_op jit(solution)/shard_map/ppermute | solution.py:554
  613.5 117.3 %collective-permute-start.37 = (bf16[2048,1024]{1,0:T(8,128)(2,1)}, bf16[2048,1024]{1,0:T(8,128)(2,1)}, u32[]{:S(2)}, u32[]{:S(2)}) collective-permute-start(bf16[2048,1024]{1,0:T(8,128)(2,1)} %get-tuple-element.47.c0_ref.ctx_ref), channel_id=1, source_target_pairs={{0,1},{1,0},{2,3},{3,2},{4,5},{5,4},{6,7},{7,6}} | collective-permute-start | bytes 12582920 | tf_op jit(solution)/shard_map/ppermute | solution.py:548
  613.8 168.7 %collective-permute-start.34 = (bf16[2048,1024]{1,0:T(8,128)(2,1)}, bf16[2048,1024]{1,0:T(8,128)(2,1)}, u32[]{:S(2)}, u32[]{:S(2)}) collective-permute-start(bf16[2048,1024]{1,0:T(8,128)(2,1)} %get-tuple-element.62.q0), channel_id=1, source_target_pairs={{0,1},{1,0},{2,3},{3,2},{4,5},{5,4},{6,7},{7,6}} | collective-permute-start | bytes 12582920 | tf_op jit(solution)/shard_map/ppermute | solution.py:548
  614.2 168.4 %collective-permute-start.35 = (bf16[2048,512]{1,0:T(8,128)(2,1)S(1)}, bf16[2048,512]{1,0:T(8,128)(2,1)}, u32[]{:S(2)}, u32[]{:S(2)}) collective-permute-start(bf16[2048,512]{1,0:T(8,128)(2,1)S(1)} %copy-done.14), channel_id=1, source_target_pairs={{0,1},{1,0},{2,3},{3,2},{4,5},{5,4},{6,7},{7,6}} | collective-permute-start | bytes 6291464 | tf_op jit(solution)/shard_map/ppermute | solution.py:548
  614.4 168.2 %collective-permute-start.36 = (bf16[2048,512]{1,0:T(8,128)(2,1)}, bf16[2048,512]{1,0:T(8,128)(2,1)}, u32[]{:S(2)}, u32[]{:S(2)}) collective-permute-start(bf16[2048,512]{1,0:T(8,128)(2,1)} %get-tuple-element.64.v0), channel_id=1, source_target_pairs={{0,1},{1,0},{2,3},{3,2},{4,5},{5,4},{6,7},{7,6}} | collective-permute-start | bytes 6291464 | tf_op jit(solution)/shard_map/ppermute | solution.py:548
  730.8 50.3 %collective-permute-start.32 = (f32[2,4608]{1,0:T(2,128)S(1)}, f32[2,4608]{1,0:T(2,128)S(1)}, u32[]{:S(2)}, u32[]{:S(2)}) collective-permute-start(f32[2,4608]{1,0:T(2,128)S(1)} %pad_maximum_fusion.2), channel_id=1, source_target_pairs={{0,1},{1,0},{2,3},{3,2},{4,5},{5,4},{6,7},{7,6}} | collective-permute-start | bytes 110600 | tf_op jit(solution)/shard_map/ppermute | solution.py:548
  781.1 101.9 %collective-permute-start.33 = (f32[2,4608]{1,0:T(2,128)S(1)}, f32[2,4608]{1,0:T(2,128)S(1)}, u32[]{:S(2)}, u32[]{:S(2)}) collective-permute-start(f32[2,4608]{1,0:T(2,128)S(1)} %fusion.1), channel_id=1, source_target_pairs={{0,2},{2,0},{1,3},{3,1},{4,6},{6,4},{5,7},{7,5}} | collective-permute-start | bytes 110600 | tf_op jit(solution)/shard_map/ppermute | solution.py:551
  (8 other events, 18.3 us)

commit v4 on v3

--- a/solution.py
+++ b/solution.py
@@ -18,7 +18,6 @@
 
 NT = (((1,), (1,)), ((), ()))
 NN = (((1,), (0,)), ((), ()))
-TN = (((0,), (0,)), ((), ()))
 
 
 def dotf(a, b, dims):
@@ -33,53 +32,57 @@
     return jnp.concatenate([cos, cos], axis=-1), jnp.concatenate([-sin, sin], axis=-1)
 
 
-QB = 256
-KB = 256
-
-
-def attn_fwd_kernel(q_ref, k_ref, v_ref, ctx_ref, lse_ref, acc_ref, sum_ref, *, k1, k2):
+QT = 512
+SB = 256
+
+
+def attn_fwd_kernel(q_ref, k_ref, v_ref, ctx_ref, lse_ref, q_s, acc_ref, sum_ref, *, k1, k2):
     i = pl.program_id(1)
-    q = jnp.concatenate([q_ref[:, :HEAD], q_ref[:, HEAD:]], axis=0)
+    nt = QT // SB
+    for t in range(nt):
+        rows = slice(t * SB, (t + 1) * SB)
+        q_s[t, :SB] = q_ref[rows, :HEAD]
+        q_s[t, SB:] = q_ref[rows, HEAD:]
     acc_ref[...] = jnp.zeros_like(acc_ref)
     sum_ref[...] = jnp.zeros_like(sum_ref)
 
-    def chunk(row0, mask):
-        k = k_ref[pl.ds(row0, KB), :]
-        v = v_ref[pl.ds(row0, KB), :]
-        s = dotf(q, k, NT)
+    def chunk(t, row0, mask):
+        k = k_ref[pl.ds(row0, SB), :]
+        v = v_ref[pl.ds(row0, SB), :]
+        s = dotf(q_s[t], k, NT)
         p = jnp.exp2(jnp.tanh(s * k1) * k2)
         if mask is not None:
             p = jnp.where(mask, p, 0.0)
         part = p[:, :128]
-        for c in range(1, KB // 128):
+        for c in range(1, SB // 128):
             part = part + p[:, c * 128:(c + 1) * 128]
         return part, dotf(p.astype(BF16), v, NN)
 
-    def pair(j, carry):
-        s0, a0 = chunk(pl.multiple_of(j * (2 * KB), 2 * KB), None)
-        s1, a1 = chunk(pl.multiple_of(j * (2 * KB) + KB, KB), None)
-        acc_ref[...] += a0 + a1
-        sum_ref[...] += s0 + s1
+    def full(j, carry):
+        for t in range(nt):
+            ps = [chunk(t, pl.multiple_of(j * QT + m * SB, SB), None) for m in range(nt)]
+            sum_ref[t] += ps[0][0] + ps[1][0]
+            acc_ref[t] += ps[0][1] + ps[1][1]
         return carry
 
-    lax.fori_loop(0, i // 2, pair, 0)
-
-    @pl.when(i % 2 == 1)
-    def _():
-        s0, a0 = chunk(pl.multiple_of((i - 1) * KB, KB), None)
-        acc_ref[...] += a0
-        sum_ref[...] += s0
-
-    rows = lax.broadcasted_iota(jnp.int32, (2 * QB, KB), 0) % QB
-    cols = lax.broadcasted_iota(jnp.int32, (2 * QB, KB), 1)
-    s0, a0 = chunk(pl.multiple_of(i * KB, KB), rows >= cols)
-    total = jnp.sum(sum_ref[...] + s0, axis=1, keepdims=True)
-    ctx = ((acc_ref[...] + a0) / total).astype(BF16)
-    ctx_ref[:, :HEAD] = ctx[:QB]
-    ctx_ref[:, HEAD:] = ctx[QB:]
-    lse = jnp.broadcast_to(jnp.log2(total), (2 * QB, 128)).T
-    lse_ref[0, 0:1, :] = lse[0:1, :QB]
-    lse_ref[0, 1:2, :] = lse[0:1, QB:]
+    lax.fori_loop(0, i, full, 0)
+
+    rows = lax.broadcasted_iota(jnp.int32, (2 * SB, SB), 0) % SB
+    cols = lax.broadcasted_iota(jnp.int32, (2 * SB, SB), 1)
+    mask = rows >= cols
+    for t in range(nt):
+        ps = [chunk(t, pl.multiple_of(i * QT + m * SB, SB), mask if m == t else None) for m in range(t + 1)]
+        tot, acc = sum_ref[t], acc_ref[t]
+        for p in ps:
+            tot, acc = tot + p[0], acc + p[1]
+        total = jnp.sum(tot, axis=1, keepdims=True)
+        ctx = (acc / total).astype(BF16)
+        r = slice(t * SB, (t + 1) * SB)
+        ctx_ref[r, :HEAD] = ctx[:SB]
+        ctx_ref[r, HEAD:] = ctx[SB:]
+        lse = jnp.broadcast_to(jnp.log2(total), (2 * SB, 128)).T
+        lse_ref[0, 0:1, r] = lse[0:1, :SB]
+        lse_ref[0, 1:2, r] = lse[0:1, SB:]
 
 
 def attn_fwd(qkv, kvh, nq):
@@ -87,21 +90,25 @@
     scale = HEAD ** -0.5
     return pl.pallas_call(
         functools.partial(attn_fwd_kernel, k1=scale / SOFT_CAP, k2=SOFT_CAP * LOG2E),
-        grid=(kvh, T // QB),
+        grid=(kvh, T // QT),
         in_specs=[
-            pl.BlockSpec((QB, 2 * HEAD), lambda h, i: (i, h)),
+            pl.BlockSpec((QT, 2 * HEAD), lambda h, i: (i, h)),
             pl.BlockSpec((T, HEAD), lambda h, i: (0, nq + h)),
             pl.BlockSpec((T, HEAD), lambda h, i: (0, nq + kvh + h)),
         ],
         out_specs=[
-            pl.BlockSpec((QB, 2 * HEAD), lambda h, i: (i, h)),
-            pl.BlockSpec((1, 2, QB), lambda h, i: (h, 0, i)),
+            pl.BlockSpec((QT, 2 * HEAD), lambda h, i: (i, h)),
+            pl.BlockSpec((1, 2, QT), lambda h, i: (h, 0, i)),
         ],
         out_shape=[
             jax.ShapeDtypeStruct((T, nq * HEAD), BF16),
             jax.ShapeDtypeStruct((kvh, 2, T), F32),
         ],
-        scratch_shapes=[pltpu.VMEM((2 * QB, HEAD), F32), pltpu.VMEM((2 * QB, 128), F32)],
+        scratch_shapes=[
+            pltpu.VMEM((QT // SB, 2 * SB, HEAD), BF16),
+            pltpu.VMEM((QT // SB, 2 * SB, HEAD), F32),
+            pltpu.VMEM((QT // SB, 2 * SB, 128), F32),
+        ],
         compiler_params=pltpu.CompilerParams(dimension_semantics=("arbitrary", "arbitrary")),
         cost_estimate=pl.CostEstimate(flops=int(2 * 2 * T * T * HEAD * kvh * 2), bytes_accessed=2 * qkv.size * 2, transcendentals=0),
         name="attn_fwd",
@@ -113,7 +120,7 @@
 
 
 def attn_bwd_kernel(q_ref, k_ref, v_ref, do_ref, ctx_ref, lse_ref, cos_ref, sin_ref, dq_ref, dk_ref, dv_ref,
-                    dqa_ref, dka_ref, dva_ref, dd_ref, *, k1, k2, scale):
+                    dqa_ref, dka_ref, dva_ref, dd_ref, kt_ref, *, k1, k2, scale):
     J = pl.program_id(1)
     nq = q_ref.shape[0] // BQ
     r = BK // BQ
@@ -131,6 +138,7 @@
     dva_ref[...] = jnp.zeros_like(dva_ref)
     k = k_ref[...]
     v = v_ref[...]
+    kt_ref[...] = k.T
 
     def tile(i, mask):
         row0 = pl.multiple_of(i * BQ, BQ)
@@ -150,7 +158,7 @@
             ds = (p * (dp - dd) * (1.0 - u * u)).astype(BF16)
             dvs.append(dotf(p.astype(BF16), do, NN))
             dks.append(dotf(ds, q, NN))
-            dqa_ref[g, rs, :] += dotf(ds, k, TN)
+            dqa_ref[g, :, rs] += dotf(kt_ref[...], ds, NN)
         dva_ref[...] += dvs[0] + dvs[1]
         dka_ref[...] += dks[0] + dks[1]
 
@@ -159,11 +167,12 @@
     for m in range(r):
         tile(J * r + m, qpos + m * BQ >= kpos)
 
-    def body(i, carry):
-        tile(i, None)
+    def body(j, carry):
+        for m in range(r):
+            tile(j * r + m, None)
         return carry
 
-    lax.fori_loop(J * r + r, nq, body, 0)
+    lax.fori_loop(J + 1, nq // r, body, 0)
 
     krow = pl.ds(pl.multiple_of(J * BK, BK), BK)
 
@@ -173,7 +182,7 @@
     dk_ref[...] = unrope(dka_ref[...], cos_ref[krow, :], sin_ref[krow, :]).astype(BF16)
     dv_ref[...] = dva_ref[...].astype(BF16)
     for g in range(2):
-        dq_ref[:, g * HEAD:(g + 1) * HEAD] = unrope(dqa_ref[g, krow, :], cos_ref[krow, :], sin_ref[krow, :]).astype(BF16)
+        dq_ref[:, g * HEAD:(g + 1) * HEAD] = unrope(dqa_ref[g, :, krow].T, cos_ref[krow, :], sin_ref[krow, :]).astype(BF16)
 
 
 def attn_bwd(qkv, kvh, nq, do, ctx, lse, cos, sin):
@@ -193,10 +202,11 @@
             jax.ShapeDtypeStruct((T, kvh * HEAD), BF16),
         ],
         scratch_shapes=[
-            pltpu.VMEM((2, T, HEAD), F32),
+            pltpu.VMEM((2, HEAD, T), F32),
             pltpu.VMEM((BK, HEAD), F32),
             pltpu.VMEM((BK, HEAD), F32),
             pltpu.VMEM((2, 1, T), F32),
+            pltpu.VMEM((HEAD, BK), BF16),
         ],
         compiler_params=pltpu.CompilerParams(dimension_semantics=("arbitrary", "arbitrary")),
         cost_estimate=pl.CostEstimate(flops=int(5 * 2 * T * T * HEAD * kvh), bytes_accessed=3 * qkv.size * 2, transcendentals=0),
@@ -206,15 +216,6 @@
 
 VMEM_LIMIT = 64_000_000
 KD = 512
-
-
-def load_pieces(pieces, layout, sc_ref, x_ref, sem):
-    cps = []
-    for i, (slot, n) in enumerate(layout):
-        blk = sc_ref[slot]
-        off = pl.multiple_of(sc_ref[slot + 1], 16)
-        cps.append(pltpu.make_async_copy(pieces[i], x_ref.at[blk, pl.ds(off, n)], sem.at[i]))
-    return cps
 
 
 def gmm_kernel(sc_ref, *refs, layout, mode, n_w, R, r0, aliased):
@@ -232,17 +233,29 @@
     last = pl.num_programs(0) - 1
     B = x_ref.shape[0]
     core = sc_ref[1]
-    cps = load_pieces(pieces, layout, sc_ref, x_ref, sem_in)
-    outs = [pltpu.make_async_copy(x_ref.at[b], all_ref.at[sc_ref[0] * B + b, pl.ds(r0, R)], sem_out.at[b]) for b in range(B)]
+
+    def cols(k):
+        return pl.ds(pl.multiple_of(k * KD, KD), KD)
+
+    def cp_in(p, k):
+        slot, n = layout[p]
+        off = pl.multiple_of(sc_ref[slot + 1], 16)
+        return pltpu.make_async_copy(pieces[p].at[:, cols(k)], x_ref.at[sc_ref[slot], pl.ds(off, n), cols(k)], sem_in.at[k])
+
+    def cp_out(b, k):
+        return pltpu.make_async_copy(x_ref.at[b, :, cols(k)], all_ref.at[sc_ref[0] * B + b, pl.ds(r0, R), cols(k)], sem_out)
 
     @pl.when(i == 0)
     def _():
-        for c in cps:
-            c.start()
-        for c in cps:
-            c.wait()
-        for c in outs:
-            c.start()
+        @pl.loop(0, last + 1)
+        def _(k):
+            for p in range(np_):
+                cp_in(p, k).start()
+
+    for p in range(np_):
+        cp_in(p, i).wait()
+    for b in range(B):
+        cp_out(b, i).start()
 
     ks = pl.ds(pl.multiple_of(i * KD, KD), KD)
 
@@ -254,12 +267,14 @@
             return [dotf(x, w_ref[0], NN), dotf(x, w_ref[1, :, half], NN), dotf(x, w_ref[2, :, half], NN)]
         return [dotf(x, ws[0][...], NT)]
 
-    if mode == "qkv":
-        for j in range(3):
-            w_ref[j] = ws[j][...].reshape(w_ref.shape[1:])
+    def prep():
+        if mode == "qkv":
+            for j in range(3):
+                w_ref[j] = ws[j][...].reshape(w_ref.shape[1:])
 
     @pl.when(i == 0)
     def _():
+        prep()
         for b in range(B):
             o = 0
             for d in products(b):
@@ -268,6 +283,7 @@
 
     @pl.when(i > 0)
     def _():
+        prep()
         for b in range(B):
             o = 0
             for d in products(b):
@@ -287,8 +303,11 @@
                 out_ref[b, :, n_rope:] = acc_ref[b, :, n_rope:].astype(BF16)
             else:
                 out_ref[b] = acc_ref[b].astype(BF16)
-        for c in outs:
-            c.wait()
+
+        @pl.loop(0, last + 1)
+        def _(k):
+            for b in range(B):
+                cp_out(b, k).wait()
 
 
 def gather_matmul(chip, core, places, pieces, ws, mode, tabs, B, R, r0, N, bufs=None):
@@ -324,8 +343,8 @@
                 pltpu.VMEM((B, R, D), BF16),
                 pltpu.VMEM((B, R, N), F32),
                 wscr,
-                pltpu.SemaphoreType.DMA((len(pieces),)),
-                pltpu.SemaphoreType.DMA((B,)),
+                pltpu.SemaphoreType.DMA((nk,)),
+                pltpu.SemaphoreType.DMA,
             ],
         ),
         out_shape=[jax.ShapeDtypeStruct((4, tokens, N), BF16), jax.ShapeDtypeStruct((4, tokens, D), BF16)],
@@ -335,24 +354,26 @@
     )(scal, *args)
 
 
-def orow_kernel(sc_ref, c0_ref, c1_ref, w_ref, out_ref):
+def orow_kernel(sc_ref, c0_ref, c1_ref, w_ref, out_ref, *, r0):
     core = sc_ref[1]
     n = c0_ref.shape[1]
+    rows = slice(r0, r0 + out_ref.shape[0])
     own = w_ref[pl.ds(pl.multiple_of(core * n, n), n), :]
     oth = w_ref[pl.ds(pl.multiple_of((1 - core) * n, n), n), :]
-    out_ref[...] = (dotf(c0_ref[...], own, NN) + dotf(c1_ref[...], oth, NN)).astype(BF16)
-
-
-def o_rows(scal, ctx, ctx_pr, w, c, nc, M, db):
+    out_ref[...] = (dotf(c0_ref[rows, :], own, NN) + dotf(c1_ref[rows, :], oth, NN)).astype(BF16)
+
+
+def o_rows(scal, ctx, ctx_pr, w, r0, M, db):
     n, D = ctx.shape[1], w.shape[1]
-    return pl.pallas_call(
-        orow_kernel,
+    tokens = ctx_pr.shape[0]
+    return pl.pallas_call(
+        functools.partial(orow_kernel, r0=r0),
         grid_spec=pltpu.PrefetchScalarGridSpec(
             num_scalar_prefetch=1,
             grid=(D // db,),
             in_specs=[
-                pl.BlockSpec((M, n), lambda i, s: (s[2] * nc + c, 0)),
-                pl.BlockSpec((M, n), lambda i, s: (c, 0)),
+                pl.BlockSpec((tokens, n), lambda i, s: (s[2], 0)),
+                pl.BlockSpec((tokens, n), lambda i, s: (0, 0)),
                 pl.BlockSpec((2 * n, db), lambda i, s: (0, i)),
             ],
             out_specs=pl.BlockSpec((M, db), lambda i, s: (0, i)),
@@ -497,11 +518,11 @@
     dg_ref[...] += jnp.sum((ga * hat).reshape(RB // 8, 8, -1), axis=0)
 
 
-def norm_call(kernel, part, peer, hidden, d_out, g, c, buf, extra):
+def norm_call(kernel, part, peer, hidden, d_out, g, r0, buf, extra):
     M, D = part.shape
     n = M // RB
     loc = pl.BlockSpec((RB, D), lambda i: (i, 0))
-    row = pl.BlockSpec((RB, D), lambda i: (c * n + i, 0))
+    row = pl.BlockSpec((RB, D), lambda i: (r0 // RB + i, 0))
     in_specs = [loc, loc, row, row, pl.BlockSpec((1, D), lambda i: (0, 0))]
     args = [part, peer, hidden, d_out, g.reshape(1, D)]
     aliases = {}
@@ -585,34 +606,31 @@
 
         ctx, lse = attn_fwd(qkv, KL, HL)
         ctx_pr = to_core(lax.dynamic_slice_in_dim(ctx, (me ^ 1) * tokens, tokens, 0))
-        nc = 4
-        M = tokens // nc
+        sizes = (128, 192, 128, 64)
+        starts = [sum(sizes[:c]) for c in range(len(sizes))]
         o_parts, o_peers = [], []
-        for c in range(nc):
-            op = o_rows(base, ctx, ctx_pr, wo2, c, nc, M, 1536)
+        for c, M in enumerate(sizes):
+            op = o_rows(base, ctx, ctx_pr, wo2, starts[c], M, 1536)
             o_parts.append(op)
             o_peers.append(to_tp(op))
         ctx_p = to_core(ctx)
 
         y_blk, gos, dgp = None, [], []
-        for c in range(nc):
-            y_blk, go, dg_ = norm_call(post_kernel, o_parts[c], o_peers[c], hidden, d_out, g_post, c, y_blk, True)
+        for c in range(len(sizes)):
+            y_blk, go, dg_ = norm_call(post_kernel, o_parts[c], o_peers[c], hidden, d_out, g_post, starts[c], y_blk, True)
             gos.append(go)
             dgp.append(dg_)
 
-        gx = [to_x(g) for g in gos[:-1]]
+        gx = [to_x(g) for g in gos]
         gp = [to_core(g) for g in gos]
-        r, r_off = two_way(gos[-1], 48)
         gxp = [to_core(g) for g in gx]
-        rp = [to_core(g) for g in r]
         HN = HL * HEAD
-        early = [c * M for c in range(nc - 1)]
-        RE = (nc - 1) * M
-        places = [(core, o) for o in early] + [(1 - core, o) for o in early]
+        RE, RL = starts[-1], sizes[-1]
+        places = [(core, o) for o in starts[:-1]] + [(1 - core, o) for o in starts[:-1]]
         bufs = gather_matmul(xi, core, places, gos[:-1] + gp[:-1], (wo2,), "nt", (), 2, RE, 0, HN)
-        bufs = gather_matmul(1 - xi, core, places, gx + gxp, (wo2,), "nt", (), 2, RE, 0, HN, bufs=bufs)
-        places = [(me, 0), (me ^ 1, 0)] + [(me ^ 2, o) for o in r_off] + [(me ^ 3, o) for o in r_off]
-        dctx, go_all = gather_matmul(0, core, places, [gos[-1], gp[-1]] + r + rp, (wo2,), "nt", (), 4, M, RE, HN, bufs=bufs)
+        bufs = gather_matmul(1 - xi, core, places, gx[:-1] + gxp[:-1], (wo2,), "nt", (), 2, RE, 0, HN, bufs=bufs)
+        places = [(me ^ rel, 0) for rel in range(4)]
+        dctx, go_all = gather_matmul(0, core, places, [gos[-1], gp[-1], gx[-1], gxp[-1]], (wo2,), "nt", (), 4, RL, RE, HN, bufs=bufs)
         dctx = dctx.reshape(T, HN)
         go_all = go_all.reshape(T, D)
 

time: 893 us -> 865 us (0.969)
  Pallas kernels: 545 us -> 521 us
    pallas_call x1, Pallas kernels: 99.8 us -> 83.4 us  [attn_bwd(): pl.pallas_call(functools.partial(attn_bwd_kernel, k1=scale / SOFT_CAP, k2...]
    pallas_call x1, Pallas kernels: 55.6 us -> 40.9 us  [attn_fwd(): pl.pallas_call(functools.partial(attn_fwd_kernel, k1=scale / SOFT_CAP, k2...]
    ppermute x8 -> x7, waiting for transfers between devices: 124 us -> 129 us  [to_x(): return lax.ppermute(v, 'cp', x_perm)]
    ppermute x7 -> x6, waiting for transfers between devices: 154 us -> 156 us  [to_tp(): return lax.ppermute(v, 'tp', tp_perm)]
  transfers between devices with their start and end apart: 38 -> 34, of which waited for: 13 -> 10; matrix products, arithmetic and copies ran while one was open for 2% -> 2% of each run, Pallas kernels for 32% -> 33%
where the time goes in v4:
time: 865 us; the launch traced here: 859 us
  Pallas kernels  521 us (60%)
  waiting for transfers between devices  288 us (33%)
  starting transfers between devices  21.9 us (3%)
  local copies, waits for them, and re-layouts  19.5 us (2%)
    ppermute x6, waiting for transfers between devices, to_tp(): return lax.ppermute(v, 'tp', tp_perm)  156 us
    ppermute x7, waiting for transfers between devices, to_x(): return lax.ppermute(v, 'cp', x_perm)  129 us
    pallas_call x5, Pallas kernels, gather_matmul(): pl.pallas_call(functools.partial(gmm_kernel, layout=layout, mode=mode, n_...  128 us
    pallas_call x1, Pallas kernels, dw_proj(): pl.pallas_call(dw_kernel, grid_spec=pltpu.PrefetchScalarGridSpec(num_scal...  100 us
    pallas_call x1, Pallas kernels, attn_bwd(): pl.pallas_call(functools.partial(attn_bwd_kernel, k1=scale / SOFT_CAP, k2...  83.4 us
    pallas_call x1, Pallas kernels, dwo_proj(): pl.pallas_call(dwo_kernel, grid_spec=pltpu.PrefetchScalarGridSpec(num_sca...  50.2 us
    pallas_call x4, Pallas kernels, o_rows(): pl.pallas_call(functools.partial(orow_kernel, r0=r0), grid_spec=pltpu.Pre...  41.2 us
    pallas_call x1, Pallas kernels, attn_fwd(): pl.pallas_call(functools.partial(attn_fwd_kernel, k1=scale / SOFT_CAP, k2...  40.9 us
  transfers between devices with their start and end apart: 34, of which 10 were waited for; matrix products, arithmetic and copies ran while one was open for 2% of the time, Pallas kernels for 33%

profile of v4, /device:TPU:0, one launch (start us, length us, event | category | flops | bytes accessed | tf_op | source)
XLA Modules:
  0.0 859.3 jit_solution(13240623408589543548)
XLA Ops:
  0.6 1.3 reshape.71.g_ref
  2.0 7.8 a_norm.1.refs_0_
  10.6 1.5 constant_dynamic-slice_fusion.4
  12.2 2.5 collective-permute-start
  14.7 36.1 %collective-permute-done.refs_0_ = bf16[176,4608]{1,0:T(8,128)(2,1)S(1)} collective-permute-done((bf16[176,4608]{1,0:T(8,128)(2,1)S(1)}, bf16[176,4608]{1,0:T(8,128)(2,1)S(1)}, u32[]{:S(2)}, u32[]{:S(2)}) %collective-permute-start) | collective-permute-done | bytes 1622048 | tf_op jit(solution)/shard_map/ppermute | solution.py:572
  50.8 1.8 collective-permute-start.1
  52.6 2.6 slice.12
  55.1 1.5 collective-permute-start.2
  56.6 3.7 fusion
  60.4 1.9 pad_maximum_fusion
  63.5 25.5 %collective-permute-done.2.refs_2_ = bf16[160,4608]{1,0:T(8,128)(2,1)} collective-permute-done((bf16[160,4608]{1,0:T(8,128)(2,1)}, bf16[160,4608]{1,0:T(8,128)(2,1)}, u32[]{:S(2)}, u32[]{:S(2)}) %collective-permute-start.2) | collective-permute-done | bytes 1474592 | tf_op jit(solution)/shard_map/ppermute | solution.py:572
  89.6 38.2 %shard_map.143 = (bf16[4,512,2048]{2,1,0:T(8,128)(2,1)}, bf16[4,512,4608]{2,1,0:T(8,128)(2,1)}) custom-call(s32[6]{0:T(128)} %stack.48.sc_ref, bf16[512,4608]{1,0:T(8,128)(2,1)} %a_norm.1.refs_0_, bf16[512,4608]{1,0:T(8,128)(2,1)} %collective-permute-done.6.refs_1_, bf16[4608,16,128]{2,1,0:T(8,128)(2,1)} %wq_ref.1, bf16[4608,8,128]{2,1,0:T(8,128)(2,1)} %wk_ref.1, ...), custom_call_target="tpu_custom_call" | custom-call | flops 19327352832 | bytes 37748736 | tf_op jit(solution)/shard_map/pallas_call | solution.py:335
  127.8 37.9 %shard_map.144 = (bf16[4,512,2048]{2,1,0:T(8,128)(2,1)}, bf16[4,512,4608]{2,1,0:T(8,128)(2,1)}) custom-call(s32[14]{0:T(128)} %stack.47.sc_ref, bf16[176,4608]{1,0:T(8,128)(2,1)} %copy-done.3, bf16[176,4608]{1,0:T(8,128)(2,1)} %collective-permute-done.1.refs_1_, ...), custom_call_target="tpu_custom_call", output_to_operand_aliasing={{0}: (12, {}), {1}: (13, {})} | custom-call | flops 19327352832 | bytes 37748736 | tf_op jit(solution)/shard_map/pallas_call | solution.py:335
  165.7 40.9 %attn_fwd.1 = (bf16[2048,1024]{1,0:T(8,128)(2,1)}, f32[4,2,2048]{2,1,0:T(2,128)}) custom-call(bf16[2048,2048]{1,0:T(8,128)(2,1)} %bitcast.31, bf16[2048,2048]{1,0:T(8,128)(2,1)} %bitcast.32, bf16[2048,2048]{1,0:T(8,128)(2,1)} %bitcast.33), custom_call_target="tpu_custom_call" | custom-call | flops 17179869184 | bytes 16777216 | tf_op jit(solution)/shard_map/attn_fwd/pallas_call | solution.py:91
  206.6 1.3 constant_dynamic-slice_fusion.3
  209.3 1.7 collective-permute-done.7.c1_ref
  212.0 11.0 %shard_map.147.p_ref = bf16[192,4608]{1,0:T(8,128)(2,1)} custom-call(s32[4]{0:T(128)} %pad_add_fusion.sc_ref, bf16[2048,1024]{1,0:T(8,128)(2,1)} %get-tuple-element.47.c0_ref.ctx_ref, bf16[512,1024]{1,0:T(8,128)(2,1)} %copy-done, bf16[2048,4608]{1,0:T(8,128)(2,1)} %bitcast.21), custom_call_target="tpu_custom_call" | custom-call | flops 3623878656 | bytes 18874368 | tf_op jit(solution)/shard_map/pallas_call | solution.py:369
  223.8 10.1 %shard_map.148.p_ref = bf16[128,4608]{1,0:T(8,128)(2,1)} custom-call(s32[4]{0:T(128)} %pad_add_fusion.sc_ref, bf16[2048,1024]{1,0:T(8,128)(2,1)} %get-tuple-element.47.c0_ref.ctx_ref, bf16[512,1024]{1,0:T(8,128)(2,1)} %copy-done, bf16[2048,4608]{1,0:T(8,128)(2,1)} %bitcast.22), custom_call_target="tpu_custom_call" | custom-call | flops 2415919104 | bytes 18874368 | tf_op jit(solution)/shard_map/pallas_call | solution.py:369
  233.9 1.2 collective-permute-start.11
  235.7 10.1 %shard_map.146.p_ref = bf16[128,4608]{1,0:T(8,128)(2,1)} custom-call(s32[4]{0:T(128)} %pad_add_fusion.sc_ref, bf16[2048,1024]{1,0:T(8,128)(2,1)} %get-tuple-element.47.c0_ref.ctx_ref, bf16[512,1024]{1,0:T(8,128)(2,1)} %copy-done, bf16[2048,4608]{1,0:T(8,128)(2,1)} %bitcast.23), custom_call_target="tpu_custom_call" | custom-call | flops 2415919104 | bytes 18874368 | tf_op jit(solution)/shard_map/pallas_call | solution.py:369
  246.6 43.4 %collective-permute-done.11.r_ref = bf16[128,4608]{1,0:T(8,128)(2,1)S(1)} collective-permute-done((bf16[128,4608]{1,0:T(8,128)(2,1)}, bf16[128,4608]{1,0:T(8,128)(2,1)S(1)}, u32[]{:S(2)}, u32[]{:S(2)}) %collective-permute-start.11) | collective-permute-done | bytes 1179680 | tf_op jit(solution)/shard_map/ppermute | solution.py:575
  289.9 1.0 copy-done.5
  291.0 5.2 shard_map.149
  296.2 1.2 copy-done.2
  297.4 6.9 shard_map.150
  304.3 1.5 collective-permute-start.16
  306.3 10.2 %shard_map.145.p_ref = bf16[64,4608]{1,0:T(8,128)(2,1)} custom-call(s32[4]{0:T(128)} %pad_add_fusion.sc_ref, bf16[2048,1024]{1,0:T(8,128)(2,1)} %get-tuple-element.47.c0_ref.ctx_ref, bf16[512,1024]{1,0:T(8,128)(2,1)} %copy-done, bf16[2048,4608]{1,0:T(8,128)(2,1)} %bitcast.24), custom_call_target="tpu_custom_call" | custom-call | flops 1207959552 | bytes 18874368 | tf_op jit(solution)/shard_map/pallas_call | solution.py:369
  317.6 5.0 shard_map.151
  322.6 10.0 %collective-permute-done.8.r_ref = bf16[64,4608]{1,0:T(8,128)(2,1)} collective-permute-done((bf16[64,4608]{1,0:T(8,128)(2,1)}, bf16[64,4608]{1,0:T(8,128)(2,1)}, u32[]{:S(2)}, u32[]{:S(2)}) %collective-permute-start.8) | collective-permute-done | bytes 589856 | tf_op jit(solution)/shard_map/ppermute | solution.py:575
  332.5 1.5 collective-permute-start.17
  334.0 37.2 %collective-permute-done.15.refs_0_ = bf16[128,4608]{1,0:T(8,128)(2,1)S(1)} collective-permute-done((bf16[128,4608]{1,0:T(8,128)(2,1)}, bf16[128,4608]{1,0:T(8,128)(2,1)S(1)}, u32[]{:S(2)}, u32[]{:S(2)}) %collective-permute-start.15) | collective-permute-done | bytes 1179680 | tf_op jit(solution)/shard_map/ppermute | solution.py:572
  371.3 3.9 shard_map.152
  375.2 1.5 collective-permute-start.13
  376.7 30.4 %collective-permute-done.13.refs_2_ = bf16[64,4608]{1,0:T(8,128)(2,1)S(1)} collective-permute-done((bf16[64,4608]{1,0:T(8,128)(2,1)}, bf16[64,4608]{1,0:T(8,128)(2,1)S(1)}, u32[]{:S(2)}, u32[]{:S(2)}) %collective-permute-start.13) | collective-permute-done | bytes 589856 | tf_op jit(solution)/shard_map/ppermute | solution.py:572
  410.4 17.4 %shard_map.153 = (bf16[4,512,1024]{2,1,0:T(8,128)(2,1)}, bf16[4,512,4608]{2,1,0:T(8,128)(2,1)}) custom-call(s32[14]{0:T(128)} %stack.103.sc_ref, bf16[128,4608]{1,0:T(8,128)(2,1)} %get-tuple-element.53.refs_0_, bf16[192,4608]{1,0:T(8,128)(2,1)} %get-tuple-element.54.refs_1_, bf16[128,4608]{1,0:T(8,128)(2,1)} %get-tuple-element.55.refs_2_, ...), custom_call_target="tpu_custom_call" | custom-call | flops 8455716864 | bytes 25952256 | tf_op jit(solution)/shard_map/pallas_call | solution.py:335
  427.8 17.4 %shard_map.154 = (bf16[4,512,1024]{2,1,0:T(8,128)(2,1)}, bf16[4,512,4608]{2,1,0:T(8,128)(2,1)}) custom-call(s32[14]{0:T(128)} %stack.102.sc_ref, bf16[128,4608]{1,0:T(8,128)(2,1)} %copy-done.4, bf16[192,4608]{1,0:T(8,128)(2,1)} %copy-done.1, bf16[128,4608]{1,0:T(8,128)(2,1)} %collective-permute-done.17.refs_2_, ...), custom_call_target="tpu_custom_call", output_to_operand_aliasing={{0}: (8, {}), {1}: (9, {})} | custom-call | flops 8455716864 | bytes 25952256 | tf_op jit(solution)/shard_map/pallas_call | solution.py:335
  445.2 17.1 %shard_map.155 = (bf16[4,512,1024]{2,1,0:T(8,128)(2,1)}, bf16[4,512,4608]{2,1,0:T(8,128)(2,1)}) custom-call(s32[10]{0:T(128)} %stack.101.sc_ref, bf16[64,4608]{1,0:T(8,128)(2,1)} %get-tuple-element.52.refs_0_, bf16[64,4608]{1,0:T(8,128)(2,1)} %collective-permute-done.12.refs_1_, ...), custom_call_target="tpu_custom_call", output_to_operand_aliasing={{0}: (6, {}), {1}: (7, {})} | custom-call | flops 2415919104 | bytes 14155776 | tf_op jit(solution)/shard_map/pallas_call | solution.py:335
  462.3 83.4 %attn_bwd.1 = (bf16[2048,1024]{1,0:T(8,128)(2,1)}, bf16[2048,512]{1,0:T(8,128)(2,1)}, bf16[2048,512]{1,0:T(8,128)(2,1)}) custom-call(bf16[2048,2048]{1,0:T(8,128)(2,1)} %bitcast.34, bf16[2048,2048]{1,0:T(8,128)(2,1)} %bitcast.35, bf16[2048,2048]{1,0:T(8,128)(2,1)} %bitcast.36, bf16[2048,1024]{1,0:T(8,128)(2,1)} %bitcast.30, ...), custom_call_target="tpu_custom_call" | custom-call | flops 21474836480 | bytes 25165824 | tf_op jit(solution)/shard_map/attn_bwd/pallas_call | solution.py:194
  545.6 1.3 constant_dynamic-slice_fusion.2
  547.5 1.1 constant_dynamic-slice_fusion.1
  548.6 1.1 constant_dynamic-slice_fusion
  550.5 1.3 collective-permute-done.26.v1
  552.5 35.2 %shard_map.156.p_ref = bf16[512,4608]{1,0:T(8,128)(2,1)} custom-call(s32[4]{0:T(128)} %pad_add_fusion.sc_ref, bf16[2048,1024]{1,0:T(8,128)(2,1)} %get-tuple-element.62.q0, bf16[2048,512]{1,0:T(8,128)(2,1)} %get-tuple-element.63.k0, bf16[2048,512]{1,0:T(8,128)(2,1)} %get-tuple-element.64.v0, bf16[512,1024]{1,0:T(8,128)(2,1)} %collective-permute-done.24.q1, ...), custom_call_target="tpu_custom_call" | custom-call | flops 19327352832 | bytes 37748736 | tf_op jit(solution)/shard_map/pallas_call | solution.py:401
  589.7 102.5 %collective-permute-done.27.r_ref = bf16[512,4608]{1,0:T(8,128)(2,1)} collective-permute-done((bf16[512,4608]{1,0:T(8,128)(2,1)}, bf16[512,4608]{1,0:T(8,128)(2,1)}, u32[]{:S(2)}, u32[]{:S(2)}) %collective-permute-start.27) | collective-permute-done | bytes 4718624 | tf_op jit(solution)/shard_map/ppermute | solution.py:575
  692.2 12.9 %shard_map.157 = (bf16[512,4608]{1,0:T(8,128)(2,1)}, f32[8,4608]{1,0:T(8,128)}) custom-call(bf16[512,4608]{1,0:T(8,128)(2,1)} %shard_map.156.p_ref, bf16[512,4608]{1,0:T(8,128)(2,1)} %collective-permute-done.27.r_ref, bf16[512,4608]{1,0:T(8,128)(2,1)} %h_ref.11, bf16[512,4608]{1,0:T(8,128)(2,1)} %dy_ref.9, f32[1,4608]{1,0:T(1,128)} %reshape.71.g_ref), custom_call_target="tpu_custom_call" | custom-call | flops 4718592000 | bytes 28311552 | tf_op jit(solution)/shard_map/pallas_call | solution.py:538
  706.2 50.2 %dwo_proj.1 = f32[2048,4608]{1,0:T(8,128)} custom-call(s32[4]{0:T(128)} %pad_add_fusion.sc_ref, bf16[2048,1024]{1,0:T(8,128)(2,1)} %get-tuple-element.47.c0_ref.ctx_ref, bf16[2048,1024]{1,0:T(8,128)(2,1)} %collective-permute-done.33.c1_ref, bf16[2048,4608]{1,0:T(8,128)(2,1)} %bitcast.28), custom_call_target="tpu_custom_call" | custom-call | flops 38654705664 | bytes 37748736 | tf_op jit(solution)/shard_map/dwo_proj/pallas_call | solution.py:467
  756.5 1.4 collective-permute-start.29
  757.9 100.4 %dw_proj.1 = (f32[73728,128]{1,0:T(8,128)}, f32[36864,128]{1,0:T(8,128)}, f32[36864,128]{1,0:T(8,128)}) custom-call(s32[4]{0:T(128)} %pad_add_fusion.sc_ref, bf16[2048,4608]{1,0:T(8,128)(2,1)} %bitcast.29, bf16[2048,1024]{1,0:T(8,128)(2,1)} %get-tuple-element.62.q0, bf16[2048,1024]{1,0:T(8,128)(2,1)} %collective-permute-done.30.q1, ...), custom_call_target="tpu_custom_call" | custom-call | flops 77309411328 | bytes 75497472 | tf_op jit(solution)/shard_map/dw_proj/pallas_call | solution.py:435
  (96 shorter events, 18.2 us)
Async XLA Ops:
  9.8 79.8 %collective-permute-start.6 = (bf16[512,4608]{1,0:T(8,128)(2,1)}, bf16[512,4608]{1,0:T(8,128)(2,1)}, u32[]{:S(2)}, u32[]{:S(2)}) collective-permute-start(bf16[512,4608]{1,0:T(8,128)(2,1)} %a_norm.1.refs_0_), channel_id=1, source_target_pairs={{0,1},{1,0},{2,3},{3,2},{4,5},{5,4},{6,7},{7,6}} | collective-permute-start | bytes 14155784 | tf_op jit(solution)/shard_map/ppermute | solution.py:569
  12.2 38.6 %collective-permute-start = (bf16[176,4608]{1,0:T(8,128)(2,1)S(1)}, bf16[176,4608]{1,0:T(8,128)(2,1)S(1)}, u32[]{:S(2)}, u32[]{:S(2)}) collective-permute-start(bf16[176,4608]{1,0:T(8,128)(2,1)S(1)} %constant_dynamic-slice_fusion.4), channel_id=1, source_target_pairs={{0,2},{2,0},{1,3},{3,1},{4,6},{6,4},{5,7},{7,5}} | collective-permute-start | bytes 4866056 | tf_op jit(solution)/shard_map/ppermute | solution.py:572
  50.8 38.2 %copy-start.3 = (bf16[176,4608]{1,0:T(8,128)(2,1)}, bf16[176,4608]{1,0:T(8,128)(2,1)S(1)}, u32[]{:S(2)}) copy-start(bf16[176,4608]{1,0:T(8,128)(2,1)S(1)} %collective-permute-done.refs_0_) | copy-start | bytes 4866052
  50.8 38.7 %collective-permute-start.1 = (bf16[176,4608]{1,0:T(8,128)(2,1)S(1)}, bf16[176,4608]{1,0:T(8,128)(2,1)}, u32[]{:S(2)}, u32[]{:S(2)}) collective-permute-start(bf16[176,4608]{1,0:T(8,128)(2,1)S(1)} %collective-permute-done.refs_0_), channel_id=1, source_target_pairs={{0,4},{4,0},{1,5},{5,1},{2,6},{6,2},{3,7},{7,3}} | collective-permute-start | bytes 4866056 | tf_op jit(solution)/shard_map/ppermute | solution.py:575
  55.1 33.9 %collective-permute-start.2 = (bf16[160,4608]{1,0:T(8,128)(2,1)}, bf16[160,4608]{1,0:T(8,128)(2,1)}, u32[]{:S(2)}, u32[]{:S(2)}) collective-permute-start(bf16[160,4608]{1,0:T(8,128)(2,1)} %slice.12), channel_id=1, source_target_pairs={{0,2},{2,0},{1,3},{3,1},{4,6},{6,4},{5,7},{7,5}} | collective-permute-start | bytes 4423688 | tf_op jit(solution)/shard_map/ppermute | solution.py:572
  89.0 38.8 %collective-permute-start.5 = (bf16[160,4608]{1,0:T(8,128)(2,1)}, bf16[160,4608]{1,0:T(8,128)(2,1)}, u32[]{:S(2)}, u32[]{:S(2)}) collective-permute-start(bf16[160,4608]{1,0:T(8,128)(2,1)} %collective-permute-done.2.refs_2_), channel_id=1, source_target_pairs={{0,1},{1,0},{2,3},{3,2},{4,5},{5,4},{6,7},{7,6}} | collective-permute-start | bytes 4423688 | tf_op jit(solution)/shard_map/ppermute | solution.py:569
  89.0 38.8 %collective-permute-start.3 = (bf16[176,4608]{1,0:T(8,128)(2,1)S(1)}, bf16[176,4608]{1,0:T(8,128)(2,1)}, u32[]{:S(2)}, u32[]{:S(2)}) collective-permute-start(bf16[176,4608]{1,0:T(8,128)(2,1)S(1)} %collective-permute-done.refs_0_), channel_id=1, source_target_pairs={{0,1},{1,0},{2,3},{3,2},{4,5},{5,4},{6,7},{7,6}} | collective-permute-start | bytes 4866056 | tf_op jit(solution)/shard_map/ppermute | solution.py:569
  89.5 38.3 %collective-permute-start.4 = (bf16[176,4608]{1,0:T(8,128)(2,1)}, bf16[176,4608]{1,0:T(8,128)(2,1)}, u32[]{:S(2)}, u32[]{:S(2)}) collective-permute-start(bf16[176,4608]{1,0:T(8,128)(2,1)} %collective-permute-done.1.refs_1_), channel_id=1, source_target_pairs={{0,1},{1,0},{2,3},{3,2},{4,5},{5,4},{6,7},{7,6}} | collective-permute-start | bytes 4866056 | tf_op jit(solution)/shard_map/ppermute | solution.py:569
  207.9 3.1 collective-permute-start.7
  211.0 1.0 copy-start
  223.0 12.1 %copy-start.12 = (f32[4608]{0:T(1024)S(1)}, f32[4608]{0:T(1024)}, u32[]{:S(2)}) copy-start(f32[4608]{0:T(1024)} %param.14) | copy-start | bytes 55300
  223.0 73.2 %collective-permute-start.10 = (bf16[192,4608]{1,0:T(8,128)(2,1)}, bf16[192,4608]{1,0:T(8,128)(2,1)S(1)}, u32[]{:S(2)}, u32[]{:S(2)}) collective-permute-start(bf16[192,4608]{1,0:T(8,128)(2,1)} %shard_map.147.p_ref), channel_id=1, source_target_pairs={{0,4},{4,0},{1,5},{5,1},{2,6},{6,2},{3,7},{7,3}} | collective-permute-start | bytes 5308424 | tf_op jit(solution)/shard_map/ppermute | solution.py:575
  233.9 56.1 %collective-permute-start.11 = (bf16[128,4608]{1,0:T(8,128)(2,1)}, bf16[128,4608]{1,0:T(8,128)(2,1)S(1)}, u32[]{:S(2)}, u32[]{:S(2)}) collective-permute-start(bf16[128,4608]{1,0:T(8,128)(2,1)} %shard_map.148.p_ref), channel_id=1, source_target_pairs={{0,4},{4,0},{1,5},{5,1},{2,6},{6,2},{3,7},{7,3}} | collective-permute-start | bytes 3538952 | tf_op jit(solution)/shard_map/ppermute | solution.py:575
  245.7 71.6 %collective-permute-start.9 = (bf16[128,4608]{1,0:T(8,128)(2,1)}, bf16[128,4608]{1,0:T(8,128)(2,1)}, u32[]{:S(2)}, u32[]{:S(2)}) collective-permute-start(bf16[128,4608]{1,0:T(8,128)(2,1)} %shard_map.146.p_ref), channel_id=1, source_target_pairs={{0,4},{4,0},{1,5},{5,1},{2,6},{6,2},{3,7},{7,3}} | collective-permute-start | bytes 3538952 | tf_op jit(solution)/shard_map/ppermute | solution.py:575
  289.9 1.0 copy-start.5
  296.2 1.2 copy-start.2
  304.3 72.4 %collective-permute-start.16 = (bf16[192,4608]{1,0:T(8,128)(2,1)}, bf16[192,4608]{1,0:T(8,128)(2,1)S(1)}, u32[]{:S(2)}, u32[]{:S(2)}) collective-permute-start(bf16[192,4608]{1,0:T(8,128)(2,1)} %get-tuple-element.54.refs_1_), channel_id=1, source_target_pairs={{0,2},{2,0},{1,3},{3,1},{4,6},{6,4},{5,7},{7,5}} | collective-permute-start | bytes 5308424 | tf_op jit(solution)/shard_map/ppermute | solution.py:572
  305.8 65.5 %collective-permute-start.15 = (bf16[128,4608]{1,0:T(8,128)(2,1)}, bf16[128,4608]{1,0:T(8,128)(2,1)S(1)}, u32[]{:S(2)}, u32[]{:S(2)}) collective-permute-start(bf16[128,4608]{1,0:T(8,128)(2,1)} %get-tuple-element.53.refs_0_), channel_id=1, source_target_pairs={{0,2},{2,0},{1,3},{3,1},{4,6},{6,4},{5,7},{7,5}} | collective-permute-start | bytes 3538952 | tf_op jit(solution)/shard_map/ppermute | solution.py:572
  306.3 68.9 %collective-permute-start.21 = (bf16[128,4608]{1,0:T(8,128)(2,1)}, bf16[128,4608]{1,0:T(8,128)(2,1)}, u32[]{:S(2)}, u32[]{:S(2)}) collective-permute-start(bf16[128,4608]{1,0:T(8,128)(2,1)} %get-tuple-element.53.refs_0_), channel_id=1, source_target_pairs={{0,1},{1,0},{2,3},{3,2},{4,5},{5,4},{6,7},{7,6}} | collective-permute-start | bytes 3538952 | tf_op jit(solution)/shard_map/ppermute | solution.py:569
  316.5 16.1 %collective-permute-start.8 = (bf16[64,4608]{1,0:T(8,128)(2,1)}, bf16[64,4608]{1,0:T(8,128)(2,1)}, u32[]{:S(2)}, u32[]{:S(2)}) collective-permute-start(bf16[64,4608]{1,0:T(8,128)(2,1)} %shard_map.145.p_ref), channel_id=1, source_target_pairs={{0,4},{4,0},{1,5},{5,1},{2,6},{6,2},{3,7},{7,3}} | collective-permute-start | bytes 1769480 | tf_op jit(solution)/shard_map/ppermute | solution.py:575
  317.3 93.0 %collective-permute-start.22 = (bf16[192,4608]{1,0:T(8,128)(2,1)}, bf16[192,4608]{1,0:T(8,128)(2,1)}, u32[]{:S(2)}, u32[]{:S(2)}) collective-permute-start(bf16[192,4608]{1,0:T(8,128)(2,1)} %get-tuple-element.54.refs_1_), channel_id=1, source_target_pairs={{0,1},{1,0},{2,3},{3,2},{4,5},{5,4},{6,7},{7,6}} | collective-permute-start | bytes 5308424 | tf_op jit(solution)/shard_map/ppermute | solution.py:569
  332.5 75.5 %collective-permute-start.17 = (bf16[128,4608]{1,0:T(8,128)(2,1)}, bf16[128,4608]{1,0:T(8,128)(2,1)}, u32[]{:S(2)}, u32[]{:S(2)}) collective-permute-start(bf16[128,4608]{1,0:T(8,128)(2,1)} %get-tuple-element.55.refs_2_), channel_id=1, source_target_pairs={{0,2},{2,0},{1,3},{3,1},{4,6},{6,4},{5,7},{7,5}} | collective-permute-start | bytes 3538952 | tf_op jit(solution)/shard_map/ppermute | solution.py:572
  371.3 35.9 %copy-start.4 = (bf16[128,4608]{1,0:T(8,128)(2,1)}, bf16[128,4608]{1,0:T(8,128)(2,1)S(1)}, u32[]{:S(2)}) copy-start(bf16[128,4608]{1,0:T(8,128)(2,1)S(1)} %collective-permute-done.15.refs_0_) | copy-start | bytes 3538948
  371.3 38.6 %collective-permute-start.23 = (bf16[128,4608]{1,0:T(8,128)(2,1)}, bf16[128,4608]{1,0:T(8,128)(2,1)}, u32[]{:S(2)}, u32[]{:S(2)}) collective-permute-start(bf16[128,4608]{1,0:T(8,128)(2,1)} %get-tuple-element.55.refs_2_), channel_id=1, source_target_pairs={{0,1},{1,0},{2,3},{3,2},{4,5},{5,4},{6,7},{7,6}} | collective-permute-start | bytes 3538952 | tf_op jit(solution)/shard_map/ppermute | solution.py:569
  375.2 32.0 %collective-permute-start.13 = (bf16[64,4608]{1,0:T(8,128)(2,1)}, bf16[64,4608]{1,0:T(8,128)(2,1)S(1)}, u32[]{:S(2)}, u32[]{:S(2)}) collective-permute-start(bf16[64,4608]{1,0:T(8,128)(2,1)} %get-tuple-element.52.refs_0_), channel_id=1, source_target_pairs={{0,2},{2,0},{1,3},{3,1},{4,6},{6,4},{5,7},{7,5}} | collective-permute-start | bytes 1769480 | tf_op jit(solution)/shard_map/ppermute | solution.py:572
  376.7 51.1 %copy-start.1 = (bf16[192,4608]{1,0:T(8,128)(2,1)}, bf16[192,4608]{1,0:T(8,128)(2,1)S(1)}, u32[]{:S(2)}) copy-start(bf16[192,4608]{1,0:T(8,128)(2,1)S(1)} %collective-permute-done.16.refs_1_) | copy-start | bytes 5308420
  376.7 51.1 %collective-permute-start.19 = (bf16[192,4608]{1,0:T(8,128)(2,1)S(1)}, bf16[192,4608]{1,0:T(8,128)(2,1)}, u32[]{:S(2)}, u32[]{:S(2)}) collective-permute-start(bf16[192,4608]{1,0:T(8,128)(2,1)S(1)} %collective-permute-done.16.refs_1_), channel_id=1, source_target_pairs={{0,1},{1,0},{2,3},{3,2},{4,5},{5,4},{6,7},{7,6}} | collective-permute-start | bytes 5308424 | tf_op jit(solution)/shard_map/ppermute | solution.py:569
  407.2 0.8 copy-start.6
  407.2 20.6 %collective-permute-start.18 = (bf16[128,4608]{1,0:T(8,128)(2,1)S(1)}, bf16[128,4608]{1,0:T(8,128)(2,1)}, u32[]{:S(2)}, u32[]{:S(2)}) collective-permute-start(bf16[128,4608]{1,0:T(8,128)(2,1)S(1)} %collective-permute-done.15.refs_0_), channel_id=1, source_target_pairs={{0,1},{1,0},{2,3},{3,2},{4,5},{5,4},{6,7},{7,6}} | collective-permute-start | bytes 3538952 | tf_op jit(solution)/shard_map/ppermute | solution.py:569
  408.0 19.8 %collective-permute-start.20 = (bf16[128,4608]{1,0:T(8,128)(2,1)}, bf16[128,4608]{1,0:T(8,128)(2,1)}, u32[]{:S(2)}, u32[]{:S(2)}) collective-permute-start(bf16[128,4608]{1,0:T(8,128)(2,1)} %collective-permute-done.17.refs_2_), channel_id=1, source_target_pairs={{0,1},{1,0},{2,3},{3,2},{4,5},{5,4},{6,7},{7,6}} | collective-permute-start | bytes 3538952 | tf_op jit(solution)/shard_map/ppermute | solution.py:569
  409.9 35.3 %collective-permute-start.12 = (bf16[64,4608]{1,0:T(8,128)(2,1)}, bf16[64,4608]{1,0:T(8,128)(2,1)}, u32[]{:S(2)}, u32[]{:S(2)}) collective-permute-start(bf16[64,4608]{1,0:T(8,128)(2,1)} %get-tuple-element.52.refs_0_), channel_id=1, source_target_pairs={{0,1},{1,0},{2,3},{3,2},{4,5},{5,4},{6,7},{7,6}} | collective-permute-start | bytes 1769480 | tf_op jit(solution)/shard_map/ppermute | solution.py:569
  410.4 34.8 %collective-permute-start.14 = (bf16[64,4608]{1,0:T(8,128)(2,1)}, bf16[64,4608]{1,0:T(8,128)(2,1)}, u32[]{:S(2)}, u32[]{:S(2)}) collective-permute-start(bf16[64,4608]{1,0:T(8,128)(2,1)} %copy-done.6), channel_id=1, source_target_pairs={{0,1},{1,0},{2,3},{3,2},{4,5},{5,4},{6,7},{7,6}} | collective-permute-start | bytes 1769480 | tf_op jit(solution)/shard_map/ppermute | solution.py:569
  546.9 5.6 collective-permute-start.24
  548.5 2.0 collective-permute-start.25
  549.7 39.1 %copy-start.7 = (f32[8,4608]{1,0:T(8,128)S(1)}, f32[8,4608]{1,0:T(8,128)}, u32[]{:S(2)}) copy-start(f32[8,4608]{1,0:T(8,128)} %get-tuple-element.67) | copy-start | bytes 442372
  549.7 39.1 %copy-start.8 = (f32[8,4608]{1,0:T(8,128)S(1)}, f32[8,4608]{1,0:T(8,128)}, u32[]{:S(2)}) copy-start(f32[8,4608]{1,0:T(8,128)} %get-tuple-element.68) | copy-start | bytes 442372
  549.7 39.1 %copy-start.9 = (f32[8,4608]{1,0:T(8,128)S(1)}, f32[8,4608]{1,0:T(8,128)}, u32[]{:S(2)}) copy-start(f32[8,4608]{1,0:T(8,128)} %get-tuple-element.69) | copy-start | bytes 442372
  549.7 39.1 %copy-start.10 = (f32[8,4608]{1,0:T(8,128)S(1)}, f32[8,4608]{1,0:T(8,128)}, u32[]{:S(2)}) copy-start(f32[8,4608]{1,0:T(8,128)} %get-tuple-element.70) | copy-start | bytes 442372
  549.7 39.5 %copy-start.11 = (bf16[2048,512]{1,0:T(8,128)(2,1)S(1)}, bf16[2048,512]{1,0:T(8,128)(2,1)}, u32[]{:S(2)}) copy-start(bf16[2048,512]{1,0:T(8,128)(2,1)} %get-tuple-element.63.k0) | copy-start | bytes 6291460
  549.7 2.0 collective-permute-start.26
  550.5 1.3 copy-start.13
  587.7 104.5 %collective-permute-start.27 = (bf16[512,4608]{1,0:T(8,128)(2,1)}, bf16[512,4608]{1,0:T(8,128)(2,1)}, u32[]{:S(2)}, u32[]{:S(2)}) collective-permute-start(bf16[512,4608]{1,0:T(8,128)(2,1)} %shard_map.156.p_ref), channel_id=1, source_target_pairs={{0,4},{4,0},{1,5},{5,1},{2,6},{6,2},{3,7},{7,3}} | collective-permute-start | bytes 14155784 | tf_op jit(solution)/shard_map/ppermute | solution.py:575
  588.6 117.6 %collective-permute-start.33 = (bf16[2048,1024]{1,0:T(8,128)(2,1)}, bf16[2048,1024]{1,0:T(8,128)(2,1)}, u32[]{:S(2)}, u32[]{:S(2)}) collective-permute-start(bf16[2048,1024]{1,0:T(8,128)(2,1)} %get-tuple-element.47.c0_ref.ctx_ref), channel_id=1, source_target_pairs={{0,1},{1,0},{2,3},{3,2},{4,5},{5,4},{6,7},{7,6}} | collective-permute-start | bytes 12582920 | tf_op jit(solution)/shard_map/ppermute | solution.py:569
  588.9 169.0 %collective-permute-start.30 = (bf16[2048,1024]{1,0:T(8,128)(2,1)}, bf16[2048,1024]{1,0:T(8,128)(2,1)}, u32[]{:S(2)}, u32[]{:S(2)}) collective-permute-start(bf16[2048,1024]{1,0:T(8,128)(2,1)} %get-tuple-element.62.q0), channel_id=1, source_target_pairs={{0,1},{1,0},{2,3},{3,2},{4,5},{5,4},{6,7},{7,6}} | collective-permute-start | bytes 12582920 | tf_op jit(solution)/shard_map/ppermute | solution.py:569
  589.2 168.7 %collective-permute-start.31 = (bf16[2048,512]{1,0:T(8,128)(2,1)S(1)}, bf16[2048,512]{1,0:T(8,128)(2,1)}, u32[]{:S(2)}, u32[]{:S(2)}) collective-permute-start(bf16[2048,512]{1,0:T(8,128)(2,1)S(1)} %copy-done.11), channel_id=1, source_target_pairs={{0,1},{1,0},{2,3},{3,2},{4,5},{5,4},{6,7},{7,6}} | collective-permute-start | bytes 6291464 | tf_op jit(solution)/shard_map/ppermute | solution.py:569
  589.4 168.5 %collective-permute-start.32 = (bf16[2048,512]{1,0:T(8,128)(2,1)}, bf16[2048,512]{1,0:T(8,128)(2,1)}, u32[]{:S(2)}, u32[]{:S(2)}) collective-permute-start(bf16[2048,512]{1,0:T(8,128)(2,1)} %get-tuple-element.64.v0), channel_id=1, source_target_pairs={{0,1},{1,0},{2,3},{3,2},{4,5},{5,4},{6,7},{7,6}} | collective-permute-start | bytes 6291464 | tf_op jit(solution)/shard_map/ppermute | solution.py:569
  706.1 50.3 %collective-permute-start.28 = (f32[2,4608]{1,0:T(2,128)S(1)}, f32[2,4608]{1,0:T(2,128)S(1)}, u32[]{:S(2)}, u32[]{:S(2)}) collective-permute-start(f32[2,4608]{1,0:T(2,128)S(1)} %pad_maximum_fusion.2), channel_id=1, source_target_pairs={{0,1},{1,0},{2,3},{3,2},{4,5},{5,4},{6,7},{7,6}} | collective-permute-start | bytes 110600 | tf_op jit(solution)/shard_map/ppermute | solution.py:569
  756.5 101.9 %collective-permute-start.29 = (f32[2,4608]{1,0:T(2,128)S(1)}, f32[2,4608]{1,0:T(2,128)S(1)}, u32[]{:S(2)}, u32[]{:S(2)}) collective-permute-start(f32[2,4608]{1,0:T(2,128)S(1)} %fusion.1), channel_id=1, source_target_pairs={{0,2},{2,0},{1,3},{3,1},{4,6},{6,4},{5,7},{7,5}} | collective-permute-start | bytes 110600 | tf_op jit(solution)/shard_map/ppermute | solution.py:572
  (1 other events, 0.8 us)

commit v5 on v4

--- a/solution.py
+++ b/solution.py
@@ -215,136 +215,97 @@
 
 
 VMEM_LIMIT = 64_000_000
-KD = 512
-
-
-def gmm_kernel(sc_ref, *refs, layout, mode, n_w, R, r0, aliased):
+
+
+def gmm_kernel(sc_ref, *refs, layout, mode, R, r0, B, n_rope, aliased):
     np_ = len(layout)
     pieces = refs[:np_]
-    ws = refs[np_:np_ + n_w]
-    rest = refs[np_ + n_w:]
+    w_ref = refs[np_]
+    rest = refs[np_ + 1:]
     if mode == "qkv":
         cos_ref, sin_ref = rest[:2]
         rest = rest[2:]
     if aliased:
         rest = rest[2:]
-    out_ref, all_ref, x_ref, acc_ref, w_ref, sem_in, sem_out = rest
-    i = pl.program_id(0)
+    out_ref, all_ref, x_ref, sem_in, sem_out = rest
+    n = pl.program_id(0)
     last = pl.num_programs(0) - 1
-    B = x_ref.shape[0]
-    core = sc_ref[1]
-
-    def cols(k):
-        return pl.ds(pl.multiple_of(k * KD, KD), KD)
-
-    def cp_in(p, k):
-        slot, n = layout[p]
-        off = pl.multiple_of(sc_ref[slot + 1], 16)
-        return pltpu.make_async_copy(pieces[p].at[:, cols(k)], x_ref.at[sc_ref[slot], pl.ds(off, n), cols(k)], sem_in.at[k])
-
-    def cp_out(b, k):
-        return pltpu.make_async_copy(x_ref.at[b, :, cols(k)], all_ref.at[sc_ref[0] * B + b, pl.ds(r0, R), cols(k)], sem_out)
-
-    @pl.when(i == 0)
+    S, M, _ = x_ref.shape
+    per = M // R
+
+    def cp_in(p):
+        slot, rows = layout[p]
+        off = pl.multiple_of(sc_ref[2 + B + p], 16)
+        return pltpu.make_async_copy(pieces[p], x_ref.at[slot, pl.ds(off, rows)], sem_in.at[p])
+
+    def cp_out(s, j):
+        return pltpu.make_async_copy(
+            x_ref.at[s, pl.ds(j * R, R)], all_ref.at[sc_ref[0] * B + sc_ref[2 + s * per + j], pl.ds(r0, R)], sem_out.at[s * per + j])
+
+    @pl.when(n == 0)
     def _():
-        @pl.loop(0, last + 1)
-        def _(k):
+        for p in range(np_):
+            cp_in(p).start()
+
+    for s in range(S):
+        @pl.when(n == 0)
+        def _(s=s):
             for p in range(np_):
-                cp_in(p, k).start()
-
-    for p in range(np_):
-        cp_in(p, i).wait()
-    for b in range(B):
-        cp_out(b, i).start()
-
-    ks = pl.ds(pl.multiple_of(i * KD, KD), KD)
-
-    def products(b):
-        x = x_ref[b, :, ks]
-        if mode == "qkv":
-            n = w_ref.shape[2] // 2
-            half = pl.ds(pl.multiple_of(core * n, n), n)
-            return [dotf(x, w_ref[0], NN), dotf(x, w_ref[1, :, half], NN), dotf(x, w_ref[2, :, half], NN)]
-        return [dotf(x, ws[0][...], NT)]
-
-    def prep():
-        if mode == "qkv":
-            for j in range(3):
-                w_ref[j] = ws[j][...].reshape(w_ref.shape[1:])
-
-    @pl.when(i == 0)
+                if layout[p][0] == s:
+                    cp_in(p).wait()
+            for j in range(per):
+                cp_out(s, j).start()
+
+        res = dotf(x_ref[s], w_ref[...], NN if mode == "qkv" else NT)
+        for j in range(per):
+            dst = sc_ref[2 + s * per + j]
+            rows = res[j * R:(j + 1) * R]
+            if mode == "qkv":
+                c = jnp.where(n < n_rope, cos_ref[dst], 1.0)
+                t = jnp.where(n < n_rope, sin_ref[dst], 0.0)
+                for h in range(rows.shape[1] // HEAD):
+                    r = rows[:, h * HEAD:(h + 1) * HEAD]
+                    out_ref[dst, :, h * HEAD:(h + 1) * HEAD] = (r * c + pltpu.roll(r, HEAD // 2, 1) * t).astype(BF16)
+            else:
+                out_ref[dst] = rows.astype(BF16)
+
+    @pl.when(n == last)
     def _():
-        prep()
-        for b in range(B):
-            o = 0
-            for d in products(b):
-                acc_ref[b, :, o:o + d.shape[1]] = d
-                o += d.shape[1]
-
-    @pl.when(i > 0)
-    def _():
-        prep()
-        for b in range(B):
-            o = 0
-            for d in products(b):
-                acc_ref[b, :, o:o + d.shape[1]] += d
-                o += d.shape[1]
-
-    @pl.when(i == last)
-    def _():
-        N = acc_ref.shape[2]
-        for b in range(B):
-            if mode == "qkv":
-                n_rope = N * 3 // 4
-                c, s = cos_ref[b], sin_ref[b]
-                for h in range(n_rope // HEAD):
-                    r = acc_ref[b, :, h * HEAD:(h + 1) * HEAD]
-                    out_ref[b, :, h * HEAD:(h + 1) * HEAD] = (r * c + pltpu.roll(r, HEAD // 2, 1) * s).astype(BF16)
-                out_ref[b, :, n_rope:] = acc_ref[b, :, n_rope:].astype(BF16)
-            else:
-                out_ref[b] = acc_ref[b].astype(BF16)
-
-        @pl.loop(0, last + 1)
-        def _(k):
-            for b in range(B):
-                cp_out(b, k).wait()
-
-
-def gather_matmul(chip, core, places, pieces, ws, mode, tabs, B, R, r0, N, bufs=None):
+        for s in range(S):
+            for j in range(per):
+                cp_out(s, j).wait()
+
+
+def gather_matmul(chip, core, places, pieces, w, mode, tabs, S, dsts, R, r0, N, bufs=None):
     D = pieces[0].shape[1]
-    tokens = 512
-    nk = D // KD
-    scal = jnp.stack([jnp.asarray(v, jnp.int32) for v in [chip, core] + [v for p in places for v in p]])
-    layout = tuple((2 + 2 * i, p.shape[0]) for i, p in enumerate(pieces))
+    tokens, nb = 512, 512
+    B = len(dsts)
+    scal = jnp.stack([jnp.asarray(v, jnp.int32) for v in [chip, core] + list(dsts) + [o for _, o in places]])
+    layout = tuple((slot, p.shape[0]) for (slot, _), p in zip(places, pieces))
     anyspec = pl.BlockSpec(memory_space=pl.ANY)
     if mode == "qkv":
-        hb = ws[1].shape[1]
-        w_specs = [pl.BlockSpec((KD, hb, HEAD), lambda i, s: (i, s[1], 0))] + [pl.BlockSpec((KD, hb, HEAD), lambda i, s: (i, 0, 0))] * 2
-        w_specs += [pl.BlockSpec((B, R, HEAD), lambda i, s: (s[0], 0, 0), pipeline_mode=pl.Buffered(1))] * 2
-        wscr = pltpu.VMEM((3, KD, hb * HEAD), BF16)
+        w_specs = [pl.BlockSpec((D, nb), lambda n, s: (0, n))]
+        w_specs += [pl.BlockSpec((B, R, HEAD), lambda n, s: (s[0], 0, 0), pipeline_mode=pl.Buffered(1))] * 2
     else:
-        w_specs = [pl.BlockSpec((N, KD), lambda i, s: (s[1], i))]
-        wscr = pltpu.VMEM((1, 16, HEAD), BF16)
+        w_specs = [pl.BlockSpec((nb, D), lambda n, s: (s[1] * (N // nb) + n, 0))]
     in_specs = [anyspec] * len(pieces) + w_specs
-    args = list(pieces) + list(ws) + [t.reshape(4, tokens, HEAD) for t in tabs]
+    args = list(pieces) + [w] + [t.reshape(4, tokens, HEAD) for t in tabs]
     aliases = {}
     if bufs is not None:
         aliases = {1 + len(args): 0, 2 + len(args): 1}
         in_specs += [anyspec, anyspec]
         args += list(bufs)
     return pl.pallas_call(
-        functools.partial(gmm_kernel, layout=layout, mode=mode, n_w=len(ws), R=R, r0=r0, aliased=bufs is not None),
+        functools.partial(gmm_kernel, layout=layout, mode=mode, R=R, r0=r0, B=B, n_rope=(N * 3 // 4) // nb, aliased=bufs is not None),
         grid_spec=pltpu.PrefetchScalarGridSpec(
             num_scalar_prefetch=1,
-            grid=(nk,),
+            grid=(N // nb,),
             in_specs=in_specs,
-            out_specs=[pl.BlockSpec((B, R, N), lambda i, s: (s[0], r0 // R, 0), pipeline_mode=pl.Buffered(1)), anyspec],
+            out_specs=[pl.BlockSpec((B, R, nb), lambda n, s: (s[0], r0 // R, n)), anyspec],
             scratch_shapes=[
-                pltpu.VMEM((B, R, D), BF16),
-                pltpu.VMEM((B, R, N), F32),
-                wscr,
-                pltpu.SemaphoreType.DMA((nk,)),
-                pltpu.SemaphoreType.DMA,
+                pltpu.VMEM((S, B * R // S, D), BF16),
+                pltpu.SemaphoreType.DMA((len(pieces),)),
+                pltpu.SemaphoreType.DMA((B,)),
             ],
         ),
         out_shape=[jax.ShapeDtypeStruct((4, tokens, N), BF16), jax.ShapeDtypeStruct((4, tokens, D), BF16)],
@@ -352,6 +313,34 @@
         compiler_params=pltpu.CompilerParams(dimension_semantics=("arbitrary",), vmem_limit_bytes=VMEM_LIMIT),
         cost_estimate=pl.CostEstimate(flops=2 * B * R * D * N, bytes_accessed=B * R * D * 4 + N * D * 2, transcendentals=0),
     )(scal, *args)
+
+
+def w_kernel(c_ref, wq_ref, wk_ref, wv_ref, out_ref, s_ref):
+    nq, n = wq_ref.shape[1] * HEAD, s_ref.shape[2] // 2
+    out_ref[:, :nq] = wq_ref[...].reshape(-1, nq)
+    half = pl.ds(pl.multiple_of(c_ref[0] * n, n), n)
+    for j, ref in enumerate((wk_ref, wv_ref)):
+        s_ref[j] = ref[...].reshape(-1, 2 * n)
+        out_ref[:, nq + j * n:nq + (j + 1) * n] = s_ref[j, :, half]
+
+
+def w_layout(c, w_q, w_k, w_v, db):
+    D, hb = w_k.shape[:2]
+    nq, n = w_q.shape[1] // 2, hb // 2
+    N = (nq + 2 * n) * HEAD
+    return pl.pallas_call(
+        w_kernel,
+        grid_spec=pltpu.PrefetchScalarGridSpec(
+            num_scalar_prefetch=1,
+            grid=(D // db,),
+            in_specs=[pl.BlockSpec((db, nq, HEAD), lambda i, s: (i, s[0], 0))] + [pl.BlockSpec((db, hb, HEAD), lambda i, s: (i, 0, 0))] * 2,
+            out_specs=pl.BlockSpec((db, N), lambda i, s: (i, 0)),
+            scratch_shapes=[pltpu.VMEM((2, db, hb * HEAD), BF16)],
+        ),
+        out_shape=jax.ShapeDtypeStruct((D, N), BF16),
+        compiler_params=pltpu.CompilerParams(dimension_semantics=("arbitrary",), vmem_limit_bytes=VMEM_LIMIT),
+        cost_estimate=pl.CostEstimate(flops=D * N * 500, bytes_accessed=D * N * 5, transcendentals=0),
+    )(jnp.reshape(c, (1,)).astype(jnp.int32), w_q, w_k, w_v)
 
 
 def orow_kernel(sc_ref, c0_ref, c1_ref, w_ref, out_ref, *, r0):
@@ -384,20 +373,20 @@
     )(scal, ctx, ctx_pr, w)
 
 
-def ga_kernel(sc_ref, q0, k0, v0, q1, k1, v1, wq_ref, wk_ref, wv_ref, out_ref, wq_s, wk_s, wv_s):
-    core = sc_ref[1]
+def ga_kernel(sc_ref, q0, k0, v0, q1, k1, v1, w0_ref, w1_ref, out_ref):
     acc = None
-    for w_ref, s_ref, own, oth in ((wq_ref, wq_s, q0, q1), (wk_ref, wk_s, k0, k1), (wv_ref, wv_s, v0, v1)):
-        s_ref[...] = w_ref[...].reshape(s_ref.shape)
-        n = own.shape[1]
-        for c, g in ((core, own), (1 - core, oth)):
-            d = dotf(g[...], s_ref[:, pl.ds(pl.multiple_of(c * n, n), n)], NT)
+    for w_ref, gs in ((w0_ref, (q0, k0, v0)), (w1_ref, (q1, k1, v1))):
+        o = 0
+        for g in gs:
+            n = g.shape[1]
+            d = dotf(g[...], w_ref[:, o:o + n], NT)
             acc = d if acc is None else acc + d
+            o += n
     out_ref[...] = acc.astype(BF16)
 
 
 def ga_rows(scal, own, oth, ws, M, db):
-    D = ws[0].shape[0]
+    D, N = ws[0].shape
     return pl.pallas_call(
         ga_kernel,
         grid_spec=pltpu.PrefetchScalarGridSpec(
@@ -405,13 +394,12 @@
             grid=(D // db,),
             in_specs=[pl.BlockSpec((M, g.shape[1]), lambda i, s: (s[2], 0)) for g in own]
             + [pl.BlockSpec((M, g.shape[1]), lambda i, s: (0, 0)) for g in oth]
-            + [pl.BlockSpec((db,) + w.shape[1:], lambda i, s: (i, 0, 0)) for w in ws],
+            + [pl.BlockSpec((db, N), lambda i, s: (i, 0)) for w in ws],
             out_specs=pl.BlockSpec((M, db), lambda i, s: (0, i)),
-            scratch_shapes=[pltpu.VMEM((db, w.shape[1] * HEAD), BF16) for w in ws],
         ),
         out_shape=jax.ShapeDtypeStruct((M, D), BF16),
         compiler_params=pltpu.CompilerParams(dimension_semantics=("arbitrary",), vmem_limit_bytes=VMEM_LIMIT),
-        cost_estimate=pl.CostEstimate(flops=2 * M * sum(w.size for w in ws), bytes_accessed=sum(w.size for w in ws) * 2, transcendentals=0),
+        cost_estimate=pl.CostEstimate(flops=4 * M * D * N, bytes_accessed=4 * D * N, transcendentals=0),
     )(scal, *own, *oth, *ws)
 
 
@@ -597,9 +585,11 @@
         a_xp = [to_core(r) for r in a_x]
         wo2 = w_o.reshape(-1, D)
         N = (HL + 2 * KL) * HEAD
-        qkv_args = ((w_q, w_k, w_v), "qkv", (cos, sin), 2, tokens, 0, N)
-        bufs = gather_matmul(xi, core, [(core, 0), (1 - core, 0)], [a_loc, a_p], *qkv_args)
-        places = [(core, o) for o in a_off] + [(1 - core, o) for o in a_off]
+        w_own = w_layout(core, w_q, w_k, w_v, 512)
+        w_oth = w_layout(1 - core, w_q, w_k, w_v, 512)
+        qkv_args = (w_own, "qkv", (cos, sin), 2, [core, 1 - core], tokens, 0, N)
+        bufs = gather_matmul(xi, core, [(0, 0), (1, 0)], [a_loc, a_p], *qkv_args)
+        places = [(0, o) for o in a_off] + [(1, o) for o in a_off]
         qkv, a_all = gather_matmul(1 - xi, core, places, a_x + a_xp, *qkv_args, bufs=bufs)
         qkv = qkv.reshape(T, N)
         a_all = a_all.reshape(T, D)
@@ -626,18 +616,20 @@
         gxp = [to_core(g) for g in gx]
         HN = HL * HEAD
         RE, RL = starts[-1], sizes[-1]
-        places = [(core, o) for o in starts[:-1]] + [(1 - core, o) for o in starts[:-1]]
-        bufs = gather_matmul(xi, core, places, gos[:-1] + gp[:-1], (wo2,), "nt", (), 2, RE, 0, HN)
-        bufs = gather_matmul(1 - xi, core, places, gx[:-1] + gxp[:-1], (wo2,), "nt", (), 2, RE, 0, HN, bufs=bufs)
-        places = [(me ^ rel, 0) for rel in range(4)]
-        dctx, go_all = gather_matmul(0, core, places, [gos[-1], gp[-1], gx[-1], gxp[-1]], (wo2,), "nt", (), 4, RL, RE, HN, bufs=bufs)
+        places = [(c, o) for c in range(2) for o in starts[:-1]]
+        pair = [core, 1 - core]
+        bufs = gather_matmul(xi, core, places, gos[:-1] + gp[:-1], wo2, "nt", (), 2, pair, RE, 0, HN)
+        bufs = gather_matmul(1 - xi, core, places, gx[:-1] + gxp[:-1], wo2, "nt", (), 2, pair, RE, 0, HN, bufs=bufs)
+        places = [(0, rel * RL) for rel in range(4)]
+        dctx, go_all = gather_matmul(0, core, places, [gos[-1], gp[-1], gx[-1], gxp[-1]], wo2, "nt", (), 1, [me ^ rel for rel in range(4)],
+                                     RL, RE, HN, bufs=bufs)
         dctx = dctx.reshape(T, HN)
         go_all = go_all.reshape(T, D)
 
         dqkv = attn_bwd(qkv, KL, HL, dctx, ctx, lse, cos, sin)
         dqkv_pr = [to_core(lax.dynamic_slice_in_dim(g, (me ^ 1) * tokens, tokens, 0)) for g in dqkv]
         dqkv_p = [to_core(g) for g in dqkv]
-        ga_part = ga_rows(base, dqkv, dqkv_pr, (w_q, w_k, w_v), tokens, 512)
+        ga_part = ga_rows(base, dqkv, dqkv_pr, (w_own, w_oth), tokens, 512)
         ga_peer = to_tp(ga_part)
 
         dwo = dwo_proj(base, ctx, ctx_p, go_all, 512).reshape(w_o.shape)

time: 865 us -> 853 us (0.986)
  waiting for transfers between devices: 288 us -> 264 us
    ppermute x7, waiting for transfers between devices: 129 us -> 109 us  [to_x(): return lax.ppermute(v, 'cp', x_perm)]
    pallas_call x5 -> x7, Pallas kernels: 128 us -> 142 us  [the longest x5 101 us: gather_matmul(): pl.pallas_call(functools.partial(gmm_kernel, layout=layout, mode=mode, R=...]
  transfers between devices with their start and end apart: 34 -> 34, of which waited for: 10 -> 9; matrix products, arithmetic and copies ran while one was open for 2% -> 2% of each run, Pallas kernels for 33% -> 38%
where the time goes in v5:
time: 853 us; the launch traced here: 844 us
  Pallas kernels  528 us (62%)
  waiting for transfers between devices  264 us (31%)
  starting transfers between devices  23.3 us (3%)
  local copies, waits for them, and re-layouts  20 us (2%)
    ppermute x6, waiting for transfers between devices, to_tp(): return lax.ppermute(v, 'tp', tp_perm)  154 us
    ppermute x7, waiting for transfers between devices, to_x(): return lax.ppermute(v, 'cp', x_perm)  109 us
    pallas_call x5, Pallas kernels, gather_matmul(): pl.pallas_call(functools.partial(gmm_kernel, layout=layout, mode=mode, R=...  101 us
    pallas_call x1, Pallas kernels, dw_proj(): pl.pallas_call(dw_kernel, grid_spec=pltpu.PrefetchScalarGridSpec(num_scal...  101 us
    pallas_call x1, Pallas kernels, attn_bwd(): pl.pallas_call(functools.partial(attn_bwd_kernel, k1=scale / SOFT_CAP, k2...  83.4 us
    pallas_call x1, Pallas kernels, dwo_proj(): pl.pallas_call(dwo_kernel, grid_spec=pltpu.PrefetchScalarGridSpec(num_sca...  50.1 us
    pallas_call x1, Pallas kernels, attn_fwd(): pl.pallas_call(functools.partial(attn_fwd_kernel, k1=scale / SOFT_CAP, k2...  41.4 us
    pallas_call x4, Pallas kernels, o_rows(): pl.pallas_call(functools.partial(orow_kernel, r0=r0), grid_spec=pltpu.Pre...  41.3 us
  transfers between devices with their start and end apart: 34, of which 9 were waited for; matrix products, arithmetic and copies ran while one was open for 2% of the time, Pallas kernels for 38%

profile of v5, /device:TPU:0, one launch (start us, length us, event | category | flops | bytes accessed | tf_op | source)
XLA Modules:
  0.0 843.8 jit_solution(10997390647643396510)
XLA Ops:
  0.6 1.3 reshape.73.g_ref
  2.0 7.8 a_norm.1.refs_0_
  10.6 1.5 constant_dynamic-slice_fusion.4
  12.2 2.5 collective-permute-start
  14.7 36.2 %collective-permute-done.refs_0_ = bf16[176,4608]{1,0:T(8,128)(2,1)} collective-permute-done((bf16[176,4608]{1,0:T(8,128)(2,1)S(1)}, bf16[176,4608]{1,0:T(8,128)(2,1)}, u32[]{:S(2)}, u32[]{:S(2)}) %collective-permute-start) | collective-permute-done | bytes 1622048 | tf_op jit(solution)/shard_map/ppermute | solution.py:560
  50.9 1.8 collective-permute-start.1
  52.7 1.5 slice.12
  54.1 1.5 collective-permute-start.2
  55.7 3.7 fusion
  59.4 1.9 pad_maximum_fusion
  62.5 20.6 %shard_map.143.refs_2_.refs_6_.w0_ref = bf16[4608,2048]{1,0:T(8,128)(2,1)} custom-call(s32[1]{0:T(128)} %bitcast.1.c_ref, bf16[4608,16,128]{2,1,0:T(8,128)(2,1)} %wq_ref.3, bf16[4608,8,128]{2,1,0:T(8,128)(2,1)} %wk_ref.3, bf16[4608,8,128]{2,1,0:T(8,128)(2,1)} %wv_ref.3), custom_call_target="tpu_custom_call" | custom-call | flops 4718592000 | bytes 47185920 | tf_op jit(solution)/shard_map/pallas_call | solution.py:331
  83.1 4.7 collective-permute-done.2.refs_2_
  88.5 29.9 %shard_map.144 = (bf16[4,512,2048]{2,1,0:T(8,128)(2,1)}, bf16[4,512,4608]{2,1,0:T(8,128)(2,1)}) custom-call(s32[6]{0:T(128)} %stack.86.sc_ref, bf16[512,4608]{1,0:T(8,128)(2,1)} %a_norm.1.refs_0_, bf16[512,4608]{1,0:T(8,128)(2,1)} %collective-permute-done.6.refs_1_, bf16[4608,2048]{1,0:T(8,128)(2,1)} %shard_map.143.refs_2_.refs_6_.w0_ref, ...), custom_call_target="tpu_custom_call" | custom-call | flops 19327352832 | bytes 37748736 | tf_op jit(solution)/shard_map/pallas_call | solution.py:298
  119.6 29.9 %shard_map.145 = (bf16[4,512,2048]{2,1,0:T(8,128)(2,1)}, bf16[4,512,4608]{2,1,0:T(8,128)(2,1)}) custom-call(s32[10]{0:T(128)} %stack.85.sc_ref, bf16[176,4608]{1,0:T(8,128)(2,1)} %collective-permute-done.refs_0_, bf16[176,4608]{1,0:T(8,128)(2,1)} %collective-permute-done.1.refs_1_, ...), custom_call_target="tpu_custom_call", output_to_operand_aliasing={{0}: (10, {}), {1}: (11, {})} | custom-call | flops 19327352832 | bytes 37748736 | tf_op jit(solution)/shard_map/pallas_call | solution.py:298
  149.5 41.4 %attn_fwd.1 = (bf16[2048,1024]{1,0:T(8,128)(2,1)}, f32[4,2,2048]{2,1,0:T(2,128)}) custom-call(bf16[2048,2048]{1,0:T(8,128)(2,1)} %bitcast.39, bf16[2048,2048]{1,0:T(8,128)(2,1)} %bitcast.40, bf16[2048,2048]{1,0:T(8,128)(2,1)} %bitcast.41), custom_call_target="tpu_custom_call" | custom-call | flops 17179869184 | bytes 16777216 | tf_op jit(solution)/shard_map/attn_fwd/pallas_call | solution.py:91
  193.4 1.7 collective-permute-done.7.c1_ref
  196.0 11.0 %shard_map.148.p_ref = bf16[192,4608]{1,0:T(8,128)(2,1)} custom-call(s32[4]{0:T(128)} %pad_add_fusion.sc_ref, bf16[2048,1024]{1,0:T(8,128)(2,1)} %get-tuple-element.47.c0_ref.ctx_ref, bf16[512,1024]{1,0:T(8,128)(2,1)} %copy-done, bf16[2048,4608]{1,0:T(8,128)(2,1)} %bitcast.21), custom_call_target="tpu_custom_call" | custom-call | flops 3623878656 | bytes 18874368 | tf_op jit(solution)/shard_map/pallas_call | solution.py:358
  207.0 1.5 collective-permute-start.10
  208.5 10.1 %shard_map.149.p_ref = bf16[128,4608]{1,0:T(8,128)(2,1)} custom-call(s32[4]{0:T(128)} %pad_add_fusion.sc_ref, bf16[2048,1024]{1,0:T(8,128)(2,1)} %get-tuple-element.47.c0_ref.ctx_ref, bf16[512,1024]{1,0:T(8,128)(2,1)} %copy-done, bf16[2048,4608]{1,0:T(8,128)(2,1)} %bitcast.22), custom_call_target="tpu_custom_call" | custom-call | flops 2415919104 | bytes 18874368 | tf_op jit(solution)/shard_map/pallas_call | solution.py:358
  219.7 10.1 %shard_map.147.p_ref = bf16[128,4608]{1,0:T(8,128)(2,1)} custom-call(s32[4]{0:T(128)} %pad_add_fusion.sc_ref, bf16[2048,1024]{1,0:T(8,128)(2,1)} %get-tuple-element.47.c0_ref.ctx_ref, bf16[512,1024]{1,0:T(8,128)(2,1)} %copy-done, bf16[2048,4608]{1,0:T(8,128)(2,1)} %bitcast.23), custom_call_target="tpu_custom_call" | custom-call | flops 2415919104 | bytes 18874368 | tf_op jit(solution)/shard_map/pallas_call | solution.py:358
  229.8 1.5 collective-permute-start.9
  231.3 42.7 %collective-permute-done.11.r_ref = bf16[128,4608]{1,0:T(8,128)(2,1)S(1)} collective-permute-done((bf16[128,4608]{1,0:T(8,128)(2,1)}, bf16[128,4608]{1,0:T(8,128)(2,1)S(1)}, u32[]{:S(2)}, u32[]{:S(2)}) %collective-permute-start.11) | collective-permute-done | bytes 1179680 | tf_op jit(solution)/shard_map/ppermute | solution.py:563
  275.0 5.1 shard_map.150
  281.3 6.9 shard_map.151
  288.2 1.5 collective-permute-start.16
  290.2 10.2 %shard_map.146.p_ref = bf16[64,4608]{1,0:T(8,128)(2,1)} custom-call(s32[4]{0:T(128)} %pad_add_fusion.sc_ref, bf16[2048,1024]{1,0:T(8,128)(2,1)} %get-tuple-element.47.c0_ref.ctx_ref, bf16[512,1024]{1,0:T(8,128)(2,1)} %copy-done, bf16[2048,4608]{1,0:T(8,128)(2,1)} %bitcast.24), custom_call_target="tpu_custom_call" | custom-call | flops 1207959552 | bytes 18874368 | tf_op jit(solution)/shard_map/pallas_call | solution.py:358
  300.4 1.5 collective-permute-start.8
  302.2 5.0 shard_map.152
  307.2 9.4 %collective-permute-done.8.r_ref = bf16[64,4608]{1,0:T(8,128)(2,1)} collective-permute-done((bf16[64,4608]{1,0:T(8,128)(2,1)}, bf16[64,4608]{1,0:T(8,128)(2,1)}, u32[]{:S(2)}, u32[]{:S(2)}) %collective-permute-start.8) | collective-permute-done | bytes 589856 | tf_op jit(solution)/shard_map/ppermute | solution.py:563
  316.6 1.3 collective-permute-start.17
  317.9 37.3 %collective-permute-done.15.refs_0_ = bf16[128,4608]{1,0:T(8,128)(2,1)S(1)} collective-permute-done((bf16[128,4608]{1,0:T(8,128)(2,1)}, bf16[128,4608]{1,0:T(8,128)(2,1)S(1)}, u32[]{:S(2)}, u32[]{:S(2)}) %collective-permute-start.15) | collective-permute-done | bytes 1179680 | tf_op jit(solution)/shard_map/ppermute | solution.py:560
  355.2 3.9 shard_map.153
  359.1 1.5 collective-permute-start.13
  360.6 30.6 %collective-permute-done.13.refs_2_ = bf16[64,4608]{1,0:T(8,128)(2,1)S(1)} collective-permute-done((bf16[64,4608]{1,0:T(8,128)(2,1)}, bf16[64,4608]{1,0:T(8,128)(2,1)S(1)}, u32[]{:S(2)}, u32[]{:S(2)}) %collective-permute-start.13) | collective-permute-done | bytes 589856 | tf_op jit(solution)/shard_map/ppermute | solution.py:560
  394.4 16.3 %shard_map.154 = (bf16[4,512,1024]{2,1,0:T(8,128)(2,1)}, bf16[4,512,4608]{2,1,0:T(8,128)(2,1)}) custom-call(s32[10]{0:T(128)} %stack.91.sc_ref, bf16[128,4608]{1,0:T(8,128)(2,1)} %get-tuple-element.53.refs_0_, bf16[192,4608]{1,0:T(8,128)(2,1)} %get-tuple-element.54.refs_1_, bf16[128,4608]{1,0:T(8,128)(2,1)} %get-tuple-element.55.refs_2_, ...), custom_call_target="tpu_custom_call" | custom-call | flops 8455716864 | bytes 25952256 | tf_op jit(solution)/shard_map/pallas_call | solution.py:298
  410.8 16.1 %shard_map.155 = (bf16[4,512,1024]{2,1,0:T(8,128)(2,1)}, bf16[4,512,4608]{2,1,0:T(8,128)(2,1)}) custom-call(s32[10]{0:T(128)} %stack.90.sc_ref, bf16[128,4608]{1,0:T(8,128)(2,1)} %copy-done.3, bf16[192,4608]{1,0:T(8,128)(2,1)} %copy-done.1, bf16[128,4608]{1,0:T(8,128)(2,1)} %collective-permute-done.17.refs_2_, ...), custom_call_target="tpu_custom_call", output_to_operand_aliasing={{0}: (8, {}), {1}: (9, {})} | custom-call | flops 8455716864 | bytes 25952256 | tf_op jit(solution)/shard_map/pallas_call | solution.py:298
  426.9 8.9 %shard_map.156 = (bf16[4,512,1024]{2,1,0:T(8,128)(2,1)}, bf16[4,512,4608]{2,1,0:T(8,128)(2,1)}) custom-call(s32[10]{0:T(128)} %stack.89.sc_ref, bf16[64,4608]{1,0:T(8,128)(2,1)} %get-tuple-element.52.refs_0_, bf16[64,4608]{1,0:T(8,128)(2,1)} %collective-permute-done.12.refs_1_, ...), custom_call_target="tpu_custom_call", output_to_operand_aliasing={{0}: (6, {}), {1}: (7, {})} | custom-call | flops 2415919104 | bytes 14155776 | tf_op jit(solution)/shard_map/pallas_call | solution.py:298
  435.8 83.4 %attn_bwd.1 = (bf16[2048,1024]{1,0:T(8,128)(2,1)}, bf16[2048,512]{1,0:T(8,128)(2,1)}, bf16[2048,512]{1,0:T(8,128)(2,1)}) custom-call(bf16[2048,2048]{1,0:T(8,128)(2,1)} %bitcast.42, bf16[2048,2048]{1,0:T(8,128)(2,1)} %bitcast.43, bf16[2048,2048]{1,0:T(8,128)(2,1)} %bitcast.44, bf16[2048,1024]{1,0:T(8,128)(2,1)} %bitcast.29, ...), custom_call_target="tpu_custom_call" | custom-call | flops 21474836480 | bytes 25165824 | tf_op jit(solution)/shard_map/attn_bwd/pallas_call | solution.py:194
  519.2 1.3 constant_dynamic-slice_fusion.2
  523.7 20.6 %shard_map.157.w1_ref = bf16[4608,2048]{1,0:T(8,128)(2,1)} custom-call(s32[1]{0:T(128)} %bitcast.5.c_ref, bf16[4608,16,128]{2,1,0:T(8,128)(2,1)} %wq_ref.3, bf16[4608,8,128]{2,1,0:T(8,128)(2,1)} %wk_ref.3, bf16[4608,8,128]{2,1,0:T(8,128)(2,1)} %wv_ref.3), custom_call_target="tpu_custom_call" | custom-call | flops 4718592000 | bytes 47185920 | tf_op jit(solution)/shard_map/pallas_call | solution.py:331
  544.4 26.8 %shard_map.158.p_ref = bf16[512,4608]{1,0:T(8,128)(2,1)} custom-call(s32[4]{0:T(128)} %pad_add_fusion.sc_ref, bf16[2048,1024]{1,0:T(8,128)(2,1)} %get-tuple-element.62.q0, bf16[2048,512]{1,0:T(8,128)(2,1)} %get-tuple-element.63.k0, bf16[2048,512]{1,0:T(8,128)(2,1)} %get-tuple-element.64.v0, bf16[512,1024]{1,0:T(8,128)(2,1)} %collective-permute-done.24.q1, ...), custom_call_target="tpu_custom_call" | custom-call | flops 19327352832 | bytes 37748736 | tf_op jit(solution)/shard_map/pallas_call | solution.py:390
  571.2 1.5 collective-permute-start.27
  573.8 101.4 %collective-permute-done.27.r_ref = bf16[512,4608]{1,0:T(8,128)(2,1)} collective-permute-done((bf16[512,4608]{1,0:T(8,128)(2,1)}, bf16[512,4608]{1,0:T(8,128)(2,1)}, u32[]{:S(2)}, u32[]{:S(2)}) %collective-permute-start.27) | collective-permute-done | bytes 4718624 | tf_op jit(solution)/shard_map/ppermute | solution.py:563
  675.2 13.0 %shard_map.159 = (bf16[512,4608]{1,0:T(8,128)(2,1)}, f32[8,4608]{1,0:T(8,128)}) custom-call(bf16[512,4608]{1,0:T(8,128)(2,1)} %shard_map.158.p_ref, bf16[512,4608]{1,0:T(8,128)(2,1)} %collective-permute-done.27.r_ref, bf16[512,4608]{1,0:T(8,128)(2,1)} %h_ref.11, bf16[512,4608]{1,0:T(8,128)(2,1)} %dy_ref.9, f32[1,4608]{1,0:T(1,128)} %reshape.73.g_ref), custom_call_target="tpu_custom_call" | custom-call | flops 4718592000 | bytes 28311552 | tf_op jit(solution)/shard_map/pallas_call | solution.py:526
  689.2 50.1 %dwo_proj.1 = f32[2048,4608]{1,0:T(8,128)} custom-call(s32[4]{0:T(128)} %pad_add_fusion.sc_ref, bf16[2048,1024]{1,0:T(8,128)(2,1)} %get-tuple-element.47.c0_ref.ctx_ref, bf16[2048,1024]{1,0:T(8,128)(2,1)} %collective-permute-done.33.c1_ref, bf16[2048,4608]{1,0:T(8,128)(2,1)} %bitcast.28), custom_call_target="tpu_custom_call" | custom-call | flops 38654705664 | bytes 37748736 | tf_op jit(solution)/shard_map/dwo_proj/pallas_call | solution.py:455
  739.4 1.3 collective-permute-start.29
  740.7 1.3 copy-done.11
  742.0 100.7 %dw_proj.1 = (f32[73728,128]{1,0:T(8,128)}, f32[36864,128]{1,0:T(8,128)}, f32[36864,128]{1,0:T(8,128)}) custom-call(s32[4]{0:T(128)} %pad_add_fusion.sc_ref, bf16[2048,4608]{1,0:T(8,128)(2,1)} %bitcast.38, bf16[2048,1024]{1,0:T(8,128)(2,1)} %get-tuple-element.62.q0, bf16[2048,1024]{1,0:T(8,128)(2,1)} %collective-permute-done.30.q1, ...), custom_call_target="tpu_custom_call" | custom-call | flops 77309411328 | bytes 75497472 | tf_op jit(solution)/shard_map/dw_proj/pallas_call | solution.py:423
  (95 shorter events, 21.0 us)
Async XLA Ops:
  9.8 78.7 %collective-permute-start.6 = (bf16[512,4608]{1,0:T(8,128)(2,1)}, bf16[512,4608]{1,0:T(8,128)(2,1)}, u32[]{:S(2)}, u32[]{:S(2)}) collective-permute-start(bf16[512,4608]{1,0:T(8,128)(2,1)} %a_norm.1.refs_0_), channel_id=1, source_target_pairs={{0,1},{1,0},{2,3},{3,2},{4,5},{5,4},{6,7},{7,6}} | collective-permute-start | bytes 14155784 | tf_op jit(solution)/shard_map/ppermute | solution.py:557
  12.2 38.7 %collective-permute-start = (bf16[176,4608]{1,0:T(8,128)(2,1)S(1)}, bf16[176,4608]{1,0:T(8,128)(2,1)}, u32[]{:S(2)}, u32[]{:S(2)}) collective-permute-start(bf16[176,4608]{1,0:T(8,128)(2,1)S(1)} %constant_dynamic-slice_fusion.4), channel_id=1, source_target_pairs={{0,2},{2,0},{1,3},{3,1},{4,6},{6,4},{5,7},{7,5}} | collective-permute-start | bytes 4866056 | tf_op jit(solution)/shard_map/ppermute | solution.py:560
  50.9 37.6 %collective-permute-start.1 = (bf16[176,4608]{1,0:T(8,128)(2,1)}, bf16[176,4608]{1,0:T(8,128)(2,1)}, u32[]{:S(2)}, u32[]{:S(2)}) collective-permute-start(bf16[176,4608]{1,0:T(8,128)(2,1)} %collective-permute-done.refs_0_), channel_id=1, source_target_pairs={{0,4},{4,0},{1,5},{5,1},{2,6},{6,2},{3,7},{7,3}} | collective-permute-start | bytes 4866056 | tf_op jit(solution)/shard_map/ppermute | solution.py:563
  54.1 33.7 %collective-permute-start.2 = (bf16[160,4608]{1,0:T(8,128)(2,1)S(1)}, bf16[160,4608]{1,0:T(8,128)(2,1)}, u32[]{:S(2)}, u32[]{:S(2)}) collective-permute-start(bf16[160,4608]{1,0:T(8,128)(2,1)S(1)} %slice.12), channel_id=1, source_target_pairs={{0,2},{2,0},{1,3},{3,1},{4,6},{6,4},{5,7},{7,5}} | collective-permute-start | bytes 4423688 | tf_op jit(solution)/shard_map/ppermute | solution.py:560
  87.8 30.6 %collective-permute-start.5 = (bf16[160,4608]{1,0:T(8,128)(2,1)}, bf16[160,4608]{1,0:T(8,128)(2,1)}, u32[]{:S(2)}, u32[]{:S(2)}) collective-permute-start(bf16[160,4608]{1,0:T(8,128)(2,1)} %collective-permute-done.2.refs_2_), channel_id=1, source_target_pairs={{0,1},{1,0},{2,3},{3,2},{4,5},{5,4},{6,7},{7,6}} | collective-permute-start | bytes 4423688 | tf_op jit(solution)/shard_map/ppermute | solution.py:557
  87.8 30.6 %collective-permute-start.3 = (bf16[176,4608]{1,0:T(8,128)(2,1)}, bf16[176,4608]{1,0:T(8,128)(2,1)S(1)}, u32[]{:S(2)}, u32[]{:S(2)}) collective-permute-start(bf16[176,4608]{1,0:T(8,128)(2,1)} %collective-permute-done.refs_0_), channel_id=1, source_target_pairs={{0,1},{1,0},{2,3},{3,2},{4,5},{5,4},{6,7},{7,6}} | collective-permute-start | bytes 4866056 | tf_op jit(solution)/shard_map/ppermute | solution.py:557
  88.5 29.9 %collective-permute-start.4 = (bf16[176,4608]{1,0:T(8,128)(2,1)}, bf16[176,4608]{1,0:T(8,128)(2,1)}, u32[]{:S(2)}, u32[]{:S(2)}) collective-permute-start(bf16[176,4608]{1,0:T(8,128)(2,1)} %collective-permute-done.1.refs_1_), channel_id=1, source_target_pairs={{0,1},{1,0},{2,3},{3,2},{4,5},{5,4},{6,7},{7,6}} | collective-permute-start | bytes 4866056 | tf_op jit(solution)/shard_map/ppermute | solution.py:557
  118.4 1.2 copy-start.12
  192.2 2.8 collective-permute-start.7
  195.1 1.0 copy-start
  207.0 12.1 %copy-start.10 = (f32[4608]{0:T(1024)S(1)}, f32[4608]{0:T(1024)}, u32[]{:S(2)}) copy-start(f32[4608]{0:T(1024)} %param.14) | copy-start | bytes 55300
  207.0 73.1 %collective-permute-start.10 = (bf16[192,4608]{1,0:T(8,128)(2,1)}, bf16[192,4608]{1,0:T(8,128)(2,1)S(1)}, u32[]{:S(2)}, u32[]{:S(2)}) collective-permute-start(bf16[192,4608]{1,0:T(8,128)(2,1)} %shard_map.148.p_ref), channel_id=1, source_target_pairs={{0,4},{4,0},{1,5},{5,1},{2,6},{6,2},{3,7},{7,3}} | collective-permute-start | bytes 5308424 | tf_op jit(solution)/shard_map/ppermute | solution.py:563
  218.5 55.4 %collective-permute-start.11 = (bf16[128,4608]{1,0:T(8,128)(2,1)}, bf16[128,4608]{1,0:T(8,128)(2,1)S(1)}, u32[]{:S(2)}, u32[]{:S(2)}) collective-permute-start(bf16[128,4608]{1,0:T(8,128)(2,1)} %shard_map.149.p_ref), channel_id=1, source_target_pairs={{0,4},{4,0},{1,5},{5,1},{2,6},{6,2},{3,7},{7,3}} | collective-permute-start | bytes 3538952 | tf_op jit(solution)/shard_map/ppermute | solution.py:563
  229.8 72.1 %collective-permute-start.9 = (bf16[128,4608]{1,0:T(8,128)(2,1)}, bf16[128,4608]{1,0:T(8,128)(2,1)}, u32[]{:S(2)}, u32[]{:S(2)}) collective-permute-start(bf16[128,4608]{1,0:T(8,128)(2,1)} %shard_map.147.p_ref), channel_id=1, source_target_pairs={{0,4},{4,0},{1,5},{5,1},{2,6},{6,2},{3,7},{7,3}} | collective-permute-start | bytes 3538952 | tf_op jit(solution)/shard_map/ppermute | solution.py:563
  274.0 1.0 copy-start.4
  280.1 1.2 copy-start.2
  288.2 72.4 %collective-permute-start.16 = (bf16[192,4608]{1,0:T(8,128)(2,1)}, bf16[192,4608]{1,0:T(8,128)(2,1)S(1)}, u32[]{:S(2)}, u32[]{:S(2)}) collective-permute-start(bf16[192,4608]{1,0:T(8,128)(2,1)} %get-tuple-element.54.refs_1_), channel_id=1, source_target_pairs={{0,2},{2,0},{1,3},{3,1},{4,6},{6,4},{5,7},{7,5}} | collective-permute-start | bytes 5308424 | tf_op jit(solution)/shard_map/ppermute | solution.py:560
  289.7 65.5 %collective-permute-start.15 = (bf16[128,4608]{1,0:T(8,128)(2,1)}, bf16[128,4608]{1,0:T(8,128)(2,1)S(1)}, u32[]{:S(2)}, u32[]{:S(2)}) collective-permute-start(bf16[128,4608]{1,0:T(8,128)(2,1)} %get-tuple-element.53.refs_0_), channel_id=1, source_target_pairs={{0,2},{2,0},{1,3},{3,1},{4,6},{6,4},{5,7},{7,5}} | collective-permute-start | bytes 3538952 | tf_op jit(solution)/shard_map/ppermute | solution.py:560
  290.2 68.9 %collective-permute-start.21 = (bf16[128,4608]{1,0:T(8,128)(2,1)}, bf16[128,4608]{1,0:T(8,128)(2,1)}, u32[]{:S(2)}, u32[]{:S(2)}) collective-permute-start(bf16[128,4608]{1,0:T(8,128)(2,1)} %get-tuple-element.53.refs_0_), channel_id=1, source_target_pairs={{0,1},{1,0},{2,3},{3,2},{4,5},{5,4},{6,7},{7,6}} | collective-permute-start | bytes 3538952 | tf_op jit(solution)/shard_map/ppermute | solution.py:557
  300.4 16.2 %collective-permute-start.8 = (bf16[64,4608]{1,0:T(8,128)(2,1)}, bf16[64,4608]{1,0:T(8,128)(2,1)}, u32[]{:S(2)}, u32[]{:S(2)}) collective-permute-start(bf16[64,4608]{1,0:T(8,128)(2,1)} %shard_map.146.p_ref), channel_id=1, source_target_pairs={{0,4},{4,0},{1,5},{5,1},{2,6},{6,2},{3,7},{7,3}} | collective-permute-start | bytes 1769480 | tf_op jit(solution)/shard_map/ppermute | solution.py:563
  301.9 92.5 %collective-permute-start.22 = (bf16[192,4608]{1,0:T(8,128)(2,1)}, bf16[192,4608]{1,0:T(8,128)(2,1)}, u32[]{:S(2)}, u32[]{:S(2)}) collective-permute-start(bf16[192,4608]{1,0:T(8,128)(2,1)} %get-tuple-element.54.refs_1_), channel_id=1, source_target_pairs={{0,1},{1,0},{2,3},{3,2},{4,5},{5,4},{6,7},{7,6}} | collective-permute-start | bytes 5308424 | tf_op jit(solution)/shard_map/ppermute | solution.py:557
  316.6 75.4 %collective-permute-start.17 = (bf16[128,4608]{1,0:T(8,128)(2,1)}, bf16[128,4608]{1,0:T(8,128)(2,1)}, u32[]{:S(2)}, u32[]{:S(2)}) collective-permute-start(bf16[128,4608]{1,0:T(8,128)(2,1)} %get-tuple-element.55.refs_2_), channel_id=1, source_target_pairs={{0,2},{2,0},{1,3},{3,1},{4,6},{6,4},{5,7},{7,5}} | collective-permute-start | bytes 3538952 | tf_op jit(solution)/shard_map/ppermute | solution.py:560
  355.2 36.0 %copy-start.3 = (bf16[128,4608]{1,0:T(8,128)(2,1)}, bf16[128,4608]{1,0:T(8,128)(2,1)S(1)}, u32[]{:S(2)}) copy-start(bf16[128,4608]{1,0:T(8,128)(2,1)S(1)} %collective-permute-done.15.refs_0_) | copy-start | bytes 3538948
  355.2 38.7 %collective-permute-start.23 = (bf16[128,4608]{1,0:T(8,128)(2,1)}, bf16[128,4608]{1,0:T(8,128)(2,1)}, u32[]{:S(2)}, u32[]{:S(2)}) collective-permute-start(bf16[128,4608]{1,0:T(8,128)(2,1)} %get-tuple-element.55.refs_2_), channel_id=1, source_target_pairs={{0,1},{1,0},{2,3},{3,2},{4,5},{5,4},{6,7},{7,6}} | collective-permute-start | bytes 3538952 | tf_op jit(solution)/shard_map/ppermute | solution.py:557
  359.1 32.1 %collective-permute-start.13 = (bf16[64,4608]{1,0:T(8,128)(2,1)}, bf16[64,4608]{1,0:T(8,128)(2,1)S(1)}, u32[]{:S(2)}, u32[]{:S(2)}) collective-permute-start(bf16[64,4608]{1,0:T(8,128)(2,1)} %get-tuple-element.52.refs_0_), channel_id=1, source_target_pairs={{0,2},{2,0},{1,3},{3,1},{4,6},{6,4},{5,7},{7,5}} | collective-permute-start | bytes 1769480 | tf_op jit(solution)/shard_map/ppermute | solution.py:560
  360.6 50.1 %copy-start.1 = (bf16[192,4608]{1,0:T(8,128)(2,1)}, bf16[192,4608]{1,0:T(8,128)(2,1)S(1)}, u32[]{:S(2)}) copy-start(bf16[192,4608]{1,0:T(8,128)(2,1)S(1)} %collective-permute-done.16.refs_1_) | copy-start | bytes 5308420
  360.6 50.2 %collective-permute-start.19 = (bf16[192,4608]{1,0:T(8,128)(2,1)S(1)}, bf16[192,4608]{1,0:T(8,128)(2,1)}, u32[]{:S(2)}, u32[]{:S(2)}) collective-permute-start(bf16[192,4608]{1,0:T(8,128)(2,1)S(1)} %collective-permute-done.16.refs_1_), channel_id=1, source_target_pairs={{0,1},{1,0},{2,3},{3,2},{4,5},{5,4},{6,7},{7,6}} | collective-permute-start | bytes 5308424 | tf_op jit(solution)/shard_map/ppermute | solution.py:557
  391.2 0.8 copy-start.5
  391.2 19.5 %collective-permute-start.18 = (bf16[128,4608]{1,0:T(8,128)(2,1)S(1)}, bf16[128,4608]{1,0:T(8,128)(2,1)}, u32[]{:S(2)}, u32[]{:S(2)}) collective-permute-start(bf16[128,4608]{1,0:T(8,128)(2,1)S(1)} %collective-permute-done.15.refs_0_), channel_id=1, source_target_pairs={{0,1},{1,0},{2,3},{3,2},{4,5},{5,4},{6,7},{7,6}} | collective-permute-start | bytes 3538952 | tf_op jit(solution)/shard_map/ppermute | solution.py:557
  392.0 18.7 %collective-permute-start.20 = (bf16[128,4608]{1,0:T(8,128)(2,1)}, bf16[128,4608]{1,0:T(8,128)(2,1)}, u32[]{:S(2)}, u32[]{:S(2)}) collective-permute-start(bf16[128,4608]{1,0:T(8,128)(2,1)} %collective-permute-done.17.refs_2_), channel_id=1, source_target_pairs={{0,1},{1,0},{2,3},{3,2},{4,5},{5,4},{6,7},{7,6}} | collective-permute-start | bytes 3538952 | tf_op jit(solution)/shard_map/ppermute | solution.py:557
  393.9 33.0 %collective-permute-start.12 = (bf16[64,4608]{1,0:T(8,128)(2,1)}, bf16[64,4608]{1,0:T(8,128)(2,1)}, u32[]{:S(2)}, u32[]{:S(2)}) collective-permute-start(bf16[64,4608]{1,0:T(8,128)(2,1)} %get-tuple-element.52.refs_0_), channel_id=1, source_target_pairs={{0,1},{1,0},{2,3},{3,2},{4,5},{5,4},{6,7},{7,6}} | collective-permute-start | bytes 1769480 | tf_op jit(solution)/shard_map/ppermute | solution.py:557
  394.4 32.5 %collective-permute-start.14 = (bf16[64,4608]{1,0:T(8,128)(2,1)}, bf16[64,4608]{1,0:T(8,128)(2,1)}, u32[]{:S(2)}, u32[]{:S(2)}) collective-permute-start(bf16[64,4608]{1,0:T(8,128)(2,1)} %copy-done.5), channel_id=1, source_target_pairs={{0,1},{1,0},{2,3},{3,2},{4,5},{5,4},{6,7},{7,6}} | collective-permute-start | bytes 1769480 | tf_op jit(solution)/shard_map/ppermute | solution.py:557
  520.5 23.9 %collective-permute-start.24 = (bf16[512,1024]{1,0:T(8,128)(2,1)S(1)}, bf16[512,1024]{1,0:T(8,128)(2,1)}, u32[]{:S(2)}, u32[]{:S(2)}) collective-permute-start(bf16[512,1024]{1,0:T(8,128)(2,1)S(1)} %constant_dynamic-slice_fusion.2), channel_id=1, source_target_pairs={{0,1},{1,0},{2,3},{3,2},{4,5},{5,4},{6,7},{7,6}} | collective-permute-start | bytes 3145736 | tf_op jit(solution)/shard_map/ppermute | solution.py:557
  522.1 22.3 %collective-permute-start.25 = (bf16[512,512]{1,0:T(8,128)(2,1)S(1)}, bf16[512,512]{1,0:T(8,128)(2,1)}, u32[]{:S(2)}, u32[]{:S(2)}) collective-permute-start(bf16[512,512]{1,0:T(8,128)(2,1)S(1)} %constant_dynamic-slice_fusion.1), channel_id=1, source_target_pairs={{0,1},{1,0},{2,3},{3,2},{4,5},{5,4},{6,7},{7,6}} | collective-permute-start | bytes 1572872 | tf_op jit(solution)/shard_map/ppermute | solution.py:557
  523.2 21.2 %collective-permute-start.26 = (bf16[512,512]{1,0:T(8,128)(2,1)S(1)}, bf16[512,512]{1,0:T(8,128)(2,1)}, u32[]{:S(2)}, u32[]{:S(2)}) collective-permute-start(bf16[512,512]{1,0:T(8,128)(2,1)S(1)} %constant_dynamic-slice_fusion), channel_id=1, source_target_pairs={{0,1},{1,0},{2,3},{3,2},{4,5},{5,4},{6,7},{7,6}} | collective-permute-start | bytes 1572872 | tf_op jit(solution)/shard_map/ppermute | solution.py:557
  544.3 28.3 %copy-start.6 = (f32[8,4608]{1,0:T(8,128)S(1)}, f32[8,4608]{1,0:T(8,128)}, u32[]{:S(2)}) copy-start(f32[8,4608]{1,0:T(8,128)} %get-tuple-element.67) | copy-start | bytes 442372
  544.3 28.3 %copy-start.7 = (f32[8,4608]{1,0:T(8,128)S(1)}, f32[8,4608]{1,0:T(8,128)}, u32[]{:S(2)}) copy-start(f32[8,4608]{1,0:T(8,128)} %get-tuple-element.68) | copy-start | bytes 442372
  544.3 28.3 %copy-start.8 = (f32[8,4608]{1,0:T(8,128)S(1)}, f32[8,4608]{1,0:T(8,128)}, u32[]{:S(2)}) copy-start(f32[8,4608]{1,0:T(8,128)} %get-tuple-element.69) | copy-start | bytes 442372
  544.3 28.3 %copy-start.9 = (f32[8,4608]{1,0:T(8,128)S(1)}, f32[8,4608]{1,0:T(8,128)}, u32[]{:S(2)}) copy-start(f32[8,4608]{1,0:T(8,128)} %get-tuple-element.70) | copy-start | bytes 442372
  571.2 104.0 %collective-permute-start.27 = (bf16[512,4608]{1,0:T(8,128)(2,1)}, bf16[512,4608]{1,0:T(8,128)(2,1)}, u32[]{:S(2)}, u32[]{:S(2)}) collective-permute-start(bf16[512,4608]{1,0:T(8,128)(2,1)} %shard_map.158.p_ref), channel_id=1, source_target_pairs={{0,4},{4,0},{1,5},{5,1},{2,6},{6,2},{3,7},{7,3}} | collective-permute-start | bytes 14155784 | tf_op jit(solution)/shard_map/ppermute | solution.py:563
  572.7 116.6 %collective-permute-start.33 = (bf16[2048,1024]{1,0:T(8,128)(2,1)}, bf16[2048,1024]{1,0:T(8,128)(2,1)}, u32[]{:S(2)}, u32[]{:S(2)}) collective-permute-start(bf16[2048,1024]{1,0:T(8,128)(2,1)} %get-tuple-element.47.c0_ref.ctx_ref), channel_id=1, source_target_pairs={{0,1},{1,0},{2,3},{3,2},{4,5},{5,4},{6,7},{7,6}} | collective-permute-start | bytes 12582920 | tf_op jit(solution)/shard_map/ppermute | solution.py:557
  572.8 167.9 %collective-permute-start.30 = (bf16[2048,1024]{1,0:T(8,128)(2,1)}, bf16[2048,1024]{1,0:T(8,128)(2,1)}, u32[]{:S(2)}, u32[]{:S(2)}) collective-permute-start(bf16[2048,1024]{1,0:T(8,128)(2,1)} %get-tuple-element.62.q0), channel_id=1, source_target_pairs={{0,1},{1,0},{2,3},{3,2},{4,5},{5,4},{6,7},{7,6}} | collective-permute-start | bytes 12582920 | tf_op jit(solution)/shard_map/ppermute | solution.py:557
  573.3 167.4 %collective-permute-start.31 = (bf16[2048,512]{1,0:T(8,128)(2,1)}, bf16[2048,512]{1,0:T(8,128)(2,1)S(1)}, u32[]{:S(2)}, u32[]{:S(2)}) collective-permute-start(bf16[2048,512]{1,0:T(8,128)(2,1)} %get-tuple-element.63.k0), channel_id=1, source_target_pairs={{0,1},{1,0},{2,3},{3,2},{4,5},{5,4},{6,7},{7,6}} | collective-permute-start | bytes 6291464 | tf_op jit(solution)/shard_map/ppermute | solution.py:557
  573.3 167.4 %collective-permute-start.32 = (bf16[2048,512]{1,0:T(8,128)(2,1)}, bf16[2048,512]{1,0:T(8,128)(2,1)}, u32[]{:S(2)}, u32[]{:S(2)}) collective-permute-start(bf16[2048,512]{1,0:T(8,128)(2,1)} %get-tuple-element.64.v0), channel_id=1, source_target_pairs={{0,1},{1,0},{2,3},{3,2},{4,5},{5,4},{6,7},{7,6}} | collective-permute-start | bytes 6291464 | tf_op jit(solution)/shard_map/ppermute | solution.py:557
  689.2 50.2 %collective-permute-start.28 = (f32[2,4608]{1,0:T(2,128)S(1)}, f32[2,4608]{1,0:T(2,128)S(1)}, u32[]{:S(2)}, u32[]{:S(2)}) collective-permute-start(f32[2,4608]{1,0:T(2,128)S(1)} %pad_maximum_fusion.2), channel_id=1, source_target_pairs={{0,1},{1,0},{2,3},{3,2},{4,5},{5,4},{6,7},{7,6}} | collective-permute-start | bytes 110600 | tf_op jit(solution)/shard_map/ppermute | solution.py:557
  739.4 103.3 %collective-permute-start.29 = (f32[2,4608]{1,0:T(2,128)S(1)}, f32[2,4608]{1,0:T(2,128)S(1)}, u32[]{:S(2)}, u32[]{:S(2)}) collective-permute-start(f32[2,4608]{1,0:T(2,128)S(1)} %fusion.1), channel_id=1, source_target_pairs={{0,2},{2,0},{1,3},{3,1},{4,6},{6,4},{5,7},{7,5}} | collective-permute-start | bytes 110600 | tf_op jit(solution)/shard_map/ppermute | solution.py:560
  740.7 1.3 copy-start.11

commit v6 on v5

--- a/solution.py
+++ b/solution.py
@@ -324,8 +324,10 @@
         out_ref[:, nq + j * n:nq + (j + 1) * n] = s_ref[j, :, half]
 
 
-def w_layout(c, w_q, w_k, w_v, db):
+def w_layout(c, w_q, w_k, w_v, db, part=0, parts=1):
     D, hb = w_k.shape[:2]
+    D //= parts
+    i0 = part * (D // db)
     nq, n = w_q.shape[1] // 2, hb // 2
     N = (nq + 2 * n) * HEAD
     return pl.pallas_call(
@@ -333,7 +335,7 @@
         grid_spec=pltpu.PrefetchScalarGridSpec(
             num_scalar_prefetch=1,
             grid=(D // db,),
-            in_specs=[pl.BlockSpec((db, nq, HEAD), lambda i, s: (i, s[0], 0))] + [pl.BlockSpec((db, hb, HEAD), lambda i, s: (i, 0, 0))] * 2,
+            in_specs=[pl.BlockSpec((db, nq, HEAD), lambda i, s: (i0 + i, s[0], 0))] + [pl.BlockSpec((db, hb, HEAD), lambda i, s: (i0 + i, 0, 0))] * 2,
             out_specs=pl.BlockSpec((db, N), lambda i, s: (i, 0)),
             scratch_shapes=[pltpu.VMEM((2, db, hb * HEAD), BF16)],
         ),
@@ -373,7 +375,18 @@
     )(scal, ctx, ctx_pr, w)
 
 
-def ga_kernel(sc_ref, q0, k0, v0, q1, k1, v1, w0_ref, w1_ref, out_ref):
+def ga_kernel(sc_ref, q0, k0, v0, q1, k1, v1, w0_ref, wa_ref, wb_ref, out_ref, w1_ref):
+    i = pl.program_id(0)
+    half = pl.num_programs(0) // 2
+
+    @pl.when(i < half)
+    def _():
+        w1_ref[...] = wa_ref[...]
+
+    @pl.when(i >= half)
+    def _():
+        w1_ref[...] = wb_ref[...]
+
     acc = None
     for w_ref, gs in ((w0_ref, (q0, k0, v0)), (w1_ref, (q1, k1, v1))):
         o = 0
@@ -387,6 +400,7 @@
 
 def ga_rows(scal, own, oth, ws, M, db):
     D, N = ws[0].shape
+    half = D // db // 2
     return pl.pallas_call(
         ga_kernel,
         grid_spec=pltpu.PrefetchScalarGridSpec(
@@ -394,8 +408,10 @@
             grid=(D // db,),
             in_specs=[pl.BlockSpec((M, g.shape[1]), lambda i, s: (s[2], 0)) for g in own]
             + [pl.BlockSpec((M, g.shape[1]), lambda i, s: (0, 0)) for g in oth]
-            + [pl.BlockSpec((db, N), lambda i, s: (i, 0)) for w in ws],
+            + [pl.BlockSpec((db, N), lambda i, s: (i, 0)), pl.BlockSpec((db, N), lambda i, s: (jnp.minimum(i, half - 1), 0)),
+               pl.BlockSpec((db, N), lambda i, s: (jnp.maximum(i - half, 0), 0))],
             out_specs=pl.BlockSpec((M, db), lambda i, s: (0, i)),
+            scratch_shapes=[pltpu.VMEM((db, N), BF16)],
         ),
         out_shape=jax.ShapeDtypeStruct((M, D), BF16),
         compiler_params=pltpu.CompilerParams(dimension_semantics=("arbitrary",), vmem_limit_bytes=VMEM_LIMIT),
@@ -586,7 +602,7 @@
         wo2 = w_o.reshape(-1, D)
         N = (HL + 2 * KL) * HEAD
         w_own = w_layout(core, w_q, w_k, w_v, 512)
-        w_oth = w_layout(1 - core, w_q, w_k, w_v, 512)
+        w_oth = [w_layout(1 - core, w_q, w_k, w_v, 384, p, 2) for p in range(2)]
         qkv_args = (w_own, "qkv", (cos, sin), 2, [core, 1 - core], tokens, 0, N)
         bufs = gather_matmul(xi, core, [(0, 0), (1, 0)], [a_loc, a_p], *qkv_args)
         places = [(0, o) for o in a_off] + [(1, o) for o in a_off]
@@ -596,7 +612,7 @@
 
         ctx, lse = attn_fwd(qkv, KL, HL)
         ctx_pr = to_core(lax.dynamic_slice_in_dim(ctx, (me ^ 1) * tokens, tokens, 0))
-        sizes = (128, 192, 128, 64)
+        sizes = (128, 128, 128, 128)
         starts = [sum(sizes[:c]) for c in range(len(sizes))]
         o_parts, o_peers = [], []
         for c, M in enumerate(sizes):
@@ -629,11 +645,11 @@
         dqkv = attn_bwd(qkv, KL, HL, dctx, ctx, lse, cos, sin)
         dqkv_pr = [to_core(lax.dynamic_slice_in_dim(g, (me ^ 1) * tokens, tokens, 0)) for g in dqkv]
         dqkv_p = [to_core(g) for g in dqkv]
-        ga_part = ga_rows(base, dqkv, dqkv_pr, (w_own, w_oth), tokens, 512)
+        ga_part = ga_rows(base, dqkv, dqkv_pr, (w_own, *w_oth), tokens, 384)
         ga_peer = to_tp(ga_part)
 
         dwo = dwo_proj(base, ctx, ctx_p, go_all, 512).reshape(w_o.shape)
-        dwq, dwk, dwv = dw_proj(base, a_all, [g for pair in zip(dqkv, dqkv_p) for g in pair], 256)
+        dwq, dwk, dwv = dw_proj(base, a_all, [g for pair in zip(dqkv, dqkv_p) for g in pair], 512)
 
         grad_h, dgr = norm_call(pre_kernel, ga_part, ga_peer, hidden, d_out, g_pre, 0, None, False)
         dg = jnp.stack([jnp.sum(dgr, axis=0), jnp.sum(sum(dgp), axis=0)])

time: 853 us -> 890 us (1.043)
  waiting for transfers between devices: 264 us -> 298 us
    ppermute x7, waiting for transfers between devices: 109 us -> 140 us  [to_x(): return lax.ppermute(v, 'cp', x_perm)]
    pallas_call x1, Pallas kernels: 26.8 us -> 36.2 us  [ga_rows(): pl.pallas_call(ga_kernel, grid_spec=pltpu.PrefetchScalarGridSpec(num_scal...]
    pallas_call x2 -> x3, Pallas kernels: 41.2 us -> 41.4 us  [w_layout(): pl.pallas_call(w_kernel, grid_spec=pltpu.PrefetchScalarGridSpec(num_scala...]
  transfers between devices with their start and end apart: 34 -> 34, of which waited for: 9 -> 12; matrix products, arithmetic and copies ran while one was open for 2% -> 2% of each run, Pallas kernels for 38% -> 35%
where the time goes in v6:
time: 890 us; the launch traced here: 880 us
  Pallas kernels  534 us (60%)
  waiting for transfers between devices  298 us (33%)
  starting transfers between devices  21.4 us (2%)
  local copies, waits for them, and re-layouts  19.1 us (2%)
    ppermute x6, waiting for transfers between devices, to_tp(): return lax.ppermute(v, 'tp', tp_perm)  155 us
    ppermute x7, waiting for transfers between devices, to_x(): return lax.ppermute(v, 'cp', x_perm)  140 us
    pallas_call x5, Pallas kernels, gather_matmul(): pl.pallas_call(functools.partial(gmm_kernel, layout=layout, mode=mode, R=...  101 us
    pallas_call x1, Pallas kernels, dw_proj(): pl.pallas_call(dw_kernel, grid_spec=pltpu.PrefetchScalarGridSpec(num_scal...  99.1 us
    pallas_call x1, Pallas kernels, attn_bwd(): pl.pallas_call(functools.partial(attn_bwd_kernel, k1=scale / SOFT_CAP, k2...  83.4 us
    pallas_call x1, Pallas kernels, dwo_proj(): pl.pallas_call(dwo_kernel, grid_spec=pltpu.PrefetchScalarGridSpec(num_sca...  50.1 us
    pallas_call x3, Pallas kernels, w_layout(): pl.pallas_call(w_kernel, grid_spec=pltpu.PrefetchScalarGridSpec(num_scala...  41.4 us
    pallas_call x1, Pallas kernels, attn_fwd(): pl.pallas_call(functools.partial(attn_fwd_kernel, k1=scale / SOFT_CAP, k2...  41.1 us
  transfers between devices with their start and end apart: 34, of which 12 were waited for; matrix products, arithmetic and copies ran while one was open for 2% of the time, Pallas kernels for 35%

profile of v6, /device:TPU:0, one launch (start us, length us, event | category | flops | bytes accessed | tf_op | source)
XLA Modules:
  0.0 880.4 jit_solution(6746703301783566269)
XLA Ops:
  0.6 1.3 reshape.74.g_ref
  2.0 7.8 a_norm.1.refs_0_
  10.6 1.5 constant_dynamic-slice_fusion.4
  12.2 2.5 collective-permute-start
  14.7 36.2 %collective-permute-done.refs_0_ = bf16[176,4608]{1,0:T(8,128)(2,1)} collective-permute-done((bf16[176,4608]{1,0:T(8,128)(2,1)S(1)}, bf16[176,4608]{1,0:T(8,128)(2,1)}, u32[]{:S(2)}, u32[]{:S(2)}) %collective-permute-start) | collective-permute-done | bytes 1622048 | tf_op jit(solution)/shard_map/ppermute | solution.py:576
  50.9 1.8 collective-permute-start.1
  52.7 1.5 slice.12
  54.1 1.5 collective-permute-start.2
  55.7 3.7 fusion
  59.4 1.9 pad_maximum_fusion
  62.5 20.6 %shard_map.143.refs_2_.refs_6_.w0_ref = bf16[4608,2048]{1,0:T(8,128)(2,1)} custom-call(s32[1]{0:T(128)} %bitcast.1.c_ref, bf16[4608,16,128]{2,1,0:T(8,128)(2,1)} %wq_ref.5, bf16[4608,8,128]{2,1,0:T(8,128)(2,1)} %wk_ref.5, bf16[4608,8,128]{2,1,0:T(8,128)(2,1)} %wv_ref.5), custom_call_target="tpu_custom_call" | custom-call | flops 4718592000 | bytes 47185920 | tf_op jit(solution)/shard_map/pallas_call | solution.py:333
  83.1 4.7 collective-permute-done.2.refs_2_
  88.5 29.9 %shard_map.144 = (bf16[4,512,2048]{2,1,0:T(8,128)(2,1)}, bf16[4,512,4608]{2,1,0:T(8,128)(2,1)}) custom-call(s32[6]{0:T(128)} %stack.86.sc_ref, bf16[512,4608]{1,0:T(8,128)(2,1)} %a_norm.1.refs_0_, bf16[512,4608]{1,0:T(8,128)(2,1)} %collective-permute-done.6.refs_1_, bf16[4608,2048]{1,0:T(8,128)(2,1)} %shard_map.143.refs_2_.refs_6_.w0_ref, ...), custom_call_target="tpu_custom_call" | custom-call | flops 19327352832 | bytes 37748736 | tf_op jit(solution)/shard_map/pallas_call | solution.py:298
  119.6 29.9 %shard_map.145 = (bf16[4,512,2048]{2,1,0:T(8,128)(2,1)}, bf16[4,512,4608]{2,1,0:T(8,128)(2,1)}) custom-call(s32[10]{0:T(128)} %stack.85.sc_ref, bf16[176,4608]{1,0:T(8,128)(2,1)} %collective-permute-done.refs_0_, bf16[176,4608]{1,0:T(8,128)(2,1)} %collective-permute-done.1.refs_1_, ...), custom_call_target="tpu_custom_call", output_to_operand_aliasing={{0}: (10, {}), {1}: (11, {})} | custom-call | flops 19327352832 | bytes 37748736 | tf_op jit(solution)/shard_map/pallas_call | solution.py:298
  149.5 41.1 %attn_fwd.1 = (bf16[2048,1024]{1,0:T(8,128)(2,1)}, f32[4,2,2048]{2,1,0:T(2,128)}) custom-call(bf16[2048,2048]{1,0:T(8,128)(2,1)} %bitcast.39, bf16[2048,2048]{1,0:T(8,128)(2,1)} %bitcast.40, bf16[2048,2048]{1,0:T(8,128)(2,1)} %bitcast.41), custom_call_target="tpu_custom_call" | custom-call | flops 17179869184 | bytes 16777216 | tf_op jit(solution)/shard_map/attn_fwd/pallas_call | solution.py:91
  193.1 1.6 collective-permute-done.7.c1_ref
  195.7 10.0 %shard_map.147.p_ref = bf16[128,4608]{1,0:T(8,128)(2,1)} custom-call(s32[4]{0:T(128)} %pad_add_fusion.sc_ref, bf16[2048,1024]{1,0:T(8,128)(2,1)} %get-tuple-element.47.c0_ref.ctx_ref, bf16[512,1024]{1,0:T(8,128)(2,1)} %copy-done, bf16[2048,4608]{1,0:T(8,128)(2,1)} %bitcast.21), custom_call_target="tpu_custom_call" | custom-call | flops 2415919104 | bytes 18874368 | tf_op jit(solution)/shard_map/pallas_call | solution.py:360
  205.7 1.5 collective-permute-start.9
  207.2 10.1 %shard_map.149.p_ref = bf16[128,4608]{1,0:T(8,128)(2,1)} custom-call(s32[4]{0:T(128)} %pad_add_fusion.sc_ref, bf16[2048,1024]{1,0:T(8,128)(2,1)} %get-tuple-element.47.c0_ref.ctx_ref, bf16[512,1024]{1,0:T(8,128)(2,1)} %copy-done, bf16[2048,4608]{1,0:T(8,128)(2,1)} %bitcast.22), custom_call_target="tpu_custom_call" | custom-call | flops 2415919104 | bytes 18874368 | tf_op jit(solution)/shard_map/pallas_call | solution.py:360
  217.9 10.1 %shard_map.148.p_ref = bf16[128,4608]{1,0:T(8,128)(2,1)} custom-call(s32[4]{0:T(128)} %pad_add_fusion.sc_ref, bf16[2048,1024]{1,0:T(8,128)(2,1)} %get-tuple-element.47.c0_ref.ctx_ref, bf16[512,1024]{1,0:T(8,128)(2,1)} %copy-done, bf16[2048,4608]{1,0:T(8,128)(2,1)} %bitcast.23), custom_call_target="tpu_custom_call" | custom-call | flops 2415919104 | bytes 18874368 | tf_op jit(solution)/shard_map/pallas_call | solution.py:360
  228.0 1.5 collective-permute-start.10
  229.5 10.0 %shard_map.146.p_ref = bf16[128,4608]{1,0:T(8,128)(2,1)} custom-call(s32[4]{0:T(128)} %pad_add_fusion.sc_ref, bf16[2048,1024]{1,0:T(8,128)(2,1)} %get-tuple-element.47.c0_ref.ctx_ref, bf16[512,1024]{1,0:T(8,128)(2,1)} %copy-done, bf16[2048,4608]{1,0:T(8,128)(2,1)} %bitcast.24), custom_call_target="tpu_custom_call" | custom-call | flops 2415919104 | bytes 18874368 | tf_op jit(solution)/shard_map/pallas_call | solution.py:360
  240.7 19.5 %collective-permute-done.11.r_ref = bf16[128,4608]{1,0:T(8,128)(2,1)} collective-permute-done((bf16[128,4608]{1,0:T(8,128)(2,1)}, bf16[128,4608]{1,0:T(8,128)(2,1)}, u32[]{:S(2)}, u32[]{:S(2)}) %collective-permute-start.11) | collective-permute-done | bytes 1179680 | tf_op jit(solution)/shard_map/ppermute | solution.py:579
  260.2 5.0 shard_map.150
  265.2 20.2 %collective-permute-done.10.r_ref = bf16[128,4608]{1,0:T(8,128)(2,1)} collective-permute-done((bf16[128,4608]{1,0:T(8,128)(2,1)}, bf16[128,4608]{1,0:T(8,128)(2,1)}, u32[]{:S(2)}, u32[]{:S(2)}) %collective-permute-start.10) | collective-permute-done | bytes 1179680 | tf_op jit(solution)/shard_map/ppermute | solution.py:579
  285.5 5.0 shard_map.151
  291.5 5.0 shard_map.152
  296.4 13.7 %collective-permute-done.8.r_ref = bf16[128,4608]{1,0:T(8,128)(2,1)S(1)} collective-permute-done((bf16[128,4608]{1,0:T(8,128)(2,1)}, bf16[128,4608]{1,0:T(8,128)(2,1)S(1)}, u32[]{:S(2)}, u32[]{:S(2)}) %collective-permute-start.8) | collective-permute-done | bytes 1179680 | tf_op jit(solution)/shard_map/ppermute | solution.py:579
  311.1 5.0 shard_map.153
  316.1 1.4 collective-permute-start.13
  318.2 1.4 collective-permute-start.16
  320.2 25.0 %collective-permute-done.13.refs_2_ = bf16[128,4608]{1,0:T(8,128)(2,1)S(1)} collective-permute-done((bf16[128,4608]{1,0:T(8,128)(2,1)}, bf16[128,4608]{1,0:T(8,128)(2,1)S(1)}, u32[]{:S(2)}, u32[]{:S(2)}) %collective-permute-start.13) | collective-permute-done | bytes 1179680 | tf_op jit(solution)/shard_map/ppermute | solution.py:576
  345.2 25.3 %collective-permute-done.15.refs_0_ = bf16[128,4608]{1,0:T(8,128)(2,1)S(1)} collective-permute-done((bf16[128,4608]{1,0:T(8,128)(2,1)}, bf16[128,4608]{1,0:T(8,128)(2,1)S(1)}, u32[]{:S(2)}, u32[]{:S(2)}) %collective-permute-start.15) | collective-permute-done | bytes 1179680 | tf_op jit(solution)/shard_map/ppermute | solution.py:576
  370.5 25.4 %collective-permute-done.16.refs_1_ = bf16[128,4608]{1,0:T(8,128)(2,1)} collective-permute-done((bf16[128,4608]{1,0:T(8,128)(2,1)}, bf16[128,4608]{1,0:T(8,128)(2,1)}, u32[]{:S(2)}, u32[]{:S(2)}) %collective-permute-start.16) | collective-permute-done | bytes 1179680 | tf_op jit(solution)/shard_map/ppermute | solution.py:576
  395.9 23.9 %collective-permute-done.17.refs_2_ = bf16[128,4608]{1,0:T(8,128)(2,1)} collective-permute-done((bf16[128,4608]{1,0:T(8,128)(2,1)}, bf16[128,4608]{1,0:T(8,128)(2,1)}, u32[]{:S(2)}, u32[]{:S(2)}) %collective-permute-start.17) | collective-permute-done | bytes 1179680 | tf_op jit(solution)/shard_map/ppermute | solution.py:576
  422.7 14.9 %shard_map.154 = (bf16[4,512,1024]{2,1,0:T(8,128)(2,1)}, bf16[4,512,4608]{2,1,0:T(8,128)(2,1)}) custom-call(s32[10]{0:T(128)} %stack.91.sc_ref, bf16[128,4608]{1,0:T(8,128)(2,1)} %get-tuple-element.53.refs_0_, bf16[128,4608]{1,0:T(8,128)(2,1)} %get-tuple-element.54.refs_1_, bf16[128,4608]{1,0:T(8,128)(2,1)} %get-tuple-element.55.refs_2_, ...), custom_call_target="tpu_custom_call" | custom-call | flops 7247757312 | bytes 23592960 | tf_op jit(solution)/shard_map/pallas_call | solution.py:298
  437.7 14.7 %shard_map.155 = (bf16[4,512,1024]{2,1,0:T(8,128)(2,1)}, bf16[4,512,4608]{2,1,0:T(8,128)(2,1)}) custom-call(s32[10]{0:T(128)} %stack.90.sc_ref, bf16[128,4608]{1,0:T(8,128)(2,1)} %copy-done.2, bf16[128,4608]{1,0:T(8,128)(2,1)} %collective-permute-done.16.refs_1_, ...), custom_call_target="tpu_custom_call", output_to_operand_aliasing={{0}: (8, {}), {1}: (9, {})} | custom-call | flops 7247757312 | bytes 23592960 | tf_op jit(solution)/shard_map/pallas_call | solution.py:298
  452.4 12.1 %shard_map.156 = (bf16[4,512,1024]{2,1,0:T(8,128)(2,1)}, bf16[4,512,4608]{2,1,0:T(8,128)(2,1)}) custom-call(s32[10]{0:T(128)} %stack.89.sc_ref, bf16[128,4608]{1,0:T(8,128)(2,1)} %get-tuple-element.52.refs_0_, bf16[128,4608]{1,0:T(8,128)(2,1)} %collective-permute-done.12.refs_1_, ...), custom_call_target="tpu_custom_call", output_to_operand_aliasing={{0}: (6, {}), {1}: (7, {})} | custom-call | flops 4831838208 | bytes 18874368 | tf_op jit(solution)/shard_map/pallas_call | solution.py:298
  464.5 83.4 %attn_bwd.1 = (bf16[2048,1024]{1,0:T(8,128)(2,1)}, bf16[2048,512]{1,0:T(8,128)(2,1)}, bf16[2048,512]{1,0:T(8,128)(2,1)}) custom-call(bf16[2048,2048]{1,0:T(8,128)(2,1)} %bitcast.42, bf16[2048,2048]{1,0:T(8,128)(2,1)} %bitcast.43, bf16[2048,2048]{1,0:T(8,128)(2,1)} %bitcast.44, bf16[2048,1024]{1,0:T(8,128)(2,1)} %bitcast.29, ...), custom_call_target="tpu_custom_call" | custom-call | flops 21474836480 | bytes 25165824 | tf_op jit(solution)/shard_map/attn_bwd/pallas_call | solution.py:194
  551.9 10.4 %shard_map.157.wa_ref = bf16[2304,2048]{1,0:T(8,128)(2,1)} custom-call(s32[1]{0:T(128)} %bitcast.5.c_ref, bf16[4608,16,128]{2,1,0:T(8,128)(2,1)} %wq_ref.5, bf16[4608,8,128]{2,1,0:T(8,128)(2,1)} %wk_ref.5, bf16[4608,8,128]{2,1,0:T(8,128)(2,1)} %wv_ref.5), custom_call_target="tpu_custom_call" | custom-call | flops 2359296000 | bytes 23592960 | tf_op jit(solution)/shard_map/pallas_call | solution.py:333
  562.3 10.4 %shard_map.158.wb_ref = bf16[2304,2048]{1,0:T(8,128)(2,1)} custom-call(s32[1]{0:T(128)} %bitcast.5.c_ref, bf16[4608,16,128]{2,1,0:T(8,128)(2,1)} %wq_ref.5, bf16[4608,8,128]{2,1,0:T(8,128)(2,1)} %wk_ref.5, bf16[4608,8,128]{2,1,0:T(8,128)(2,1)} %wv_ref.5), custom_call_target="tpu_custom_call" | custom-call | flops 2359296000 | bytes 23592960 | tf_op jit(solution)/shard_map/pallas_call | solution.py:333
  572.8 36.2 %shard_map.159.p_ref = bf16[512,4608]{1,0:T(8,128)(2,1)} custom-call(s32[4]{0:T(128)} %pad_add_fusion.sc_ref, bf16[2048,1024]{1,0:T(8,128)(2,1)} %get-tuple-element.62.q0, bf16[2048,512]{1,0:T(8,128)(2,1)} %get-tuple-element.63.k0, bf16[2048,512]{1,0:T(8,128)(2,1)} %get-tuple-element.64.v0, bf16[512,1024]{1,0:T(8,128)(2,1)} %collective-permute-done.24.q1, ...), custom_call_target="tpu_custom_call" | custom-call | flops 19327352832 | bytes 37748736 | tf_op jit(solution)/shard_map/pallas_call | solution.py:404
  609.0 1.5 collective-permute-start.27
  611.6 101.8 %collective-permute-done.27.r_ref = bf16[512,4608]{1,0:T(8,128)(2,1)} collective-permute-done((bf16[512,4608]{1,0:T(8,128)(2,1)}, bf16[512,4608]{1,0:T(8,128)(2,1)}, u32[]{:S(2)}, u32[]{:S(2)}) %collective-permute-start.27) | collective-permute-done | bytes 4718624 | tf_op jit(solution)/shard_map/ppermute | solution.py:579
  713.5 13.0 %shard_map.160 = (bf16[512,4608]{1,0:T(8,128)(2,1)}, f32[8,4608]{1,0:T(8,128)}) custom-call(bf16[512,4608]{1,0:T(8,128)(2,1)} %shard_map.159.p_ref, bf16[512,4608]{1,0:T(8,128)(2,1)} %collective-permute-done.27.r_ref, bf16[512,4608]{1,0:T(8,128)(2,1)} %h_ref.11, bf16[512,4608]{1,0:T(8,128)(2,1)} %dy_ref.9, f32[1,4608]{1,0:T(1,128)} %reshape.74.g_ref), custom_call_target="tpu_custom_call" | custom-call | flops 4718592000 | bytes 28311552 | tf_op jit(solution)/shard_map/pallas_call | solution.py:542
  727.5 50.1 %dwo_proj.1 = f32[2048,4608]{1,0:T(8,128)} custom-call(s32[4]{0:T(128)} %pad_add_fusion.sc_ref, bf16[2048,1024]{1,0:T(8,128)(2,1)} %get-tuple-element.47.c0_ref.ctx_ref, bf16[2048,1024]{1,0:T(8,128)(2,1)} %collective-permute-done.33.c1_ref, bf16[2048,4608]{1,0:T(8,128)(2,1)} %bitcast.28), custom_call_target="tpu_custom_call" | custom-call | flops 38654705664 | bytes 37748736 | tf_op jit(solution)/shard_map/dwo_proj/pallas_call | solution.py:471
  777.6 1.4 collective-permute-start.29
  780.4 99.1 %dw_proj.1 = (f32[73728,128]{1,0:T(8,128)}, f32[36864,128]{1,0:T(8,128)}, f32[36864,128]{1,0:T(8,128)}) custom-call(s32[4]{0:T(128)} %pad_add_fusion.sc_ref, bf16[2048,4608]{1,0:T(8,128)(2,1)} %bitcast.38, bf16[2048,1024]{1,0:T(8,128)(2,1)} %get-tuple-element.62.q0, bf16[2048,1024]{1,0:T(8,128)(2,1)} %collective-permute-done.30.q1, ...), custom_call_target="tpu_custom_call" | custom-call | flops 77309411328 | bytes 75497472 | tf_op jit(solution)/shard_map/dw_proj/pallas_call | solution.py:439
  (94 shorter events, 23.7 us)
Async XLA Ops:
  9.8 78.7 %collective-permute-start.6 = (bf16[512,4608]{1,0:T(8,128)(2,1)}, bf16[512,4608]{1,0:T(8,128)(2,1)}, u32[]{:S(2)}, u32[]{:S(2)}) collective-permute-start(bf16[512,4608]{1,0:T(8,128)(2,1)} %a_norm.1.refs_0_), channel_id=1, source_target_pairs={{0,1},{1,0},{2,3},{3,2},{4,5},{5,4},{6,7},{7,6}} | collective-permute-start | bytes 14155784 | tf_op jit(solution)/shard_map/ppermute | solution.py:573
  12.2 38.7 %collective-permute-start = (bf16[176,4608]{1,0:T(8,128)(2,1)S(1)}, bf16[176,4608]{1,0:T(8,128)(2,1)}, u32[]{:S(2)}, u32[]{:S(2)}) collective-permute-start(bf16[176,4608]{1,0:T(8,128)(2,1)S(1)} %constant_dynamic-slice_fusion.4), channel_id=1, source_target_pairs={{0,2},{2,0},{1,3},{3,1},{4,6},{6,4},{5,7},{7,5}} | collective-permute-start | bytes 4866056 | tf_op jit(solution)/shard_map/ppermute | solution.py:576
  50.9 37.6 %collective-permute-start.1 = (bf16[176,4608]{1,0:T(8,128)(2,1)}, bf16[176,4608]{1,0:T(8,128)(2,1)}, u32[]{:S(2)}, u32[]{:S(2)}) collective-permute-start(bf16[176,4608]{1,0:T(8,128)(2,1)} %collective-permute-done.refs_0_), channel_id=1, source_target_pairs={{0,4},{4,0},{1,5},{5,1},{2,6},{6,2},{3,7},{7,3}} | collective-permute-start | bytes 4866056 | tf_op jit(solution)/shard_map/ppermute | solution.py:579
  54.1 33.7 %collective-permute-start.2 = (bf16[160,4608]{1,0:T(8,128)(2,1)S(1)}, bf16[160,4608]{1,0:T(8,128)(2,1)}, u32[]{:S(2)}, u32[]{:S(2)}) collective-permute-start(bf16[160,4608]{1,0:T(8,128)(2,1)S(1)} %slice.12), channel_id=1, source_target_pairs={{0,2},{2,0},{1,3},{3,1},{4,6},{6,4},{5,7},{7,5}} | collective-permute-start | bytes 4423688 | tf_op jit(solution)/shard_map/ppermute | solution.py:576
  87.8 30.6 %collective-permute-start.5 = (bf16[160,4608]{1,0:T(8,128)(2,1)}, bf16[160,4608]{1,0:T(8,128)(2,1)}, u32[]{:S(2)}, u32[]{:S(2)}) collective-permute-start(bf16[160,4608]{1,0:T(8,128)(2,1)} %collective-permute-done.2.refs_2_), channel_id=1, source_target_pairs={{0,1},{1,0},{2,3},{3,2},{4,5},{5,4},{6,7},{7,6}} | collective-permute-start | bytes 4423688 | tf_op jit(solution)/shard_map/ppermute | solution.py:573
  87.8 30.6 %collective-permute-start.3 = (bf16[176,4608]{1,0:T(8,128)(2,1)}, bf16[176,4608]{1,0:T(8,128)(2,1)S(1)}, u32[]{:S(2)}, u32[]{:S(2)}) collective-permute-start(bf16[176,4608]{1,0:T(8,128)(2,1)} %collective-permute-done.refs_0_), channel_id=1, source_target_pairs={{0,1},{1,0},{2,3},{3,2},{4,5},{5,4},{6,7},{7,6}} | collective-permute-start | bytes 4866056 | tf_op jit(solution)/shard_map/ppermute | solution.py:573
  88.5 29.9 %collective-permute-start.4 = (bf16[176,4608]{1,0:T(8,128)(2,1)}, bf16[176,4608]{1,0:T(8,128)(2,1)}, u32[]{:S(2)}, u32[]{:S(2)}) collective-permute-start(bf16[176,4608]{1,0:T(8,128)(2,1)} %collective-permute-done.1.refs_1_), channel_id=1, source_target_pairs={{0,1},{1,0},{2,3},{3,2},{4,5},{5,4},{6,7},{7,6}} | collective-permute-start | bytes 4866056 | tf_op jit(solution)/shard_map/ppermute | solution.py:573
  118.4 1.2 copy-start.11
  191.9 2.8 collective-permute-start.7
  194.7 1.0 copy-start
  205.7 84.7 %collective-permute-start.9 = (bf16[128,4608]{1,0:T(8,128)(2,1)}, bf16[128,4608]{1,0:T(8,128)(2,1)S(1)}, u32[]{:S(2)}, u32[]{:S(2)}) collective-permute-start(bf16[128,4608]{1,0:T(8,128)(2,1)} %shard_map.147.p_ref), channel_id=1, source_target_pairs={{0,4},{4,0},{1,5},{5,1},{2,6},{6,2},{3,7},{7,3}} | collective-permute-start | bytes 3538952 | tf_op jit(solution)/shard_map/ppermute | solution.py:579
  217.4 42.8 %collective-permute-start.11 = (bf16[128,4608]{1,0:T(8,128)(2,1)}, bf16[128,4608]{1,0:T(8,128)(2,1)}, u32[]{:S(2)}, u32[]{:S(2)}) collective-permute-start(bf16[128,4608]{1,0:T(8,128)(2,1)} %shard_map.149.p_ref), channel_id=1, source_target_pairs={{0,4},{4,0},{1,5},{5,1},{2,6},{6,2},{3,7},{7,3}} | collective-permute-start | bytes 3538952 | tf_op jit(solution)/shard_map/ppermute | solution.py:579
  228.0 12.1 %copy-start.9 = (f32[4608]{0:T(1024)S(1)}, f32[4608]{0:T(1024)}, u32[]{:S(2)}) copy-start(f32[4608]{0:T(1024)} %param.14) | copy-start | bytes 55300
  228.0 57.5 %collective-permute-start.10 = (bf16[128,4608]{1,0:T(8,128)(2,1)}, bf16[128,4608]{1,0:T(8,128)(2,1)}, u32[]{:S(2)}, u32[]{:S(2)}) collective-permute-start(bf16[128,4608]{1,0:T(8,128)(2,1)} %shard_map.148.p_ref), channel_id=1, source_target_pairs={{0,4},{4,0},{1,5},{5,1},{2,6},{6,2},{3,7},{7,3}} | collective-permute-start | bytes 3538952 | tf_op jit(solution)/shard_map/ppermute | solution.py:579
  239.5 70.6 %collective-permute-start.8 = (bf16[128,4608]{1,0:T(8,128)(2,1)}, bf16[128,4608]{1,0:T(8,128)(2,1)S(1)}, u32[]{:S(2)}, u32[]{:S(2)}) collective-permute-start(bf16[128,4608]{1,0:T(8,128)(2,1)} %shard_map.146.p_ref), channel_id=1, source_target_pairs={{0,4},{4,0},{1,5},{5,1},{2,6},{6,2},{3,7},{7,3}} | collective-permute-start | bytes 3538952 | tf_op jit(solution)/shard_map/ppermute | solution.py:579
  290.4 1.0 copy-start.3
  310.1 1.0 copy-start.4
  316.1 29.1 %collective-permute-start.13 = (bf16[128,4608]{1,0:T(8,128)(2,1)}, bf16[128,4608]{1,0:T(8,128)(2,1)S(1)}, u32[]{:S(2)}, u32[]{:S(2)}) collective-permute-start(bf16[128,4608]{1,0:T(8,128)(2,1)} %get-tuple-element.52.refs_0_), channel_id=1, source_target_pairs={{0,2},{2,0},{1,3},{3,1},{4,6},{6,4},{5,7},{7,5}} | collective-permute-start | bytes 3538952 | tf_op jit(solution)/shard_map/ppermute | solution.py:576
  317.5 52.9 %collective-permute-start.15 = (bf16[128,4608]{1,0:T(8,128)(2,1)}, bf16[128,4608]{1,0:T(8,128)(2,1)S(1)}, u32[]{:S(2)}, u32[]{:S(2)}) collective-permute-start(bf16[128,4608]{1,0:T(8,128)(2,1)} %get-tuple-element.53.refs_0_), channel_id=1, source_target_pairs={{0,2},{2,0},{1,3},{3,1},{4,6},{6,4},{5,7},{7,5}} | collective-permute-start | bytes 3538952 | tf_op jit(solution)/shard_map/ppermute | solution.py:576
  318.2 77.7 %collective-permute-start.16 = (bf16[128,4608]{1,0:T(8,128)(2,1)}, bf16[128,4608]{1,0:T(8,128)(2,1)}, u32[]{:S(2)}, u32[]{:S(2)}) collective-permute-start(bf16[128,4608]{1,0:T(8,128)(2,1)} %get-tuple-element.54.refs_1_), channel_id=1, source_target_pairs={{0,2},{2,0},{1,3},{3,1},{4,6},{6,4},{5,7},{7,5}} | collective-permute-start | bytes 3538952 | tf_op jit(solution)/shard_map/ppermute | solution.py:576
  319.6 100.2 %collective-permute-start.17 = (bf16[128,4608]{1,0:T(8,128)(2,1)}, bf16[128,4608]{1,0:T(8,128)(2,1)}, u32[]{:S(2)}, u32[]{:S(2)}) collective-permute-start(bf16[128,4608]{1,0:T(8,128)(2,1)} %get-tuple-element.55.refs_2_), channel_id=1, source_target_pairs={{0,2},{2,0},{1,3},{3,1},{4,6},{6,4},{5,7},{7,5}} | collective-permute-start | bytes 3538952 | tf_op jit(solution)/shard_map/ppermute | solution.py:576
  320.2 99.5 %collective-permute-start.21 = (bf16[128,4608]{1,0:T(8,128)(2,1)}, bf16[128,4608]{1,0:T(8,128)(2,1)}, u32[]{:S(2)}, u32[]{:S(2)}) collective-permute-start(bf16[128,4608]{1,0:T(8,128)(2,1)} %get-tuple-element.53.refs_0_), channel_id=1, source_target_pairs={{0,1},{1,0},{2,3},{3,2},{4,5},{5,4},{6,7},{7,6}} | collective-permute-start | bytes 3538952 | tf_op jit(solution)/shard_map/ppermute | solution.py:573
  345.2 92.5 %copy-start.1 = (bf16[128,4608]{1,0:T(8,128)(2,1)}, bf16[128,4608]{1,0:T(8,128)(2,1)S(1)}, u32[]{:S(2)}) copy-start(bf16[128,4608]{1,0:T(8,128)(2,1)S(1)} %collective-permute-done.13.refs_2_) | copy-start | bytes 3538948
  345.2 77.0 %collective-permute-start.22 = (bf16[128,4608]{1,0:T(8,128)(2,1)}, bf16[128,4608]{1,0:T(8,128)(2,1)}, u32[]{:S(2)}, u32[]{:S(2)}) collective-permute-start(bf16[128,4608]{1,0:T(8,128)(2,1)} %get-tuple-element.54.refs_1_), channel_id=1, source_target_pairs={{0,1},{1,0},{2,3},{3,2},{4,5},{5,4},{6,7},{7,6}} | collective-permute-start | bytes 3538952 | tf_op jit(solution)/shard_map/ppermute | solution.py:573
  370.5 67.2 %copy-start.2 = (bf16[128,4608]{1,0:T(8,128)(2,1)}, bf16[128,4608]{1,0:T(8,128)(2,1)S(1)}, u32[]{:S(2)}) copy-start(bf16[128,4608]{1,0:T(8,128)(2,1)S(1)} %collective-permute-done.15.refs_0_) | copy-start | bytes 3538948
  370.5 51.8 %collective-permute-start.23 = (bf16[128,4608]{1,0:T(8,128)(2,1)}, bf16[128,4608]{1,0:T(8,128)(2,1)}, u32[]{:S(2)}, u32[]{:S(2)}) collective-permute-start(bf16[128,4608]{1,0:T(8,128)(2,1)} %get-tuple-element.55.refs_2_), channel_id=1, source_target_pairs={{0,1},{1,0},{2,3},{3,2},{4,5},{5,4},{6,7},{7,6}} | collective-permute-start | bytes 3538952 | tf_op jit(solution)/shard_map/ppermute | solution.py:573
  395.9 41.8 %collective-permute-start.18 = (bf16[128,4608]{1,0:T(8,128)(2,1)S(1)}, bf16[128,4608]{1,0:T(8,128)(2,1)}, u32[]{:S(2)}, u32[]{:S(2)}) collective-permute-start(bf16[128,4608]{1,0:T(8,128)(2,1)S(1)} %collective-permute-done.15.refs_0_), channel_id=1, source_target_pairs={{0,1},{1,0},{2,3},{3,2},{4,5},{5,4},{6,7},{7,6}} | collective-permute-start | bytes 3538952 | tf_op jit(solution)/shard_map/ppermute | solution.py:573
  419.7 17.9 %collective-permute-start.19 = (bf16[128,4608]{1,0:T(8,128)(2,1)}, bf16[128,4608]{1,0:T(8,128)(2,1)}, u32[]{:S(2)}, u32[]{:S(2)}) collective-permute-start(bf16[128,4608]{1,0:T(8,128)(2,1)} %collective-permute-done.16.refs_1_), channel_id=1, source_target_pairs={{0,1},{1,0},{2,3},{3,2},{4,5},{5,4},{6,7},{7,6}} | collective-permute-start | bytes 3538952 | tf_op jit(solution)/shard_map/ppermute | solution.py:573
  419.7 17.9 %collective-permute-start.20 = (bf16[128,4608]{1,0:T(8,128)(2,1)}, bf16[128,4608]{1,0:T(8,128)(2,1)}, u32[]{:S(2)}, u32[]{:S(2)}) collective-permute-start(bf16[128,4608]{1,0:T(8,128)(2,1)} %collective-permute-done.17.refs_2_), channel_id=1, source_target_pairs={{0,1},{1,0},{2,3},{3,2},{4,5},{5,4},{6,7},{7,6}} | collective-permute-start | bytes 3538952 | tf_op jit(solution)/shard_map/ppermute | solution.py:573
  422.2 30.2 %collective-permute-start.12 = (bf16[128,4608]{1,0:T(8,128)(2,1)}, bf16[128,4608]{1,0:T(8,128)(2,1)}, u32[]{:S(2)}, u32[]{:S(2)}) collective-permute-start(bf16[128,4608]{1,0:T(8,128)(2,1)} %get-tuple-element.52.refs_0_), channel_id=1, source_target_pairs={{0,1},{1,0},{2,3},{3,2},{4,5},{5,4},{6,7},{7,6}} | collective-permute-start | bytes 3538952 | tf_op jit(solution)/shard_map/ppermute | solution.py:573
  422.2 30.2 %collective-permute-start.14 = (bf16[128,4608]{1,0:T(8,128)(2,1)S(1)}, bf16[128,4608]{1,0:T(8,128)(2,1)}, u32[]{:S(2)}, u32[]{:S(2)}) collective-permute-start(bf16[128,4608]{1,0:T(8,128)(2,1)S(1)} %collective-permute-done.13.refs_2_), channel_id=1, source_target_pairs={{0,1},{1,0},{2,3},{3,2},{4,5},{5,4},{6,7},{7,6}} | collective-permute-start | bytes 3538952 | tf_op jit(solution)/shard_map/ppermute | solution.py:573
  549.2 23.6 %collective-permute-start.24 = (bf16[512,1024]{1,0:T(8,128)(2,1)S(1)}, bf16[512,1024]{1,0:T(8,128)(2,1)}, u32[]{:S(2)}, u32[]{:S(2)}) collective-permute-start(bf16[512,1024]{1,0:T(8,128)(2,1)S(1)} %constant_dynamic-slice_fusion.2), channel_id=1, source_target_pairs={{0,1},{1,0},{2,3},{3,2},{4,5},{5,4},{6,7},{7,6}} | collective-permute-start | bytes 3145736 | tf_op jit(solution)/shard_map/ppermute | solution.py:573
  550.3 22.4 %collective-permute-start.25 = (bf16[512,512]{1,0:T(8,128)(2,1)S(1)}, bf16[512,512]{1,0:T(8,128)(2,1)}, u32[]{:S(2)}, u32[]{:S(2)}) collective-permute-start(bf16[512,512]{1,0:T(8,128)(2,1)S(1)} %constant_dynamic-slice_fusion.1), channel_id=1, source_target_pairs={{0,1},{1,0},{2,3},{3,2},{4,5},{5,4},{6,7},{7,6}} | collective-permute-start | bytes 1572872 | tf_op jit(solution)/shard_map/ppermute | solution.py:573
  551.9 20.9 %collective-permute-start.26 = (bf16[512,512]{1,0:T(8,128)(2,1)S(1)}, bf16[512,512]{1,0:T(8,128)(2,1)}, u32[]{:S(2)}, u32[]{:S(2)}) collective-permute-start(bf16[512,512]{1,0:T(8,128)(2,1)S(1)} %constant_dynamic-slice_fusion), channel_id=1, source_target_pairs={{0,1},{1,0},{2,3},{3,2},{4,5},{5,4},{6,7},{7,6}} | collective-permute-start | bytes 1572872 | tf_op jit(solution)/shard_map/ppermute | solution.py:573
  572.7 37.9 %copy-start.5 = (f32[8,4608]{1,0:T(8,128)S(1)}, f32[8,4608]{1,0:T(8,128)}, u32[]{:S(2)}) copy-start(f32[8,4608]{1,0:T(8,128)} %get-tuple-element.67) | copy-start | bytes 442372
  572.7 37.9 %copy-start.6 = (f32[8,4608]{1,0:T(8,128)S(1)}, f32[8,4608]{1,0:T(8,128)}, u32[]{:S(2)}) copy-start(f32[8,4608]{1,0:T(8,128)} %get-tuple-element.68) | copy-start | bytes 442372
  572.7 37.9 %copy-start.7 = (f32[8,4608]{1,0:T(8,128)S(1)}, f32[8,4608]{1,0:T(8,128)}, u32[]{:S(2)}) copy-start(f32[8,4608]{1,0:T(8,128)} %get-tuple-element.69) | copy-start | bytes 442372
  572.7 37.9 %copy-start.8 = (f32[8,4608]{1,0:T(8,128)S(1)}, f32[8,4608]{1,0:T(8,128)}, u32[]{:S(2)}) copy-start(f32[8,4608]{1,0:T(8,128)} %get-tuple-element.70) | copy-start | bytes 442372
  609.0 104.5 %collective-permute-start.27 = (bf16[512,4608]{1,0:T(8,128)(2,1)}, bf16[512,4608]{1,0:T(8,128)(2,1)}, u32[]{:S(2)}, u32[]{:S(2)}) collective-permute-start(bf16[512,4608]{1,0:T(8,128)(2,1)} %shard_map.159.p_ref), channel_id=1, source_target_pairs={{0,4},{4,0},{1,5},{5,1},{2,6},{6,2},{3,7},{7,3}} | collective-permute-start | bytes 14155784 | tf_op jit(solution)/shard_map/ppermute | solution.py:579
  610.5 117.0 %collective-permute-start.33 = (bf16[2048,1024]{1,0:T(8,128)(2,1)}, bf16[2048,1024]{1,0:T(8,128)(2,1)}, u32[]{:S(2)}, u32[]{:S(2)}) collective-permute-start(bf16[2048,1024]{1,0:T(8,128)(2,1)} %get-tuple-element.47.c0_ref.ctx_ref), channel_id=1, source_target_pairs={{0,1},{1,0},{2,3},{3,2},{4,5},{5,4},{6,7},{7,6}} | collective-permute-start | bytes 12582920 | tf_op jit(solution)/shard_map/ppermute | solution.py:573
  610.8 168.3 %collective-permute-start.30 = (bf16[2048,1024]{1,0:T(8,128)(2,1)}, bf16[2048,1024]{1,0:T(8,128)(2,1)}, u32[]{:S(2)}, u32[]{:S(2)}) collective-permute-start(bf16[2048,1024]{1,0:T(8,128)(2,1)} %get-tuple-element.62.q0), channel_id=1, source_target_pairs={{0,1},{1,0},{2,3},{3,2},{4,5},{5,4},{6,7},{7,6}} | collective-permute-start | bytes 12582920 | tf_op jit(solution)/shard_map/ppermute | solution.py:573
  611.1 167.9 %collective-permute-start.31 = (bf16[2048,512]{1,0:T(8,128)(2,1)}, bf16[2048,512]{1,0:T(8,128)(2,1)S(1)}, u32[]{:S(2)}, u32[]{:S(2)}) collective-permute-start(bf16[2048,512]{1,0:T(8,128)(2,1)} %get-tuple-element.63.k0), channel_id=1, source_target_pairs={{0,1},{1,0},{2,3},{3,2},{4,5},{5,4},{6,7},{7,6}} | collective-permute-start | bytes 6291464 | tf_op jit(solution)/shard_map/ppermute | solution.py:573
  611.3 167.7 %collective-permute-start.32 = (bf16[2048,512]{1,0:T(8,128)(2,1)}, bf16[2048,512]{1,0:T(8,128)(2,1)}, u32[]{:S(2)}, u32[]{:S(2)}) collective-permute-start(bf16[2048,512]{1,0:T(8,128)(2,1)} %get-tuple-element.64.v0), channel_id=1, source_target_pairs={{0,1},{1,0},{2,3},{3,2},{4,5},{5,4},{6,7},{7,6}} | collective-permute-start | bytes 6291464 | tf_op jit(solution)/shard_map/ppermute | solution.py:573
  727.4 50.1 %collective-permute-start.28 = (f32[2,4608]{1,0:T(2,128)S(1)}, f32[2,4608]{1,0:T(2,128)S(1)}, u32[]{:S(2)}, u32[]{:S(2)}) collective-permute-start(f32[2,4608]{1,0:T(2,128)S(1)} %pad_maximum_fusion.2), channel_id=1, source_target_pairs={{0,1},{1,0},{2,3},{3,2},{4,5},{5,4},{6,7},{7,6}} | collective-permute-start | bytes 110600 | tf_op jit(solution)/shard_map/ppermute | solution.py:573
  777.6 101.9 %collective-permute-start.29 = (f32[2,4608]{1,0:T(2,128)S(1)}, f32[2,4608]{1,0:T(2,128)S(1)}, u32[]{:S(2)}, u32[]{:S(2)}) collective-permute-start(f32[2,4608]{1,0:T(2,128)S(1)} %fusion.1), channel_id=1, source_target_pairs={{0,2},{2,0},{1,3},{3,1},{4,6},{6,4},{5,7},{7,5}} | collective-permute-start | bytes 110600 | tf_op jit(solution)/shard_map/ppermute | solution.py:576
  779.0 1.4 copy-start.10

commit v7 on v5

--- a/solution.py
+++ b/solution.py
@@ -315,7 +315,8 @@
     )(scal, *args)
 
 
-def w_kernel(c_ref, wq_ref, wk_ref, wv_ref, out_ref, s_ref):
+def w_kernel(c_ref, wq_ref, wk_ref, wv_ref, *rest):
+    out_ref, s_ref = rest[-2:]
     nq, n = wq_ref.shape[1] * HEAD, s_ref.shape[2] // 2
     out_ref[:, :nq] = wq_ref[...].reshape(-1, nq)
     half = pl.ds(pl.multiple_of(c_ref[0] * n, n), n)
@@ -324,23 +325,31 @@
         out_ref[:, nq + j * n:nq + (j + 1) * n] = s_ref[j, :, half]
 
 
-def w_layout(c, w_q, w_k, w_v, db):
+def w_layout(c, w_q, w_k, w_v, db, i0=0, n_blocks=None, buf=None):
     D, hb = w_k.shape[:2]
     nq, n = w_q.shape[1] // 2, hb // 2
     N = (nq + 2 * n) * HEAD
+    steps = D // db if n_blocks is None else n_blocks
+    in_specs = [pl.BlockSpec((db, nq, HEAD), lambda i, s: (i0 + i, s[0], 0))] + [pl.BlockSpec((db, hb, HEAD), lambda i, s: (i0 + i, 0, 0))] * 2
+    args, aliases = [w_q, w_k, w_v], {}
+    if buf is not None:
+        in_specs.append(pl.BlockSpec(memory_space=pl.ANY))
+        args.append(buf)
+        aliases = {4: 0}
     return pl.pallas_call(
         w_kernel,
         grid_spec=pltpu.PrefetchScalarGridSpec(
             num_scalar_prefetch=1,
-            grid=(D // db,),
-            in_specs=[pl.BlockSpec((db, nq, HEAD), lambda i, s: (i, s[0], 0))] + [pl.BlockSpec((db, hb, HEAD), lambda i, s: (i, 0, 0))] * 2,
-            out_specs=pl.BlockSpec((db, N), lambda i, s: (i, 0)),
+            grid=(steps,),
+            in_specs=in_specs,
+            out_specs=pl.BlockSpec((db, N), lambda i, s: (i0 + i, 0)),
             scratch_shapes=[pltpu.VMEM((2, db, hb * HEAD), BF16)],
         ),
         out_shape=jax.ShapeDtypeStruct((D, N), BF16),
+        input_output_aliases=aliases,
         compiler_params=pltpu.CompilerParams(dimension_semantics=("arbitrary",), vmem_limit_bytes=VMEM_LIMIT),
-        cost_estimate=pl.CostEstimate(flops=D * N * 500, bytes_accessed=D * N * 5, transcendentals=0),
-    )(jnp.reshape(c, (1,)).astype(jnp.int32), w_q, w_k, w_v)
+        cost_estimate=pl.CostEstimate(flops=steps * db * N * 500, bytes_accessed=steps * db * N * 5, transcendentals=0),
+    )(jnp.reshape(c, (1,)).astype(jnp.int32), *args)
 
 
 def orow_kernel(sc_ref, c0_ref, c1_ref, w_ref, out_ref, *, r0):
@@ -403,9 +412,12 @@
     )(scal, *own, *oth, *ws)
 
 
-def dw_kernel(sc_ref, a_ref, q0, q1, k0, k1, v0, v1, oq_ref, ok_ref, ov_ref):
+def dw_kernel(sc_ref, a_ref, q0, q1, k0, k1, v0, v1, h0_ref, h1_ref, oq_ref, ok_ref, ov_ref, oo_ref):
     db = a_ref.shape[1]
     core = sc_ref[1]
+    nr = h0_ref.shape[0]
+    oo_ref[pl.ds(pl.multiple_of(core * nr, nr), nr), :] = h0_ref[...]
+    oo_ref[pl.ds(pl.multiple_of((1 - core) * nr, nr), nr), :] = h1_ref[...]
     at = a_ref[...].T
     for pair, out_ref in (((q0, q1), oq_ref), ((k0, k1), ok_ref), ((v0, v1), ov_ref)):
         hh = pair[0].shape[1] // HEAD
@@ -417,7 +429,7 @@
                 out_ref[pl.ds(c * hh + h, db, stride=nh), :] = res[:, h * HEAD:(h + 1) * HEAD]
 
 
-def dw_proj(scal, a, gs, db):
+def dw_proj(scal, a, gs, halves, db):
     T, D = a.shape
     nhs = [2 * gs[0].shape[1] // HEAD, 2 * gs[2].shape[1] // HEAD, 2 * gs[4].shape[1] // HEAD]
     outs = pl.pallas_call(
@@ -426,47 +438,41 @@
             num_scalar_prefetch=1,
             grid=(D // db,),
             in_specs=[pl.BlockSpec((T, db), lambda i, s: (0, i))]
-            + [pl.BlockSpec(g.shape, lambda i, s: (0, 0), pipeline_mode=pl.Buffered(1)) for g in gs],
-            out_specs=[pl.BlockSpec((db * nh, HEAD), lambda i, s: (i, 0)) for nh in nhs],
+            + [pl.BlockSpec(g.shape, lambda i, s: (0, 0), pipeline_mode=pl.Buffered(1)) for g in gs]
+            + [pl.BlockSpec((h.shape[0], db), lambda i, s: (0, i)) for h in halves],
+            out_specs=[pl.BlockSpec((db * nh, HEAD), lambda i, s: (i, 0)) for nh in nhs]
+            + [pl.BlockSpec((2 * halves[0].shape[0], db), lambda i, s: (0, i))],
         ),
-        out_shape=[jax.ShapeDtypeStruct((D * nh, HEAD), F32) for nh in nhs],
+        out_shape=[jax.ShapeDtypeStruct((D * nh, HEAD), F32) for nh in nhs] + [jax.ShapeDtypeStruct((2 * halves[0].shape[0], D), F32)],
         compiler_params=pltpu.CompilerParams(dimension_semantics=("arbitrary",), vmem_limit_bytes=VMEM_LIMIT),
         cost_estimate=pl.CostEstimate(flops=2 * T * D * sum(nhs) * HEAD, bytes_accessed=D * sum(nhs) * HEAD * 4, transcendentals=0),
         name="dw_proj",
-    )(scal, a, *gs)
-    return [o.reshape(D, nh, HEAD) for o, nh in zip(outs, nhs)]
-
-
-def dwo_kernel(sc_ref, c0_ref, c1_ref, g_ref, out_ref, t_ref):
-    core = sc_ref[1]
-    n = c0_ref.shape[1]
-
+    )(scal, a, *gs, *halves)
+    return [o.reshape(D, nh, HEAD) for o, nh in zip(outs, nhs)] + [outs[3]]
+
+
+def dwo_kernel(c_ref, g_ref, out_ref, t_ref):
     @pl.when(pl.program_id(0) == 0)
     def _():
-        t_ref[pl.ds(pl.multiple_of(core * n, n), n), :] = c0_ref[...].T
-        t_ref[pl.ds(pl.multiple_of((1 - core) * n, n), n), :] = c1_ref[...].T
+        t_ref[...] = c_ref[...].T
 
     out_ref[...] = dotf(t_ref[...], g_ref[...], NN)
 
 
-def dwo_proj(scal, c0, c1, go, db):
+def dwo_proj(ctx, go, db):
     T, D = go.shape
-    n = c0.shape[1]
+    n = ctx.shape[1]
     return pl.pallas_call(
         dwo_kernel,
-        grid_spec=pltpu.PrefetchScalarGridSpec(
-            num_scalar_prefetch=1,
-            grid=(D // db,),
-            in_specs=[pl.BlockSpec((T, n), lambda i, s: (0, 0), pipeline_mode=pl.Buffered(1))] * 2
-            + [pl.BlockSpec((T, db), lambda i, s: (0, i))],
-            out_specs=pl.BlockSpec((2 * n, db), lambda i, s: (0, i)),
-            scratch_shapes=[pltpu.VMEM((2 * n, T), BF16)],
-        ),
-        out_shape=jax.ShapeDtypeStruct((2 * n, D), F32),
+        grid=(D // db,),
+        in_specs=[pl.BlockSpec((T, n), lambda i: (0, 0), pipeline_mode=pl.Buffered(1)), pl.BlockSpec((T, db), lambda i: (0, i))],
+        out_specs=pl.BlockSpec((n, db), lambda i: (0, i)),
+        scratch_shapes=[pltpu.VMEM((n, T), BF16)],
+        out_shape=jax.ShapeDtypeStruct((n, D), F32),
         compiler_params=pltpu.CompilerParams(dimension_semantics=("arbitrary",), vmem_limit_bytes=VMEM_LIMIT),
-        cost_estimate=pl.CostEstimate(flops=4 * T * D * n, bytes_accessed=2 * n * D * 4, transcendentals=0),
+        cost_estimate=pl.CostEstimate(flops=2 * T * D * n, bytes_accessed=n * D * 4, transcendentals=0),
         name="dwo_proj",
-    )(scal, c0, c1, go)
+    )(ctx, go)
 
 
 RB = 64
@@ -580,13 +586,14 @@
             return [r1, r2, r3], [tp * n, (1 - tp) * n, 2 * n]
 
         a_loc = a_call(hidden, g_pre)
-        a_x, a_off = two_way(a_loc, 176)
+        a_x, a_off = two_way(a_loc, 160)
         a_p = to_core(a_loc)
         a_xp = [to_core(r) for r in a_x]
         wo2 = w_o.reshape(-1, D)
         N = (HL + 2 * KL) * HEAD
         w_own = w_layout(core, w_q, w_k, w_v, 512)
-        w_oth = w_layout(1 - core, w_q, w_k, w_v, 512)
+        w_oth = w_layout(1 - core, w_q, w_k, w_v, 512, 0, 4)
+        w_oth = w_layout(1 - core, w_q, w_k, w_v, 512, 4, 5, w_oth)
         qkv_args = (w_own, "qkv", (cos, sin), 2, [core, 1 - core], tokens, 0, N)
         bufs = gather_matmul(xi, core, [(0, 0), (1, 0)], [a_loc, a_p], *qkv_args)
         places = [(0, o) for o in a_off] + [(1, o) for o in a_off]
@@ -596,14 +603,13 @@
 
         ctx, lse = attn_fwd(qkv, KL, HL)
         ctx_pr = to_core(lax.dynamic_slice_in_dim(ctx, (me ^ 1) * tokens, tokens, 0))
-        sizes = (128, 192, 128, 64)
+        sizes = (128, 128, 128, 128)
         starts = [sum(sizes[:c]) for c in range(len(sizes))]
         o_parts, o_peers = [], []
         for c, M in enumerate(sizes):
             op = o_rows(base, ctx, ctx_pr, wo2, starts[c], M, 1536)
             o_parts.append(op)
             o_peers.append(to_tp(op))
-        ctx_p = to_core(ctx)
 
         y_blk, gos, dgp = None, [], []
         for c in range(len(sizes)):
@@ -626,14 +632,17 @@
         dctx = dctx.reshape(T, HN)
         go_all = go_all.reshape(T, D)
 
+        dwo_own = dwo_proj(ctx, go_all, 512)
+        dwo_peer = to_core(dwo_own)
         dqkv = attn_bwd(qkv, KL, HL, dctx, ctx, lse, cos, sin)
         dqkv_pr = [to_core(lax.dynamic_slice_in_dim(g, (me ^ 1) * tokens, tokens, 0)) for g in dqkv]
         dqkv_p = [to_core(g) for g in dqkv]
         ga_part = ga_rows(base, dqkv, dqkv_pr, (w_own, w_oth), tokens, 512)
         ga_peer = to_tp(ga_part)
 
-        dwo = dwo_proj(base, ctx, ctx_p, go_all, 512).reshape(w_o.shape)
-        dwq, dwk, dwv = dw_proj(base, a_all, [g for pair in zip(dqkv, dqkv_p) for g in pair], 256)
+        pairs = [g for pair in zip(dqkv, dqkv_p) for g in pair]
+        dwq, dwk, dwv, dwo = dw_proj(base, a_all, pairs, (dwo_own, dwo_peer), 256)
+        dwo = dwo.reshape(w_o.shape)
 
         grad_h, dgr = norm_call(pre_kernel, ga_part, ga_peer, hidden, d_out, g_pre, 0, None, False)
         dg = jnp.stack([jnp.sum(dgr, axis=0), jnp.sum(sum(dgp), axis=0)])

time: 853 us -> 864 us (1.013)
  waiting for transfers between devices: 264 us -> 299 us
  Pallas kernels: 528 us -> 505 us
    ppermute x7, waiting for transfers between devices: 109 us -> 141 us  [to_x(): return lax.ppermute(v, 'cp', x_perm)]
    pallas_call x1, Pallas kernels: 50.1 us -> 26.5 us  [dwo_proj(): pl.pallas_call(dwo_kernel, grid=(D // db,), in_specs=[pl.BlockSpec((T, n)...]
    pallas_call x2 -> x3, Pallas kernels: 41.2 us -> 41.9 us  [w_layout(): pl.pallas_call(w_kernel, grid_spec=pltpu.PrefetchScalarGridSpec(num_scala...]
  transfers between devices with their start and end apart: 34 -> 34, of which waited for: 9 -> 13; matrix products, arithmetic and copies ran while one was open for 2% -> 2% of each run, Pallas kernels for 38% -> 32%
where the time goes in v7:
time: 864 us; the launch traced here: 854 us
  Pallas kernels  505 us (58%)
  waiting for transfers between devices  299 us (35%)
  local copies, waits for them, and re-layouts  20.6 us (2%)
  starting transfers between devices  20.4 us (2%)
    ppermute x6, waiting for transfers between devices, to_tp(): return lax.ppermute(v, 'tp', tp_perm)  156 us
    ppermute x7, waiting for transfers between devices, to_x(): return lax.ppermute(v, 'cp', x_perm)  141 us
    pallas_call x1, Pallas kernels, dw_proj(): pl.pallas_call(dw_kernel, grid_spec=pltpu.PrefetchScalarGridSpec(num_scal...  103 us
    pallas_call x5, Pallas kernels, gather_matmul(): pl.pallas_call(functools.partial(gmm_kernel, layout=layout, mode=mode, R=...  101 us
    pallas_call x1, Pallas kernels, attn_bwd(): pl.pallas_call(functools.partial(attn_bwd_kernel, k1=scale / SOFT_CAP, k2...  83.5 us
    pallas_call x3, Pallas kernels, w_layout(): pl.pallas_call(w_kernel, grid_spec=pltpu.PrefetchScalarGridSpec(num_scala...  41.9 us
    pallas_call x1, Pallas kernels, attn_fwd(): pl.pallas_call(functools.partial(attn_fwd_kernel, k1=scale / SOFT_CAP, k2...  41.4 us
    pallas_call x4, Pallas kernels, o_rows(): pl.pallas_call(functools.partial(orow_kernel, r0=r0), grid_spec=pltpu.Pre...  40.4 us
  transfers between devices with their start and end apart: 34, of which 13 were waited for; matrix products, arithmetic and copies ran while one was open for 2% of the time, Pallas kernels for 32%

profile of v7, /device:TPU:0, one launch (start us, length us, event | category | flops | bytes accessed | tf_op | source)
XLA Modules:
  0.0 854.1 jit_solution(3573206761138640266)
XLA Ops:
  2.0 7.8 a_norm.1.refs_0_
  10.6 1.5 constant_dynamic-slice_fusion.4
  12.1 2.5 collective-permute-start
  14.6 1.6 slice.12
  16.2 31.6 %collective-permute-done.refs_0_ = bf16[160,4608]{1,0:T(8,128)(2,1)} collective-permute-done((bf16[160,4608]{1,0:T(8,128)(2,1)S(1)}, bf16[160,4608]{1,0:T(8,128)(2,1)}, u32[]{:S(2)}, u32[]{:S(2)}) %collective-permute-start) | collective-permute-done | bytes 1474592 | tf_op jit(solution)/shard_map/ppermute | solution.py:566
  47.9 2.0 collective-permute-start.1
  49.9 3.7 fusion
  53.6 1.9 pad_maximum_fusion
  56.8 20.6 %shard_map.143.refs_2_.refs_6_.w0_ref = bf16[4608,2048]{1,0:T(8,128)(2,1)} custom-call(s32[1]{0:T(128)} %bitcast.1.c_ref, bf16[4608,16,128]{2,1,0:T(8,128)(2,1)} %wq_ref.5, bf16[4608,8,128]{2,1,0:T(8,128)(2,1)} %wk_ref.5, bf16[4608,8,128]{2,1,0:T(8,128)(2,1)} %wv_ref.5), custom_call_target="tpu_custom_call" | custom-call | flops 4718592000 | bytes 47185920 | tf_op jit(solution)/shard_map/pallas_call | solution.py:339
  77.4 8.2 collective-permute-done.2.refs_2_
  86.1 29.9 %shard_map.144 = (bf16[4,512,2048]{2,1,0:T(8,128)(2,1)}, bf16[4,512,4608]{2,1,0:T(8,128)(2,1)}) custom-call(s32[6]{0:T(128)} %stack.86.sc_ref, bf16[512,4608]{1,0:T(8,128)(2,1)} %a_norm.1.refs_0_, bf16[512,4608]{1,0:T(8,128)(2,1)} %collective-permute-done.6.refs_1_, bf16[4608,2048]{1,0:T(8,128)(2,1)} %shard_map.143.refs_2_.refs_6_.w0_ref, ...), custom_call_target="tpu_custom_call" | custom-call | flops 19327352832 | bytes 37748736 | tf_op jit(solution)/shard_map/pallas_call | solution.py:298
  117.2 29.9 %shard_map.145 = (bf16[4,512,2048]{2,1,0:T(8,128)(2,1)}, bf16[4,512,4608]{2,1,0:T(8,128)(2,1)}) custom-call(s32[10]{0:T(128)} %stack.85.sc_ref, bf16[160,4608]{1,0:T(8,128)(2,1)} %collective-permute-done.refs_0_, bf16[160,4608]{1,0:T(8,128)(2,1)} %collective-permute-done.1.refs_1_, ...), custom_call_target="tpu_custom_call", output_to_operand_aliasing={{0}: (10, {}), {1}: (11, {})} | custom-call | flops 19327352832 | bytes 37748736 | tf_op jit(solution)/shard_map/pallas_call | solution.py:298
  147.2 41.4 %attn_fwd.1 = (bf16[2048,1024]{1,0:T(8,128)(2,1)}, f32[4,2,2048]{2,1,0:T(2,128)}) custom-call(bf16[2048,2048]{1,0:T(8,128)(2,1)} %bitcast.39, bf16[2048,2048]{1,0:T(8,128)(2,1)} %bitcast.40, bf16[2048,2048]{1,0:T(8,128)(2,1)} %bitcast.41), custom_call_target="tpu_custom_call" | custom-call | flops 17179869184 | bytes 16777216 | tf_op jit(solution)/shard_map/attn_fwd/pallas_call | solution.py:91
  190.5 2.1 collective-permute-done.7.c1_ref
  193.6 10.1 %shard_map.147.p_ref = bf16[128,4608]{1,0:T(8,128)(2,1)} custom-call(s32[4]{0:T(128)} %pad_add_fusion.sc_ref, bf16[2048,1024]{1,0:T(8,128)(2,1)} %get-tuple-element.48.c0_ref.ctx_ref.c_ref, bf16[512,1024]{1,0:T(8,128)(2,1)} %copy-done, bf16[2048,4608]{1,0:T(8,128)(2,1)} %bitcast.21), custom_call_target="tpu_custom_call" | custom-call | flops 2415919104 | bytes 18874368 | tf_op jit(solution)/shard_map/pallas_call | solution.py:367
  203.6 1.8 collective-permute-start.9
  205.4 10.1 %shard_map.149.p_ref = bf16[128,4608]{1,0:T(8,128)(2,1)} custom-call(s32[4]{0:T(128)} %pad_add_fusion.sc_ref, bf16[2048,1024]{1,0:T(8,128)(2,1)} %get-tuple-element.48.c0_ref.ctx_ref.c_ref, bf16[512,1024]{1,0:T(8,128)(2,1)} %copy-done, bf16[2048,4608]{1,0:T(8,128)(2,1)} %bitcast.22), custom_call_target="tpu_custom_call" | custom-call | flops 2415919104 | bytes 18874368 | tf_op jit(solution)/shard_map/pallas_call | solution.py:367
  215.8 10.1 %shard_map.148.p_ref = bf16[128,4608]{1,0:T(8,128)(2,1)} custom-call(s32[4]{0:T(128)} %pad_add_fusion.sc_ref, bf16[2048,1024]{1,0:T(8,128)(2,1)} %get-tuple-element.48.c0_ref.ctx_ref.c_ref, bf16[512,1024]{1,0:T(8,128)(2,1)} %copy-done, bf16[2048,4608]{1,0:T(8,128)(2,1)} %bitcast.23), custom_call_target="tpu_custom_call" | custom-call | flops 2415919104 | bytes 18874368 | tf_op jit(solution)/shard_map/pallas_call | solution.py:367
  225.9 1.8 collective-permute-start.10
  227.6 10.1 %shard_map.146.p_ref = bf16[128,4608]{1,0:T(8,128)(2,1)} custom-call(s32[4]{0:T(128)} %pad_add_fusion.sc_ref, bf16[2048,1024]{1,0:T(8,128)(2,1)} %get-tuple-element.48.c0_ref.ctx_ref.c_ref, bf16[512,1024]{1,0:T(8,128)(2,1)} %copy-done, bf16[2048,4608]{1,0:T(8,128)(2,1)} %bitcast.24), custom_call_target="tpu_custom_call" | custom-call | flops 2415919104 | bytes 18874368 | tf_op jit(solution)/shard_map/pallas_call | solution.py:367
  238.6 19.5 %collective-permute-done.11.r_ref = bf16[128,4608]{1,0:T(8,128)(2,1)} collective-permute-done((bf16[128,4608]{1,0:T(8,128)(2,1)}, bf16[128,4608]{1,0:T(8,128)(2,1)}, u32[]{:S(2)}, u32[]{:S(2)}) %collective-permute-start.11) | collective-permute-done | bytes 1179680 | tf_op jit(solution)/shard_map/ppermute | solution.py:569
  258.1 4.9 shard_map.150
  263.0 20.3 %collective-permute-done.10.r_ref = bf16[128,4608]{1,0:T(8,128)(2,1)} collective-permute-done((bf16[128,4608]{1,0:T(8,128)(2,1)}, bf16[128,4608]{1,0:T(8,128)(2,1)}, u32[]{:S(2)}, u32[]{:S(2)}) %collective-permute-start.10) | collective-permute-done | bytes 1179680 | tf_op jit(solution)/shard_map/ppermute | solution.py:569
  283.4 5.0 shard_map.151
  289.4 5.0 shard_map.152
  294.4 13.3 %collective-permute-done.8.r_ref = bf16[128,4608]{1,0:T(8,128)(2,1)S(1)} collective-permute-done((bf16[128,4608]{1,0:T(8,128)(2,1)}, bf16[128,4608]{1,0:T(8,128)(2,1)S(1)}, u32[]{:S(2)}, u32[]{:S(2)}) %collective-permute-start.8) | collective-permute-done | bytes 1179680 | tf_op jit(solution)/shard_map/ppermute | solution.py:569
  308.7 5.0 shard_map.153
  313.7 1.8 collective-permute-start.13
  315.7 1.7 collective-permute-start.16
  317.8 25.0 %collective-permute-done.13.refs_2_ = bf16[128,4608]{1,0:T(8,128)(2,1)S(1)} collective-permute-done((bf16[128,4608]{1,0:T(8,128)(2,1)}, bf16[128,4608]{1,0:T(8,128)(2,1)S(1)}, u32[]{:S(2)}, u32[]{:S(2)}) %collective-permute-start.13) | collective-permute-done | bytes 1179680 | tf_op jit(solution)/shard_map/ppermute | solution.py:566
  343.3 24.8 %collective-permute-done.17.refs_2_ = bf16[128,4608]{1,0:T(8,128)(2,1)S(1)} collective-permute-done((bf16[128,4608]{1,0:T(8,128)(2,1)}, bf16[128,4608]{1,0:T(8,128)(2,1)S(1)}, u32[]{:S(2)}, u32[]{:S(2)}) %collective-permute-start.17) | collective-permute-done | bytes 1179680 | tf_op jit(solution)/shard_map/ppermute | solution.py:566
  368.0 25.4 %collective-permute-done.16.refs_1_ = bf16[128,4608]{1,0:T(8,128)(2,1)} collective-permute-done((bf16[128,4608]{1,0:T(8,128)(2,1)}, bf16[128,4608]{1,0:T(8,128)(2,1)}, u32[]{:S(2)}, u32[]{:S(2)}) %collective-permute-start.16) | collective-permute-done | bytes 1179680 | tf_op jit(solution)/shard_map/ppermute | solution.py:566
  393.4 23.6 %collective-permute-done.15.refs_0_ = bf16[128,4608]{1,0:T(8,128)(2,1)} collective-permute-done((bf16[128,4608]{1,0:T(8,128)(2,1)}, bf16[128,4608]{1,0:T(8,128)(2,1)}, u32[]{:S(2)}, u32[]{:S(2)}) %collective-permute-start.15) | collective-permute-done | bytes 1179680 | tf_op jit(solution)/shard_map/ppermute | solution.py:566
  419.5 14.8 %shard_map.154 = (bf16[4,512,1024]{2,1,0:T(8,128)(2,1)}, bf16[4,512,4608]{2,1,0:T(8,128)(2,1)}) custom-call(s32[10]{0:T(128)} %stack.91.sc_ref, bf16[128,4608]{1,0:T(8,128)(2,1)} %get-tuple-element.54.refs_0_, bf16[128,4608]{1,0:T(8,128)(2,1)} %get-tuple-element.55.refs_1_, bf16[128,4608]{1,0:T(8,128)(2,1)} %get-tuple-element.56.refs_2_, ...), custom_call_target="tpu_custom_call" | custom-call | flops 7247757312 | bytes 23592960 | tf_op jit(solution)/shard_map/pallas_call | solution.py:298
  434.4 14.7 %shard_map.155 = (bf16[4,512,1024]{2,1,0:T(8,128)(2,1)}, bf16[4,512,4608]{2,1,0:T(8,128)(2,1)}) custom-call(s32[10]{0:T(128)} %stack.90.sc_ref, bf16[128,4608]{1,0:T(8,128)(2,1)} %collective-permute-done.15.refs_0_, bf16[128,4608]{1,0:T(8,128)(2,1)} %collective-permute-done.16.refs_1_, ...), custom_call_target="tpu_custom_call", output_to_operand_aliasing={{0}: (8, {}), {1}: (9, {})} | custom-call | flops 7247757312 | bytes 23592960 | tf_op jit(solution)/shard_map/pallas_call | solution.py:298
  449.1 12.1 %shard_map.156 = (bf16[4,512,1024]{2,1,0:T(8,128)(2,1)}, bf16[4,512,4608]{2,1,0:T(8,128)(2,1)}) custom-call(s32[10]{0:T(128)} %stack.89.sc_ref, bf16[128,4608]{1,0:T(8,128)(2,1)} %get-tuple-element.53.refs_0_, bf16[128,4608]{1,0:T(8,128)(2,1)} %collective-permute-done.12.refs_1_, ...), custom_call_target="tpu_custom_call", output_to_operand_aliasing={{0}: (6, {}), {1}: (7, {})} | custom-call | flops 4831838208 | bytes 18874368 | tf_op jit(solution)/shard_map/pallas_call | solution.py:298
  461.2 26.5 %dwo_proj.1.h0_ref = f32[1024,4608]{1,0:T(8,128)} custom-call(bf16[2048,1024]{1,0:T(8,128)(2,1)} %get-tuple-element.48.c0_ref.ctx_ref.c_ref, bf16[2048,4608]{1,0:T(8,128)(2,1)} %bitcast.28), custom_call_target="tpu_custom_call" | custom-call | flops 19327352832 | bytes 18874368 | tf_op jit(solution)/shard_map/dwo_proj/pallas_call | solution.py:465
  488.2 83.5 %attn_bwd.1 = (bf16[2048,1024]{1,0:T(8,128)(2,1)}, bf16[2048,512]{1,0:T(8,128)(2,1)}, bf16[2048,512]{1,0:T(8,128)(2,1)}) custom-call(bf16[2048,2048]{1,0:T(8,128)(2,1)} %bitcast.42, bf16[2048,2048]{1,0:T(8,128)(2,1)} %bitcast.43, bf16[2048,2048]{1,0:T(8,128)(2,1)} %bitcast.44, bf16[2048,1024]{1,0:T(8,128)(2,1)} %bitcast.29, ...), custom_call_target="tpu_custom_call" | custom-call | flops 21474836480 | bytes 25165824 | tf_op jit(solution)/shard_map/attn_bwd/pallas_call | solution.py:194
  575.8 9.1 %shard_map.157.rest_0_ = bf16[4608,2048]{1,0:T(8,128)(2,1)} custom-call(s32[1]{0:T(128)} %bitcast.5.c_ref, bf16[4608,16,128]{2,1,0:T(8,128)(2,1)} %wq_ref.5, bf16[4608,8,128]{2,1,0:T(8,128)(2,1)} %wk_ref.5, bf16[4608,8,128]{2,1,0:T(8,128)(2,1)} %wv_ref.5), custom_call_target="tpu_custom_call" | custom-call | flops 2097152000 | bytes 20971520 | tf_op jit(solution)/shard_map/pallas_call | solution.py:339
  584.9 12.3 %shard_map.158.w1_ref = bf16[4608,2048]{1,0:T(8,128)(2,1)} custom-call(s32[1]{0:T(128)} %bitcast.5.c_ref, bf16[4608,16,128]{2,1,0:T(8,128)(2,1)} %wq_ref.5, bf16[4608,8,128]{2,1,0:T(8,128)(2,1)} %wk_ref.5, bf16[4608,8,128]{2,1,0:T(8,128)(2,1)} %wv_ref.5, bf16[4608,2048]{1,0:T(8,128)(2,1)} %shard_map.157.rest_0_), custom_call_target="tpu_custom_call", output_to_operand_aliasing={{}: (4, {})} | custom-call | flops 2621440000 | bytes 26214400 | tf_op jit(solution)/shard_map/pallas_call | solution.py:339
  597.2 26.6 %shard_map.159.p_ref = bf16[512,4608]{1,0:T(8,128)(2,1)} custom-call(s32[4]{0:T(128)} %pad_add_fusion.sc_ref, bf16[2048,1024]{1,0:T(8,128)(2,1)} %get-tuple-element.63.q0, bf16[2048,512]{1,0:T(8,128)(2,1)} %get-tuple-element.64.k0, bf16[2048,512]{1,0:T(8,128)(2,1)} %get-tuple-element.65.v0, bf16[512,1024]{1,0:T(8,128)(2,1)} %collective-permute-done.24.q1, ...), custom_call_target="tpu_custom_call" | custom-call | flops 19327352832 | bytes 37748736 | tf_op jit(solution)/shard_map/pallas_call | solution.py:399
  623.8 1.7 collective-permute-start.27
  625.8 102.5 %collective-permute-done.27.r_ref = bf16[512,4608]{1,0:T(8,128)(2,1)} collective-permute-done((bf16[512,4608]{1,0:T(8,128)(2,1)}, bf16[512,4608]{1,0:T(8,128)(2,1)}, u32[]{:S(2)}, u32[]{:S(2)}) %collective-permute-start.27) | collective-permute-done | bytes 4718624 | tf_op jit(solution)/shard_map/ppermute | solution.py:569
  728.3 12.9 %shard_map.160 = (bf16[512,4608]{1,0:T(8,128)(2,1)}, f32[8,4608]{1,0:T(8,128)}) custom-call(bf16[512,4608]{1,0:T(8,128)(2,1)} %shard_map.159.p_ref, bf16[512,4608]{1,0:T(8,128)(2,1)} %collective-permute-done.27.r_ref, bf16[512,4608]{1,0:T(8,128)(2,1)} %h_ref.11, bf16[512,4608]{1,0:T(8,128)(2,1)} %dy_ref.9, f32[1,4608]{1,0:T(1,128)} %reshape.74.g_ref), custom_call_target="tpu_custom_call" | custom-call | flops 4718592000 | bytes 28311552 | tf_op jit(solution)/shard_map/pallas_call | solution.py:532
  743.4 1.8 collective-permute-start.29
  745.2 2.2 collective-permute-done.29
  748.2 1.4 copy-done.11
  750.9 103.0 %dw_proj.1 = (f32[73728,128]{1,0:T(8,128)}, f32[36864,128]{1,0:T(8,128)}, f32[36864,128]{1,0:T(8,128)}, f32[2048,4608]{1,0:T(8,128)}) custom-call(s32[4]{0:T(128)} %pad_add_fusion.sc_ref, bf16[2048,4608]{1,0:T(8,128)(2,1)} %bitcast.38, bf16[2048,1024]{1,0:T(8,128)(2,1)} %get-tuple-element.63.q0, bf16[2048,1024]{1,0:T(8,128)(2,1)} %collective-permute-done.30.q1, ...), custom_call_target="tpu_custom_call" | custom-call | flops 77309411328 | bytes 75497472 | tf_op jit(solution)/shard_map/dw_proj/pallas_call | solution.py:435
  (100 shorter events, 24.0 us)
Async XLA Ops:
  9.8 76.3 %collective-permute-start.6 = (bf16[512,4608]{1,0:T(8,128)(2,1)}, bf16[512,4608]{1,0:T(8,128)(2,1)}, u32[]{:S(2)}, u32[]{:S(2)}) collective-permute-start(bf16[512,4608]{1,0:T(8,128)(2,1)} %a_norm.1.refs_0_), channel_id=1, source_target_pairs={{0,1},{1,0},{2,3},{3,2},{4,5},{5,4},{6,7},{7,6}} | collective-permute-start | bytes 14155784 | tf_op jit(solution)/shard_map/ppermute | solution.py:563
  12.1 35.7 %collective-permute-start = (bf16[160,4608]{1,0:T(8,128)(2,1)S(1)}, bf16[160,4608]{1,0:T(8,128)(2,1)}, u32[]{:S(2)}, u32[]{:S(2)}) collective-permute-start(bf16[160,4608]{1,0:T(8,128)(2,1)S(1)} %constant_dynamic-slice_fusion.4), channel_id=1, source_target_pairs={{0,2},{2,0},{1,3},{3,1},{4,6},{6,4},{5,7},{7,5}} | collective-permute-start | bytes 4423688 | tf_op jit(solution)/shard_map/ppermute | solution.py:566
  16.2 69.4 %collective-permute-start.2 = (bf16[192,4608]{1,0:T(8,128)(2,1)S(1)}, bf16[192,4608]{1,0:T(8,128)(2,1)}, u32[]{:S(2)}, u32[]{:S(2)}) collective-permute-start(bf16[192,4608]{1,0:T(8,128)(2,1)S(1)} %slice.12), channel_id=1, source_target_pairs={{0,2},{2,0},{1,3},{3,1},{4,6},{6,4},{5,7},{7,5}} | collective-permute-start | bytes 5308424 | tf_op jit(solution)/shard_map/ppermute | solution.py:566
  47.9 37.7 %collective-permute-start.1 = (bf16[160,4608]{1,0:T(8,128)(2,1)}, bf16[160,4608]{1,0:T(8,128)(2,1)}, u32[]{:S(2)}, u32[]{:S(2)}) collective-permute-start(bf16[160,4608]{1,0:T(8,128)(2,1)} %collective-permute-done.refs_0_), channel_id=1, source_target_pairs={{0,4},{4,0},{1,5},{5,1},{2,6},{6,2},{3,7},{7,3}} | collective-permute-start | bytes 4423688 | tf_op jit(solution)/shard_map/ppermute | solution.py:569
  77.4 38.6 %collective-permute-start.3 = (bf16[160,4608]{1,0:T(8,128)(2,1)}, bf16[160,4608]{1,0:T(8,128)(2,1)}, u32[]{:S(2)}, u32[]{:S(2)}) collective-permute-start(bf16[160,4608]{1,0:T(8,128)(2,1)} %collective-permute-done.refs_0_), channel_id=1, source_target_pairs={{0,1},{1,0},{2,3},{3,2},{4,5},{5,4},{6,7},{7,6}} | collective-permute-start | bytes 4423688 | tf_op jit(solution)/shard_map/ppermute | solution.py:563
  85.6 30.4 %collective-permute-start.5 = (bf16[192,4608]{1,0:T(8,128)(2,1)}, bf16[192,4608]{1,0:T(8,128)(2,1)S(1)}, u32[]{:S(2)}, u32[]{:S(2)}) collective-permute-start(bf16[192,4608]{1,0:T(8,128)(2,1)} %collective-permute-done.2.refs_2_), channel_id=1, source_target_pairs={{0,1},{1,0},{2,3},{3,2},{4,5},{5,4},{6,7},{7,6}} | collective-permute-start | bytes 5308424 | tf_op jit(solution)/shard_map/ppermute | solution.py:563
  85.6 30.5 %collective-permute-start.4 = (bf16[160,4608]{1,0:T(8,128)(2,1)}, bf16[160,4608]{1,0:T(8,128)(2,1)}, u32[]{:S(2)}, u32[]{:S(2)}) collective-permute-start(bf16[160,4608]{1,0:T(8,128)(2,1)} %collective-permute-done.1.refs_1_), channel_id=1, source_target_pairs={{0,1},{1,0},{2,3},{3,2},{4,5},{5,4},{6,7},{7,6}} | collective-permute-start | bytes 4423688 | tf_op jit(solution)/shard_map/ppermute | solution.py:563
  116.0 1.2 copy-start.13
  189.9 2.7 collective-permute-start.7
  203.6 84.7 %collective-permute-start.9 = (bf16[128,4608]{1,0:T(8,128)(2,1)}, bf16[128,4608]{1,0:T(8,128)(2,1)S(1)}, u32[]{:S(2)}, u32[]{:S(2)}) collective-permute-start(bf16[128,4608]{1,0:T(8,128)(2,1)} %shard_map.147.p_ref), channel_id=1, source_target_pairs={{0,4},{4,0},{1,5},{5,1},{2,6},{6,2},{3,7},{7,3}} | collective-permute-start | bytes 3538952 | tf_op jit(solution)/shard_map/ppermute | solution.py:569
  215.5 42.6 %collective-permute-start.11 = (bf16[128,4608]{1,0:T(8,128)(2,1)}, bf16[128,4608]{1,0:T(8,128)(2,1)}, u32[]{:S(2)}, u32[]{:S(2)}) collective-permute-start(bf16[128,4608]{1,0:T(8,128)(2,1)} %shard_map.149.p_ref), channel_id=1, source_target_pairs={{0,4},{4,0},{1,5},{5,1},{2,6},{6,2},{3,7},{7,3}} | collective-permute-start | bytes 3538952 | tf_op jit(solution)/shard_map/ppermute | solution.py:569
  225.9 12.1 %copy-start.10 = (f32[4608]{0:T(1024)S(1)}, f32[4608]{0:T(1024)}, u32[]{:S(2)}) copy-start(f32[4608]{0:T(1024)} %param.14) | copy-start | bytes 55300
  225.9 57.5 %collective-permute-start.10 = (bf16[128,4608]{1,0:T(8,128)(2,1)}, bf16[128,4608]{1,0:T(8,128)(2,1)}, u32[]{:S(2)}, u32[]{:S(2)}) collective-permute-start(bf16[128,4608]{1,0:T(8,128)(2,1)} %shard_map.148.p_ref), channel_id=1, source_target_pairs={{0,4},{4,0},{1,5},{5,1},{2,6},{6,2},{3,7},{7,3}} | collective-permute-start | bytes 3538952 | tf_op jit(solution)/shard_map/ppermute | solution.py:569
  237.7 70.0 %collective-permute-start.8 = (bf16[128,4608]{1,0:T(8,128)(2,1)}, bf16[128,4608]{1,0:T(8,128)(2,1)S(1)}, u32[]{:S(2)}, u32[]{:S(2)}) collective-permute-start(bf16[128,4608]{1,0:T(8,128)(2,1)} %shard_map.146.p_ref), channel_id=1, source_target_pairs={{0,4},{4,0},{1,5},{5,1},{2,6},{6,2},{3,7},{7,3}} | collective-permute-start | bytes 3538952 | tf_op jit(solution)/shard_map/ppermute | solution.py:569
  288.3 1.1 copy-start.3
  307.7 1.0 copy-start.4
  313.7 29.1 %collective-permute-start.13 = (bf16[128,4608]{1,0:T(8,128)(2,1)}, bf16[128,4608]{1,0:T(8,128)(2,1)S(1)}, u32[]{:S(2)}, u32[]{:S(2)}) collective-permute-start(bf16[128,4608]{1,0:T(8,128)(2,1)} %get-tuple-element.53.refs_0_), channel_id=1, source_target_pairs={{0,2},{2,0},{1,3},{3,1},{4,6},{6,4},{5,7},{7,5}} | collective-permute-start | bytes 3538952 | tf_op jit(solution)/shard_map/ppermute | solution.py:566
  315.4 27.3 %collective-permute-start.23 = (bf16[128,4608]{1,0:T(8,128)(2,1)}, bf16[128,4608]{1,0:T(8,128)(2,1)S(1)}, u32[]{:S(2)}, u32[]{:S(2)}) collective-permute-start(bf16[128,4608]{1,0:T(8,128)(2,1)} %get-tuple-element.56.refs_2_), channel_id=1, source_target_pairs={{0,1},{1,0},{2,3},{3,2},{4,5},{5,4},{6,7},{7,6}} | collective-permute-start | bytes 3538952 | tf_op jit(solution)/shard_map/ppermute | solution.py:563
  315.4 52.6 %collective-permute-start.17 = (bf16[128,4608]{1,0:T(8,128)(2,1)}, bf16[128,4608]{1,0:T(8,128)(2,1)S(1)}, u32[]{:S(2)}, u32[]{:S(2)}) collective-permute-start(bf16[128,4608]{1,0:T(8,128)(2,1)} %get-tuple-element.56.refs_2_), channel_id=1, source_target_pairs={{0,2},{2,0},{1,3},{3,1},{4,6},{6,4},{5,7},{7,5}} | collective-permute-start | bytes 3538952 | tf_op jit(solution)/shard_map/ppermute | solution.py:566
  315.7 77.7 %collective-permute-start.16 = (bf16[128,4608]{1,0:T(8,128)(2,1)}, bf16[128,4608]{1,0:T(8,128)(2,1)}, u32[]{:S(2)}, u32[]{:S(2)}) collective-permute-start(bf16[128,4608]{1,0:T(8,128)(2,1)} %get-tuple-element.55.refs_1_), channel_id=1, source_target_pairs={{0,2},{2,0},{1,3},{3,1},{4,6},{6,4},{5,7},{7,5}} | collective-permute-start | bytes 3538952 | tf_op jit(solution)/shard_map/ppermute | solution.py:566
  317.5 99.6 %collective-permute-start.15 = (bf16[128,4608]{1,0:T(8,128)(2,1)}, bf16[128,4608]{1,0:T(8,128)(2,1)}, u32[]{:S(2)}, u32[]{:S(2)}) collective-permute-start(bf16[128,4608]{1,0:T(8,128)(2,1)} %get-tuple-element.54.refs_0_), channel_id=1, source_target_pairs={{0,2},{2,0},{1,3},{3,1},{4,6},{6,4},{5,7},{7,5}} | collective-permute-start | bytes 3538952 | tf_op jit(solution)/shard_map/ppermute | solution.py:566
  342.8 91.6 %copy-start.1 = (bf16[128,4608]{1,0:T(8,128)(2,1)}, bf16[128,4608]{1,0:T(8,128)(2,1)S(1)}, u32[]{:S(2)}) copy-start(bf16[128,4608]{1,0:T(8,128)(2,1)S(1)} %collective-permute-done.13.refs_2_) | copy-start | bytes 3538948
  342.8 76.2 %collective-permute-start.22 = (bf16[128,4608]{1,0:T(8,128)(2,1)}, bf16[128,4608]{1,0:T(8,128)(2,1)}, u32[]{:S(2)}, u32[]{:S(2)}) collective-permute-start(bf16[128,4608]{1,0:T(8,128)(2,1)} %get-tuple-element.55.refs_1_), channel_id=1, source_target_pairs={{0,1},{1,0},{2,3},{3,2},{4,5},{5,4},{6,7},{7,6}} | collective-permute-start | bytes 3538952 | tf_op jit(solution)/shard_map/ppermute | solution.py:563
  342.8 25.3 %copy-start.14 = (bf16[128,4608]{1,0:T(8,128)(2,1)}, bf16[128,4608]{1,0:T(8,128)(2,1)S(1)}, u32[]{:S(2)}) copy-start(bf16[128,4608]{1,0:T(8,128)(2,1)S(1)} %collective-permute-done.23.refs_5_) | copy-start | bytes 3538948
  342.8 76.7 %collective-permute-start.21 = (bf16[128,4608]{1,0:T(8,128)(2,1)}, bf16[128,4608]{1,0:T(8,128)(2,1)}, u32[]{:S(2)}, u32[]{:S(2)}) collective-permute-start(bf16[128,4608]{1,0:T(8,128)(2,1)} %get-tuple-element.54.refs_0_), channel_id=1, source_target_pairs={{0,1},{1,0},{2,3},{3,2},{4,5},{5,4},{6,7},{7,6}} | collective-permute-start | bytes 3538952 | tf_op jit(solution)/shard_map/ppermute | solution.py:563
  368.0 66.3 %copy-start.2 = (bf16[128,4608]{1,0:T(8,128)(2,1)}, bf16[128,4608]{1,0:T(8,128)(2,1)S(1)}, u32[]{:S(2)}) copy-start(bf16[128,4608]{1,0:T(8,128)(2,1)S(1)} %collective-permute-done.17.refs_2_) | copy-start | bytes 3538948
  368.0 66.3 %collective-permute-start.20 = (bf16[128,4608]{1,0:T(8,128)(2,1)S(1)}, bf16[128,4608]{1,0:T(8,128)(2,1)}, u32[]{:S(2)}, u32[]{:S(2)}) collective-permute-start(bf16[128,4608]{1,0:T(8,128)(2,1)S(1)} %collective-permute-done.17.refs_2_), channel_id=1, source_target_pairs={{0,1},{1,0},{2,3},{3,2},{4,5},{5,4},{6,7},{7,6}} | collective-permute-start | bytes 3538952 | tf_op jit(solution)/shard_map/ppermute | solution.py:563
  393.4 41.0 %collective-permute-start.19 = (bf16[128,4608]{1,0:T(8,128)(2,1)}, bf16[128,4608]{1,0:T(8,128)(2,1)}, u32[]{:S(2)}, u32[]{:S(2)}) collective-permute-start(bf16[128,4608]{1,0:T(8,128)(2,1)} %collective-permute-done.16.refs_1_), channel_id=1, source_target_pairs={{0,1},{1,0},{2,3},{3,2},{4,5},{5,4},{6,7},{7,6}} | collective-permute-start | bytes 3538952 | tf_op jit(solution)/shard_map/ppermute | solution.py:563
  417.0 17.4 %collective-permute-start.18 = (bf16[128,4608]{1,0:T(8,128)(2,1)}, bf16[128,4608]{1,0:T(8,128)(2,1)}, u32[]{:S(2)}, u32[]{:S(2)}) collective-permute-start(bf16[128,4608]{1,0:T(8,128)(2,1)} %collective-permute-done.15.refs_0_), channel_id=1, source_target_pairs={{0,1},{1,0},{2,3},{3,2},{4,5},{5,4},{6,7},{7,6}} | collective-permute-start | bytes 3538952 | tf_op jit(solution)/shard_map/ppermute | solution.py:563
  418.9 30.1 %collective-permute-start.12 = (bf16[128,4608]{1,0:T(8,128)(2,1)}, bf16[128,4608]{1,0:T(8,128)(2,1)}, u32[]{:S(2)}, u32[]{:S(2)}) collective-permute-start(bf16[128,4608]{1,0:T(8,128)(2,1)} %get-tuple-element.53.refs_0_), channel_id=1, source_target_pairs={{0,1},{1,0},{2,3},{3,2},{4,5},{5,4},{6,7},{7,6}} | collective-permute-start | bytes 3538952 | tf_op jit(solution)/shard_map/ppermute | solution.py:563
  419.5 29.6 %collective-permute-start.14 = (bf16[128,4608]{1,0:T(8,128)(2,1)S(1)}, bf16[128,4608]{1,0:T(8,128)(2,1)}, u32[]{:S(2)}, u32[]{:S(2)}) collective-permute-start(bf16[128,4608]{1,0:T(8,128)(2,1)S(1)} %collective-permute-done.13.refs_2_), channel_id=1, source_target_pairs={{0,1},{1,0},{2,3},{3,2},{4,5},{5,4},{6,7},{7,6}} | collective-permute-start | bytes 3538952 | tf_op jit(solution)/shard_map/ppermute | solution.py:563
  487.7 263.2 %collective-permute-start.33 = (f32[1024,4608]{1,0:T(8,128)}, f32[1024,4608]{1,0:T(8,128)}, u32[]{:S(2)}, u32[]{:S(2)}) collective-permute-start(f32[1024,4608]{1,0:T(8,128)} %dwo_proj.1.h0_ref), channel_id=1, source_target_pairs={{0,1},{1,0},{2,3},{3,2},{4,5},{5,4},{6,7},{7,6}} | collective-permute-start | bytes 56623112 | tf_op jit(solution)/shard_map/ppermute | solution.py:563
  573.0 24.2 %collective-permute-start.24 = (bf16[512,1024]{1,0:T(8,128)(2,1)S(1)}, bf16[512,1024]{1,0:T(8,128)(2,1)}, u32[]{:S(2)}, u32[]{:S(2)}) collective-permute-start(bf16[512,1024]{1,0:T(8,128)(2,1)S(1)} %constant_dynamic-slice_fusion.2), channel_id=1, source_target_pairs={{0,1},{1,0},{2,3},{3,2},{4,5},{5,4},{6,7},{7,6}} | collective-permute-start | bytes 3145736 | tf_op jit(solution)/shard_map/ppermute | solution.py:563
  575.3 21.9 %collective-permute-start.26 = (bf16[512,512]{1,0:T(8,128)(2,1)S(1)}, bf16[512,512]{1,0:T(8,128)(2,1)}, u32[]{:S(2)}, u32[]{:S(2)}) collective-permute-start(bf16[512,512]{1,0:T(8,128)(2,1)S(1)} %constant_dynamic-slice_fusion), channel_id=1, source_target_pairs={{0,1},{1,0},{2,3},{3,2},{4,5},{5,4},{6,7},{7,6}} | collective-permute-start | bytes 1572872 | tf_op jit(solution)/shard_map/ppermute | solution.py:563
  575.8 21.4 %collective-permute-start.25 = (bf16[512,512]{1,0:T(8,128)(2,1)S(1)}, bf16[512,512]{1,0:T(8,128)(2,1)}, u32[]{:S(2)}, u32[]{:S(2)}) collective-permute-start(bf16[512,512]{1,0:T(8,128)(2,1)S(1)} %constant_dynamic-slice_fusion.1), channel_id=1, source_target_pairs={{0,1},{1,0},{2,3},{3,2},{4,5},{5,4},{6,7},{7,6}} | collective-permute-start | bytes 1572872 | tf_op jit(solution)/shard_map/ppermute | solution.py:563
  597.2 28.5 %copy-start.5 = (f32[8,4608]{1,0:T(8,128)S(1)}, f32[8,4608]{1,0:T(8,128)}, u32[]{:S(2)}) copy-start(f32[8,4608]{1,0:T(8,128)} %get-tuple-element.68) | copy-start | bytes 442372
  597.2 28.5 %copy-start.6 = (f32[8,4608]{1,0:T(8,128)S(1)}, f32[8,4608]{1,0:T(8,128)}, u32[]{:S(2)}) copy-start(f32[8,4608]{1,0:T(8,128)} %get-tuple-element.69) | copy-start | bytes 442372
  597.2 28.5 %copy-start.7 = (f32[8,4608]{1,0:T(8,128)S(1)}, f32[8,4608]{1,0:T(8,128)}, u32[]{:S(2)}) copy-start(f32[8,4608]{1,0:T(8,128)} %get-tuple-element.70) | copy-start | bytes 442372
  597.2 28.5 %copy-start.8 = (f32[8,4608]{1,0:T(8,128)S(1)}, f32[8,4608]{1,0:T(8,128)}, u32[]{:S(2)}) copy-start(f32[8,4608]{1,0:T(8,128)} %get-tuple-element.71) | copy-start | bytes 442372
  623.8 104.5 %collective-permute-start.27 = (bf16[512,4608]{1,0:T(8,128)(2,1)}, bf16[512,4608]{1,0:T(8,128)(2,1)}, u32[]{:S(2)}, u32[]{:S(2)}) collective-permute-start(bf16[512,4608]{1,0:T(8,128)(2,1)} %shard_map.159.p_ref), channel_id=1, source_target_pairs={{0,4},{4,0},{1,5},{5,1},{2,6},{6,2},{3,7},{7,3}} | collective-permute-start | bytes 14155784 | tf_op jit(solution)/shard_map/ppermute | solution.py:569
  625.5 125.4 %collective-permute-start.30 = (bf16[2048,1024]{1,0:T(8,128)(2,1)}, bf16[2048,1024]{1,0:T(8,128)(2,1)}, u32[]{:S(2)}, u32[]{:S(2)}) collective-permute-start(bf16[2048,1024]{1,0:T(8,128)(2,1)} %get-tuple-element.63.q0), channel_id=1, source_target_pairs={{0,1},{1,0},{2,3},{3,2},{4,5},{5,4},{6,7},{7,6}} | collective-permute-start | bytes 12582920 | tf_op jit(solution)/shard_map/ppermute | solution.py:563
  625.8 116.4 %copy-start.9 = (bf16[2048,512]{1,0:T(8,128)(2,1)S(1)}, bf16[2048,512]{1,0:T(8,128)(2,1)}, u32[]{:S(2)}) copy-start(bf16[2048,512]{1,0:T(8,128)(2,1)} %get-tuple-element.64.k0) | copy-start | bytes 6291460
  742.1 1.2 collective-permute-start.28
  742.2 6.0 collective-permute-start.31
  742.7 6.9 collective-permute-start.32
  743.4 4.0 collective-permute-start.29
  748.2 1.4 copy-start.11
  749.5 1.3 copy-start.12
  (1 other events, 1.0 us)

commit v8 on v7

--- a/solution.py
+++ b/solution.py
@@ -119,7 +119,7 @@
 BK = 512
 
 
-def attn_bwd_kernel(q_ref, k_ref, v_ref, do_ref, ctx_ref, lse_ref, cos_ref, sin_ref, dq_ref, dk_ref, dv_ref,
+def attn_bwd_kernel(sc_ref, q_ref, k_ref, v_ref, do_ref, ctx_ref, lse_ref, cos_ref, sin_ref, dq_ref, dk_ref, dv_ref, pq_ref, pk_ref, pv_ref,
                     dqa_ref, dka_ref, dva_ref, dd_ref, kt_ref, *, k1, k2, scale):
     J = pl.program_id(1)
     nq = q_ref.shape[0] // BQ
@@ -184,34 +184,47 @@
     for g in range(2):
         dq_ref[:, g * HEAD:(g + 1) * HEAD] = unrope(dqa_ref[g, :, krow].T, cos_ref[krow, :], sin_ref[krow, :]).astype(BF16)
 
-
-def attn_bwd(qkv, kvh, nq, do, ctx, lse, cos, sin):
+    @pl.when(J == sc_ref[3])
+    def _():
+        pq_ref[...] = dq_ref[...]
+        pk_ref[...] = dk_ref[...]
+        pv_ref[...] = dv_ref[...]
+
+
+def attn_bwd(scal, qkv, kvh, nq, do, ctx, lse, cos, sin):
     T = qkv.shape[0]
     scale = HEAD ** -0.5
-    full2 = pl.BlockSpec((T, 2 * HEAD), lambda h, j: (0, h))
-    kblk = pl.BlockSpec((BK, HEAD), lambda h, j: (j, h))
-    tab = pl.BlockSpec((T, HEAD), lambda h, j: (0, 0))
+    full2 = pl.BlockSpec((T, 2 * HEAD), lambda h, j, s: (0, h))
+    kblk = pl.BlockSpec((BK, HEAD), lambda h, j, s: (j, h))
+    tab = pl.BlockSpec((T, HEAD), lambda h, j, s: (0, 0))
     return pl.pallas_call(
         functools.partial(attn_bwd_kernel, k1=scale / SOFT_CAP, k2=SOFT_CAP * LOG2E, scale=scale),
-        grid=(kvh, T // BK),
-        in_specs=[full2, pl.BlockSpec((BK, HEAD), lambda h, j: (j, nq + h)), pl.BlockSpec((BK, HEAD), lambda h, j: (j, nq + kvh + h)), full2, full2, pl.BlockSpec((1, 2, T), lambda h, j: (h, 0, 0)), tab, tab],
-        out_specs=[pl.BlockSpec((BK, 2 * HEAD), lambda h, j: (j, h)), kblk, kblk],
+        grid_spec=pltpu.PrefetchScalarGridSpec(
+            num_scalar_prefetch=1,
+            grid=(kvh, T // BK),
+            in_specs=[full2, pl.BlockSpec((BK, HEAD), lambda h, j, s: (j, nq + h)), pl.BlockSpec((BK, HEAD), lambda h, j, s: (j, nq + kvh + h)), full2, full2, pl.BlockSpec((1, 2, T), lambda h, j, s: (h, 0, 0)), tab, tab],
+            out_specs=[pl.BlockSpec((BK, 2 * HEAD), lambda h, j, s: (j, h)), kblk, kblk,
+                       pl.BlockSpec((BK, 2 * HEAD), lambda h, j, s: (0, h))] + [pl.BlockSpec((BK, HEAD), lambda h, j, s: (0, h))] * 2,
+            scratch_shapes=[
+                pltpu.VMEM((2, HEAD, T), F32),
+                pltpu.VMEM((BK, HEAD), F32),
+                pltpu.VMEM((BK, HEAD), F32),
+                pltpu.VMEM((2, 1, T), F32),
+                pltpu.VMEM((HEAD, BK), BF16),
+            ],
+        ),
         out_shape=[
             jax.ShapeDtypeStruct((T, nq * HEAD), BF16),
             jax.ShapeDtypeStruct((T, kvh * HEAD), BF16),
             jax.ShapeDtypeStruct((T, kvh * HEAD), BF16),
-        ],
-        scratch_shapes=[
-            pltpu.VMEM((2, HEAD, T), F32),
-            pltpu.VMEM((BK, HEAD), F32),
-            pltpu.VMEM((BK, HEAD), F32),
-            pltpu.VMEM((2, 1, T), F32),
-            pltpu.VMEM((HEAD, BK), BF16),
+            jax.ShapeDtypeStruct((BK, nq * HEAD), BF16),
+            jax.ShapeDtypeStruct((BK, kvh * HEAD), BF16),
+            jax.ShapeDtypeStruct((BK, kvh * HEAD), BF16),
         ],
         compiler_params=pltpu.CompilerParams(dimension_semantics=("arbitrary", "arbitrary")),
         cost_estimate=pl.CostEstimate(flops=int(5 * 2 * T * T * HEAD * kvh), bytes_accessed=3 * qkv.size * 2, transcendentals=0),
         name="attn_bwd",
-    )(qkv, qkv, qkv, do, ctx, lse, cos, sin)
+    )(scal, qkv, qkv, qkv, do, ctx, lse, cos, sin)
 
 
 VMEM_LIMIT = 64_000_000
@@ -536,22 +549,26 @@
     )(*args)
 
 
-def a_kernel(h_ref, g_ref, a_ref):
+def a_kernel(s_ref, h_ref, g_ref, a_ref):
     h = h_ref[...].astype(F32)
     inv = lax.rsqrt(jnp.mean(h * h, axis=-1, keepdims=True) + NORM_EPS)
     a_ref[...] = (h * inv * g_ref[...]).astype(BF16)
 
 
-def a_call(hidden, g):
-    M, D = hidden.shape
-    row = pl.BlockSpec((RB, D), lambda i: (i, 0))
-    return pl.pallas_call(
-        a_kernel, grid=(M // RB,), in_specs=[row, pl.BlockSpec((1, D), lambda i: (0, 0))], out_specs=row,
+def a_call(hidden, g, idx, M, rb):
+    D = hidden.shape[1]
+    return pl.pallas_call(
+        a_kernel,
+        grid_spec=pltpu.PrefetchScalarGridSpec(
+            num_scalar_prefetch=1,
+            grid=(M // rb,),
+            in_specs=[pl.BlockSpec((rb, D), lambda i, s: (s[0] * (M // rb) + i, 0)), pl.BlockSpec((1, D), lambda i, s: (0, 0))],
+            out_specs=pl.BlockSpec((rb, D), lambda i, s: (i, 0)),
+        ),
         out_shape=jax.ShapeDtypeStruct((M, D), BF16),
         compiler_params=pltpu.CompilerParams(dimension_semantics=("arbitrary",)),
         cost_estimate=pl.CostEstimate(flops=M * D * 1000, bytes_accessed=M * D * 4, transcendentals=0),
-        name="a_norm",
-    )(hidden, g.reshape(1, D))
+    )(jnp.reshape(idx, (1,)).astype(jnp.int32), hidden, g.reshape(1, D))
 
 
 def solution(mesh):
@@ -579,14 +596,15 @@
         cos, sin = lax.optimization_barrier(rope_tables(T))
         base = jnp.stack([xi, core, me, me ^ 1]).astype(jnp.int32)
 
-        def two_way(blk, n):
-            r1 = to_x(lax.dynamic_slice_in_dim(blk, tp * n, n, 0))
+        def two_way(first, blk, n):
+            r1 = to_x(first)
             r3 = to_x(blk[2 * n:])
             r2 = to_tp(r1)
             return [r1, r2, r3], [tp * n, (1 - tp) * n, 2 * n]
 
-        a_loc = a_call(hidden, g_pre)
-        a_x, a_off = two_way(a_loc, 160)
+        a_first = a_call(hidden, g_pre, tp, 160, 32)
+        a_loc = a_call(hidden, g_pre, jnp.int32(0), tokens, 64)
+        a_x, a_off = two_way(a_first, a_loc, 160)
         a_p = to_core(a_loc)
         a_xp = [to_core(r) for r in a_x]
         wo2 = w_o.reshape(-1, D)
@@ -634,8 +652,9 @@
 
         dwo_own = dwo_proj(ctx, go_all, 512)
         dwo_peer = to_core(dwo_own)
-        dqkv = attn_bwd(qkv, KL, HL, dctx, ctx, lse, cos, sin)
-        dqkv_pr = [to_core(lax.dynamic_slice_in_dim(g, (me ^ 1) * tokens, tokens, 0)) for g in dqkv]
+        grads = attn_bwd(base, qkv, KL, HL, dctx, ctx, lse, cos, sin)
+        dqkv = grads[:3]
+        dqkv_pr = [to_core(g) for g in grads[3:]]
         dqkv_p = [to_core(g) for g in dqkv]
         ga_part = ga_rows(base, dqkv, dqkv_pr, (w_own, w_oth), tokens, 512)
         ga_peer = to_tp(ga_part)

time: 864 us -> 866 us (level)
  no operation moved by 1% of the time
where the time goes in v8:
time: 866 us; the launch traced here: 857 us
  Pallas kernels  511 us (59%)
  waiting for transfers between devices  299 us (35%)
  starting transfers between devices  20.3 us (2%)
  local copies, waits for them, and re-layouts  16.9 us (2%)
    ppermute x6, waiting for transfers between devices, to_tp(): return lax.ppermute(v, 'tp', tp_perm)  156 us
    ppermute x7, waiting for transfers between devices, to_x(): return lax.ppermute(v, 'cp', x_perm)  141 us
    pallas_call x1, Pallas kernels, dw_proj(): pl.pallas_call(dw_kernel, grid_spec=pltpu.PrefetchScalarGridSpec(num_scal...  103 us
    pallas_call x5, Pallas kernels, gather_matmul(): pl.pallas_call(functools.partial(gmm_kernel, layout=layout, mode=mode, R=...  101 us
    pallas_call x1, Pallas kernels, attn_bwd(): pl.pallas_call(functools.partial(attn_bwd_kernel, k1=scale / SOFT_CAP, k2...  85.1 us
    pallas_call x3, Pallas kernels, w_layout(): pl.pallas_call(w_kernel, grid_spec=pltpu.PrefetchScalarGridSpec(num_scala...  41.9 us
    pallas_call x1, Pallas kernels, attn_fwd(): pl.pallas_call(functools.partial(attn_fwd_kernel, k1=scale / SOFT_CAP, k2...  41.4 us
    pallas_call x4, Pallas kernels, o_rows(): pl.pallas_call(functools.partial(orow_kernel, r0=r0), grid_spec=pltpu.Pre...  40.3 us
  transfers between devices with their start and end apart: 34, of which 13 were waited for; matrix products, arithmetic and copies ran while one was open for 2% of the time, Pallas kernels for 32%

profile of v8, /device:TPU:0, one launch (start us, length us, event | category | flops | bytes accessed | tf_op | source)
XLA Modules:
  0.0 856.6 jit_solution(6403828536280031048)
XLA Ops:
  2.0 7.8 shard_map.144.refs_0_
  10.6 4.4 shard_map.143
  15.1 2.5 collective-permute-start
  17.6 1.6 slice.12
  19.2 31.8 %collective-permute-done.refs_0_ = bf16[160,4608]{1,0:T(8,128)(2,1)} collective-permute-done((bf16[160,4608]{1,0:T(8,128)(2,1)}, bf16[160,4608]{1,0:T(8,128)(2,1)}, u32[]{:S(2)}, u32[]{:S(2)}) %collective-permute-start) | collective-permute-done | bytes 1474592 | tf_op jit(solution)/shard_map/ppermute | solution.py:583
  51.0 2.1 collective-permute-start.1
  53.1 3.7 fusion
  56.8 2.0 pad_maximum_fusion
  60.0 20.6 %shard_map.145.refs_2_.refs_6_.w0_ref = bf16[4608,2048]{1,0:T(8,128)(2,1)} custom-call(s32[1]{0:T(128)} %bitcast.1.c_ref, bf16[4608,16,128]{2,1,0:T(8,128)(2,1)} %wq_ref.5, bf16[4608,8,128]{2,1,0:T(8,128)(2,1)} %wk_ref.5, bf16[4608,8,128]{2,1,0:T(8,128)(2,1)} %wv_ref.5), custom_call_target="tpu_custom_call" | custom-call | flops 4718592000 | bytes 47185920 | tf_op jit(solution)/shard_map/pallas_call | solution.py:352
  80.6 8.2 collective-permute-done.2.refs_2_
  89.3 29.9 %shard_map.146 = (bf16[4,512,2048]{2,1,0:T(8,128)(2,1)}, bf16[4,512,4608]{2,1,0:T(8,128)(2,1)}) custom-call(s32[6]{0:T(128)} %stack.86.sc_ref, bf16[512,4608]{1,0:T(8,128)(2,1)} %shard_map.144.refs_0_, bf16[512,4608]{1,0:T(8,128)(2,1)} %collective-permute-done.6.refs_1_, bf16[4608,2048]{1,0:T(8,128)(2,1)} %shard_map.145.refs_2_.refs_6_.w0_ref, ...), custom_call_target="tpu_custom_call" | custom-call | flops 19327352832 | bytes 37748736 | tf_op jit(solution)/shard_map/pallas_call | solution.py:311
  120.4 29.9 %shard_map.147 = (bf16[4,512,2048]{2,1,0:T(8,128)(2,1)}, bf16[4,512,4608]{2,1,0:T(8,128)(2,1)}) custom-call(s32[10]{0:T(128)} %stack.85.sc_ref, bf16[160,4608]{1,0:T(8,128)(2,1)} %collective-permute-done.refs_0_, bf16[160,4608]{1,0:T(8,128)(2,1)} %collective-permute-done.1.refs_1_, ...), custom_call_target="tpu_custom_call", output_to_operand_aliasing={{0}: (10, {}), {1}: (11, {})} | custom-call | flops 19327352832 | bytes 37748736 | tf_op jit(solution)/shard_map/pallas_call | solution.py:311
  150.4 41.4 %attn_fwd.1 = (bf16[2048,1024]{1,0:T(8,128)(2,1)}, f32[4,2,2048]{2,1,0:T(2,128)}) custom-call(bf16[2048,2048]{1,0:T(8,128)(2,1)} %bitcast.40, bf16[2048,2048]{1,0:T(8,128)(2,1)} %bitcast.41, bf16[2048,2048]{1,0:T(8,128)(2,1)} %bitcast.42), custom_call_target="tpu_custom_call" | custom-call | flops 17179869184 | bytes 16777216 | tf_op jit(solution)/shard_map/attn_fwd/pallas_call | solution.py:91
  193.8 2.0 collective-permute-done.7.c1_ref
  196.7 10.1 %shard_map.149.p_ref = bf16[128,4608]{1,0:T(8,128)(2,1)} custom-call(s32[4]{0:T(128)} %pad_add_fusion.sc_ref, bf16[2048,1024]{1,0:T(8,128)(2,1)} %get-tuple-element.51.c0_ref.ctx_ref.c_ref, bf16[512,1024]{1,0:T(8,128)(2,1)} %copy-done, bf16[2048,4608]{1,0:T(8,128)(2,1)} %bitcast.22), custom_call_target="tpu_custom_call" | custom-call | flops 2415919104 | bytes 18874368 | tf_op jit(solution)/shard_map/pallas_call | solution.py:380
  206.8 1.8 collective-permute-start.9
  208.6 10.1 %shard_map.151.p_ref = bf16[128,4608]{1,0:T(8,128)(2,1)} custom-call(s32[4]{0:T(128)} %pad_add_fusion.sc_ref, bf16[2048,1024]{1,0:T(8,128)(2,1)} %get-tuple-element.51.c0_ref.ctx_ref.c_ref, bf16[512,1024]{1,0:T(8,128)(2,1)} %copy-done, bf16[2048,4608]{1,0:T(8,128)(2,1)} %bitcast.23), custom_call_target="tpu_custom_call" | custom-call | flops 2415919104 | bytes 18874368 | tf_op jit(solution)/shard_map/pallas_call | solution.py:380
  218.9 10.1 %shard_map.150.p_ref = bf16[128,4608]{1,0:T(8,128)(2,1)} custom-call(s32[4]{0:T(128)} %pad_add_fusion.sc_ref, bf16[2048,1024]{1,0:T(8,128)(2,1)} %get-tuple-element.51.c0_ref.ctx_ref.c_ref, bf16[512,1024]{1,0:T(8,128)(2,1)} %copy-done, bf16[2048,4608]{1,0:T(8,128)(2,1)} %bitcast.24), custom_call_target="tpu_custom_call" | custom-call | flops 2415919104 | bytes 18874368 | tf_op jit(solution)/shard_map/pallas_call | solution.py:380
  229.0 1.8 collective-permute-start.10
  230.8 10.1 %shard_map.148.p_ref = bf16[128,4608]{1,0:T(8,128)(2,1)} custom-call(s32[4]{0:T(128)} %pad_add_fusion.sc_ref, bf16[2048,1024]{1,0:T(8,128)(2,1)} %get-tuple-element.51.c0_ref.ctx_ref.c_ref, bf16[512,1024]{1,0:T(8,128)(2,1)} %copy-done, bf16[2048,4608]{1,0:T(8,128)(2,1)} %bitcast.25), custom_call_target="tpu_custom_call" | custom-call | flops 2415919104 | bytes 18874368 | tf_op jit(solution)/shard_map/pallas_call | solution.py:380
  241.7 19.5 %collective-permute-done.11.r_ref = bf16[128,4608]{1,0:T(8,128)(2,1)} collective-permute-done((bf16[128,4608]{1,0:T(8,128)(2,1)}, bf16[128,4608]{1,0:T(8,128)(2,1)}, u32[]{:S(2)}, u32[]{:S(2)}) %collective-permute-start.11) | collective-permute-done | bytes 1179680 | tf_op jit(solution)/shard_map/ppermute | solution.py:586
  261.2 4.9 shard_map.152
  266.2 20.3 %collective-permute-done.10.r_ref = bf16[128,4608]{1,0:T(8,128)(2,1)} collective-permute-done((bf16[128,4608]{1,0:T(8,128)(2,1)}, bf16[128,4608]{1,0:T(8,128)(2,1)}, u32[]{:S(2)}, u32[]{:S(2)}) %collective-permute-start.10) | collective-permute-done | bytes 1179680 | tf_op jit(solution)/shard_map/ppermute | solution.py:586
  286.5 5.0 shard_map.153
  292.6 5.0 shard_map.154
  297.5 13.3 %collective-permute-done.8.r_ref = bf16[128,4608]{1,0:T(8,128)(2,1)S(1)} collective-permute-done((bf16[128,4608]{1,0:T(8,128)(2,1)}, bf16[128,4608]{1,0:T(8,128)(2,1)S(1)}, u32[]{:S(2)}, u32[]{:S(2)}) %collective-permute-start.8) | collective-permute-done | bytes 1179680 | tf_op jit(solution)/shard_map/ppermute | solution.py:586
  311.9 5.0 shard_map.155
  316.9 1.8 collective-permute-start.13
  318.9 1.7 collective-permute-start.16
  320.9 25.0 %collective-permute-done.13.refs_2_ = bf16[128,4608]{1,0:T(8,128)(2,1)S(1)} collective-permute-done((bf16[128,4608]{1,0:T(8,128)(2,1)}, bf16[128,4608]{1,0:T(8,128)(2,1)S(1)}, u32[]{:S(2)}, u32[]{:S(2)}) %collective-permute-start.13) | collective-permute-done | bytes 1179680 | tf_op jit(solution)/shard_map/ppermute | solution.py:583
  346.5 24.8 %collective-permute-done.17.refs_2_ = bf16[128,4608]{1,0:T(8,128)(2,1)S(1)} collective-permute-done((bf16[128,4608]{1,0:T(8,128)(2,1)}, bf16[128,4608]{1,0:T(8,128)(2,1)S(1)}, u32[]{:S(2)}, u32[]{:S(2)}) %collective-permute-start.17) | collective-permute-done | bytes 1179680 | tf_op jit(solution)/shard_map/ppermute | solution.py:583
  371.2 25.4 %collective-permute-done.16.refs_1_ = bf16[128,4608]{1,0:T(8,128)(2,1)} collective-permute-done((bf16[128,4608]{1,0:T(8,128)(2,1)}, bf16[128,4608]{1,0:T(8,128)(2,1)}, u32[]{:S(2)}, u32[]{:S(2)}) %collective-permute-start.16) | collective-permute-done | bytes 1179680 | tf_op jit(solution)/shard_map/ppermute | solution.py:583
  396.6 23.6 %collective-permute-done.15.refs_0_ = bf16[128,4608]{1,0:T(8,128)(2,1)} collective-permute-done((bf16[128,4608]{1,0:T(8,128)(2,1)}, bf16[128,4608]{1,0:T(8,128)(2,1)}, u32[]{:S(2)}, u32[]{:S(2)}) %collective-permute-start.15) | collective-permute-done | bytes 1179680 | tf_op jit(solution)/shard_map/ppermute | solution.py:583
  422.6 14.9 %shard_map.156 = (bf16[4,512,1024]{2,1,0:T(8,128)(2,1)}, bf16[4,512,4608]{2,1,0:T(8,128)(2,1)}) custom-call(s32[10]{0:T(128)} %stack.91.sc_ref, bf16[128,4608]{1,0:T(8,128)(2,1)} %get-tuple-element.57.refs_0_, bf16[128,4608]{1,0:T(8,128)(2,1)} %get-tuple-element.58.refs_1_, bf16[128,4608]{1,0:T(8,128)(2,1)} %get-tuple-element.59.refs_2_, ...), custom_call_target="tpu_custom_call" | custom-call | flops 7247757312 | bytes 23592960 | tf_op jit(solution)/shard_map/pallas_call | solution.py:311
  437.5 14.7 %shard_map.157 = (bf16[4,512,1024]{2,1,0:T(8,128)(2,1)}, bf16[4,512,4608]{2,1,0:T(8,128)(2,1)}) custom-call(s32[10]{0:T(128)} %stack.90.sc_ref, bf16[128,4608]{1,0:T(8,128)(2,1)} %collective-permute-done.15.refs_0_, bf16[128,4608]{1,0:T(8,128)(2,1)} %collective-permute-done.16.refs_1_, ...), custom_call_target="tpu_custom_call", output_to_operand_aliasing={{0}: (8, {}), {1}: (9, {})} | custom-call | flops 7247757312 | bytes 23592960 | tf_op jit(solution)/shard_map/pallas_call | solution.py:311
  452.2 12.1 %shard_map.158 = (bf16[4,512,1024]{2,1,0:T(8,128)(2,1)}, bf16[4,512,4608]{2,1,0:T(8,128)(2,1)}) custom-call(s32[10]{0:T(128)} %stack.89.sc_ref, bf16[128,4608]{1,0:T(8,128)(2,1)} %get-tuple-element.56.refs_0_, bf16[128,4608]{1,0:T(8,128)(2,1)} %collective-permute-done.12.refs_1_, ...), custom_call_target="tpu_custom_call", output_to_operand_aliasing={{0}: (6, {}), {1}: (7, {})} | custom-call | flops 4831838208 | bytes 18874368 | tf_op jit(solution)/shard_map/pallas_call | solution.py:311
  464.3 26.5 %dwo_proj.1.h0_ref = f32[1024,4608]{1,0:T(8,128)} custom-call(bf16[2048,1024]{1,0:T(8,128)(2,1)} %get-tuple-element.51.c0_ref.ctx_ref.c_ref, bf16[2048,4608]{1,0:T(8,128)(2,1)} %bitcast.29), custom_call_target="tpu_custom_call" | custom-call | flops 19327352832 | bytes 18874368 | tf_op jit(solution)/shard_map/dwo_proj/pallas_call | solution.py:478
  491.3 85.1 %attn_bwd.1 = (bf16[2048,1024]{1,0:T(8,128)(2,1)}, bf16[2048,512]{1,0:T(8,128)(2,1)}, bf16[2048,512]{1,0:T(8,128)(2,1)}, bf16[512,1024]{1,0:T(8,128)(2,1)}, bf16...) custom-call(s32[4]{0:T(128)} %pad_add_fusion.sc_ref, bf16[2048,2048]{1,0:T(8,128)(2,1)} %bitcast.43, ...), custom_call_target="tpu_custom_call" | custom-call | flops 21474836480 | bytes 25165824 | tf_op jit(solution)/shard_map/attn_bwd/pallas_call | solution.py:200
  577.0 9.1 %shard_map.159.rest_0_ = bf16[4608,2048]{1,0:T(8,128)(2,1)} custom-call(s32[1]{0:T(128)} %bitcast.5.c_ref, bf16[4608,16,128]{2,1,0:T(8,128)(2,1)} %wq_ref.5, bf16[4608,8,128]{2,1,0:T(8,128)(2,1)} %wk_ref.5, bf16[4608,8,128]{2,1,0:T(8,128)(2,1)} %wv_ref.5), custom_call_target="tpu_custom_call" | custom-call | flops 2097152000 | bytes 20971520 | tf_op jit(solution)/shard_map/pallas_call | solution.py:352
  586.1 12.3 %shard_map.160.w1_ref = bf16[4608,2048]{1,0:T(8,128)(2,1)} custom-call(s32[1]{0:T(128)} %bitcast.5.c_ref, bf16[4608,16,128]{2,1,0:T(8,128)(2,1)} %wq_ref.5, bf16[4608,8,128]{2,1,0:T(8,128)(2,1)} %wk_ref.5, bf16[4608,8,128]{2,1,0:T(8,128)(2,1)} %wv_ref.5, bf16[4608,2048]{1,0:T(8,128)(2,1)} %shard_map.159.rest_0_), custom_call_target="tpu_custom_call", output_to_operand_aliasing={{}: (4, {})} | custom-call | flops 2621440000 | bytes 26214400 | tf_op jit(solution)/shard_map/pallas_call | solution.py:352
  599.7 26.7 %shard_map.161.p_ref = bf16[512,4608]{1,0:T(8,128)(2,1)} custom-call(s32[4]{0:T(128)} %pad_add_fusion.sc_ref, bf16[2048,1024]{1,0:T(8,128)(2,1)} %get-tuple-element.66.q0, bf16[2048,512]{1,0:T(8,128)(2,1)} %get-tuple-element.67.k0, bf16[2048,512]{1,0:T(8,128)(2,1)} %get-tuple-element.68.v0, bf16[512,1024]{1,0:T(8,128)(2,1)} %copy-done.15, ...), custom_call_target="tpu_custom_call" | custom-call | flops 19327352832 | bytes 37748736 | tf_op jit(solution)/shard_map/pallas_call | solution.py:412
  626.3 1.7 collective-permute-start.27
  628.2 102.5 %collective-permute-done.27.r_ref = bf16[512,4608]{1,0:T(8,128)(2,1)} collective-permute-done((bf16[512,4608]{1,0:T(8,128)(2,1)}, bf16[512,4608]{1,0:T(8,128)(2,1)}, u32[]{:S(2)}, u32[]{:S(2)}) %collective-permute-start.27) | collective-permute-done | bytes 4718624 | tf_op jit(solution)/shard_map/ppermute | solution.py:586
  730.7 12.9 %shard_map.162 = (bf16[512,4608]{1,0:T(8,128)(2,1)}, f32[8,4608]{1,0:T(8,128)}) custom-call(bf16[512,4608]{1,0:T(8,128)(2,1)} %shard_map.161.p_ref, bf16[512,4608]{1,0:T(8,128)(2,1)} %collective-permute-done.27.r_ref, bf16[512,4608]{1,0:T(8,128)(2,1)} %h_ref.13, bf16[512,4608]{1,0:T(8,128)(2,1)} %dy_ref.9, f32[1,4608]{1,0:T(1,128)} %reshape.79.g_ref), custom_call_target="tpu_custom_call" | custom-call | flops 4718592000 | bytes 28311552 | tf_op jit(solution)/shard_map/pallas_call | solution.py:545
  745.9 1.8 collective-permute-start.29
  747.7 2.2 collective-permute-done.29
  750.6 1.4 copy-done.11
  753.4 103.0 %dw_proj.1 = (f32[73728,128]{1,0:T(8,128)}, f32[36864,128]{1,0:T(8,128)}, f32[36864,128]{1,0:T(8,128)}, f32[2048,4608]{1,0:T(8,128)}) custom-call(s32[4]{0:T(128)} %pad_add_fusion.sc_ref, bf16[2048,4608]{1,0:T(8,128)(2,1)} %bitcast.39, bf16[2048,1024]{1,0:T(8,128)(2,1)} %get-tuple-element.66.q0, bf16[2048,1024]{1,0:T(8,128)(2,1)} %collective-permute-done.30.q1, ...), custom_call_target="tpu_custom_call" | custom-call | flops 77309411328 | bytes 75497472 | tf_op jit(solution)/shard_map/dw_proj/pallas_call | solution.py:448
  (103 shorter events, 21.7 us)
Async XLA Ops:
  9.8 79.5 %collective-permute-start.6 = (bf16[512,4608]{1,0:T(8,128)(2,1)}, bf16[512,4608]{1,0:T(8,128)(2,1)}, u32[]{:S(2)}, u32[]{:S(2)}) collective-permute-start(bf16[512,4608]{1,0:T(8,128)(2,1)} %shard_map.144.refs_0_), channel_id=1, source_target_pairs={{0,1},{1,0},{2,3},{3,2},{4,5},{5,4},{6,7},{7,6}} | collective-permute-start | bytes 14155784 | tf_op jit(solution)/shard_map/ppermute | solution.py:580
  15.1 35.9 %collective-permute-start = (bf16[160,4608]{1,0:T(8,128)(2,1)}, bf16[160,4608]{1,0:T(8,128)(2,1)}, u32[]{:S(2)}, u32[]{:S(2)}) collective-permute-start(bf16[160,4608]{1,0:T(8,128)(2,1)} %shard_map.143), channel_id=1, source_target_pairs={{0,2},{2,0},{1,3},{3,1},{4,6},{6,4},{5,7},{7,5}} | collective-permute-start | bytes 4423688 | tf_op jit(solution)/shard_map/ppermute | solution.py:583
  19.2 69.6 %collective-permute-start.2 = (bf16[192,4608]{1,0:T(8,128)(2,1)S(1)}, bf16[192,4608]{1,0:T(8,128)(2,1)}, u32[]{:S(2)}, u32[]{:S(2)}) collective-permute-start(bf16[192,4608]{1,0:T(8,128)(2,1)S(1)} %slice.12), channel_id=1, source_target_pairs={{0,2},{2,0},{1,3},{3,1},{4,6},{6,4},{5,7},{7,5}} | collective-permute-start | bytes 5308424 | tf_op jit(solution)/shard_map/ppermute | solution.py:583
  51.0 37.7 %collective-permute-start.1 = (bf16[160,4608]{1,0:T(8,128)(2,1)}, bf16[160,4608]{1,0:T(8,128)(2,1)}, u32[]{:S(2)}, u32[]{:S(2)}) collective-permute-start(bf16[160,4608]{1,0:T(8,128)(2,1)} %collective-permute-done.refs_0_), channel_id=1, source_target_pairs={{0,4},{4,0},{1,5},{5,1},{2,6},{6,2},{3,7},{7,3}} | collective-permute-start | bytes 4423688 | tf_op jit(solution)/shard_map/ppermute | solution.py:586
  80.6 38.6 %collective-permute-start.3 = (bf16[160,4608]{1,0:T(8,128)(2,1)}, bf16[160,4608]{1,0:T(8,128)(2,1)}, u32[]{:S(2)}, u32[]{:S(2)}) collective-permute-start(bf16[160,4608]{1,0:T(8,128)(2,1)} %collective-permute-done.refs_0_), channel_id=1, source_target_pairs={{0,1},{1,0},{2,3},{3,2},{4,5},{5,4},{6,7},{7,6}} | collective-permute-start | bytes 4423688 | tf_op jit(solution)/shard_map/ppermute | solution.py:580
  88.7 30.4 %collective-permute-start.5 = (bf16[192,4608]{1,0:T(8,128)(2,1)}, bf16[192,4608]{1,0:T(8,128)(2,1)S(1)}, u32[]{:S(2)}, u32[]{:S(2)}) collective-permute-start(bf16[192,4608]{1,0:T(8,128)(2,1)} %collective-permute-done.2.refs_2_), channel_id=1, source_target_pairs={{0,1},{1,0},{2,3},{3,2},{4,5},{5,4},{6,7},{7,6}} | collective-permute-start | bytes 5308424 | tf_op jit(solution)/shard_map/ppermute | solution.py:580
  88.8 30.5 %collective-permute-start.4 = (bf16[160,4608]{1,0:T(8,128)(2,1)}, bf16[160,4608]{1,0:T(8,128)(2,1)}, u32[]{:S(2)}, u32[]{:S(2)}) collective-permute-start(bf16[160,4608]{1,0:T(8,128)(2,1)} %collective-permute-done.1.refs_1_), channel_id=1, source_target_pairs={{0,1},{1,0},{2,3},{3,2},{4,5},{5,4},{6,7},{7,6}} | collective-permute-start | bytes 4423688 | tf_op jit(solution)/shard_map/ppermute | solution.py:580
  119.2 1.2 copy-start.13
  193.1 2.7 collective-permute-start.7
  206.8 84.7 %collective-permute-start.9 = (bf16[128,4608]{1,0:T(8,128)(2,1)}, bf16[128,4608]{1,0:T(8,128)(2,1)S(1)}, u32[]{:S(2)}, u32[]{:S(2)}) collective-permute-start(bf16[128,4608]{1,0:T(8,128)(2,1)} %shard_map.149.p_ref), channel_id=1, source_target_pairs={{0,4},{4,0},{1,5},{5,1},{2,6},{6,2},{3,7},{7,3}} | collective-permute-start | bytes 3538952 | tf_op jit(solution)/shard_map/ppermute | solution.py:586
  218.7 42.6 %collective-permute-start.11 = (bf16[128,4608]{1,0:T(8,128)(2,1)}, bf16[128,4608]{1,0:T(8,128)(2,1)}, u32[]{:S(2)}, u32[]{:S(2)}) collective-permute-start(bf16[128,4608]{1,0:T(8,128)(2,1)} %shard_map.151.p_ref), channel_id=1, source_target_pairs={{0,4},{4,0},{1,5},{5,1},{2,6},{6,2},{3,7},{7,3}} | collective-permute-start | bytes 3538952 | tf_op jit(solution)/shard_map/ppermute | solution.py:586
  229.0 12.1 %copy-start.9 = (f32[4608]{0:T(1024)S(1)}, f32[4608]{0:T(1024)}, u32[]{:S(2)}) copy-start(f32[4608]{0:T(1024)} %param.14) | copy-start | bytes 55300
  229.0 57.5 %collective-permute-start.10 = (bf16[128,4608]{1,0:T(8,128)(2,1)}, bf16[128,4608]{1,0:T(8,128)(2,1)}, u32[]{:S(2)}, u32[]{:S(2)}) collective-permute-start(bf16[128,4608]{1,0:T(8,128)(2,1)} %shard_map.150.p_ref), channel_id=1, source_target_pairs={{0,4},{4,0},{1,5},{5,1},{2,6},{6,2},{3,7},{7,3}} | collective-permute-start | bytes 3538952 | tf_op jit(solution)/shard_map/ppermute | solution.py:586
  240.9 70.0 %collective-permute-start.8 = (bf16[128,4608]{1,0:T(8,128)(2,1)}, bf16[128,4608]{1,0:T(8,128)(2,1)S(1)}, u32[]{:S(2)}, u32[]{:S(2)}) collective-permute-start(bf16[128,4608]{1,0:T(8,128)(2,1)} %shard_map.148.p_ref), channel_id=1, source_target_pairs={{0,4},{4,0},{1,5},{5,1},{2,6},{6,2},{3,7},{7,3}} | collective-permute-start | bytes 3538952 | tf_op jit(solution)/shard_map/ppermute | solution.py:586
  291.5 1.1 copy-start.3
  316.9 29.1 %collective-permute-start.13 = (bf16[128,4608]{1,0:T(8,128)(2,1)}, bf16[128,4608]{1,0:T(8,128)(2,1)S(1)}, u32[]{:S(2)}, u32[]{:S(2)}) collective-permute-start(bf16[128,4608]{1,0:T(8,128)(2,1)} %get-tuple-element.56.refs_0_), channel_id=1, source_target_pairs={{0,2},{2,0},{1,3},{3,1},{4,6},{6,4},{5,7},{7,5}} | collective-permute-start | bytes 3538952 | tf_op jit(solution)/shard_map/ppermute | solution.py:583
  318.6 27.3 %collective-permute-start.23 = (bf16[128,4608]{1,0:T(8,128)(2,1)}, bf16[128,4608]{1,0:T(8,128)(2,1)S(1)}, u32[]{:S(2)}, u32[]{:S(2)}) collective-permute-start(bf16[128,4608]{1,0:T(8,128)(2,1)} %get-tuple-element.59.refs_2_), channel_id=1, source_target_pairs={{0,1},{1,0},{2,3},{3,2},{4,5},{5,4},{6,7},{7,6}} | collective-permute-start | bytes 3538952 | tf_op jit(solution)/shard_map/ppermute | solution.py:580
  318.6 52.6 %collective-permute-start.17 = (bf16[128,4608]{1,0:T(8,128)(2,1)}, bf16[128,4608]{1,0:T(8,128)(2,1)S(1)}, u32[]{:S(2)}, u32[]{:S(2)}) collective-permute-start(bf16[128,4608]{1,0:T(8,128)(2,1)} %get-tuple-element.59.refs_2_), channel_id=1, source_target_pairs={{0,2},{2,0},{1,3},{3,1},{4,6},{6,4},{5,7},{7,5}} | collective-permute-start | bytes 3538952 | tf_op jit(solution)/shard_map/ppermute | solution.py:583
  318.9 77.7 %collective-permute-start.16 = (bf16[128,4608]{1,0:T(8,128)(2,1)}, bf16[128,4608]{1,0:T(8,128)(2,1)}, u32[]{:S(2)}, u32[]{:S(2)}) collective-permute-start(bf16[128,4608]{1,0:T(8,128)(2,1)} %get-tuple-element.58.refs_1_), channel_id=1, source_target_pairs={{0,2},{2,0},{1,3},{3,1},{4,6},{6,4},{5,7},{7,5}} | collective-permute-start | bytes 3538952 | tf_op jit(solution)/shard_map/ppermute | solution.py:583
  320.6 99.6 %collective-permute-start.15 = (bf16[128,4608]{1,0:T(8,128)(2,1)}, bf16[128,4608]{1,0:T(8,128)(2,1)}, u32[]{:S(2)}, u32[]{:S(2)}) collective-permute-start(bf16[128,4608]{1,0:T(8,128)(2,1)} %get-tuple-element.57.refs_0_), channel_id=1, source_target_pairs={{0,2},{2,0},{1,3},{3,1},{4,6},{6,4},{5,7},{7,5}} | collective-permute-start | bytes 3538952 | tf_op jit(solution)/shard_map/ppermute | solution.py:583
  345.9 91.5 %copy-start.1 = (bf16[128,4608]{1,0:T(8,128)(2,1)}, bf16[128,4608]{1,0:T(8,128)(2,1)S(1)}, u32[]{:S(2)}) copy-start(bf16[128,4608]{1,0:T(8,128)(2,1)S(1)} %collective-permute-done.13.refs_2_) | copy-start | bytes 3538948
  345.9 76.1 %collective-permute-start.22 = (bf16[128,4608]{1,0:T(8,128)(2,1)}, bf16[128,4608]{1,0:T(8,128)(2,1)}, u32[]{:S(2)}, u32[]{:S(2)}) collective-permute-start(bf16[128,4608]{1,0:T(8,128)(2,1)} %get-tuple-element.58.refs_1_), channel_id=1, source_target_pairs={{0,1},{1,0},{2,3},{3,2},{4,5},{5,4},{6,7},{7,6}} | collective-permute-start | bytes 3538952 | tf_op jit(solution)/shard_map/ppermute | solution.py:580
  345.9 25.3 %copy-start.14 = (bf16[128,4608]{1,0:T(8,128)(2,1)}, bf16[128,4608]{1,0:T(8,128)(2,1)S(1)}, u32[]{:S(2)}) copy-start(bf16[128,4608]{1,0:T(8,128)(2,1)S(1)} %collective-permute-done.23.refs_5_) | copy-start | bytes 3538948
  346.0 76.6 %collective-permute-start.21 = (bf16[128,4608]{1,0:T(8,128)(2,1)}, bf16[128,4608]{1,0:T(8,128)(2,1)}, u32[]{:S(2)}, u32[]{:S(2)}) collective-permute-start(bf16[128,4608]{1,0:T(8,128)(2,1)} %get-tuple-element.57.refs_0_), channel_id=1, source_target_pairs={{0,1},{1,0},{2,3},{3,2},{4,5},{5,4},{6,7},{7,6}} | collective-permute-start | bytes 3538952 | tf_op jit(solution)/shard_map/ppermute | solution.py:580
  371.2 66.3 %copy-start.2 = (bf16[128,4608]{1,0:T(8,128)(2,1)}, bf16[128,4608]{1,0:T(8,128)(2,1)S(1)}, u32[]{:S(2)}) copy-start(bf16[128,4608]{1,0:T(8,128)(2,1)S(1)} %collective-permute-done.17.refs_2_) | copy-start | bytes 3538948
  371.2 66.3 %collective-permute-start.20 = (bf16[128,4608]{1,0:T(8,128)(2,1)S(1)}, bf16[128,4608]{1,0:T(8,128)(2,1)}, u32[]{:S(2)}, u32[]{:S(2)}) collective-permute-start(bf16[128,4608]{1,0:T(8,128)(2,1)S(1)} %collective-permute-done.17.refs_2_), channel_id=1, source_target_pairs={{0,1},{1,0},{2,3},{3,2},{4,5},{5,4},{6,7},{7,6}} | collective-permute-start | bytes 3538952 | tf_op jit(solution)/shard_map/ppermute | solution.py:580
  396.6 40.9 %collective-permute-start.19 = (bf16[128,4608]{1,0:T(8,128)(2,1)}, bf16[128,4608]{1,0:T(8,128)(2,1)}, u32[]{:S(2)}, u32[]{:S(2)}) collective-permute-start(bf16[128,4608]{1,0:T(8,128)(2,1)} %collective-permute-done.16.refs_1_), channel_id=1, source_target_pairs={{0,1},{1,0},{2,3},{3,2},{4,5},{5,4},{6,7},{7,6}} | collective-permute-start | bytes 3538952 | tf_op jit(solution)/shard_map/ppermute | solution.py:580
  420.2 17.3 %collective-permute-start.18 = (bf16[128,4608]{1,0:T(8,128)(2,1)}, bf16[128,4608]{1,0:T(8,128)(2,1)}, u32[]{:S(2)}, u32[]{:S(2)}) collective-permute-start(bf16[128,4608]{1,0:T(8,128)(2,1)} %collective-permute-done.15.refs_0_), channel_id=1, source_target_pairs={{0,1},{1,0},{2,3},{3,2},{4,5},{5,4},{6,7},{7,6}} | collective-permute-start | bytes 3538952 | tf_op jit(solution)/shard_map/ppermute | solution.py:580
  422.1 30.1 %collective-permute-start.12 = (bf16[128,4608]{1,0:T(8,128)(2,1)}, bf16[128,4608]{1,0:T(8,128)(2,1)}, u32[]{:S(2)}, u32[]{:S(2)}) collective-permute-start(bf16[128,4608]{1,0:T(8,128)(2,1)} %get-tuple-element.56.refs_0_), channel_id=1, source_target_pairs={{0,1},{1,0},{2,3},{3,2},{4,5},{5,4},{6,7},{7,6}} | collective-permute-start | bytes 3538952 | tf_op jit(solution)/shard_map/ppermute | solution.py:580
  422.6 29.6 %collective-permute-start.14 = (bf16[128,4608]{1,0:T(8,128)(2,1)S(1)}, bf16[128,4608]{1,0:T(8,128)(2,1)}, u32[]{:S(2)}, u32[]{:S(2)}) collective-permute-start(bf16[128,4608]{1,0:T(8,128)(2,1)S(1)} %collective-permute-done.13.refs_2_), channel_id=1, source_target_pairs={{0,1},{1,0},{2,3},{3,2},{4,5},{5,4},{6,7},{7,6}} | collective-permute-start | bytes 3538952 | tf_op jit(solution)/shard_map/ppermute | solution.py:580
  490.9 262.5 %collective-permute-start.33 = (f32[1024,4608]{1,0:T(8,128)}, f32[1024,4608]{1,0:T(8,128)}, u32[]{:S(2)}, u32[]{:S(2)}) collective-permute-start(f32[1024,4608]{1,0:T(8,128)} %dwo_proj.1.h0_ref), channel_id=1, source_target_pairs={{0,1},{1,0},{2,3},{3,2},{4,5},{5,4},{6,7},{7,6}} | collective-permute-start | bytes 56623112 | tf_op jit(solution)/shard_map/ppermute | solution.py:580
  576.4 21.9 %collective-permute-start.24 = (bf16[512,1024]{1,0:T(8,128)(2,1)}, bf16[512,1024]{1,0:T(8,128)(2,1)S(1)}, u32[]{:S(2)}, u32[]{:S(2)}) collective-permute-start(bf16[512,1024]{1,0:T(8,128)(2,1)} %get-tuple-element.69), channel_id=1, source_target_pairs={{0,1},{1,0},{2,3},{3,2},{4,5},{5,4},{6,7},{7,6}} | collective-permute-start | bytes 3145736 | tf_op jit(solution)/shard_map/ppermute | solution.py:580
  576.5 21.9 %collective-permute-start.25 = (bf16[512,512]{1,0:T(8,128)(2,1)}, bf16[512,512]{1,0:T(8,128)(2,1)S(1)}, u32[]{:S(2)}, u32[]{:S(2)}) collective-permute-start(bf16[512,512]{1,0:T(8,128)(2,1)} %get-tuple-element.70), channel_id=1, source_target_pairs={{0,1},{1,0},{2,3},{3,2},{4,5},{5,4},{6,7},{7,6}} | collective-permute-start | bytes 1572872 | tf_op jit(solution)/shard_map/ppermute | solution.py:580
  576.9 21.4 %collective-permute-start.26 = (bf16[512,512]{1,0:T(8,128)(2,1)}, bf16[512,512]{1,0:T(8,128)(2,1)S(1)}, u32[]{:S(2)}, u32[]{:S(2)}) collective-permute-start(bf16[512,512]{1,0:T(8,128)(2,1)} %get-tuple-element.71), channel_id=1, source_target_pairs={{0,1},{1,0},{2,3},{3,2},{4,5},{5,4},{6,7},{7,6}} | collective-permute-start | bytes 1572872 | tf_op jit(solution)/shard_map/ppermute | solution.py:580
  598.4 1.3 copy-start.15
  599.7 28.5 %copy-start.5 = (f32[8,4608]{1,0:T(8,128)S(1)}, f32[8,4608]{1,0:T(8,128)}, u32[]{:S(2)}) copy-start(f32[8,4608]{1,0:T(8,128)} %get-tuple-element.74) | copy-start | bytes 442372
  599.7 28.5 %copy-start.6 = (f32[8,4608]{1,0:T(8,128)S(1)}, f32[8,4608]{1,0:T(8,128)}, u32[]{:S(2)}) copy-start(f32[8,4608]{1,0:T(8,128)} %get-tuple-element.75) | copy-start | bytes 442372
  599.7 28.5 %copy-start.7 = (f32[8,4608]{1,0:T(8,128)S(1)}, f32[8,4608]{1,0:T(8,128)}, u32[]{:S(2)}) copy-start(f32[8,4608]{1,0:T(8,128)} %get-tuple-element.76) | copy-start | bytes 442372
  599.7 28.5 %copy-start.8 = (f32[8,4608]{1,0:T(8,128)S(1)}, f32[8,4608]{1,0:T(8,128)}, u32[]{:S(2)}) copy-start(f32[8,4608]{1,0:T(8,128)} %get-tuple-element.77) | copy-start | bytes 442372
  626.3 104.4 %collective-permute-start.27 = (bf16[512,4608]{1,0:T(8,128)(2,1)}, bf16[512,4608]{1,0:T(8,128)(2,1)}, u32[]{:S(2)}, u32[]{:S(2)}) collective-permute-start(bf16[512,4608]{1,0:T(8,128)(2,1)} %shard_map.161.p_ref), channel_id=1, source_target_pairs={{0,4},{4,0},{1,5},{5,1},{2,6},{6,2},{3,7},{7,3}} | collective-permute-start | bytes 14155784 | tf_op jit(solution)/shard_map/ppermute | solution.py:586
  628.0 125.3 %collective-permute-start.30 = (bf16[2048,1024]{1,0:T(8,128)(2,1)}, bf16[2048,1024]{1,0:T(8,128)(2,1)}, u32[]{:S(2)}, u32[]{:S(2)}) collective-permute-start(bf16[2048,1024]{1,0:T(8,128)(2,1)} %get-tuple-element.66.q0), channel_id=1, source_target_pairs={{0,1},{1,0},{2,3},{3,2},{4,5},{5,4},{6,7},{7,6}} | collective-permute-start | bytes 12582920 | tf_op jit(solution)/shard_map/ppermute | solution.py:580
  628.2 116.4 %copy-start.10 = (bf16[2048,512]{1,0:T(8,128)(2,1)S(1)}, bf16[2048,512]{1,0:T(8,128)(2,1)}, u32[]{:S(2)}) copy-start(bf16[2048,512]{1,0:T(8,128)(2,1)} %get-tuple-element.67.k0) | copy-start | bytes 6291460
  744.6 1.2 collective-permute-start.28
  744.7 6.0 collective-permute-start.31
  745.1 6.9 collective-permute-start.32
  745.9 4.0 collective-permute-start.29
  750.6 1.4 copy-start.11
  752.0 1.4 copy-start.12
  (4 other events, 3.7 us)
